TPU v7x, 8 devices: a whole 2x2x1 slice. The times are simulated.
8 devices in a mesh: dp: 1 (over z), tp: 2 (over y), ep: 4 (over x, core).
Axes of the slice: x: 2, y: 2, z: 1, core: 2. Of those that a mesh axis runs over, the one named last changes fastest.
Arguments:
- tokens_a: bfloat16 [16384, 2048], P(('dp', 'ep', 'tp'))
- expert_ids_a: int32 [16384, 2], P(('dp', 'ep', 'tp'))
- gates_a: float32 [16384, 2], P(('dp', 'ep', 'tp'))
- tokens_b: bfloat16 [16384, 2048], P(('dp', 'ep', 'tp'))
- expert_ids_b: int32 [16384, 2], P(('dp', 'ep', 'tp'))
- gates_b: float32 [16384, 2], P(('dp', 'ep', 'tp'))
- w_gate: bfloat16 [8, 2048, 5632], P('ep', None, 'tp')
- w_up: bfloat16 [8, 2048, 5632], P('ep', None, 'tp')
- w_down: bfloat16 [8, 5632, 2048], P('ep', 'tp')
Outputs:
- output 1: bfloat16 [16384, 2048], P(('dp', 'ep', 'tp'))
- output 2: bfloat16 [16384, 2048], P(('dp', 'ep', 'tp'))
All inputs are finite; a program needn't handle non-finite values.
Results may differ from a plain program's by a relative error of at most 0.00149.
Values are sent between devices in bfloat16 or wider.
A program may use at most 1 GiB of HBM per device.

v0:
```python
import jax
import jax.numpy as jnp
from jax import lax
from jax.sharding import PartitionSpec as P


def solution(mesh):
    ep_size = mesh.shape["ep"]
    row_spec = P(("dp", "ep", "tp"), None)
    gate_spec = P("ep", None, "tp")
    down_spec = P("ep", "tp", None)

    def moe_local(tokens, expert_ids, gate_vals, w_gate, w_up, w_down):
        tok_loc, model_dim = tokens.shape
        top_k = expert_ids.shape[1]
        num_experts = w_gate.shape[0] * ep_size
        mean_load = top_k * tok_loc // num_experts
        capacity = mean_load + mean_load // 4
        flat_ids = expert_ids.reshape(tok_loc * top_k)
        onehot = (flat_ids[:, None] == jnp.arange(num_experts, dtype=jnp.int32)[None, :]).astype(jnp.int32)
        position = jnp.sum(jnp.cumsum(onehot, axis=0) * onehot, axis=1) - 1
        slot_ids = jnp.where(position < capacity, flat_ids * capacity + position, num_experts * capacity)
        copy_tok = jnp.arange(tok_loc * top_k, dtype=jnp.int32) // top_k
        source = jnp.full((num_experts * capacity,), tok_loc, jnp.int32).at[slot_ids].set(copy_tok, mode="drop")
        slot_rows = jnp.take(tokens, source, axis=0, mode="fill", fill_value=0).reshape(num_experts, capacity, model_dim)
        received = lax.all_to_all(slot_rows, "ep", 0, 1, tiled=True)
        gathered = lax.all_gather(received, "tp", axis=1, tiled=True)
        gate_act = jnp.einsum("erd,edf->erf", gathered, w_gate, preferred_element_type=jnp.float32)
        up_lin = jnp.einsum("erd,edf->erf", gathered, w_up, preferred_element_type=jnp.float32)
        hidden = (jax.nn.silu(gate_act) * up_lin).astype(jnp.bfloat16)
        partial_out = jnp.einsum("erf,efd->erd", hidden, w_down, preferred_element_type=jnp.float32)
        summed = lax.psum_scatter(partial_out, "tp", scatter_dimension=1, tiled=True)
        returned = lax.all_to_all(summed.astype(jnp.bfloat16), "ep", 1, 0, tiled=True)
        copies = jnp.take(returned.reshape(num_experts * capacity, model_dim), slot_ids, axis=0, mode="fill", fill_value=0)
        weighted = copies.reshape(tok_loc, top_k, model_dim).astype(jnp.float32) * gate_vals[:, :, None]
        return jnp.sum(weighted, axis=1).astype(jnp.bfloat16)

    def group_body(tokens_a, expert_ids_a, gates_a, tokens_b, expert_ids_b, gates_b, w_gate, w_up, w_down):
        out_a = moe_local(tokens_a, expert_ids_a, gates_a, w_gate, w_up, w_down)
        out_b = moe_local(tokens_b, expert_ids_b, gates_b, w_gate, w_up, w_down)
        return (out_a, out_b)

    in_specs = (row_spec, row_spec, row_spec, row_spec, row_spec, row_spec, gate_spec, gate_spec, down_spec)
    return jax.shard_map(group_body, mesh=mesh, in_specs=in_specs, out_specs=(row_spec, row_spec), check_vma=False)
```

profile of v0, /device:TPU:0, one launch (start us, length us, event | category | flops | bytes accessed | tf_op | source)
XLA Modules:
  0.0 3657.5 jit_solution(13170971734961614216)
XLA Ops:
  7.2 1.1 copy.27
  8.3 0.5 eq.54
  8.8 0.5 eq.50
  9.2 0.7 broadcast_multiply_fusion.1
  10.0 2.3 reduce-window.14
  12.3 0.3 slice_reduce_fusion.1
  12.6 0.2 reduce-window.15
  12.8 0.1 add_bitcast_fusion.1
  12.9 0.1 fusion.5
  13.1 0.6 copy-done.6
  13.6 0.6 broadcast_clamp_fusion.1
  14.2 0.4 copy.29
  14.6 0.6 mul.67
  15.3 15.5 scatter_custom_fusion
  30.9 43.3 %gather_fusion = bf16[5120,2048]{1,0:T(8,128)(2,1)} fusion(bf16[2048,2048]{1,0:T(8,128)(2,1)} %param.13, s32[5120]{0:T(1024)S(1)} %fusion.8), kind=kCustom, calls=%fused_computation.clone | custom fusion | bytes 41963520 | tf_op jit(solution)/shard_map/jit(_take)/gather | solution.py:25
  74.2 11.1 broadcast_select_fusion.1
  85.3 232.3 %all_to_all.66 = bf16[8,640,2048]{2,1,0:T(8,128)(2,1)S(1)} all-to-all(bf16[8,640,2048]{2,1,0:T(8,128)(2,1)S(1)} %bitcast.67), channel_id=1, replica_groups=mesh['dp'=1,'tp'=2,'ep'=4] {'ep'}, dimensions={0} | all-to-all | bytes 41943040 | tf_op jit(solution)/shard_map/all_to_all | solution.py:26
  317.7 7.2 copy.30
  324.9 0.0 all-gather.5.cloned.1.call-start
  325.0 0.4 copy.34
  325.3 0.5 eq.62
  325.8 0.5 eq.58
  326.3 2.3 reduce-window.16
  328.6 0.3 slice_reduce_fusion
  328.9 0.2 reduce-window.19
  329.1 0.4 copy.36
  329.5 0.6 mul.75
  330.1 0.1 add_bitcast_fusion
  330.2 0.1 fusion.3
  330.4 0.6 broadcast_clamp_fusion
  331.0 16.0 scatter_custom_fusion.1
  347.1 43.3 %gather_fusion.2 = bf16[5120,2048]{1,0:T(8,128)(2,1)} fusion(bf16[2048,2048]{1,0:T(8,128)(2,1)} %param.16, s32[5120]{0:T(1024)S(1)} %fusion.9), kind=kCustom, calls=%fused_computation.2.clone | custom fusion | bytes 41963520 | tf_op jit(solution)/shard_map/jit(_take)/gather | solution.py:25
  390.4 11.2 broadcast_select_fusion
  401.6 231.2 %all_to_all.67 = bf16[8,640,2048]{2,1,0:T(8,128)(2,1)S(1)} all-to-all(bf16[8,640,2048]{2,1,0:T(8,128)(2,1)S(1)} %bitcast.68), channel_id=1, replica_groups=mesh['dp'=1,'tp'=2,'ep'=4] {'ep'}, dimensions={0} | all-to-all | bytes 41943040 | tf_op jit(solution)/shard_map/all_to_all | solution.py:26
  632.8 7.2 copy.37
  640.0 0.0 reduce-scatter.3.cloned.1.call-start
  640.0 167.1 %all-gather.3.cloned.1.call-done = bf16[2,5120,2048]{2,1,0:T(8,128)(2,1)} async-done(((bf16[2,2560,2048]{2,1,0:T(8,128)(2,1)}), bf16[2,5120,2048]{2,1,0:T(8,128)(2,1)}) %all-gather.3.cloned.1.call-update) | async-done | bytes 41943056 | tf_op jit(solution)/shard_map/all_gather | solution.py:27
  807.2 130.4 %fusion.19 = f32[2,5120,2816]{2,1,0:T(8,128)} fusion(bf16[2,5120,2048]{2,1,0:T(8,128)(2,1)} %all-gather.3.cloned.1.call-done, bf16[2,2048,2816]{2,1,0:T(8,128)(2,1)} %param.19), kind=kOutput, calls=%fused_computation.65 | convolution fusion | flops 118111600640 | bytes 180355072 | tf_op jit(solution)/shard_map/erd,edf->erf/dot_general | solution.py:28
  937.6 130.7 %fusion.20 = f32[2,5120,2816]{2,1,0:T(8,128)} fusion(bf16[2,5120,2048]{2,1,0:T(8,128)(2,1)} %all-gather.3.cloned.1.call-done, bf16[2,2048,2816]{2,1,0:T(8,128)(2,1)} %param.20), kind=kOutput, calls=%fused_computation.66 | convolution fusion | flops 118111600640 | bytes 180355072 | tf_op jit(solution)/shard_map/erd,edf->erf/dot_general | solution.py:29
  1068.2 138.1 %fusion = f32[2,5120,2048]{2,1,0:T(8,128)} fusion(bf16[2,2816,2048]{2,1,0:T(8,128)(2,1)} %param.21, f32[2,5120,2816]{2,1,0:T(8,128)} %fusion.20, f32[2,5120,2816]{2,1,0:T(8,128)} %fusion.19), kind=kOutput, calls=%fused_computation.8 | convolution fusion | flops 118284615680 | bytes 337641472 | tf_op jit(solution)/shard_map/erf,efd->erd/dot_general | solution.py:31
  1206.4 83.7 %all-gather.5.cloned.1.call-done = bf16[2,5120,2048]{2,1,0:T(8,128)(2,1)} async-done(((bf16[2,2560,2048]{2,1,0:T(8,128)(2,1)}), bf16[2,5120,2048]{2,1,0:T(8,128)(2,1)}) %all-gather.5.cloned.1.call-update) | async-done | bytes 41943056 | tf_op jit(solution)/shard_map/all_gather | solution.py:27
  1290.1 130.4 %fusion.21 = f32[2,5120,2816]{2,1,0:T(8,128)} fusion(bf16[2,5120,2048]{2,1,0:T(8,128)(2,1)} %all-gather.5.cloned.1.call-done, bf16[2,2048,2816]{2,1,0:T(8,128)(2,1)} %param.19), kind=kOutput, calls=%fused_computation.67 | convolution fusion | flops 118111600640 | bytes 180355072 | tf_op jit(solution)/shard_map/erd,edf->erf/dot_general | solution.py:28
  1420.5 130.9 %fusion.22 = f32[2,5120,2816]{2,1,0:T(8,128)} fusion(bf16[2,5120,2048]{2,1,0:T(8,128)(2,1)} %all-gather.5.cloned.1.call-done, bf16[2,2048,2816]{2,1,0:T(8,128)(2,1)} %param.20), kind=kOutput, calls=%fused_computation.68 | convolution fusion | flops 118111600640 | bytes 180355072 | tf_op jit(solution)/shard_map/erd,edf->erf/dot_general | solution.py:29
  1551.4 138.1 %fusion.1 = f32[2,5120,2048]{2,1,0:T(8,128)} fusion(bf16[2,2816,2048]{2,1,0:T(8,128)(2,1)} %param.21, f32[2,5120,2816]{2,1,0:T(8,128)} %fusion.22, f32[2,5120,2816]{2,1,0:T(8,128)} %fusion.21), kind=kOutput, calls=%fused_computation.9 | convolution fusion | flops 118284615680 | bytes 337641472 | tf_op jit(solution)/shard_map/erf,efd->erd/dot_general | solution.py:31
  1689.5 508.4 %reduce-scatter.3.cloned.1.call-done = f32[2,2560,2048]{2,1,0:T(8,128)} async-done(((f32[2,5120,2048]{2,1,0:T(8,128)}), f32[2,2560,2048]{2,1,0:T(8,128)}) %reduce-scatter.3.cloned.1.call-update) | async-done | bytes 41943056 | tf_op jit(solution)/shard_map/reduce_scatter | solution.py:32
  2197.9 14.8 convert_element_type.42
  2212.7 60.9 %copy.31 = bf16[2,2560,2048]{2,0,1:T(2,128)(2,1)} copy(bf16[2,2560,2048]{2,1,0:T(8,128)(2,1)S(1)} %convert_element_type.42) | data formatting | bytes 41943040 | tf_op jit(solution)/shard_map/convert_element_type | solution.py:33
  2273.6 7.8 all-to-all-start.1
  2281.3 824.3 %reduce-scatter.5.cloned.1.call-done = f32[2,2560,2048]{2,1,0:T(8,128)} async-done(((f32[2,5120,2048]{2,1,0:T(8,128)}), f32[2,2560,2048]{2,1,0:T(8,128)}) %reduce-scatter.5.cloned.1.call-update) | async-done | bytes 41943056 | tf_op jit(solution)/shard_map/reduce_scatter | solution.py:32
  3105.6 14.8 convert_element_type.48
  3120.4 60.9 %copy.38 = bf16[2,2560,2048]{2,0,1:T(2,128)(2,1)} copy(bf16[2,2560,2048]{2,1,0:T(8,128)(2,1)S(1)} %convert_element_type.48) | data formatting | bytes 41943040 | tf_op jit(solution)/shard_map/convert_element_type | solution.py:33
  3181.3 8.1 all-to-all-start.3
  3189.4 1.3 copy.33
  3190.8 1.3 copy.40
  3192.2 21.4 copy.32
  3213.6 41.0 %gather_fusion.1 = bf16[4096,2048]{1,0:T(8,128)(2,1)} fusion(bf16[5120,2048]{1,0:T(8,128)(2,1)} %bitcast.63, s32[4096]{0:T(1024)S(1)} %copy-done.11), kind=kCustom, calls=%fused_computation.1.clone | custom fusion | bytes 33570816 | tf_op jit(solution)/shard_map/jit(_take)/gather | solution.py:34
  3254.6 18.7 select_convert_fusion.1
  3273.2 39.0 %reshape.156 = f32[2048,2,2048]{2,1,0:T(2,128)} reshape(f32[4096,2048]{1,0:T(8,128)} %select_convert_fusion.1) | data formatting | bytes 67108864 | tf_op jit(solution)/shard_map/convert_element_type | solution.py:35
  3312.2 104.8 %all-to-all-done.3 = bf16[2,2560,2048]{2,0,1:T(2,128)(2,1)} async-done(((bf16[2,2560,2048]{2,0,1:T(2,128)(2,1)}), bf16[2,2560,2048]{2,0,1:T(2,128)(2,1)}, u32[]{:S(2)}, u32[]{:S(2)}) %all-to-all-start.3) | async-done | bytes 20971552 | tf_op jit(solution)/shard_map/all_to_all | solution.py:33
  3417.1 21.4 copy.39
  3438.4 41.0 %gather_fusion.3 = bf16[4096,2048]{1,0:T(8,128)(2,1)} fusion(bf16[5120,2048]{1,0:T(8,128)(2,1)} %bitcast.64, s32[4096]{0:T(1024)S(1)} %copy-done.12), kind=kCustom, calls=%fused_computation.3.clone | custom fusion | bytes 33570816 | tf_op jit(solution)/shard_map/jit(_take)/gather | solution.py:34
  3479.4 18.9 select_convert_fusion
  3498.3 39.1 %reshape.157 = f32[2048,2,2048]{2,1,0:T(2,128)} reshape(f32[4096,2048]{1,0:T(8,128)} %select_convert_fusion) | data formatting | bytes 67108864 | tf_op jit(solution)/shard_map/convert_element_type | solution.py:35
  3537.4 113.1 %multiply_reduce_fusion = (bf16[2048,2048]{1,0:T(8,128)(2,1)}, bf16[2048,2048]{1,0:T(8,128)(2,1)}) fusion(f32[2048,2,2048]{2,1,0:T(2,128)} %reshape.157, f32[2048,2]{1,0:T(8,128)S(1)} %copy-done.1, f32[2048,2,2048]{2,1,0:T(2,128)} %reshape.156, f32[2048,2]{1,0:T(8,128)S(1)} %copy-done), kind=kLoop, calls=%fused_computation.10 | loop fusion | flops 25165824 | bytes 83918848 | tf_op jit(solution)/shard_map/reduce_sum | solution.py:36
  (48 shorter events, 0.4 us)
Async XLA Ops:
  7.2 800.0 %all-gather.3.cloned.1.call-start = ((), (), s32[]{:S(2)}) async-start(), calls=%async_computation.6 | async-start | bytes 62914560 | tf_op jit(solution)/shard_map/all_gather | solution.py:27
  9.2 65.0 %copy-start.2 = (s32[4096]{0:T(1024)}, s32[4096]{0:T(1024)S(1)}, u32[]{:S(2)}) copy-start(s32[4096]{0:T(1024)S(1)} %eq.50) | copy-start | bytes 49156
  13.0 0.6 copy-start.6
  317.7 7.3 copy-start.10
  324.9 965.2 %all-gather.5.cloned.1.call-start = ((), (), s32[]{:S(2)}) async-start(), calls=%async_computation.8 | async-start | bytes 62914560 | tf_op jit(solution)/shard_map/all_gather | solution.py:27
  326.3 64.1 %copy-start.4 = (s32[4096]{0:T(1024)}, s32[4096]{0:T(1024)S(1)}, u32[]{:S(2)}) copy-start(s32[4096]{0:T(1024)S(1)} %eq.58) | copy-start | bytes 49156
  330.4 0.7 copy-start.8
  640.0 1557.9 %reduce-scatter.3.cloned.1.call-start = ((), (), s32[]{:S(2)}) async-start(), calls=%async_computation.7 | async-start | bytes 125829120 | tf_op jit(solution)/shard_map/reduce_scatter | solution.py:32
  1206.4 1899.2 %reduce-scatter.5.cloned.1.call-start = ((), (), s32[]{:S(2)}) async-start(), calls=%async_computation.9 | async-start | bytes 125829120 | tf_op jit(solution)/shard_map/reduce_scatter | solution.py:32
  2273.6 907.7 %all-to-all-start.1 = ((bf16[2,2560,2048]{2,0,1:T(2,128)(2,1)}), bf16[2,2560,2048]{2,0,1:T(2,128)(2,1)}, u32[]{:S(2)}, u32[]{:S(2)}) async-start(bf16[2,2560,2048]{2,0,1:T(2,128)(2,1)} %copy.31), calls=%async_computation.2 | async-start | bytes 41943040 | tf_op jit(solution)/shard_map/all_to_all | solution.py:33
  3181.3 8.2 copy-start.13
  3181.3 9.5 copy-start.14
  3181.3 10.9 copy-start.3
  3181.3 10.9 copy-start.7
  3181.3 10.9 copy-start.5
  3181.3 10.9 copy-start.9
  3181.3 235.7 %all-to-all-start.3 = ((bf16[2,2560,2048]{2,0,1:T(2,128)(2,1)}), bf16[2,2560,2048]{2,0,1:T(2,128)(2,1)}, u32[]{:S(2)}, u32[]{:S(2)}) async-start(bf16[2,2560,2048]{2,0,1:T(2,128)(2,1)} %copy.38), calls=%async_computation.5 | async-start | bytes 41943040 | tf_op jit(solution)/shard_map/all_to_all | solution.py:33
  3189.4 24.2 copy-start.11
  3312.2 126.2 %copy-start.12 = (s32[4096]{0:T(1024)S(1)}, s32[4096]{0:T(1024)}, u32[]{:S(2)}) copy-start(s32[4096]{0:T(1024)} %get-tuple-element.4) | copy-start | bytes 49156
  3498.3 39.1 %copy-start = (f32[2048,2]{1,0:T(8,128)S(1)}, f32[2048,2]{1,0:T(8,128)}, u32[]{:S(2)}) copy-start(f32[2048,2]{1,0:T(8,128)} %copy.33) | copy-start | bytes 49156
  3498.3 39.1 %copy-start.1 = (f32[2048,2]{1,0:T(8,128)S(1)}, f32[2048,2]{1,0:T(8,128)}, u32[]{:S(2)}) copy-start(f32[2048,2]{1,0:T(8,128)} %copy.40) | copy-start | bytes 49156
Sparse Core Ops, SparseCore 0:
  325.0 482.0 all-gather.2
  808.7 481.3 all-gather.4
  1292.4 905.5 reduce-scatter.2
  2200.1 905.5 reduce-scatter.4
where the time goes:
time: 3670 us; the launch traced here: 3660 us
  waiting for transfers between devices  1690 us (46%)
  matrix products  799 us (22%)
  local copies, waits for them, and re-layouts  466 us (13%)
  blocking collectives  464 us (13%)
  other arithmetic  210 us (6%)
    reduce_scatter x2, waiting for transfers between devices, moe_local(): lax.psum_scatter(partial_out, 'tp', scatter_dimension=1, tiled=True)  1330 us
    all_to_all x2, blocking collectives, moe_local(): received = lax.all_to_all(slot_rows, 'ep', 0, 1, tiled=True)  464 us
    dot_general x2, matrix products, moe_local(): jnp.einsum('erf,efd->erd', hidden, w_down, preferred_element_type=jnp.flo...  276 us
    dot_general x2, matrix products, moe_local(): jnp.einsum('erd,edf->erf', gathered, w_up, preferred_element_type=jnp.flo...  262 us
    dot_general x2, matrix products, moe_local(): jnp.einsum('erd,edf->erf', gathered, w_gate, preferred_element_type=jnp.f...  261 us
    all_gather x2, waiting for transfers between devices, moe_local(): gathered = lax.all_gather(received, 'tp', axis=1, tiled=True)  251 us
    convert_element_type x2, local copies, waits for them, and re-layouts, moe_local(): summed.astype(jnp.bfloat16)  122 us
    reduce_sum x1, other arithmetic, moe_local(): return jnp.sum(weighted, axis=1).astype(jnp.bfloat16)  113 us
  transfers between devices with their start and end apart: 6, of which 5 were waited for; matrix products, arithmetic and copies ran while one was open for 32% of the time, Pallas kernels for 0%

commit v1 on v0

v1 whole, which is shorter than its diff:
```python
import functools

import jax
import jax.numpy as jnp
from jax import lax
from jax.experimental import pallas as pl
from jax.experimental.pallas import tpu as pltpu
from jax.sharding import PartitionSpec as P


TP_SWAP = [(0, 1), (1, 0)]
BF16 = jnp.bfloat16
F32 = jnp.float32
MASKS = 4
TN = 256
VMEM_LIMIT = 60 * 1024 * 1024


def mm(a, b):
    return jnp.dot(a, b, preferred_element_type=F32)


def call(kernel, flops, nbytes, **kw):
    params = pltpu.CompilerParams(vmem_limit_bytes=VMEM_LIMIT)
    cost = pl.CostEstimate(flops=int(flops), bytes_accessed=int(nbytes), transcendentals=0)
    return pl.pallas_call(kernel, compiler_params=params, cost_estimate=cost, **kw)


def any_spec():
    return pl.BlockSpec(memory_space=pl.ANY)


def dispatch_kernel(pos_ref, tok_ref, *outs):
    step = pl.program_id(0)
    cap, model = outs[0].shape[1:]
    slots = lax.broadcasted_iota(jnp.int32, (cap, tok_ref.shape[0]), 0)
    onehot = (slots == pos_ref[0]).astype(BF16)
    for m, out in enumerate(outs):

        @pl.when(step // 2 == m)
        def _():
            for lo in range(0, model, 512):
                out[0, :, lo:lo + 512] = mm(onehot, tok_ref[:, lo:lo + 512]).astype(BF16)


def dispatch(pos, tokens, cap):
    n = pos.shape[0] // 2
    toks, model = tokens.shape
    out = jax.ShapeDtypeStruct((2, cap, model), BF16)
    return call(
        dispatch_kernel, 2 * n * 2 * cap * toks * model, toks * model * 2 + 2 * n * cap * model * 2,
        grid=(2 * n,),
        in_specs=[pl.BlockSpec((1, 1, toks), lambda i: (i, 0, 0)), pl.BlockSpec((toks, model), lambda i: (0, 0))],
        out_specs=[pl.BlockSpec((1, cap, model), functools.partial(lambda m, i: (jnp.clip(i - 2 * m, 0, 1), 0, 0), m)) for m in range(n)],
        out_shape=[out] * n,
    )(pos, tokens)


def hidden_kernel(*refs):
    xs, (wg, wu), h = refs[:MASKS], refs[MASKS:MASKS + 2], refs[-1]
    g = wg[...].reshape(wg.shape[-2:])
    u = wu[...].reshape(wu.shape[-2:])
    for m in range(MASKS):
        x = xs[m][0]
        a = mm(x, g)
        h[m] = (a * jax.nn.sigmoid(a) * mm(x, u)).astype(BF16)


def weight_spec(w, k, cols, off):
    if w.ndim == 3:
        return pl.BlockSpec((1, w.shape[1], cols), lambda n: (k, 0, n + off))
    return pl.BlockSpec((w.shape[0], cols), lambda n: (0, n + off))


def hidden(xs, wg, wu, k, width, off=0, wu_off=0, steps=None, into=None):
    _, cap, model = xs[0].shape
    steps = width // TN if steps is None else steps
    in_specs = [pl.BlockSpec((1, cap, model), lambda n: (k, 0, 0)) for _ in xs]
    in_specs += [weight_spec(wg, k, TN, off), weight_spec(wu, k, TN, wu_off)]
    args = [*xs, wg, wu]
    kw = {}
    if into is not None:
        args.append(into)
        in_specs.append(any_spec())
        kw["input_output_aliases"] = {len(args) - 1: 0}
    rows = MASKS * cap
    return call(
        hidden_kernel, 4 * rows * model * TN * steps, 2 * (rows * model + 2 * model * TN * steps + rows * TN * steps),
        grid=(steps,), in_specs=in_specs,
        out_specs=pl.BlockSpec((MASKS, cap, TN), lambda n: (0, 0, n + off)),
        out_shape=jax.ShapeDtypeStruct((MASKS, cap, width), BF16), **kw,
    )(*args)


def part_kernel(h, wd, out):
    for m in range(MASKS):
        out[m] = mm(h[m], wd[0])


def part(h, wd, k):
    _, cap, width = h.shape
    model = wd.shape[2]
    rows = MASKS * cap
    return call(
        part_kernel, 2 * rows * width * model, 2 * (rows * width + width * model) + 4 * rows * model,
        grid=(model // TN,),
        in_specs=[pl.BlockSpec((MASKS, cap, width), lambda n: (0, 0, 0)), pl.BlockSpec((1, width, TN), lambda n: (k, 0, n))],
        out_specs=pl.BlockSpec((MASKS, cap, TN), lambda n: (0, 0, n)),
        out_shape=jax.ShapeDtypeStruct((MASKS, cap, model), F32),
    )(h, wd)


def final_kernel(h_a, h_b, p_a, p_b, wd, *outs):
    i = pl.program_id(0)
    for b, (h, p) in enumerate(((h_a, p_a), (h_b, p_b))):
        for m, out in enumerate(outs):

            @pl.when(i == b * MASKS + m)
            def _():
                out[0] = (p[0] + mm(h[0], wd[...])).astype(BF16)


def final(h_a, h_b, p_a, p_b, wd, lo):
    _, cap, width = h_a.shape
    cols = wd.shape[1]
    first = lambda i: jnp.minimum(i, MASKS - 1)
    second = lambda i: jnp.maximum(i - MASKS, 0)
    at = lo // cols
    rows = 2 * MASKS * cap
    return call(
        final_kernel, 2 * rows * width * cols, 2 * (rows * width + width * cols) + 6 * rows * cols,
        grid=(2 * MASKS,),
        in_specs=[
            pl.BlockSpec((1, cap, width), lambda i: (first(i), 0, 0)),
            pl.BlockSpec((1, cap, width), lambda i: (second(i), 0, 0)),
            pl.BlockSpec((1, cap, cols), lambda i: (first(i), 0, at)),
            pl.BlockSpec((1, cap, cols), lambda i: (second(i), 0, at)),
            pl.BlockSpec((width, cols), lambda i: (0, 0)),
        ],
        out_specs=[pl.BlockSpec((1, cap, cols), functools.partial(lambda m, i: (jnp.where(i >= MASKS + m, 1, 0), 0, 0), m)) for m in range(MASKS)],
        out_shape=[jax.ShapeDtypeStruct((2, cap, cols), BF16)] * MASKS,
    )(h_a, h_b, p_a, p_b, wd)


TB = 512


def picked(k, ys, pos, gate):
    slots = lax.broadcasted_iota(jnp.int32, (TB, ys[0].shape[1]), 1)
    total = None
    for m in range(MASKS):
        e = 2 * m + k
        onehot = (slots == pos[0, :, e:e + 1]).astype(BF16)
        term = gate[0, :, e:e + 1] * mm(onehot, ys[m][0])
        total = term if total is None else total + term
    return total


def combine_first_kernel(k, *refs):
    refs[-1][...] = picked(k, refs[:MASKS], refs[MASKS], refs[MASKS + 1])


def combine_kernel(k, *refs):
    acc, outs = refs[MASKS + 2], refs[-2:]
    i, blocks = pl.program_id(0), pl.num_programs(0) // 2
    total = acc[...] + picked(k, refs[:MASKS], refs[MASKS], refs[MASKS + 1])
    for b, out in enumerate(outs):

        @pl.when(i // blocks == b)
        def _():
            out[...] = total.astype(BF16)


def combine(ys, pos, gate, k, lo, acc, into):
    _, cap, cols = ys[0].shape
    toks = pos.shape[1]
    blocks = toks // TB
    model = acc.shape[1]
    at = lo // cols
    in_specs = [pl.BlockSpec((1, cap, cols), lambda i: (i // blocks, 0, 0)) for _ in ys]
    in_specs += [pl.BlockSpec((1, TB, pos.shape[2]), lambda i: (i // blocks, i % blocks, 0))] * 2
    args = [*ys, pos, gate]
    args.append(acc)
    in_specs.append(pl.BlockSpec((TB, cols), lambda i: (i, at)))
    out_specs = [
        pl.BlockSpec((TB, cols), lambda i: (jnp.minimum(i, blocks - 1), at)),
        pl.BlockSpec((TB, cols), lambda i: (jnp.maximum(i - blocks, 0), at)),
    ]
    kw = {}
    if into is not None:
        for j, buf in enumerate(into):
            args.append(buf)
            in_specs.append(any_spec())
            kw.setdefault("input_output_aliases", {})[len(args) - 1] = j
    return call(
        functools.partial(combine_kernel, k), 2 * 2 * toks * MASKS * cap * cols, 2 * toks * cols * 6,
        grid=(2 * blocks,), in_specs=in_specs, out_specs=out_specs,
        out_shape=[jax.ShapeDtypeStruct((toks, model), BF16)] * 2, **kw,
    )(*args)


def combine_first(ys, pos, gate, k, lo, model, into):
    _, cap, cols = ys[0].shape
    toks = pos.shape[1]
    blocks = toks // TB
    at = lo // cols
    in_specs = [pl.BlockSpec((1, cap, cols), lambda i: (i // blocks, 0, 0)) for _ in ys]
    in_specs += [pl.BlockSpec((1, TB, pos.shape[2]), lambda i: (i // blocks, i % blocks, 0))] * 2
    args = [*ys, pos, gate]
    kw = {}
    if into is not None:
        args.append(into)
        in_specs.append(any_spec())
        kw["input_output_aliases"] = {len(args) - 1: 0}

    return call(
        functools.partial(combine_first_kernel, k), 2 * 2 * toks * MASKS * cap * cols, 2 * toks * cols * 6,
        grid=(2 * blocks,), in_specs=in_specs,
        out_specs=pl.BlockSpec((TB, cols), lambda i: (i, at)),
        out_shape=jax.ShapeDtypeStruct((2 * toks, model), F32), **kw,
    )(*args)


def cuts(sizes):
    out, at = [], 0
    for size in sizes:
        out.append((at, at + size))
        at += size
    return out


def solution(mesh):
    ep_size = mesh.shape["ep"]
    row_spec = P(("dp", "ep", "tp"), None)
    gate_spec = P("ep", None, "tp")
    down_spec = P("ep", "tp", None)

    def ep_swap(value, mask):
        return lax.ppermute(value, "ep", [(i, i ^ mask) for i in range(ep_size)])

    def tp_swap(value):
        return lax.ppermute(value, "tp", TP_SWAP)

    def routing(ids, gates, me):
        toks, top_k = ids.shape[1:]
        n_exp = 2 * ep_size
        mean_load = top_k * toks // n_exp
        cap = mean_load + mean_load // 4
        code = ((ids // 2) ^ me) * 2 + ids % 2
        hit = code[:, None] == jnp.arange(n_exp, dtype=jnp.int32)[None, :, None, None]
        has = jnp.any(hit, axis=3)
        count = has.astype(jnp.int32)
        pos = jnp.cumsum(count, axis=2) - count
        pos = jnp.where(has & (pos < cap), pos, -1)
        gate = jnp.sum(jnp.where(hit, gates[:, None], 0.0), axis=3)
        return pos, gate, cap

    def group_body(tokens_a, ids_a, gates_a, tokens_b, ids_b, gates_b, w_gate, w_up, w_down):
        me = lax.axis_index("ep")
        width, model = w_down.shape[1:]
        up_cuts = cuts([1024, 1024, 512, 256])
        d0_cuts = cuts([1024, 1024])
        d1_cuts = cuts([128, 128] + [256] * 6 + [128, 128])
        g_r = tp_swap(w_gate)
        u0_r = tp_swap(w_up[0])
        d0_r = [tp_swap(w_down[0][:, lo:hi]) for lo, hi in d0_cuts]
        u1_r = [tp_swap(w_up[1][:, lo:hi]) for lo, hi in up_cuts]
        d1_r = [tp_swap(w_down[1][:, lo:hi]) for lo, hi in d1_cuts]

        pos, gate, cap = routing(jnp.stack([ids_a, ids_b]), jnp.stack([gates_a, gates_b]), me)
        pos_t, gate_t = pos.transpose(0, 2, 1), gate.transpose(0, 2, 1)

        xs = []
        for b, tokens in enumerate((tokens_a, tokens_b)):
            rows = pos[b][:, None, :]
            far = dispatch(rows[4:], tokens, cap)
            far = [ep_swap(far[0], 2), ep_swap(far[1], 3)]
            near = dispatch(rows[:4], tokens, cap)
            xs.append([near[0], ep_swap(near[1], 1), *far])

        def bring_back(ys):
            return [ys[0], ep_swap(ys[1], 1), ep_swap(ys[2], 2), ep_swap(ys[3], 3)]

        h_l, p = [[None] * 2, [None] * 2], [[None] * 2, [None] * 2]
        for b in range(2):
            for k in range(2):
                h_l[b][k] = hidden(xs[b], w_gate, w_up, k, width)
            for k in range(2):
                p[b][k] = part(h_l[b][k], w_down, k)

        h_r = []
        for b in range(2):
            h_r.append(hidden(xs[b], g_r, u0_r, 0, width))
        acc = None
        for n, (lo, hi) in enumerate(d0_cuts):
            ys = final(h_r[0], h_r[1], p[0][0], p[1][0], d0_r[n], lo)
            ys = bring_back(ys)
            acc = combine_first(ys, pos_t, gate_t, 0, lo, model, acc)

        h_r = [None, None]
        for n, (lo, hi) in enumerate(up_cuts):
            for b in range(2):
                h_r[b] = hidden(xs[b], g_r, u1_r[n], 1, width, lo // TN, steps=(hi - lo) // TN, into=h_r[b])
        outs = None
        for n, (lo, hi) in enumerate(d1_cuts):
            ys = final(h_r[0], h_r[1], p[0][1], p[1][1], d1_r[n], lo)
            ys = bring_back(ys)
            outs = combine(ys, pos_t, gate_t, 1, lo, acc, outs)
        return tuple(outs)

    in_specs = (row_spec, row_spec, row_spec, row_spec, row_spec, row_spec, gate_spec, gate_spec, down_spec)
    return jax.shard_map(group_body, mesh=mesh, in_specs=in_specs, out_specs=(row_spec, row_spec), check_vma=False)
```

time: 3670 us -> 2080 us (0.57)
  Pallas kernels: 0 us -> 1300 us
  waiting for transfers between devices: 1690 us -> 646 us
  matrix products: 799 us -> 0 us
  blocking collectives: 464 us -> 0 us
  local copies, waits for them, and re-layouts: 466 us -> 61.2 us
  other arithmetic: 210 us -> 6.57 us
  starting transfers between devices: 16 us -> 59.1 us
    reduce_scatter x2 -> x0, waiting for transfers between devices: 1330 us -> none  [moe_local(): lax.psum_scatter(partial_out, 'tp', scatter_dimension=1, tiled=True)]
    pallas_call x0 -> x46, Pallas kernels: none -> 1300 us  [the longest x14 577 us: hidden(): call(hidden_kernel, 4 * rows * model * TN * steps, 2 * (rows * model + 2...]
    dot_general x6 -> x0, matrix products: 799 us -> none  [the longest x2 276 us: moe_local(): jnp.einsum('erf,efd->erd', hidden, w_down, preferred_element_type=jnp.flo...]
    ppermute x0 -> x60, waiting for transfers between devices: none -> 646 us  [the longest x42 334 us: ep_swap(): return lax.ppermute(value, 'ep', [(i, i ^ mask) for i in range(ep_size)])]
    all_to_all x2 -> x0, blocking collectives: 464 us -> none  [moe_local(): received = lax.all_to_all(slot_rows, 'ep', 0, 1, tiled=True)]
    all_gather x2 -> x0, waiting for transfers between devices: 251 us -> none  [moe_local(): gathered = lax.all_gather(received, 'tp', axis=1, tiled=True)]
    convert_element_type x4 -> x1, local copies, waits for them, and re-layouts: 200 us -> 0.56 us  [routing(): count = has.astype(jnp.int32)]
    gather x4 -> x0, local copies, waits for them, and re-layouts: 169 us -> none  [the longest x2 86.6 us: moe_local(): jnp.take(tokens, source, axis=0, mode='fill', fill_value=0)]
  transfers between devices with their start and end apart: 6 -> 60, of which waited for: 5 -> 20; matrix products, arithmetic and copies ran while one was open for 32% -> 2% of each run, Pallas kernels for 0% -> 61%
where the time goes in v1:
time: 2080 us; the launch traced here: 2070 us
  Pallas kernels  1300 us (62%)
  waiting for transfers between devices  646 us (31%)
  local copies, waits for them, and re-layouts  61.2 us (3%)
  starting transfers between devices  59.1 us (3%)
    pallas_call x14, Pallas kernels, hidden(): call(hidden_kernel, 4 * rows * model * TN * steps, 2 * (rows * model + 2...  577 us
    ppermute x42, waiting for transfers between devices, ep_swap(): return lax.ppermute(value, 'ep', [(i, i ^ mask) for i in range(ep_size)])  334 us
    ppermute x18, waiting for transfers between devices, tp_swap(): return lax.ppermute(value, 'tp', TP_SWAP)  312 us
    pallas_call x12, Pallas kernels, final(): call(final_kernel, 2 * rows * width * cols, 2 * (rows * width + width * c...  259 us
    pallas_call x4, Pallas kernels, part(): call(part_kernel, 2 * rows * width * model, 2 * (rows * width + width * m...  153 us
    pallas_call x4, Pallas kernels, dispatch(): call(dispatch_kernel, 2 * n * 2 * cap * toks * model, toks * model * 2 +...  124 us
    pallas_call x10, Pallas kernels, combine(): call(functools.partial(combine_kernel, k), 2 * 2 * toks * MASKS * cap * c...  118 us
    pallas_call x2, Pallas kernels, combine_first(): call(functools.partial(combine_first_kernel, k), 2 * 2 * toks * MASKS * c...  65.7 us
  transfers between devices with their start and end apart: 60, of which 20 were waited for; matrix products, arithmetic and copies ran while one was open for 2% of the time, Pallas kernels for 61%

profile of v1, /device:TPU:0, one launch (start us, length us, event | category | flops | bytes accessed | tf_op | source)
XLA Modules:
  0.0 2070.8 jit_solution(2297166625919969916)
XLA Ops:
  3.1 4.6 reduce-window.6
  13.8 30.7 %shard_map.104 = (bf16[2,640,2048]{2,1,0:T(8,128)(2,1)}, bf16[2,640,2048]{2,1,0:T(8,128)(2,1)}) custom-call(s32[4,1,2048]{2,1,0:T(1,128)} %copy.56.pos_ref, bf16[2048,2048]{1,0:T(8,128)(2,1)} %tok_ref.5), custom_call_target="tpu_custom_call" | custom-call | flops 21474836480 | bytes 18874368 | tf_op jit(solution)/shard_map/pallas_call | solution.py:50
  46.3 31.0 %shard_map.105 = (bf16[2,640,2048]{2,1,0:T(8,128)(2,1)}, bf16[2,640,2048]{2,1,0:T(8,128)(2,1)}) custom-call(s32[4,1,2048]{2,1,0:T(1,128)} %copy.57.pos_ref, bf16[2048,2048]{1,0:T(8,128)(2,1)} %tok_ref.5), custom_call_target="tpu_custom_call" | custom-call | flops 21474836480 | bytes 18874368 | tf_op jit(solution)/shard_map/pallas_call | solution.py:50
  81.7 14.2 slice_bitcast_fusion.1
  103.8 6.0 slice_bitcast_fusion
  121.6 10.1 fusion.4
  131.8 31.0 %shard_map.110 = (bf16[2,640,2048]{2,1,0:T(8,128)(2,1)}, bf16[2,640,2048]{2,1,0:T(8,128)(2,1)}) custom-call(s32[4,1,2048]{2,1,0:T(1,128)} %copy.58.pos_ref, bf16[2048,2048]{1,0:T(8,128)(2,1)} %tok_ref.7), custom_call_target="tpu_custom_call" | custom-call | flops 21474836480 | bytes 18874368 | tf_op jit(solution)/shard_map/pallas_call | solution.py:50
  162.8 30.8 %shard_map.111 = (bf16[2,640,2048]{2,1,0:T(8,128)(2,1)}, bf16[2,640,2048]{2,1,0:T(8,128)(2,1)}) custom-call(s32[4,1,2048]{2,1,0:T(1,128)} %copy.59.pos_ref, bf16[2048,2048]{1,0:T(8,128)(2,1)} %tok_ref.7), custom_call_target="tpu_custom_call" | custom-call | flops 21474836480 | bytes 18874368 | tf_op jit(solution)/shard_map/pallas_call | solution.py:50
  196.0 110.0 %collective-permute-done.2.refs_3_ = bf16[2,640,2048]{2,1,0:T(8,128)(2,1)} collective-permute-done((bf16[2,640,2048]{2,1,0:T(8,128)(2,1)}, bf16[2,640,2048]{2,1,0:T(8,128)(2,1)}, u32[]{:S(2)}, u32[]{:S(2)}) %collective-permute-start.2) | collective-permute-done | bytes 5242912 | tf_op jit(solution)/shard_map/ppermute | solution.py:239
  308.1 67.6 %shard_map.116.h = bf16[4,640,2816]{2,1,0:T(8,128)(2,1)} custom-call(bf16[2,640,2048]{2,1,0:T(8,128)(2,1)} %get-tuple-element.76.refs_0_, bf16[2,640,2048]{2,1,0:T(8,128)(2,1)} %collective-permute-done.refs_1_, bf16[2,640,2048]{2,1,0:T(8,128)(2,1)} %collective-permute-done.1.refs_2_, bf16[2,640,2048]{2,1,0:T(8,128)(2,1)} %collective-permute-done.2.refs_3_, ...), custom_call_target="tpu_custom_call" | custom-call | flops 59055800320 | bytes 47972352 | tf_op jit(solution)/shard_map/pallas_call | solution.py:87
  375.7 68.0 %shard_map.123.h = bf16[4,640,2816]{2,1,0:T(8,128)(2,1)} custom-call(bf16[2,640,2048]{2,1,0:T(8,128)(2,1)} %get-tuple-element.76.refs_0_, bf16[2,640,2048]{2,1,0:T(8,128)(2,1)} %collective-permute-done.refs_1_, bf16[2,640,2048]{2,1,0:T(8,128)(2,1)} %collective-permute-done.1.refs_2_, bf16[2,640,2048]{2,1,0:T(8,128)(2,1)} %collective-permute-done.2.refs_3_, ...), custom_call_target="tpu_custom_call" | custom-call | flops 59055800320 | bytes 47972352 | tf_op jit(solution)/shard_map/pallas_call | solution.py:87
  443.7 38.3 %shard_map.117.p_a = f32[4,640,2048]{2,1,0:T(8,128)} custom-call(bf16[4,640,2816]{2,1,0:T(8,128)(2,1)} %shard_map.116.h, bf16[2,2816,2048]{2,1,0:T(8,128)(2,1)} %wd.7), custom_call_target="tpu_custom_call" | custom-call | flops 29527900160 | bytes 46923776 | tf_op jit(solution)/shard_map/pallas_call | solution.py:104
  484.1 46.6 %collective-permute-done.10.refs_3_ = bf16[2,640,2048]{2,1,0:T(8,128)(2,1)} collective-permute-done((bf16[2,640,2048]{2,1,0:T(8,128)(2,1)}, bf16[2,640,2048]{2,1,0:T(8,128)(2,1)}, u32[]{:S(2)}, u32[]{:S(2)}) %collective-permute-start.10) | collective-permute-done | bytes 5242912 | tf_op jit(solution)/shard_map/ppermute | solution.py:239
  532.2 67.7 %shard_map.118.h = bf16[4,640,2816]{2,1,0:T(8,128)(2,1)} custom-call(bf16[2,640,2048]{2,1,0:T(8,128)(2,1)} %get-tuple-element.80.refs_0_, bf16[2,640,2048]{2,1,0:T(8,128)(2,1)} %collective-permute-done.8.refs_1_, bf16[2,640,2048]{2,1,0:T(8,128)(2,1)} %collective-permute-done.9.refs_2_, bf16[2,640,2048]{2,1,0:T(8,128)(2,1)} %collective-permute-done.10.refs_3_, ...), custom_call_target="tpu_custom_call" | custom-call | flops 59055800320 | bytes 47972352 | tf_op jit(solution)/shard_map/pallas_call | solution.py:87
  599.9 38.2 %shard_map.119.p_b = f32[4,640,2048]{2,1,0:T(8,128)} custom-call(bf16[4,640,2816]{2,1,0:T(8,128)(2,1)} %shard_map.118.h, bf16[2,2816,2048]{2,1,0:T(8,128)(2,1)} %wd.7), custom_call_target="tpu_custom_call" | custom-call | flops 29527900160 | bytes 46923776 | tf_op jit(solution)/shard_map/pallas_call | solution.py:104
  638.1 38.4 %shard_map.124.p_a = f32[4,640,2048]{2,1,0:T(8,128)} custom-call(bf16[4,640,2816]{2,1,0:T(8,128)(2,1)} %shard_map.123.h, bf16[2,2816,2048]{2,1,0:T(8,128)(2,1)} %wd.7), custom_call_target="tpu_custom_call" | custom-call | flops 29527900160 | bytes 46923776 | tf_op jit(solution)/shard_map/pallas_call | solution.py:104
  676.5 67.6 %shard_map.125.h = bf16[4,640,2816]{2,1,0:T(8,128)(2,1)} custom-call(bf16[2,640,2048]{2,1,0:T(8,128)(2,1)} %get-tuple-element.80.refs_0_, bf16[2,640,2048]{2,1,0:T(8,128)(2,1)} %collective-permute-done.8.refs_1_, bf16[2,640,2048]{2,1,0:T(8,128)(2,1)} %collective-permute-done.9.refs_2_, bf16[2,640,2048]{2,1,0:T(8,128)(2,1)} %collective-permute-done.10.refs_3_, ...), custom_call_target="tpu_custom_call" | custom-call | flops 59055800320 | bytes 47972352 | tf_op jit(solution)/shard_map/pallas_call | solution.py:87
  744.1 38.4 %shard_map.126.p_b = f32[4,640,2048]{2,1,0:T(8,128)} custom-call(bf16[4,640,2816]{2,1,0:T(8,128)(2,1)} %shard_map.125.h, bf16[2,2816,2048]{2,1,0:T(8,128)(2,1)} %wd.7), custom_call_target="tpu_custom_call" | custom-call | flops 29527900160 | bytes 46923776 | tf_op jit(solution)/shard_map/pallas_call | solution.py:104
  782.5 199.5 %collective-permute-done.15.refs_5_ = bf16[2048,2816]{1,0:T(8,128)(2,1)} collective-permute-done((bf16[2048,2816]{1,0:T(8,128)(2,1)}, bf16[2048,2816]{1,0:T(8,128)(2,1)}, u32[]{:S(2)}, u32[]{:S(2)}) %collective-permute-start.15) | collective-permute-done | bytes 11534368 | tf_op jit(solution)/shard_map/ppermute | solution.py:242
  984.0 67.6 %shard_map.121.h_a = bf16[4,640,2816]{2,1,0:T(8,128)(2,1)} custom-call(bf16[2,640,2048]{2,1,0:T(8,128)(2,1)} %get-tuple-element.76.refs_0_, bf16[2,640,2048]{2,1,0:T(8,128)(2,1)} %collective-permute-done.refs_1_, bf16[2,640,2048]{2,1,0:T(8,128)(2,1)} %collective-permute-done.1.refs_2_, bf16[2,640,2048]{2,1,0:T(8,128)(2,1)} %collective-permute-done.2.refs_3_, ...), custom_call_target="tpu_custom_call" | custom-call | flops 59055800320 | bytes 47972352 | tf_op jit(solution)/shard_map/pallas_call | solution.py:87
  1051.6 67.6 %shard_map.122.h_b = bf16[4,640,2816]{2,1,0:T(8,128)(2,1)} custom-call(bf16[2,640,2048]{2,1,0:T(8,128)(2,1)} %get-tuple-element.80.refs_0_, bf16[2,640,2048]{2,1,0:T(8,128)(2,1)} %collective-permute-done.8.refs_1_, bf16[2,640,2048]{2,1,0:T(8,128)(2,1)} %collective-permute-done.9.refs_2_, bf16[2,640,2048]{2,1,0:T(8,128)(2,1)} %collective-permute-done.10.refs_3_, ...), custom_call_target="tpu_custom_call" | custom-call | flops 59055800320 | bytes 47972352 | tf_op jit(solution)/shard_map/pallas_call | solution.py:87
  1120.9 28.3 %shard_map.106.refs_6_ = bf16[4,640,2816]{2,1,0:T(8,128)(2,1)} custom-call(bf16[2,640,2048]{2,1,0:T(8,128)(2,1)} %get-tuple-element.76.refs_0_, bf16[2,640,2048]{2,1,0:T(8,128)(2,1)} %collective-permute-done.refs_1_, bf16[2,640,2048]{2,1,0:T(8,128)(2,1)} %collective-permute-done.1.refs_2_, bf16[2,640,2048]{2,1,0:T(8,128)(2,1)} %collective-permute-done.2.refs_3_, ...), custom_call_target="tpu_custom_call" | custom-call | flops 21474836480 | bytes 24117248 | tf_op jit(solution)/shard_map/pallas_call | solution.py:87
  1149.2 50.1 %collective-permute-done.16.wd = bf16[2816,1024]{1,0:T(8,128)(2,1)} collective-permute-done((bf16[2816,1024]{1,0:T(8,128)(2,1)}, bf16[2816,1024]{1,0:T(8,128)(2,1)}, u32[]{:S(2)}, u32[]{:S(2)}) %collective-permute-start.16) | collective-permute-done | bytes 5767200 | tf_op jit(solution)/shard_map/ppermute | solution.py:242
  1201.0 41.3 %shard_map.127 = (bf16[2,640,1024]{2,1,0:T(8,128)(2,1)}, bf16[2,640,1024]{2,1,0:T(8,128)(2,1)}, bf16[2,640,1024]{2,1,0:T(8,128)(2,1)}, bf16[2,640,1024]{2,1,0:T(8,128)(2,1)}) custom-call(bf16[4,640,2816]{2,1,0:T(8,128)(2,1)} %shard_map.121.h_a, bf16[4,640,2816]{2,1,0:T(8,128)(2,1)} %shard_map.122.h_b, f32[4,640,2048]{2,1,0:T(8,128)} %shard_map.124.p_a, ...), custom_call_target="tpu_custom_call" | custom-call | flops 29527900160 | bytes 66060288 | tf_op jit(solution)/shard_map/pallas_call | solution.py:130
  1242.4 28.5 %shard_map.112.refs_6_ = bf16[4,640,2816]{2,1,0:T(8,128)(2,1)} custom-call(bf16[2,640,2048]{2,1,0:T(8,128)(2,1)} %get-tuple-element.80.refs_0_, bf16[2,640,2048]{2,1,0:T(8,128)(2,1)} %collective-permute-done.8.refs_1_, bf16[2,640,2048]{2,1,0:T(8,128)(2,1)} %collective-permute-done.9.refs_2_, bf16[2,640,2048]{2,1,0:T(8,128)(2,1)} %collective-permute-done.10.refs_3_, ...), custom_call_target="tpu_custom_call" | custom-call | flops 21474836480 | bytes 24117248 | tf_op jit(solution)/shard_map/pallas_call | solution.py:87
  1270.9 52.0 %collective-permute-done.20.wd = bf16[2816,1024]{1,0:T(8,128)(2,1)} collective-permute-done((bf16[2816,1024]{1,0:T(8,128)(2,1)}, bf16[2816,1024]{1,0:T(8,128)(2,1)}, u32[]{:S(2)}, u32[]{:S(2)}) %collective-permute-start.20) | collective-permute-done | bytes 5767200 | tf_op jit(solution)/shard_map/ppermute | solution.py:242
  1324.6 41.4 %shard_map.128 = (bf16[2,640,1024]{2,1,0:T(8,128)(2,1)}, bf16[2,640,1024]{2,1,0:T(8,128)(2,1)}, bf16[2,640,1024]{2,1,0:T(8,128)(2,1)}, bf16[2,640,1024]{2,1,0:T(8,128)(2,1)}) custom-call(bf16[4,640,2816]{2,1,0:T(8,128)(2,1)} %shard_map.121.h_a, bf16[4,640,2816]{2,1,0:T(8,128)(2,1)} %shard_map.122.h_b, f32[4,640,2048]{2,1,0:T(8,128)} %shard_map.124.p_a, ...), custom_call_target="tpu_custom_call" | custom-call | flops 29527900160 | bytes 66060288 | tf_op jit(solution)/shard_map/pallas_call | solution.py:130
  1366.4 28.3 %shard_map.107.refs_6_ = bf16[4,640,2816]{2,1,0:T(8,128)(2,1)} custom-call(bf16[2,640,2048]{2,1,0:T(8,128)(2,1)} %get-tuple-element.76.refs_0_, bf16[2,640,2048]{2,1,0:T(8,128)(2,1)} %collective-permute-done.refs_1_, bf16[2,640,2048]{2,1,0:T(8,128)(2,1)} %collective-permute-done.1.refs_2_, ...), custom_call_target="tpu_custom_call", output_to_operand_aliasing={{}: (6, {})} | custom-call | flops 21474836480 | bytes 24117248 | tf_op jit(solution)/shard_map/pallas_call | solution.py:87
  1394.7 28.4 %shard_map.113.refs_6_ = bf16[4,640,2816]{2,1,0:T(8,128)(2,1)} custom-call(bf16[2,640,2048]{2,1,0:T(8,128)(2,1)} %get-tuple-element.80.refs_0_, bf16[2,640,2048]{2,1,0:T(8,128)(2,1)} %collective-permute-done.8.refs_1_, bf16[2,640,2048]{2,1,0:T(8,128)(2,1)} %collective-permute-done.9.refs_2_, ...), custom_call_target="tpu_custom_call", output_to_operand_aliasing={{}: (6, {})} | custom-call | flops 21474836480 | bytes 24117248 | tf_op jit(solution)/shard_map/pallas_call | solution.py:87
  1424.8 17.1 shard_map.108.refs_6_
  1441.9 17.4 shard_map.114.refs_6_
  1459.6 11.3 shard_map.109.h_a
  1470.9 11.5 shard_map.115.h_b
  1484.1 18.1 shard_map.132
  1502.5 18.3 shard_map.133
  1522.6 17.9 shard_map.134
  1540.9 17.9 shard_map.135
  1560.5 10.5 collective-permute-done.52.wd
  1571.0 16.9 shard_map.120
  1588.2 16.9 shard_map.138
  1605.2 18.2 shard_map.136
  1625.3 17.2 shard_map.139
  1643.5 38.5 %collective-permute-done.54.refs_2_ = bf16[2,640,128]{2,1,0:T(8,128)(2,1)S(1)} collective-permute-done((bf16[2,640,128]{2,1,0:T(8,128)(2,1)S(1)}, bf16[2,640,128]{2,1,0:T(8,128)(2,1)S(1)}, u32[]{:S(2)}, u32[]{:S(2)}) %collective-permute-start.54) | collective-permute-done | bytes 327712 | tf_op jit(solution)/shard_map/ppermute | solution.py:239
  1682.0 16.9 shard_map.131
  1701.8 18.2 shard_map.137
  1721.8 32.9 %shard_map.129.refs_6_ = f32[4096,2048]{1,0:T(8,128)} custom-call(bf16[2,640,1024]{2,1,0:T(8,128)(2,1)} %get-tuple-element.92.refs_0_, bf16[2,640,1024]{2,1,0:T(8,128)(2,1)} %collective-permute-done.21.refs_1_, bf16[2,640,1024]{2,1,0:T(8,128)(2,1)} %collective-permute-done.22.refs_2_, bf16[2,640,1024]{2,1,0:T(8,128)(2,1)} %collective-permute-done.23.refs_3_, ...), custom_call_target="tpu_custom_call" | custom-call | flops 21474836480 | bytes 25165824 | tf_op jit(solution)/shard_map/pallas_call | solution.py:216
  1754.7 68.6 %collective-permute-done.58.refs_2_ = bf16[2,640,128]{2,1,0:T(8,128)(2,1)S(1)} collective-permute-done((bf16[2,640,128]{2,1,0:T(8,128)(2,1)S(1)}, bf16[2,640,128]{2,1,0:T(8,128)(2,1)S(1)}, u32[]{:S(2)}, u32[]{:S(2)}) %collective-permute-start.58) | collective-permute-done | bytes 327712 | tf_op jit(solution)/shard_map/ppermute | solution.py:239
  1831.8 32.8 %shard_map.130.refs_6_ = f32[4096,2048]{1,0:T(8,128)} custom-call(bf16[2,640,1024]{2,1,0:T(8,128)(2,1)} %get-tuple-element.88.refs_0_, bf16[2,640,1024]{2,1,0:T(8,128)(2,1)} %copy-done.1, bf16[2,640,1024]{2,1,0:T(8,128)(2,1)} %collective-permute-done.18.refs_2_, ...), custom_call_target="tpu_custom_call", output_to_operand_aliasing={{}: (6, {})} | custom-call | flops 21474836480 | bytes 25165824 | tf_op jit(solution)/shard_map/pallas_call | solution.py:216
  1864.7 11.1 shard_map.140
  1877.8 10.9 shard_map.141
  1890.5 12.3 shard_map.142
  1909.2 12.3 shard_map.143
  1923.7 11.7 collective-permute-done.43.refs_3_
  1937.3 12.3 shard_map.144
  1951.8 11.7 collective-permute-done.39.refs_3_
  1965.3 12.3 shard_map.145
  1978.2 13.3 collective-permute-done.35.refs_3_
  1992.2 12.3 shard_map.146
  2007.9 11.7 collective-permute-done.31.refs_3_
  2021.4 12.3 shard_map.147
  2033.8 7.7 collective-permute-done.26.refs_2_
  2041.4 5.5 collective-permute-done.27.refs_3_
  2047.7 10.8 shard_map.148
  2059.5 10.8 shard_map.149
  (220 shorter events, 100.9 us)
Async XLA Ops:
  44.5 149.1 %collective-permute-start = (bf16[2,640,2048]{2,1,0:T(8,128)(2,1)}, bf16[2,640,2048]{2,1,0:T(8,128)(2,1)}, u32[]{:S(2)}, u32[]{:S(2)}) collective-permute-start(bf16[2,640,2048]{2,1,0:T(8,128)(2,1)} %get-tuple-element.77), channel_id=1, source_target_pairs={{0,1},{1,0},{2,3},{3,2},{4,5},{5,4},{6,7},{7,6}} | collective-permute-start | bytes 15728648 | tf_op jit(solution)/shard_map/ppermute | solution.py:239
  77.3 116.9 %collective-permute-start.1 = (bf16[2,640,2048]{2,1,0:T(8,128)(2,1)}, bf16[2,640,2048]{2,1,0:T(8,128)(2,1)}, u32[]{:S(2)}, u32[]{:S(2)}) collective-permute-start(bf16[2,640,2048]{2,1,0:T(8,128)(2,1)} %get-tuple-element.78), channel_id=1, source_target_pairs={{0,2},{1,3},{2,0},{3,1},{4,6},{5,7},{6,4},{7,5}} | collective-permute-start | bytes 15728648 | tf_op jit(solution)/shard_map/ppermute | solution.py:239
  79.8 226.2 %collective-permute-start.2 = (bf16[2,640,2048]{2,1,0:T(8,128)(2,1)}, bf16[2,640,2048]{2,1,0:T(8,128)(2,1)}, u32[]{:S(2)}, u32[]{:S(2)}) collective-permute-start(bf16[2,640,2048]{2,1,0:T(8,128)(2,1)} %get-tuple-element.79), channel_id=1, source_target_pairs={{0,3},{1,2},{2,1},{3,0},{4,7},{5,6},{6,5},{7,4}} | collective-permute-start | bytes 15728648 | tf_op jit(solution)/shard_map/ppermute | solution.py:239
  79.9 903.8 %collective-permute-start.3 = (bf16[2,2048,2816]{2,1,0:T(8,128)(2,1)}, bf16[2,2048,2816]{2,1,0:T(8,128)(2,1)}, u32[]{:S(2)}, u32[]{:S(2)}) collective-permute-start(bf16[2,2048,2816]{2,1,0:T(8,128)(2,1)} %refs_4_.7), channel_id=1, source_target_pairs={{0,4},{4,0},{1,5},{5,1},{2,6},{6,2},{3,7},{7,3}} | collective-permute-start | bytes 69206024 | tf_op jit(solution)/shard_map/ppermute | solution.py:242
  81.7 21.5 %slice-start.3 = ((s8[23068672]{0:T(1024)(128)(4,1)}), s8[4194304]{0:T(1024)(128)(4,1)S(1)}, s32[]{:S(2)}) async-start(s8[23068672]{0:T(1024)(128)(4,1)} %bitcast.52), calls=%async_computation.3 | async-start | bytes 8388608
  97.0 1362.2 %collective-permute-start.4 = (bf16[2048,256]{1,0:T(8,128)(2,1)}, bf16[2048,256]{1,0:T(8,128)(2,1)}, u32[]{:S(2)}, u32[]{:S(2)}) collective-permute-start(bf16[2048,256]{1,0:T(8,128)(2,1)} %slice.143), channel_id=1, source_target_pairs={{0,4},{4,0},{1,5},{5,1},{2,6},{6,2},{3,7},{7,3}} | collective-permute-start | bytes 3145736 | tf_op jit(solution)/shard_map/ppermute | solution.py:242
  193.6 288.4 %collective-permute-start.8 = (bf16[2,640,2048]{2,1,0:T(8,128)(2,1)}, bf16[2,640,2048]{2,1,0:T(8,128)(2,1)}, u32[]{:S(2)}, u32[]{:S(2)}) collective-permute-start(bf16[2,640,2048]{2,1,0:T(8,128)(2,1)} %get-tuple-element.81), channel_id=1, source_target_pairs={{0,1},{1,0},{2,3},{3,2},{4,5},{5,4},{6,7},{7,6}} | collective-permute-start | bytes 15728648 | tf_op jit(solution)/shard_map/ppermute | solution.py:239
  194.3 289.3 %collective-permute-start.9 = (bf16[2,640,2048]{2,1,0:T(8,128)(2,1)}, bf16[2,640,2048]{2,1,0:T(8,128)(2,1)}, u32[]{:S(2)}, u32[]{:S(2)}) collective-permute-start(bf16[2,640,2048]{2,1,0:T(8,128)(2,1)} %get-tuple-element.82), channel_id=1, source_target_pairs={{0,2},{1,3},{2,0},{3,1},{4,6},{5,7},{6,4},{7,5}} | collective-permute-start | bytes 15728648 | tf_op jit(solution)/shard_map/ppermute | solution.py:239
  306.0 224.7 %collective-permute-start.10 = (bf16[2,640,2048]{2,1,0:T(8,128)(2,1)}, bf16[2,640,2048]{2,1,0:T(8,128)(2,1)}, u32[]{:S(2)}, u32[]{:S(2)}) collective-permute-start(bf16[2,640,2048]{2,1,0:T(8,128)(2,1)} %get-tuple-element.83), channel_id=1, source_target_pairs={{0,3},{1,2},{2,1},{3,0},{4,7},{5,6},{6,5},{7,4}} | collective-permute-start | bytes 15728648 | tf_op jit(solution)/shard_map/ppermute | solution.py:239
  482.0 941.1 %collective-permute-start.5 = (bf16[2048,512]{1,0:T(8,128)(2,1)}, bf16[2048,512]{1,0:T(8,128)(2,1)}, u32[]{:S(2)}, u32[]{:S(2)}) collective-permute-start(bf16[2048,512]{1,0:T(8,128)(2,1)} %slice.144), channel_id=1, source_target_pairs={{0,4},{4,0},{1,5},{5,1},{2,6},{6,2},{3,7},{7,3}} | collective-permute-start | bytes 6291464 | tf_op jit(solution)/shard_map/ppermute | solution.py:242
  483.6 882.5 %collective-permute-start.6 = (bf16[2048,1024]{1,0:T(8,128)(2,1)}, bf16[2048,1024]{1,0:T(8,128)(2,1)}, u32[]{:S(2)}, u32[]{:S(2)}) collective-permute-start(bf16[2048,1024]{1,0:T(8,128)(2,1)} %get-tuple-element.167), channel_id=1, source_target_pairs={{0,4},{4,0},{1,5},{5,1},{2,6},{6,2},{3,7},{7,3}} | collective-permute-start | bytes 12582920 | tf_op jit(solution)/shard_map/ppermute | solution.py:242
  530.7 451.2 %collective-permute-start.15 = (bf16[2048,2816]{1,0:T(8,128)(2,1)}, bf16[2048,2816]{1,0:T(8,128)(2,1)}, u32[]{:S(2)}, u32[]{:S(2)}) collective-permute-start(bf16[2048,2816]{1,0:T(8,128)(2,1)} %get-tuple-element.152), channel_id=1, source_target_pairs={{0,4},{4,0},{1,5},{5,1},{2,6},{6,2},{3,7},{7,3}} | collective-permute-start | bytes 34603016 | tf_op jit(solution)/shard_map/ppermute | solution.py:242
  982.0 137.2 %collective-permute-start.7 = (bf16[2048,1024]{1,0:T(8,128)(2,1)}, bf16[2048,1024]{1,0:T(8,128)(2,1)}, u32[]{:S(2)}, u32[]{:S(2)}) collective-permute-start(bf16[2048,1024]{1,0:T(8,128)(2,1)} %get-tuple-element.166), channel_id=1, source_target_pairs={{0,4},{4,0},{1,5},{5,1},{2,6},{6,2},{3,7},{7,3}} | collective-permute-start | bytes 12582920 | tf_op jit(solution)/shard_map/ppermute | solution.py:242
  983.7 215.6 %collective-permute-start.16 = (bf16[2816,1024]{1,0:T(8,128)(2,1)}, bf16[2816,1024]{1,0:T(8,128)(2,1)}, u32[]{:S(2)}, u32[]{:S(2)}) collective-permute-start(bf16[2816,1024]{1,0:T(8,128)(2,1)} %get-tuple-element.165), channel_id=1, source_target_pairs={{0,4},{4,0},{1,5},{5,1},{2,6},{6,2},{3,7},{7,3}} | collective-permute-start | bytes 17301512 | tf_op jit(solution)/shard_map/ppermute | solution.py:242
  1119.1 203.7 %collective-permute-start.20 = (bf16[2816,1024]{1,0:T(8,128)(2,1)}, bf16[2816,1024]{1,0:T(8,128)(2,1)}, u32[]{:S(2)}, u32[]{:S(2)}) collective-permute-start(bf16[2816,1024]{1,0:T(8,128)(2,1)} %get-tuple-element.164), channel_id=1, source_target_pairs={{0,4},{4,0},{1,5},{5,1},{2,6},{6,2},{3,7},{7,3}} | collective-permute-start | bytes 17301512 | tf_op jit(solution)/shard_map/ppermute | solution.py:242
  1199.3 341.2 %collective-permute-start.11 = (bf16[2816,128]{1,0:T(8,128)(2,1)}, bf16[2816,128]{1,0:T(8,128)(2,1)}, u32[]{:S(2)}, u32[]{:S(2)}) collective-permute-start(bf16[2816,128]{1,0:T(8,128)(2,1)} %get-tuple-element.157), channel_id=1, source_target_pairs={{0,4},{4,0},{1,5},{5,1},{2,6},{6,2},{3,7},{7,3}} | collective-permute-start | bytes 2162696 | tf_op jit(solution)/shard_map/ppermute | solution.py:242
  1322.9 43.2 %copy-start.5 = (bf16[2816,256]{1,0:T(8,128)(2,1)S(1)}, bf16[2816,256]{1,0:T(8,128)(2,1)}, u32[]{:S(2)}) copy-start(bf16[2816,256]{1,0:T(8,128)(2,1)} %get-tuple-element.163) | copy-start | bytes 4325380
  1322.9 236.0 %collective-permute-start.24 = (bf16[2816,128]{1,0:T(8,128)(2,1)}, bf16[2816,128]{1,0:T(8,128)(2,1)}, u32[]{:S(2)}, u32[]{:S(2)}) collective-permute-start(bf16[2816,128]{1,0:T(8,128)(2,1)} %get-tuple-element.156), channel_id=1, source_target_pairs={{0,4},{4,0},{1,5},{5,1},{2,6},{6,2},{3,7},{7,3}} | collective-permute-start | bytes 2162696 | tf_op jit(solution)/shard_map/ppermute | solution.py:242
  1366.1 116.2 %collective-permute-start.28 = (bf16[2816,256]{1,0:T(8,128)(2,1)S(1)}, bf16[2816,256]{1,0:T(8,128)(2,1)}, u32[]{:S(2)}, u32[]{:S(2)}) collective-permute-start(bf16[2816,256]{1,0:T(8,128)(2,1)S(1)} %copy-done.5), channel_id=1, source_target_pairs={{0,4},{4,0},{1,5},{5,1},{2,6},{6,2},{3,7},{7,3}} | collective-permute-start | bytes 4325384 | tf_op jit(solution)/shard_map/ppermute | solution.py:242
  1423.1 79.1 %collective-permute-start.32 = (bf16[2816,256]{1,0:T(8,128)(2,1)}, bf16[2816,256]{1,0:T(8,128)(2,1)}, u32[]{:S(2)}, u32[]{:S(2)}) collective-permute-start(bf16[2816,256]{1,0:T(8,128)(2,1)} %get-tuple-element.162), channel_id=1, source_target_pairs={{0,4},{4,0},{1,5},{5,1},{2,6},{6,2},{3,7},{7,3}} | collective-permute-start | bytes 4325384 | tf_op jit(solution)/shard_map/ppermute | solution.py:242
  1459.3 61.5 %collective-permute-start.36 = (bf16[2816,256]{1,0:T(8,128)(2,1)S(1)}, bf16[2816,256]{1,0:T(8,128)(2,1)}, u32[]{:S(2)}, u32[]{:S(2)}) collective-permute-start(bf16[2816,256]{1,0:T(8,128)(2,1)S(1)} %copy-done.4), channel_id=1, source_target_pairs={{0,4},{4,0},{1,5},{5,1},{2,6},{6,2},{3,7},{7,3}} | collective-permute-start | bytes 4325384 | tf_op jit(solution)/shard_map/ppermute | solution.py:242
  1482.3 58.6 %collective-permute-start.40 = (bf16[2816,256]{1,0:T(8,128)(2,1)}, bf16[2816,256]{1,0:T(8,128)(2,1)}, u32[]{:S(2)}, u32[]{:S(2)}) collective-permute-start(bf16[2816,256]{1,0:T(8,128)(2,1)} %get-tuple-element.160), channel_id=1, source_target_pairs={{0,4},{4,0},{1,5},{5,1},{2,6},{6,2},{3,7},{7,3}} | collective-permute-start | bytes 4325384 | tf_op jit(solution)/shard_map/ppermute | solution.py:242
  1502.2 85.7 %collective-permute-start.44 = (bf16[2816,256]{1,0:T(8,128)(2,1)S(1)}, bf16[2816,256]{1,0:T(8,128)(2,1)}, u32[]{:S(2)}, u32[]{:S(2)}) collective-permute-start(bf16[2816,256]{1,0:T(8,128)(2,1)S(1)} %copy-done.3), channel_id=1, source_target_pairs={{0,4},{4,0},{1,5},{5,1},{2,6},{6,2},{3,7},{7,3}} | collective-permute-start | bytes 4325384 | tf_op jit(solution)/shard_map/ppermute | solution.py:242
  1520.8 50.2 %collective-permute-start.52 = (bf16[2816,128]{1,0:T(8,128)(2,1)}, bf16[2816,128]{1,0:T(8,128)(2,1)S(1)}, u32[]{:S(2)}, u32[]{:S(2)}) collective-permute-start(bf16[2816,128]{1,0:T(8,128)(2,1)} %get-tuple-element.155), channel_id=1, source_target_pairs={{0,4},{4,0},{1,5},{5,1},{2,6},{6,2},{3,7},{7,3}} | collective-permute-start | bytes 2162696 | tf_op jit(solution)/shard_map/ppermute | solution.py:242
  1540.5 84.4 %collective-permute-start.48 = (bf16[2816,256]{1,0:T(8,128)(2,1)S(1)}, bf16[2816,256]{1,0:T(8,128)(2,1)}, u32[]{:S(2)}, u32[]{:S(2)}) collective-permute-start(bf16[2816,256]{1,0:T(8,128)(2,1)S(1)} %copy-done.2), channel_id=1, source_target_pairs={{0,4},{4,0},{1,5},{5,1},{2,6},{6,2},{3,7},{7,3}} | collective-permute-start | bytes 4325384 | tf_op jit(solution)/shard_map/ppermute | solution.py:242
  1540.9 160.9 %collective-permute-start.21 = (bf16[2,640,1024]{2,1,0:T(8,128)(2,1)}, bf16[2,640,1024]{2,1,0:T(8,128)(2,1)}, u32[]{:S(2)}, u32[]{:S(2)}) collective-permute-start(bf16[2,640,1024]{2,1,0:T(8,128)(2,1)} %get-tuple-element.93), channel_id=1, source_target_pairs={{0,1},{1,0},{2,3},{3,2},{4,5},{5,4},{6,7},{7,6}} | collective-permute-start | bytes 7864328 | tf_op jit(solution)/shard_map/ppermute | solution.py:239
  1558.8 161.1 %collective-permute-start.22 = (bf16[2,640,1024]{2,1,0:T(8,128)(2,1)}, bf16[2,640,1024]{2,1,0:T(8,128)(2,1)}, u32[]{:S(2)}, u32[]{:S(2)}) collective-permute-start(bf16[2,640,1024]{2,1,0:T(8,128)(2,1)} %get-tuple-element.94), channel_id=1, source_target_pairs={{0,2},{1,3},{2,0},{3,1},{4,6},{5,7},{6,4},{7,5}} | collective-permute-start | bytes 7864328 | tf_op jit(solution)/shard_map/ppermute | solution.py:239
  1571.0 150.3 %collective-permute-start.23 = (bf16[2,640,1024]{2,1,0:T(8,128)(2,1)}, bf16[2,640,1024]{2,1,0:T(8,128)(2,1)}, u32[]{:S(2)}, u32[]{:S(2)}) collective-permute-start(bf16[2,640,1024]{2,1,0:T(8,128)(2,1)} %get-tuple-element.95), channel_id=1, source_target_pairs={{0,3},{1,2},{2,1},{3,0},{4,7},{5,6},{6,5},{7,4}} | collective-permute-start | bytes 7864328 | tf_op jit(solution)/shard_map/ppermute | solution.py:239
  1587.9 35.4 %collective-permute-start.56 = (bf16[2816,128]{1,0:T(8,128)(2,1)}, bf16[2816,128]{1,0:T(8,128)(2,1)S(1)}, u32[]{:S(2)}, u32[]{:S(2)}) collective-permute-start(bf16[2816,128]{1,0:T(8,128)(2,1)} %get-tuple-element.154), channel_id=1, source_target_pairs={{0,4},{4,0},{1,5},{5,1},{2,6},{6,2},{3,7},{7,3}} | collective-permute-start | bytes 2162696 | tf_op jit(solution)/shard_map/ppermute | solution.py:242
  1623.4 19.0 collective-permute-start.53
  1624.9 57.1 %collective-permute-start.54 = (bf16[2,640,128]{2,1,0:T(8,128)(2,1)S(1)}, bf16[2,640,128]{2,1,0:T(8,128)(2,1)S(1)}, u32[]{:S(2)}, u32[]{:S(2)}) collective-permute-start(bf16[2,640,128]{2,1,0:T(8,128)(2,1)S(1)} %copy-done.37), channel_id=1, source_target_pairs={{0,2},{1,3},{2,0},{3,1},{4,6},{5,7},{6,4},{7,5}} | collective-permute-start | bytes 983048 | tf_op jit(solution)/shard_map/ppermute | solution.py:239
  1642.4 56.5 %copy-start.19 = (bf16[2,640,128]{2,1,0:T(8,128)(2,1)}, bf16[2,640,128]{2,1,0:T(8,128)(2,1)S(1)}, u32[]{:S(2)}) copy-start(bf16[2,640,128]{2,1,0:T(8,128)(2,1)S(1)} %collective-permute-done.53.refs_1_) | copy-start | bytes 983044
  1642.5 56.5 %collective-permute-start.55 = (bf16[2,640,128]{2,1,0:T(8,128)(2,1)S(1)}, bf16[2,640,128]{2,1,0:T(8,128)(2,1)S(1)}, u32[]{:S(2)}, u32[]{:S(2)}) collective-permute-start(bf16[2,640,128]{2,1,0:T(8,128)(2,1)S(1)} %copy-done.36), channel_id=1, source_target_pairs={{0,3},{1,2},{2,1},{3,0},{4,7},{5,6},{6,5},{7,4}} | collective-permute-start | bytes 983048 | tf_op jit(solution)/shard_map/ppermute | solution.py:239
  1682.0 18.1 collective-permute-start.57
  1699.6 130.3 %collective-permute-start.17 = (bf16[2,640,1024]{2,1,0:T(8,128)(2,1)}, bf16[2,640,1024]{2,1,0:T(8,128)(2,1)S(1)}, u32[]{:S(2)}, u32[]{:S(2)}) collective-permute-start(bf16[2,640,1024]{2,1,0:T(8,128)(2,1)} %get-tuple-element.89), channel_id=1, source_target_pairs={{0,1},{1,0},{2,3},{3,2},{4,5},{5,4},{6,7},{7,6}} | collective-permute-start | bytes 7864328 | tf_op jit(solution)/shard_map/ppermute | solution.py:239
  1700.1 129.8 %collective-permute-start.18 = (bf16[2,640,1024]{2,1,0:T(8,128)(2,1)}, bf16[2,640,1024]{2,1,0:T(8,128)(2,1)}, u32[]{:S(2)}, u32[]{:S(2)}) collective-permute-start(bf16[2,640,1024]{2,1,0:T(8,128)(2,1)} %get-tuple-element.90), channel_id=1, source_target_pairs={{0,2},{1,3},{2,0},{3,1},{4,6},{5,7},{6,4},{7,5}} | collective-permute-start | bytes 7864328 | tf_op jit(solution)/shard_map/ppermute | solution.py:239
  1701.8 129.8 %collective-permute-start.19 = (bf16[2,640,1024]{2,1,0:T(8,128)(2,1)}, bf16[2,640,1024]{2,1,0:T(8,128)(2,1)}, u32[]{:S(2)}, u32[]{:S(2)}) collective-permute-start(bf16[2,640,1024]{2,1,0:T(8,128)(2,1)} %get-tuple-element.91), channel_id=1, source_target_pairs={{0,3},{1,2},{2,1},{3,0},{4,7},{5,6},{6,5},{7,4}} | collective-permute-start | bytes 7864328 | tf_op jit(solution)/shard_map/ppermute | solution.py:239
  1720.0 103.3 %collective-permute-start.58 = (bf16[2,640,128]{2,1,0:T(8,128)(2,1)S(1)}, bf16[2,640,128]{2,1,0:T(8,128)(2,1)S(1)}, u32[]{:S(2)}, u32[]{:S(2)}) collective-permute-start(bf16[2,640,128]{2,1,0:T(8,128)(2,1)S(1)} %copy-done.35), channel_id=1, source_target_pairs={{0,2},{1,3},{2,0},{3,1},{4,6},{5,7},{6,4},{7,5}} | collective-permute-start | bytes 983048 | tf_op jit(solution)/shard_map/ppermute | solution.py:239
  1721.3 107.2 %collective-permute-start.59 = (bf16[2,640,128]{2,1,0:T(8,128)(2,1)S(1)}, bf16[2,640,128]{2,1,0:T(8,128)(2,1)S(1)}, u32[]{:S(2)}, u32[]{:S(2)}) collective-permute-start(bf16[2,640,128]{2,1,0:T(8,128)(2,1)S(1)} %copy-done.34), channel_id=1, source_target_pairs={{0,3},{1,2},{2,1},{3,0},{4,7},{5,6},{6,5},{7,4}} | collective-permute-start | bytes 983048 | tf_op jit(solution)/shard_map/ppermute | solution.py:239
  1824.0 51.8 %collective-permute-start.33 = (bf16[2,640,256]{2,1,0:T(8,128)(2,1)}, bf16[2,640,256]{2,1,0:T(8,128)(2,1)S(1)}, u32[]{:S(2)}, u32[]{:S(2)}) collective-permute-start(bf16[2,640,256]{2,1,0:T(8,128)(2,1)} %get-tuple-element.105), channel_id=1, source_target_pairs={{0,1},{1,0},{2,3},{3,2},{4,5},{5,4},{6,7},{7,6}} | collective-permute-start | bytes 1966088 | tf_op jit(solution)/shard_map/ppermute | solution.py:239
  1829.3 46.9 %collective-permute-start.41 = (bf16[2,640,256]{2,1,0:T(8,128)(2,1)}, bf16[2,640,256]{2,1,0:T(8,128)(2,1)S(1)}, u32[]{:S(2)}, u32[]{:S(2)}) collective-permute-start(bf16[2,640,256]{2,1,0:T(8,128)(2,1)} %get-tuple-element.113), channel_id=1, source_target_pairs={{0,1},{1,0},{2,3},{3,2},{4,5},{5,4},{6,7},{7,6}} | collective-permute-start | bytes 1966088 | tf_op jit(solution)/shard_map/ppermute | solution.py:239
  1829.9 47.8 %collective-permute-start.49 = (bf16[2,640,256]{2,1,0:T(8,128)(2,1)}, bf16[2,640,256]{2,1,0:T(8,128)(2,1)}, u32[]{:S(2)}, u32[]{:S(2)}) collective-permute-start(bf16[2,640,256]{2,1,0:T(8,128)(2,1)} %get-tuple-element.121), channel_id=1, source_target_pairs={{0,1},{1,0},{2,3},{3,2},{4,5},{5,4},{6,7},{7,6}} | collective-permute-start | bytes 1966088 | tf_op jit(solution)/shard_map/ppermute | solution.py:239
  1830.0 58.7 %collective-permute-start.50 = (bf16[2,640,256]{2,1,0:T(8,128)(2,1)}, bf16[2,640,256]{2,1,0:T(8,128)(2,1)}, u32[]{:S(2)}, u32[]{:S(2)}) collective-permute-start(bf16[2,640,256]{2,1,0:T(8,128)(2,1)} %get-tuple-element.122), channel_id=1, source_target_pairs={{0,2},{1,3},{2,0},{3,1},{4,6},{5,7},{6,4},{7,5}} | collective-permute-start | bytes 1966088 | tf_op jit(solution)/shard_map/ppermute | solution.py:239
  1831.6 58.6 %collective-permute-start.51 = (bf16[2,640,256]{2,1,0:T(8,128)(2,1)}, bf16[2,640,256]{2,1,0:T(8,128)(2,1)}, u32[]{:S(2)}, u32[]{:S(2)}) collective-permute-start(bf16[2,640,256]{2,1,0:T(8,128)(2,1)} %get-tuple-element.123), channel_id=1, source_target_pairs={{0,3},{1,2},{2,1},{3,0},{4,7},{5,6},{6,5},{7,4}} | collective-permute-start | bytes 1966088 | tf_op jit(solution)/shard_map/ppermute | solution.py:239
  1875.8 27.0 %collective-permute-start.45 = (bf16[2,640,256]{2,1,0:T(8,128)(2,1)S(1)}, bf16[2,640,256]{2,1,0:T(8,128)(2,1)S(1)}, u32[]{:S(2)}, u32[]{:S(2)}) collective-permute-start(bf16[2,640,256]{2,1,0:T(8,128)(2,1)S(1)} %copy-done.33), channel_id=1, source_target_pairs={{0,1},{1,0},{2,3},{3,2},{4,5},{5,4},{6,7},{7,6}} | collective-permute-start | bytes 1966088 | tf_op jit(solution)/shard_map/ppermute | solution.py:239
  1876.2 27.0 %collective-permute-start.46 = (bf16[2,640,256]{2,1,0:T(8,128)(2,1)}, bf16[2,640,256]{2,1,0:T(8,128)(2,1)S(1)}, u32[]{:S(2)}, u32[]{:S(2)}) collective-permute-start(bf16[2,640,256]{2,1,0:T(8,128)(2,1)} %get-tuple-element.118), channel_id=1, source_target_pairs={{0,2},{1,3},{2,0},{3,1},{4,6},{5,7},{6,4},{7,5}} | collective-permute-start | bytes 1966088 | tf_op jit(solution)/shard_map/ppermute | solution.py:239
  1877.8 29.5 %collective-permute-start.47 = (bf16[2,640,256]{2,1,0:T(8,128)(2,1)}, bf16[2,640,256]{2,1,0:T(8,128)(2,1)}, u32[]{:S(2)}, u32[]{:S(2)}) collective-permute-start(bf16[2,640,256]{2,1,0:T(8,128)(2,1)} %get-tuple-element.119), channel_id=1, source_target_pairs={{0,3},{1,2},{2,1},{3,0},{4,7},{5,6},{6,5},{7,4}} | collective-permute-start | bytes 1966088 | tf_op jit(solution)/shard_map/ppermute | solution.py:239
  1888.7 33.4 %collective-permute-start.42 = (bf16[2,640,256]{2,1,0:T(8,128)(2,1)}, bf16[2,640,256]{2,1,0:T(8,128)(2,1)S(1)}, u32[]{:S(2)}, u32[]{:S(2)}) collective-permute-start(bf16[2,640,256]{2,1,0:T(8,128)(2,1)} %get-tuple-element.114), channel_id=1, source_target_pairs={{0,2},{1,3},{2,0},{3,1},{4,6},{5,7},{6,4},{7,5}} | collective-permute-start | bytes 1966088 | tf_op jit(solution)/shard_map/ppermute | solution.py:239
  1890.2 45.1 %collective-permute-start.43 = (bf16[2,640,256]{2,1,0:T(8,128)(2,1)}, bf16[2,640,256]{2,1,0:T(8,128)(2,1)}, u32[]{:S(2)}, u32[]{:S(2)}) collective-permute-start(bf16[2,640,256]{2,1,0:T(8,128)(2,1)} %get-tuple-element.115), channel_id=1, source_target_pairs={{0,3},{1,2},{2,1},{3,0},{4,7},{5,6},{6,5},{7,4}} | collective-permute-start | bytes 1966088 | tf_op jit(solution)/shard_map/ppermute | solution.py:239
  1902.9 46.7 %collective-permute-start.37 = (bf16[2,640,256]{2,1,0:T(8,128)(2,1)}, bf16[2,640,256]{2,1,0:T(8,128)(2,1)S(1)}, u32[]{:S(2)}, u32[]{:S(2)}) collective-permute-start(bf16[2,640,256]{2,1,0:T(8,128)(2,1)} %get-tuple-element.109), channel_id=1, source_target_pairs={{0,1},{1,0},{2,3},{3,2},{4,5},{5,4},{6,7},{7,6}} | collective-permute-start | bytes 1966088 | tf_op jit(solution)/shard_map/ppermute | solution.py:239
  1903.2 47.0 %collective-permute-start.38 = (bf16[2,640,256]{2,1,0:T(8,128)(2,1)}, bf16[2,640,256]{2,1,0:T(8,128)(2,1)S(1)}, u32[]{:S(2)}, u32[]{:S(2)}) collective-permute-start(bf16[2,640,256]{2,1,0:T(8,128)(2,1)} %get-tuple-element.110), channel_id=1, source_target_pairs={{0,2},{1,3},{2,0},{3,1},{4,6},{5,7},{6,4},{7,5}} | collective-permute-start | bytes 1966088 | tf_op jit(solution)/shard_map/ppermute | solution.py:239
  1907.3 56.2 %collective-permute-start.39 = (bf16[2,640,256]{2,1,0:T(8,128)(2,1)}, bf16[2,640,256]{2,1,0:T(8,128)(2,1)}, u32[]{:S(2)}, u32[]{:S(2)}) collective-permute-start(bf16[2,640,256]{2,1,0:T(8,128)(2,1)} %get-tuple-element.111), channel_id=1, source_target_pairs={{0,3},{1,2},{2,1},{3,0},{4,7},{5,6},{6,5},{7,4}} | collective-permute-start | bytes 1966088 | tf_op jit(solution)/shard_map/ppermute | solution.py:239
  1922.1 56.2 %collective-permute-start.34 = (bf16[2,640,256]{2,1,0:T(8,128)(2,1)}, bf16[2,640,256]{2,1,0:T(8,128)(2,1)S(1)}, u32[]{:S(2)}, u32[]{:S(2)}) collective-permute-start(bf16[2,640,256]{2,1,0:T(8,128)(2,1)} %get-tuple-element.106), channel_id=1, source_target_pairs={{0,2},{1,3},{2,0},{3,1},{4,6},{5,7},{6,4},{7,5}} | collective-permute-start | bytes 1966088 | tf_op jit(solution)/shard_map/ppermute | solution.py:239
  1935.3 56.2 %collective-permute-start.35 = (bf16[2,640,256]{2,1,0:T(8,128)(2,1)}, bf16[2,640,256]{2,1,0:T(8,128)(2,1)}, u32[]{:S(2)}, u32[]{:S(2)}) collective-permute-start(bf16[2,640,256]{2,1,0:T(8,128)(2,1)} %get-tuple-element.107), channel_id=1, source_target_pairs={{0,3},{1,2},{2,1},{3,0},{4,7},{5,6},{6,5},{7,4}} | collective-permute-start | bytes 1966088 | tf_op jit(solution)/shard_map/ppermute | solution.py:239
  1949.6 56.6 %collective-permute-start.29 = (bf16[2,640,256]{2,1,0:T(8,128)(2,1)}, bf16[2,640,256]{2,1,0:T(8,128)(2,1)S(1)}, u32[]{:S(2)}, u32[]{:S(2)}) collective-permute-start(bf16[2,640,256]{2,1,0:T(8,128)(2,1)} %get-tuple-element.101), channel_id=1, source_target_pairs={{0,1},{1,0},{2,3},{3,2},{4,5},{5,4},{6,7},{7,6}} | collective-permute-start | bytes 1966088 | tf_op jit(solution)/shard_map/ppermute | solution.py:239
  1950.1 56.2 %collective-permute-start.30 = (bf16[2,640,256]{2,1,0:T(8,128)(2,1)}, bf16[2,640,256]{2,1,0:T(8,128)(2,1)S(1)}, u32[]{:S(2)}, u32[]{:S(2)}) collective-permute-start(bf16[2,640,256]{2,1,0:T(8,128)(2,1)} %get-tuple-element.102), channel_id=1, source_target_pairs={{0,2},{1,3},{2,0},{3,1},{4,6},{5,7},{6,4},{7,5}} | collective-permute-start | bytes 1966088 | tf_op jit(solution)/shard_map/ppermute | solution.py:239
  1963.4 56.2 %collective-permute-start.31 = (bf16[2,640,256]{2,1,0:T(8,128)(2,1)}, bf16[2,640,256]{2,1,0:T(8,128)(2,1)S(1)}, u32[]{:S(2)}, u32[]{:S(2)}) collective-permute-start(bf16[2,640,256]{2,1,0:T(8,128)(2,1)} %get-tuple-element.103), channel_id=1, source_target_pairs={{0,3},{1,2},{2,1},{3,0},{4,7},{5,6},{6,5},{7,4}} | collective-permute-start | bytes 1966088 | tf_op jit(solution)/shard_map/ppermute | solution.py:239
  1978.2 80.3 %collective-permute-start.12 = (bf16[2,640,128]{2,1,0:T(8,128)(2,1)}, bf16[2,640,128]{2,1,0:T(8,128)(2,1)S(1)}, u32[]{:S(2)}, u32[]{:S(2)}) collective-permute-start(bf16[2,640,128]{2,1,0:T(8,128)(2,1)} %get-tuple-element.85), channel_id=1, source_target_pairs={{0,1},{1,0},{2,3},{3,2},{4,5},{5,4},{6,7},{7,6}} | collective-permute-start | bytes 983048 | tf_op jit(solution)/shard_map/ppermute | solution.py:239
  1991.5 13.0 collective-permute-start.25
  2004.5 29.2 %copy-start.26 = (bf16[2,640,128]{2,1,0:T(8,128)(2,1)}, bf16[2,640,128]{2,1,0:T(8,128)(2,1)S(1)}, u32[]{:S(2)}) copy-start(bf16[2,640,128]{2,1,0:T(8,128)(2,1)S(1)} %collective-permute-done.25.refs_1_) | copy-start | bytes 983044
  2004.5 54.0 %collective-permute-start.13 = (bf16[2,640,128]{2,1,0:T(8,128)(2,1)}, bf16[2,640,128]{2,1,0:T(8,128)(2,1)S(1)}, u32[]{:S(2)}, u32[]{:S(2)}) collective-permute-start(bf16[2,640,128]{2,1,0:T(8,128)(2,1)} %get-tuple-element.86), channel_id=1, source_target_pairs={{0,2},{1,3},{2,0},{3,1},{4,6},{5,7},{6,4},{7,5}} | collective-permute-start | bytes 983048 | tf_op jit(solution)/shard_map/ppermute | solution.py:239
  2006.2 52.4 %collective-permute-start.14 = (bf16[2,640,128]{2,1,0:T(8,128)(2,1)}, bf16[2,640,128]{2,1,0:T(8,128)(2,1)S(1)}, u32[]{:S(2)}, u32[]{:S(2)}) collective-permute-start(bf16[2,640,128]{2,1,0:T(8,128)(2,1)} %get-tuple-element.87), channel_id=1, source_target_pairs={{0,3},{1,2},{2,1},{3,0},{4,7},{5,6},{6,5},{7,4}} | collective-permute-start | bytes 983048 | tf_op jit(solution)/shard_map/ppermute | solution.py:239
  2006.3 35.1 %collective-permute-start.26 = (bf16[2,640,128]{2,1,0:T(8,128)(2,1)}, bf16[2,640,128]{2,1,0:T(8,128)(2,1)S(1)}, u32[]{:S(2)}, u32[]{:S(2)}) collective-permute-start(bf16[2,640,128]{2,1,0:T(8,128)(2,1)} %get-tuple-element.98), channel_id=1, source_target_pairs={{0,2},{1,3},{2,0},{3,1},{4,6},{5,7},{6,4},{7,5}} | collective-permute-start | bytes 983048 | tf_op jit(solution)/shard_map/ppermute | solution.py:239
  2019.6 27.3 %collective-permute-start.27 = (bf16[2,640,128]{2,1,0:T(8,128)(2,1)}, bf16[2,640,128]{2,1,0:T(8,128)(2,1)S(1)}, u32[]{:S(2)}, u32[]{:S(2)}) collective-permute-start(bf16[2,640,128]{2,1,0:T(8,128)(2,1)} %get-tuple-element.99), channel_id=1, source_target_pairs={{0,3},{1,2},{2,1},{3,0},{4,7},{5,6},{6,5},{7,4}} | collective-permute-start | bytes 983048 | tf_op jit(solution)/shard_map/ppermute | solution.py:239
  (41 other events, 453.6 us)

commit v2 on v1

v2 whole, which is shorter than its diff:
```python
import functools

import jax
import jax.numpy as jnp
from jax import lax
from jax.experimental import pallas as pl
from jax.experimental.pallas import tpu as pltpu
from jax.sharding import PartitionSpec as P


TP_SWAP = [(0, 1), (1, 0)]
BF16 = jnp.bfloat16
F32 = jnp.float32
MASKS = 4
TN = 256
TB = 512
VMEM_LIMIT = 60 * 1024 * 1024


def mm(a, b):
    return jnp.dot(a, b, preferred_element_type=F32)


def call(kernel, flops, nbytes, **kw):
    params = pltpu.CompilerParams(vmem_limit_bytes=VMEM_LIMIT)
    cost = pl.CostEstimate(flops=int(flops), bytes_accessed=int(nbytes), transcendentals=0)
    return pl.pallas_call(kernel, compiler_params=params, cost_estimate=cost, **kw)


def filled_further(into, args, in_specs):
    if into is None:
        return {}
    args.append(into)
    in_specs.append(pl.BlockSpec(memory_space=pl.ANY))
    return {"input_output_aliases": {len(args) - 1: 0}}


def dispatch_kernel(pos_ref, tok_ref, *outs):
    step = pl.program_id(0)
    cap, model = outs[0].shape[1:]
    slots = lax.broadcasted_iota(jnp.int32, (cap, tok_ref.shape[0]), 0)
    onehot = (slots == pos_ref[0]).astype(BF16)
    for lo in range(0, model, 512):
        rows = mm(onehot, tok_ref[:, lo:lo + 512]).astype(BF16)
        for m, out in enumerate(outs):

            @pl.when(step // 2 == m)
            def _():
                out[0, :, lo:lo + 512] = rows


def dispatch(pos, tokens, cap):
    n = pos.shape[0] // 2
    toks, model = tokens.shape
    out = jax.ShapeDtypeStruct((2, cap, model), BF16)
    return call(
        dispatch_kernel, 2 * n * 2 * cap * toks * model, toks * model * 2 + 2 * n * cap * model * 2,
        grid=(2 * n,),
        in_specs=[pl.BlockSpec((1, 1, toks), lambda i: (i, 0, 0)), pl.BlockSpec((toks, model), lambda i: (0, 0))],
        out_specs=[pl.BlockSpec((1, cap, model), functools.partial(lambda m, i: (jnp.clip(i - 2 * m, 0, 1), 0, 0), m)) for m in range(n)],
        out_shape=[out] * n,
    )(pos, tokens)


def hidden_kernel(*refs):
    xs, (wg, wu), h = refs[:MASKS], refs[MASKS:MASKS + 2], refs[-1]
    g = wg[...].reshape(wg.shape[-2:])
    u = wu[...].reshape(wu.shape[-2:])
    for m in range(MASKS):
        x = xs[m][0]
        a = mm(x, g)
        h[0, m] = (a * jax.nn.sigmoid(a) * mm(x, u)).astype(BF16)


def hidden_local(xs, wg, wu):
    _, cap, model = xs[0].shape
    width = wg.shape[2]
    rows = 2 * MASKS * cap
    return call(
        hidden_kernel, 4 * rows * model * width, 2 * (rows * model + 4 * model * width + rows * width),
        grid=(2, width // TN),
        in_specs=[pl.BlockSpec((1, cap, model), lambda k, n: (k, 0, 0)) for _ in xs]
        + [pl.BlockSpec((1, model, TN), lambda k, n: (k, 0, n))] * 2,
        out_specs=pl.BlockSpec((1, MASKS, cap, TN), lambda k, n: (k, 0, 0, n)),
        out_shape=jax.ShapeDtypeStruct((2, MASKS, cap, width), BF16),
    )(*xs, wg, wu)


def hidden(xs, b, k, wg, wu, lo, into):
    _, cap, model = xs[0].shape
    width, cols = wg.shape[1], wu.shape[1]
    off, steps = lo // TN, cols // TN
    in_specs = [pl.BlockSpec((1, cap, model), lambda n: (k, 0, 0)) for _ in xs]
    in_specs += [pl.BlockSpec((model, TN), lambda n: (0, n + off)), pl.BlockSpec((model, TN), lambda n: (0, n))]
    args = [*xs, wg, wu]
    kw = filled_further(into, args, in_specs)
    rows = MASKS * cap
    return call(
        hidden_kernel, 4 * rows * model * cols, 2 * (rows * model + 2 * model * cols + rows * cols),
        grid=(steps,), in_specs=in_specs,
        out_specs=pl.BlockSpec((1, MASKS, cap, TN), lambda n: (b, 0, 0, n + off)),
        out_shape=jax.ShapeDtypeStruct((2, MASKS, cap, width), BF16), **kw,
    )(*args)


def part_kernel(h, wd, *refs):
    for m in range(MASKS):
        refs[-1][0, 0, m] = mm(h[0, m], wd[0])


def part(h, b, wd, into):
    _, _, cap, width = h.shape
    model = wd.shape[2]
    rows = 2 * MASKS * cap
    in_specs = [pl.BlockSpec((1, MASKS, cap, width), lambda k, n: (k, 0, 0, 0)), pl.BlockSpec((1, width, TN), lambda k, n: (k, 0, n))]
    args = [h, wd]
    kw = filled_further(into, args, in_specs)
    return call(
        part_kernel, 2 * rows * width * model, 2 * (rows * width + 2 * width * model) + 4 * rows * model,
        grid=(2, model // TN), in_specs=in_specs,
        out_specs=pl.BlockSpec((1, 1, MASKS, cap, TN), lambda k, n: (k, b, 0, 0, n)),
        out_shape=jax.ShapeDtypeStruct((2, 2, MASKS, cap, model), F32), **kw,
    )(*args)


def final_kernel(h, p, wd, *outs):
    m = pl.program_id(0) % len(outs)
    cap = h.shape[2]
    for lo in range(0, cap, cap // 2):
        rows = slice(lo, lo + cap // 2)
        y = (p[0, 0, 0, rows] + mm(h[0, 0, rows], wd[...])).astype(BF16)
        for j, out in enumerate(outs):

            @pl.when(m == j)
            def _():
                out[0, rows] = y


def final(h, p, k, wd, lo, masks):
    _, _, cap, width = h.shape
    cols = wd.shape[1]
    at, n, m0 = lo // cols, len(masks), masks[0]
    rows = 2 * n * cap
    return call(
        final_kernel, 2 * rows * width * cols, 2 * (rows * width + width * cols) + 6 * rows * cols,
        grid=(2 * n,),
        in_specs=[
            pl.BlockSpec((1, 1, cap, width), lambda i: (i // n, m0 + i % n, 0, 0)),
            pl.BlockSpec((1, 1, 1, cap, cols), lambda i: (k, i // n, m0 + i % n, 0, at)),
            pl.BlockSpec((width, cols), lambda i: (0, 0)),
        ],
        out_specs=[pl.BlockSpec((1, cap, cols), functools.partial(lambda m, i: (jnp.where(i >= n + m, 1, 0), 0, 0), m)) for m in range(n)],
        out_shape=[jax.ShapeDtypeStruct((2, cap, cols), BF16)] * n,
    )(h, p, wd)


def picked(k, ys, pick, gate):
    total = None
    for m in range(MASKS):
        e = 2 * m + k
        term = gate[0, :, e:e + 1] * mm(pick[0, m], ys[m][0])
        total = term if total is None else total + term
    return total


def combine_first_kernel(k, *refs):
    refs[-1][...] = picked(k, refs[:MASKS], refs[MASKS], refs[MASKS + 1])


def combine_kernel(k, *refs):
    acc, outs = refs[MASKS + 2], refs[-2:]
    i, blocks = pl.program_id(0), pl.num_programs(0) // 2
    total = (acc[...] + picked(k, refs[:MASKS], refs[MASKS], refs[MASKS + 1])).astype(BF16)
    for b, out in enumerate(outs):

        @pl.when(i // blocks == b)
        def _():
            out[...] = total


def combine(ys, pick, gate, k, lo, model, acc=None, into=None):
    _, cap, cols = ys[0].shape
    toks = pick.shape[2]
    blocks = toks // TB
    at = lo // cols
    in_specs = [pl.BlockSpec((1, cap, cols), lambda i: (i // blocks, 0, 0)) for _ in ys]
    in_specs += [
        pl.BlockSpec((1, MASKS, TB, cap), lambda i: (i // blocks, 0, i % blocks, 0)),
        pl.BlockSpec((1, TB, gate.shape[2]), lambda i: (i // blocks, i % blocks, 0)),
    ]
    args = [*ys, pick, gate]
    flops, nbytes = 2 * 2 * toks * MASKS * cap * cols, 2 * 2 * toks * MASKS * cap + 2 * toks * cols * 6
    if acc is None:
        kw = filled_further(into, args, in_specs)
        return call(
            functools.partial(combine_first_kernel, k), flops, nbytes,
            grid=(2 * blocks,), in_specs=in_specs,
            out_specs=pl.BlockSpec((TB, cols), lambda i: (i, at)),
            out_shape=jax.ShapeDtypeStruct((2 * toks, model), F32), **kw,
        )(*args)
    args.append(acc)
    in_specs.append(pl.BlockSpec((TB, cols), lambda i: (i, at)))
    kw = {}
    if into is not None:
        kw["input_output_aliases"] = {len(args): 0, len(args) + 1: 1}
        args += into
        in_specs += [pl.BlockSpec(memory_space=pl.ANY)] * 2
    return call(
        functools.partial(combine_kernel, k), flops, nbytes,
        grid=(2 * blocks,), in_specs=in_specs,
        out_specs=[
            pl.BlockSpec((TB, cols), lambda i: (jnp.minimum(i, blocks - 1), at)),
            pl.BlockSpec((TB, cols), lambda i: (jnp.maximum(i - blocks, 0), at)),
        ],
        out_shape=[jax.ShapeDtypeStruct((toks, model), BF16)] * 2, **kw,
    )(*args)


def cuts(sizes):
    out, at = [], 0
    for size in sizes:
        out.append((at, at + size))
        at += size
    return out


def solution(mesh):
    ep_size = mesh.shape["ep"]
    row_spec = P(("dp", "ep", "tp"), None)
    gate_spec = P("ep", None, "tp")
    down_spec = P("ep", "tp", None)
    up1_cuts = cuts([512, 1024, 1024, 256])
    down_cuts = [cuts([1024] + [256] * 4), cuts([256] * 7 + [128, 128])]
    late = [(0, n) for n in range(1, 5)] + [(1, n) for n in range(9)]
    halves = [(1, 7), (1, 8)]

    def ep_swap(value, mask):
        return lax.ppermute(value, "ep", [(i, i ^ mask) for i in range(ep_size)])

    def tp_swap(w, k, lo=0, hi=None):
        piece = lax.slice(w, (k, 0, lo), (k + 1, w.shape[1], w.shape[2] if hi is None else hi))
        return lax.ppermute(piece, "tp", TP_SWAP)[0]

    def routing(ids, gates, me):
        toks, top_k = ids.shape[1:]
        n_exp = 2 * ep_size
        mean_load = top_k * toks // n_exp
        cap = mean_load + mean_load // 4
        code = ((ids // 2) ^ me) * 2 + ids % 2
        hit = code[:, None] == jnp.arange(n_exp, dtype=jnp.int32)[None, :, None, None]
        has = jnp.any(hit, axis=3)
        count = has.astype(jnp.int32)
        pos = jnp.cumsum(count, axis=2) - count
        pos = jnp.where(has & (pos < cap), pos, -1)
        gate = jnp.sum(jnp.where(hit, gates[:, None], 0.0), axis=3)
        return pos, gate, cap

    def group_body(tokens_a, ids_a, gates_a, tokens_b, ids_b, gates_b, w_gate, w_up, w_down):
        me = lax.axis_index("ep")
        model = w_down.shape[2]
        up1 = [None] * len(up1_cuts)
        up1[0] = tp_swap(w_up, 1, *up1_cuts[0])
        gate0 = tp_swap(w_gate, 0)
        up0 = tp_swap(w_up, 0)
        down = [[None] * len(c) for c in down_cuts]
        down[0][0] = tp_swap(w_down, 0, *down_cuts[0][0])
        gate1 = tp_swap(w_gate, 1)
        for n, (lo, hi) in list(enumerate(up1_cuts))[1:]:
            up1[n] = tp_swap(w_up, 1, lo, hi)
        for k, n in late:
            lo, hi = down_cuts[k][n]
            down[k][n] = tp_swap(w_down, k, lo, hi)

        pos, gate, cap = routing(jnp.stack([ids_a, ids_b]), jnp.stack([gates_a, gates_b]), me)
        gate_t = gate.transpose(0, 2, 1)

        xs = []
        for b, tokens in enumerate((tokens_a, tokens_b)):
            rows = pos[b][:, None, :]
            far = dispatch(rows[4:], tokens, cap)
            far = [ep_swap(far[0], 2), ep_swap(far[1], 3)]
            near = dispatch(rows[:4], tokens, cap)
            xs.append([near[0], ep_swap(near[1], 1), *far])
        slots = jnp.arange(cap, dtype=jnp.int32)
        picks = [(pos.reshape(2, MASKS, 2, -1)[:, :, k, :, None] == slots).astype(BF16) for k in range(2)]

        p, h_l = None, []
        for b in range(2):
            h_l.append(hidden_local(xs[b], w_gate, w_up))
        for b in range(2):
            p = part(h_l[b], b, w_down, p)

        h_r = [None, None]
        for b in range(2):
            h_r[0] = hidden(xs[b], b, 0, gate0, up0, 0, h_r[0])
        for n, (lo, hi) in enumerate(up1_cuts):
            for b in range(2):
                h_r[1] = hidden(xs[b], b, 1, gate1, up1[n], lo, h_r[1])

        acc, outs = None, None
        for k, n in [(0, 0)] + late:
            lo, hi = down_cuts[k][n]
            if (k, n) in halves:
                far = final(h_r[k], p, k, down[k][n], lo, (2, 3))
                near = final(h_r[k], p, k, down[k][n], lo, (0, 1))
            else:
                *near, y2, y3 = final(h_r[k], p, k, down[k][n], lo, (0, 1, 2, 3))
                far = [y2, y3]
            far = [ep_swap(far[0], 2), ep_swap(far[1], 3)]
            near = [near[0], ep_swap(near[1], 1)]
            if k == 0:
                acc = combine(near + far, picks[0], gate_t, 0, lo, model, None, acc)
            else:
                outs = combine(near + far, picks[1], gate_t, 1, lo, model, acc, outs)
        return tuple(outs)

    in_specs = (row_spec, row_spec, row_spec, row_spec, row_spec, row_spec, gate_spec, gate_spec, down_spec)
    return jax.shard_map(group_body, mesh=mesh, in_specs=in_specs, out_specs=(row_spec, row_spec), check_vma=False)
```

time: 2080 us -> 2170 us (1.043)
  Pallas kernels: 1300 us -> 1380 us
    pallas_call x12 -> x16, Pallas kernels: 259 us -> 321 us  [final(): call(final_kernel, 2 * rows * width * cols, 2 * (rows * width + width * c...]
    pallas_call x30 -> x28, Pallas kernels: 913 us -> 936 us  [the longest x10 306 us: hidden(): call(hidden_kernel, 4 * rows * model * cols, 2 * (rows * model + 2 * mode...]
    ppermute x42 -> x48, waiting for transfers between devices: 334 us -> 320 us  [ep_swap(): return lax.ppermute(value, 'ep', [(i, i ^ mask) for i in range(ep_size)])]
    ppermute x18 -> x21, waiting for transfers between devices: 312 us -> 325 us  [tp_swap(): return lax.ppermute(piece, 'tp', TP_SWAP)[0]]
  transfers between devices with their start and end apart: 60 -> 69, of which waited for: 20 -> 15; matrix products, arithmetic and copies ran while one was open for 2% -> 3% of each run, Pallas kernels for 61% -> 62%
where the time goes in v2:
time: 2170 us; the launch traced here: 2160 us
  Pallas kernels  1380 us (64%)
  waiting for transfers between devices  645 us (30%)
  starting transfers between devices  56.4 us (3%)
  local copies, waits for them, and re-layouts  52.9 us (2%)
  other arithmetic  26.4 us (1%)
    ppermute x21, waiting for transfers between devices, tp_swap(): return lax.ppermute(piece, 'tp', TP_SWAP)[0]  325 us
    pallas_call x16, Pallas kernels, final(): call(final_kernel, 2 * rows * width * cols, 2 * (rows * width + width * c...  321 us
    ppermute x48, waiting for transfers between devices, ep_swap(): return lax.ppermute(value, 'ep', [(i, i ^ mask) for i in range(ep_size)])  320 us
    pallas_call x10, Pallas kernels, hidden(): call(hidden_kernel, 4 * rows * model * cols, 2 * (rows * model + 2 * mode...  306 us
    pallas_call x2, Pallas kernels, hidden_local(): call(hidden_kernel, 4 * rows * model * width, 2 * (rows * model + 4 * mod...  259 us
    pallas_call x2, Pallas kernels, part(): call(part_kernel, 2 * rows * width * model, 2 * (rows * width + 2 * width...  146 us
    pallas_call x9, Pallas kernels, combine(): call(functools.partial(combine_kernel, k), flops, nbytes, grid=(2 * block...  132 us
    pallas_call x4, Pallas kernels, dispatch(): call(dispatch_kernel, 2 * n * 2 * cap * toks * model, toks * model * 2 +...  125 us
  transfers between devices with their start and end apart: 69, of which 15 were waited for; matrix products, arithmetic and copies ran while one was open for 3% of the time, Pallas kernels for 62%

profile of v2, /device:TPU:0, one launch (start us, length us, event | category | flops | bytes accessed | tf_op | source)
XLA Modules:
  0.0 2164.9 jit_solution(13553699933643256892)
XLA Ops:
  8.1 31.1 %shard_map.106 = (bf16[2,640,2048]{2,1,0:T(8,128)(2,1)}, bf16[2,640,2048]{2,1,0:T(8,128)(2,1)}) custom-call(s32[4,1,2048]{2,1,0:T(1,128)} %get-tuple-element.182.pos_ref, bf16[2048,2048]{1,0:T(8,128)(2,1)} %tok_ref.7), custom_call_target="tpu_custom_call" | custom-call | flops 21474836480 | bytes 18874368 | tf_op jit(solution)/shard_map/pallas_call | solution.py:56
  40.1 31.2 %shard_map.107 = (bf16[2,640,2048]{2,1,0:T(8,128)(2,1)}, bf16[2,640,2048]{2,1,0:T(8,128)(2,1)}) custom-call(s32[4,1,2048]{2,1,0:T(1,128)} %get-tuple-element.181.pos_ref, bf16[2048,2048]{1,0:T(8,128)(2,1)} %tok_ref.7), custom_call_target="tpu_custom_call" | custom-call | flops 21474836480 | bytes 18874368 | tf_op jit(solution)/shard_map/pallas_call | solution.py:56
  73.9 31.2 %shard_map.104 = (bf16[2,640,2048]{2,1,0:T(8,128)(2,1)}, bf16[2,640,2048]{2,1,0:T(8,128)(2,1)}) custom-call(s32[4,1,2048]{2,1,0:T(1,128)} %get-tuple-element.184.pos_ref, bf16[2048,2048]{1,0:T(8,128)(2,1)} %tok_ref.5), custom_call_target="tpu_custom_call" | custom-call | flops 21474836480 | bytes 18874368 | tf_op jit(solution)/shard_map/pallas_call | solution.py:56
  105.2 31.6 %shard_map.105 = (bf16[2,640,2048]{2,1,0:T(8,128)(2,1)}, bf16[2,640,2048]{2,1,0:T(8,128)(2,1)}) custom-call(s32[4,1,2048]{2,1,0:T(1,128)} %get-tuple-element.183.pos_ref, bf16[2048,2048]{1,0:T(8,128)(2,1)} %tok_ref.5), custom_call_target="tpu_custom_call" | custom-call | flops 21474836480 | bytes 18874368 | tf_op jit(solution)/shard_map/pallas_call | solution.py:56
  144.9 12.6 fusion.4
  177.4 10.6 fusion.1.refs_4_
  188.0 9.4 fusion.refs_4_
  207.0 92.9 %collective-permute-done.7.refs_3_ = bf16[2,640,2048]{2,1,0:T(8,128)(2,1)} collective-permute-done((bf16[2,640,2048]{2,1,0:T(8,128)(2,1)}, bf16[2,640,2048]{2,1,0:T(8,128)(2,1)}, u32[]{:S(2)}, u32[]{:S(2)}) %collective-permute-start.7) | collective-permute-done | bytes 5242912 | tf_op jit(solution)/shard_map/ppermute | solution.py:238
  301.5 129.6 %shard_map.117.h = bf16[2,4,640,2816]{3,2,1,0:T(8,128)(2,1)} custom-call(bf16[2,640,2048]{2,1,0:T(8,128)(2,1)} %get-tuple-element.86.refs_0_, bf16[2,640,2048]{2,1,0:T(8,128)(2,1)} %collective-permute-done.5.refs_1_, bf16[2,640,2048]{2,1,0:T(8,128)(2,1)} %collective-permute-done.6.refs_2_, bf16[2,640,2048]{2,1,0:T(8,128)(2,1)} %collective-permute-done.7.refs_3_, ...), custom_call_target="tpu_custom_call" | custom-call | flops 118111600640 | bytes 95944704 | tf_op jit(solution)/shard_map/pallas_call | solution.py:79
  433.1 91.6 %collective-permute-done.2.refs_3_ = bf16[2,640,2048]{2,1,0:T(8,128)(2,1)} collective-permute-done((bf16[2,640,2048]{2,1,0:T(8,128)(2,1)}, bf16[2,640,2048]{2,1,0:T(8,128)(2,1)}, u32[]{:S(2)}, u32[]{:S(2)}) %collective-permute-start.2) | collective-permute-done | bytes 5242912 | tf_op jit(solution)/shard_map/ppermute | solution.py:238
  526.2 129.9 %shard_map.116.h = bf16[2,4,640,2816]{3,2,1,0:T(8,128)(2,1)} custom-call(bf16[2,640,2048]{2,1,0:T(8,128)(2,1)} %get-tuple-element.82.refs_0_, bf16[2,640,2048]{2,1,0:T(8,128)(2,1)} %collective-permute-done.refs_1_, bf16[2,640,2048]{2,1,0:T(8,128)(2,1)} %collective-permute-done.1.refs_2_, bf16[2,640,2048]{2,1,0:T(8,128)(2,1)} %collective-permute-done.2.refs_3_, ...), custom_call_target="tpu_custom_call" | custom-call | flops 118111600640 | bytes 95944704 | tf_op jit(solution)/shard_map/pallas_call | solution.py:79
  656.0 72.8 %shard_map.118.refs_0_ = f32[2,2,4,640,2048]{4,3,2,1,0:T(8,128)} custom-call(bf16[2,4,640,2816]{3,2,1,0:T(8,128)(2,1)} %shard_map.117.h, bf16[2,2816,2048]{2,1,0:T(8,128)(2,1)} %wd.3), custom_call_target="tpu_custom_call" | custom-call | flops 59055800320 | bytes 93847552 | tf_op jit(solution)/shard_map/pallas_call | solution.py:118
  728.9 72.8 %shard_map.119.p = f32[2,2,4,640,2048]{4,3,2,1,0:T(8,128)} custom-call(bf16[2,4,640,2816]{3,2,1,0:T(8,128)(2,1)} %shard_map.116.h, bf16[2,2816,2048]{2,1,0:T(8,128)(2,1)} %wd.3, f32[2,2,4,640,2048]{4,3,2,1,0:T(8,128)} %shard_map.118.refs_0_), custom_call_target="tpu_custom_call", output_to_operand_aliasing={{}: (2, {})} | custom-call | flops 59055800320 | bytes 93847552 | tf_op jit(solution)/shard_map/pallas_call | solution.py:118
  803.7 67.6 %shard_map.122.refs_6_ = bf16[2,4,640,2816]{3,2,1,0:T(8,128)(2,1)} custom-call(bf16[2,640,2048]{2,1,0:T(8,128)(2,1)} %get-tuple-element.86.refs_0_, bf16[2,640,2048]{2,1,0:T(8,128)(2,1)} %collective-permute-done.5.refs_1_, bf16[2,640,2048]{2,1,0:T(8,128)(2,1)} %collective-permute-done.6.refs_2_, bf16[2,640,2048]{2,1,0:T(8,128)(2,1)} %collective-permute-done.7.refs_3_, ...), custom_call_target="tpu_custom_call" | custom-call | flops 59055800320 | bytes 47972352 | tf_op jit(solution)/shard_map/pallas_call | solution.py:98
  871.3 67.9 %shard_map.123.h = bf16[2,4,640,2816]{3,2,1,0:T(8,128)(2,1)} custom-call(bf16[2,640,2048]{2,1,0:T(8,128)(2,1)} %get-tuple-element.82.refs_0_, bf16[2,640,2048]{2,1,0:T(8,128)(2,1)} %collective-permute-done.refs_1_, bf16[2,640,2048]{2,1,0:T(8,128)(2,1)} %collective-permute-done.1.refs_2_, ...), custom_call_target="tpu_custom_call", output_to_operand_aliasing={{}: (6, {})} | custom-call | flops 59055800320 | bytes 47972352 | tf_op jit(solution)/shard_map/pallas_call | solution.py:98
  939.2 211.0 %collective-permute-done.10 = bf16[1,2048,512]{2,1,0:T(8,128)(2,1)S(1)} collective-permute-done((bf16[1,2048,512]{2,1,0:T(8,128)(2,1)}, bf16[1,2048,512]{2,1,0:T(8,128)(2,1)S(1)}, u32[]{:S(2)}, u32[]{:S(2)}) %collective-permute-start.10) | collective-permute-done | bytes 2097184 | tf_op jit(solution)/shard_map/ppermute | solution.py:242
  1152.3 17.1 shard_map.108.refs_6_
  1169.4 17.0 shard_map.109.refs_6_
  1186.4 53.8 %collective-permute-done.9 = bf16[1,2048,1024]{2,1,0:T(8,128)(2,1)} collective-permute-done((bf16[1,2048,1024]{2,1,0:T(8,128)(2,1)}, bf16[1,2048,1024]{2,1,0:T(8,128)(2,1)}, u32[]{:S(2)}, u32[]{:S(2)}) %collective-permute-start.9) | collective-permute-done | bytes 4194336 | tf_op jit(solution)/shard_map/ppermute | solution.py:242
  1241.8 28.8 %shard_map.110.refs_6_ = bf16[2,4,640,2816]{3,2,1,0:T(8,128)(2,1)} custom-call(bf16[2,640,2048]{2,1,0:T(8,128)(2,1)} %get-tuple-element.86.refs_0_, bf16[2,640,2048]{2,1,0:T(8,128)(2,1)} %collective-permute-done.5.refs_1_, bf16[2,640,2048]{2,1,0:T(8,128)(2,1)} %collective-permute-done.6.refs_2_, ...), custom_call_target="tpu_custom_call", output_to_operand_aliasing={{}: (6, {})} | custom-call | flops 21474836480 | bytes 24117248 | tf_op jit(solution)/shard_map/pallas_call | solution.py:98
  1270.5 28.4 %shard_map.111.refs_6_ = bf16[2,4,640,2816]{3,2,1,0:T(8,128)(2,1)} custom-call(bf16[2,640,2048]{2,1,0:T(8,128)(2,1)} %get-tuple-element.82.refs_0_, bf16[2,640,2048]{2,1,0:T(8,128)(2,1)} %collective-permute-done.refs_1_, bf16[2,640,2048]{2,1,0:T(8,128)(2,1)} %collective-permute-done.1.refs_2_, ...), custom_call_target="tpu_custom_call", output_to_operand_aliasing={{}: (6, {})} | custom-call | flops 21474836480 | bytes 24117248 | tf_op jit(solution)/shard_map/pallas_call | solution.py:98
  1299.4 41.1 %shard_map.128 = (bf16[2,640,1024]{2,1,0:T(8,128)(2,1)}, bf16[2,640,1024]{2,1,0:T(8,128)(2,1)}, bf16[2,640,1024]{2,1,0:T(8,128)(2,1)}, bf16[2,640,1024]{2,1,0:T(8,128)(2,1)}) custom-call(bf16[2,4,640,2816]{3,2,1,0:T(8,128)(2,1)} %shard_map.123.h, f32[2,2,4,640,2048]{4,3,2,1,0:T(8,128)} %shard_map.119.p, bf16[2816,1024]{1,0:T(8,128)(2,1)} %bitcast.21.wd), custom_call_target="tpu_custom_call" | custom-call | flops 29527900160 | bytes 66060288 | tf_op jit(solution)/shard_map/pallas_call | solution.py:144
  1340.5 51.4 %collective-permute-done.8 = bf16[1,2048,1024]{2,1,0:T(8,128)(2,1)} collective-permute-done((bf16[1,2048,1024]{2,1,0:T(8,128)(2,1)}, bf16[1,2048,1024]{2,1,0:T(8,128)(2,1)}, u32[]{:S(2)}, u32[]{:S(2)}) %collective-permute-start.8) | collective-permute-done | bytes 4194336 | tf_op jit(solution)/shard_map/ppermute | solution.py:242
  1393.5 28.5 %shard_map.112.refs_6_ = bf16[2,4,640,2816]{3,2,1,0:T(8,128)(2,1)} custom-call(bf16[2,640,2048]{2,1,0:T(8,128)(2,1)} %get-tuple-element.86.refs_0_, bf16[2,640,2048]{2,1,0:T(8,128)(2,1)} %collective-permute-done.5.refs_1_, bf16[2,640,2048]{2,1,0:T(8,128)(2,1)} %collective-permute-done.6.refs_2_, ...), custom_call_target="tpu_custom_call", output_to_operand_aliasing={{}: (6, {})} | custom-call | flops 21474836480 | bytes 24117248 | tf_op jit(solution)/shard_map/pallas_call | solution.py:98
  1421.9 28.4 %shard_map.113.refs_6_ = bf16[2,4,640,2816]{3,2,1,0:T(8,128)(2,1)} custom-call(bf16[2,640,2048]{2,1,0:T(8,128)(2,1)} %get-tuple-element.82.refs_0_, bf16[2,640,2048]{2,1,0:T(8,128)(2,1)} %collective-permute-done.refs_1_, bf16[2,640,2048]{2,1,0:T(8,128)(2,1)} %collective-permute-done.1.refs_2_, ...), custom_call_target="tpu_custom_call", output_to_operand_aliasing={{}: (6, {})} | custom-call | flops 21474836480 | bytes 24117248 | tf_op jit(solution)/shard_map/pallas_call | solution.py:98
  1450.8 21.9 %shard_map.127 = (bf16[2,640,256]{2,1,0:T(8,128)(2,1)}, bf16[2,640,256]{2,1,0:T(8,128)(2,1)}, bf16[2,640,256]{2,1,0:T(8,128)(2,1)}, bf16[2,640,256]{2,1,0:T(8,128)(2,1)}) custom-call(bf16[2,4,640,2816]{3,2,1,0:T(8,128)(2,1)} %shard_map.123.h, f32[2,2,4,640,2048]{4,3,2,1,0:T(8,128)} %shard_map.119.p, bf16[2816,256]{1,0:T(8,128)(2,1)} %bitcast.20.wd), custom_call_target="tpu_custom_call" | custom-call | flops 7381975040 | bytes 38141952 | tf_op jit(solution)/shard_map/pallas_call | solution.py:144
  1474.3 22.2 %shard_map.126 = (bf16[2,640,256]{2,1,0:T(8,128)(2,1)}, bf16[2,640,256]{2,1,0:T(8,128)(2,1)}, bf16[2,640,256]{2,1,0:T(8,128)(2,1)}, bf16[2,640,256]{2,1,0:T(8,128)(2,1)}) custom-call(bf16[2,4,640,2816]{3,2,1,0:T(8,128)(2,1)} %shard_map.123.h, f32[2,2,4,640,2048]{4,3,2,1,0:T(8,128)} %shard_map.119.p, bf16[2816,256]{1,0:T(8,128)(2,1)} %bitcast.19.wd), custom_call_target="tpu_custom_call" | custom-call | flops 7381975040 | bytes 38141952 | tf_op jit(solution)/shard_map/pallas_call | solution.py:144
  1497.5 11.4 shard_map.114.refs_6_
  1508.9 11.4 shard_map.115.h
  1520.3 9.1 collective-permute-done.37
  1530.3 9.5 shard_map.134
  1539.8 9.5 shard_map.135
  1550.5 21.9 %shard_map.125 = (bf16[2,640,256]{2,1,0:T(8,128)(2,1)}, bf16[2,640,256]{2,1,0:T(8,128)(2,1)}, bf16[2,640,256]{2,1,0:T(8,128)(2,1)}, bf16[2,640,256]{2,1,0:T(8,128)(2,1)}) custom-call(bf16[2,4,640,2816]{3,2,1,0:T(8,128)(2,1)} %shard_map.123.h, f32[2,2,4,640,2048]{4,3,2,1,0:T(8,128)} %shard_map.119.p, bf16[2816,256]{1,0:T(8,128)(2,1)} %bitcast.18.wd), custom_call_target="tpu_custom_call" | custom-call | flops 7381975040 | bytes 38141952 | tf_op jit(solution)/shard_map/pallas_call | solution.py:144
  1573.2 9.5 shard_map.121
  1583.9 22.3 %shard_map.124 = (bf16[2,640,256]{2,1,0:T(8,128)(2,1)}, bf16[2,640,256]{2,1,0:T(8,128)(2,1)}, bf16[2,640,256]{2,1,0:T(8,128)(2,1)}, bf16[2,640,256]{2,1,0:T(8,128)(2,1)}) custom-call(bf16[2,4,640,2816]{3,2,1,0:T(8,128)(2,1)} %shard_map.123.h, f32[2,2,4,640,2048]{4,3,2,1,0:T(8,128)} %shard_map.119.p, bf16[2816,256]{1,0:T(8,128)(2,1)} %bitcast.17.wd), custom_call_target="tpu_custom_call" | custom-call | flops 7381975040 | bytes 38141952 | tf_op jit(solution)/shard_map/pallas_call | solution.py:144
  1607.1 21.9 %shard_map.142 = (bf16[2,640,256]{2,1,0:T(8,128)(2,1)}, bf16[2,640,256]{2,1,0:T(8,128)(2,1)}, bf16[2,640,256]{2,1,0:T(8,128)(2,1)}, bf16[2,640,256]{2,1,0:T(8,128)(2,1)}) custom-call(bf16[2,4,640,2816]{3,2,1,0:T(8,128)(2,1)} %shard_map.115.h, f32[2,2,4,640,2048]{4,3,2,1,0:T(8,128)} %shard_map.119.p, bf16[2816,256]{1,0:T(8,128)(2,1)} %bitcast.29.wd), custom_call_target="tpu_custom_call" | custom-call | flops 7381975040 | bytes 38141952 | tf_op jit(solution)/shard_map/pallas_call | solution.py:144
  1630.2 21.9 %shard_map.141 = (bf16[2,640,256]{2,1,0:T(8,128)(2,1)}, bf16[2,640,256]{2,1,0:T(8,128)(2,1)}, bf16[2,640,256]{2,1,0:T(8,128)(2,1)}, bf16[2,640,256]{2,1,0:T(8,128)(2,1)}) custom-call(bf16[2,4,640,2816]{3,2,1,0:T(8,128)(2,1)} %shard_map.115.h, f32[2,2,4,640,2048]{4,3,2,1,0:T(8,128)} %shard_map.119.p, bf16[2816,256]{1,0:T(8,128)(2,1)} %bitcast.28.wd), custom_call_target="tpu_custom_call" | custom-call | flops 7381975040 | bytes 38141952 | tf_op jit(solution)/shard_map/pallas_call | solution.py:144
  1652.1 9.5 shard_map.120
  1661.6 22.0 %shard_map.140 = (bf16[2,640,256]{2,1,0:T(8,128)(2,1)}, bf16[2,640,256]{2,1,0:T(8,128)(2,1)}, bf16[2,640,256]{2,1,0:T(8,128)(2,1)}, bf16[2,640,256]{2,1,0:T(8,128)(2,1)}) custom-call(bf16[2,4,640,2816]{3,2,1,0:T(8,128)(2,1)} %shard_map.115.h, f32[2,2,4,640,2048]{4,3,2,1,0:T(8,128)} %shard_map.119.p, bf16[2816,256]{1,0:T(8,128)(2,1)} %bitcast.27.wd), custom_call_target="tpu_custom_call" | custom-call | flops 7381975040 | bytes 38141952 | tf_op jit(solution)/shard_map/pallas_call | solution.py:144
  1685.4 22.0 %shard_map.139 = (bf16[2,640,256]{2,1,0:T(8,128)(2,1)}, bf16[2,640,256]{2,1,0:T(8,128)(2,1)}, bf16[2,640,256]{2,1,0:T(8,128)(2,1)}, bf16[2,640,256]{2,1,0:T(8,128)(2,1)}) custom-call(bf16[2,4,640,2816]{3,2,1,0:T(8,128)(2,1)} %shard_map.115.h, f32[2,2,4,640,2048]{4,3,2,1,0:T(8,128)} %shard_map.119.p, bf16[2816,256]{1,0:T(8,128)(2,1)} %bitcast.26.wd), custom_call_target="tpu_custom_call" | custom-call | flops 7381975040 | bytes 38141952 | tf_op jit(solution)/shard_map/pallas_call | solution.py:144
  1707.8 22.0 %shard_map.138 = (bf16[2,640,256]{2,1,0:T(8,128)(2,1)}, bf16[2,640,256]{2,1,0:T(8,128)(2,1)}, bf16[2,640,256]{2,1,0:T(8,128)(2,1)}, bf16[2,640,256]{2,1,0:T(8,128)(2,1)}) custom-call(bf16[2,4,640,2816]{3,2,1,0:T(8,128)(2,1)} %shard_map.115.h, f32[2,2,4,640,2048]{4,3,2,1,0:T(8,128)} %shard_map.119.p, bf16[2816,256]{1,0:T(8,128)(2,1)} %bitcast.25.wd), custom_call_target="tpu_custom_call" | custom-call | flops 7381975040 | bytes 38141952 | tf_op jit(solution)/shard_map/pallas_call | solution.py:144
  1731.4 22.2 %shard_map.137 = (bf16[2,640,256]{2,1,0:T(8,128)(2,1)}, bf16[2,640,256]{2,1,0:T(8,128)(2,1)}, bf16[2,640,256]{2,1,0:T(8,128)(2,1)}, bf16[2,640,256]{2,1,0:T(8,128)(2,1)}) custom-call(bf16[2,4,640,2816]{3,2,1,0:T(8,128)(2,1)} %shard_map.115.h, f32[2,2,4,640,2048]{4,3,2,1,0:T(8,128)} %shard_map.119.p, bf16[2816,256]{1,0:T(8,128)(2,1)} %bitcast.24.wd), custom_call_target="tpu_custom_call" | custom-call | flops 7381975040 | bytes 38141952 | tf_op jit(solution)/shard_map/pallas_call | solution.py:144
  1753.6 60.2 %collective-permute-done.31.refs_2_ = bf16[2,640,256]{2,1,0:T(8,128)(2,1)S(1)} collective-permute-done((bf16[2,640,256]{2,1,0:T(8,128)(2,1)S(1)}, bf16[2,640,256]{2,1,0:T(8,128)(2,1)S(1)}, u32[]{:S(2)}, u32[]{:S(2)}) %collective-permute-start.31) | collective-permute-done | bytes 655392 | tf_op jit(solution)/shard_map/ppermute | solution.py:238
  1813.8 12.9 collective-permute-done.32.refs_3_
  1828.2 21.9 %shard_map.136 = (bf16[2,640,256]{2,1,0:T(8,128)(2,1)}, bf16[2,640,256]{2,1,0:T(8,128)(2,1)}, bf16[2,640,256]{2,1,0:T(8,128)(2,1)}, bf16[2,640,256]{2,1,0:T(8,128)(2,1)}) custom-call(bf16[2,4,640,2816]{3,2,1,0:T(8,128)(2,1)} %shard_map.115.h, f32[2,2,4,640,2048]{4,3,2,1,0:T(8,128)} %shard_map.119.p, bf16[2816,256]{1,0:T(8,128)(2,1)} %bitcast.23.wd), custom_call_target="tpu_custom_call" | custom-call | flops 7381975040 | bytes 38141952 | tf_op jit(solution)/shard_map/pallas_call | solution.py:144
  1853.0 33.4 %shard_map.129.refs_6_ = f32[4096,2048]{1,0:T(8,128)} custom-call(bf16[2,640,1024]{2,1,0:T(8,128)(2,1)} %get-tuple-element.110.refs_0_, bf16[2,640,1024]{2,1,0:T(8,128)(2,1)} %collective-permute-done.34.refs_1_, bf16[2,640,1024]{2,1,0:T(8,128)(2,1)} %collective-permute-done.35.refs_2_, bf16[2,640,1024]{2,1,0:T(8,128)(2,1)} %collective-permute-done.36.refs_3_, ...), custom_call_target="tpu_custom_call" | custom-call | flops 21474836480 | bytes 46137344 | tf_op jit(solution)/shard_map/pallas_call | solution.py:195
  1888.7 14.7 shard_map.130.refs_6_
  1905.0 14.8 shard_map.131.refs_6_
  1925.2 14.7 shard_map.132.refs_6_
  1940.3 11.1 collective-permute-done.68.refs_3_
  1952.9 14.7 shard_map.133.refs_6_
  1970.1 9.6 collective-permute-done.64.refs_3_
  1980.2 14.9 shard_map.143
  1996.8 14.9 shard_map.144
  2022.2 15.2 shard_map.145
  2039.1 15.0 shard_map.146
  2054.6 9.3 collective-permute-done.52.refs_3_
  2065.6 15.0 shard_map.147
  2081.1 10.9 collective-permute-done.48.refs_3_
  2092.5 15.2 shard_map.148
  2110.7 9.2 collective-permute-done.44.refs_3_
  2120.8 14.9 shard_map.149
  2136.7 13.5 shard_map.150
  2151.1 13.5 shard_map.151
  (271 shorter events, 115.2 us)
Async XLA Ops:
  39.3 166.2 %collective-permute-start.5 = (bf16[2,640,2048]{2,1,0:T(8,128)(2,1)}, bf16[2,640,2048]{2,1,0:T(8,128)(2,1)}, u32[]{:S(2)}, u32[]{:S(2)}) collective-permute-start(bf16[2,640,2048]{2,1,0:T(8,128)(2,1)} %get-tuple-element.87), channel_id=1, source_target_pairs={{0,1},{1,0},{2,3},{3,2},{4,5},{5,4},{6,7},{7,6}} | collective-permute-start | bytes 15728648 | tf_op jit(solution)/shard_map/ppermute | solution.py:238
  71.3 134.2 %collective-permute-start.6 = (bf16[2,640,2048]{2,1,0:T(8,128)(2,1)}, bf16[2,640,2048]{2,1,0:T(8,128)(2,1)}, u32[]{:S(2)}, u32[]{:S(2)}) collective-permute-start(bf16[2,640,2048]{2,1,0:T(8,128)(2,1)} %get-tuple-element.88), channel_id=1, source_target_pairs={{0,2},{1,3},{2,0},{3,1},{4,6},{5,7},{6,4},{7,5}} | collective-permute-start | bytes 15728648 | tf_op jit(solution)/shard_map/ppermute | solution.py:238
  73.8 226.1 %collective-permute-start.7 = (bf16[2,640,2048]{2,1,0:T(8,128)(2,1)}, bf16[2,640,2048]{2,1,0:T(8,128)(2,1)}, u32[]{:S(2)}, u32[]{:S(2)}) collective-permute-start(bf16[2,640,2048]{2,1,0:T(8,128)(2,1)} %get-tuple-element.89), channel_id=1, source_target_pairs={{0,3},{1,2},{2,1},{3,0},{4,7},{5,6},{6,5},{7,4}} | collective-permute-start | bytes 15728648 | tf_op jit(solution)/shard_map/ppermute | solution.py:238
  105.1 326.0 %collective-permute-start = (bf16[2,640,2048]{2,1,0:T(8,128)(2,1)}, bf16[2,640,2048]{2,1,0:T(8,128)(2,1)}, u32[]{:S(2)}, u32[]{:S(2)}) collective-permute-start(bf16[2,640,2048]{2,1,0:T(8,128)(2,1)} %get-tuple-element.83), channel_id=1, source_target_pairs={{0,1},{1,0},{2,3},{3,2},{4,5},{5,4},{6,7},{7,6}} | collective-permute-start | bytes 15728648 | tf_op jit(solution)/shard_map/ppermute | solution.py:238
  136.7 294.8 %collective-permute-start.1 = (bf16[2,640,2048]{2,1,0:T(8,128)(2,1)}, bf16[2,640,2048]{2,1,0:T(8,128)(2,1)}, u32[]{:S(2)}, u32[]{:S(2)}) collective-permute-start(bf16[2,640,2048]{2,1,0:T(8,128)(2,1)} %get-tuple-element.84), channel_id=1, source_target_pairs={{0,2},{1,3},{2,0},{3,1},{4,6},{5,7},{6,4},{7,5}} | collective-permute-start | bytes 15728648 | tf_op jit(solution)/shard_map/ppermute | solution.py:238
  205.5 319.2 %collective-permute-start.2 = (bf16[2,640,2048]{2,1,0:T(8,128)(2,1)}, bf16[2,640,2048]{2,1,0:T(8,128)(2,1)}, u32[]{:S(2)}, u32[]{:S(2)}) collective-permute-start(bf16[2,640,2048]{2,1,0:T(8,128)(2,1)} %get-tuple-element.85), channel_id=1, source_target_pairs={{0,3},{1,2},{2,1},{3,0},{4,7},{5,6},{6,5},{7,4}} | collective-permute-start | bytes 15728648 | tf_op jit(solution)/shard_map/ppermute | solution.py:238
  205.5 596.2 %collective-permute-start.15 = (bf16[1,2048,2816]{2,1,0:T(8,128)(2,1)}, bf16[1,2048,2816]{2,1,0:T(8,128)(2,1)}, u32[]{:S(2)}, u32[]{:S(2)}) collective-permute-start(bf16[1,2048,2816]{2,1,0:T(8,128)(2,1)} %get-tuple-element.175), channel_id=1, source_target_pairs={{0,4},{4,0},{1,5},{5,1},{2,6},{6,2},{3,7},{7,3}} | collective-permute-start | bytes 34603016 | tf_op jit(solution)/shard_map/ppermute | solution.py:242
  299.9 502.3 %collective-permute-start.16 = (bf16[1,2048,2816]{2,1,0:T(8,128)(2,1)}, bf16[1,2048,2816]{2,1,0:T(8,128)(2,1)}, u32[]{:S(2)}, u32[]{:S(2)}) collective-permute-start(bf16[1,2048,2816]{2,1,0:T(8,128)(2,1)} %slice.123), channel_id=1, source_target_pairs={{0,4},{4,0},{1,5},{5,1},{2,6},{6,2},{3,7},{7,3}} | collective-permute-start | bytes 34603016 | tf_op jit(solution)/shard_map/ppermute | solution.py:242
  431.0 867.9 %collective-permute-start.33 = (bf16[1,2816,1024]{2,1,0:T(8,128)(2,1)}, bf16[1,2816,1024]{2,1,0:T(8,128)(2,1)}, u32[]{:S(2)}, u32[]{:S(2)}) collective-permute-start(bf16[1,2816,1024]{2,1,0:T(8,128)(2,1)} %slice.129), channel_id=1, source_target_pairs={{0,4},{4,0},{1,5},{5,1},{2,6},{6,2},{3,7},{7,3}} | collective-permute-start | bytes 17301512 | tf_op jit(solution)/shard_map/ppermute | solution.py:242
  431.6 1018.8 %collective-permute-start.29 = (bf16[1,2816,256]{2,1,0:T(8,128)(2,1)}, bf16[1,2816,256]{2,1,0:T(8,128)(2,1)}, u32[]{:S(2)}, u32[]{:S(2)}) collective-permute-start(bf16[1,2816,256]{2,1,0:T(8,128)(2,1)} %get-tuple-element.168), channel_id=1, source_target_pairs={{0,4},{4,0},{1,5},{5,1},{2,6},{6,2},{3,7},{7,3}} | collective-permute-start | bytes 4325384 | tf_op jit(solution)/shard_map/ppermute | solution.py:242
  524.6 627.1 %collective-permute-start.3 = (bf16[1,2048,2816]{2,1,0:T(8,128)(2,1)}, bf16[1,2048,2816]{2,1,0:T(8,128)(2,1)}, u32[]{:S(2)}, u32[]{:S(2)}) collective-permute-start(bf16[1,2048,2816]{2,1,0:T(8,128)(2,1)} %get-tuple-element.176), channel_id=1, source_target_pairs={{0,4},{4,0},{1,5},{5,1},{2,6},{6,2},{3,7},{7,3}} | collective-permute-start | bytes 34603016 | tf_op jit(solution)/shard_map/ppermute | solution.py:242
  801.7 348.5 %collective-permute-start.10 = (bf16[1,2048,512]{2,1,0:T(8,128)(2,1)}, bf16[1,2048,512]{2,1,0:T(8,128)(2,1)S(1)}, u32[]{:S(2)}, u32[]{:S(2)}) collective-permute-start(bf16[1,2048,512]{2,1,0:T(8,128)(2,1)} %slice.119), channel_id=1, source_target_pairs={{0,4},{4,0},{1,5},{5,1},{2,6},{6,2},{3,7},{7,3}} | collective-permute-start | bytes 6291464 | tf_op jit(solution)/shard_map/ppermute | solution.py:242
  802.2 438.0 %collective-permute-start.9 = (bf16[1,2048,1024]{2,1,0:T(8,128)(2,1)}, bf16[1,2048,1024]{2,1,0:T(8,128)(2,1)}, u32[]{:S(2)}, u32[]{:S(2)}) collective-permute-start(bf16[1,2048,1024]{2,1,0:T(8,128)(2,1)} %get-tuple-element.177), channel_id=1, source_target_pairs={{0,4},{4,0},{1,5},{5,1},{2,6},{6,2},{3,7},{7,3}} | collective-permute-start | bytes 12582920 | tf_op jit(solution)/shard_map/ppermute | solution.py:242
  1150.2 322.4 %collective-permute-start.25 = (bf16[1,2816,256]{2,1,0:T(8,128)(2,1)}, bf16[1,2816,256]{2,1,0:T(8,128)(2,1)}, u32[]{:S(2)}, u32[]{:S(2)}) collective-permute-start(bf16[1,2816,256]{2,1,0:T(8,128)(2,1)} %get-tuple-element.169), channel_id=1, source_target_pairs={{0,4},{4,0},{1,5},{5,1},{2,6},{6,2},{3,7},{7,3}} | collective-permute-start | bytes 4325384 | tf_op jit(solution)/shard_map/ppermute | solution.py:242
  1151.8 397.5 %collective-permute-start.21 = (bf16[1,2816,256]{2,1,0:T(8,128)(2,1)}, bf16[1,2816,256]{2,1,0:T(8,128)(2,1)}, u32[]{:S(2)}, u32[]{:S(2)}) collective-permute-start(bf16[1,2816,256]{2,1,0:T(8,128)(2,1)} %get-tuple-element.170), channel_id=1, source_target_pairs={{0,4},{4,0},{1,5},{5,1},{2,6},{6,2},{3,7},{7,3}} | collective-permute-start | bytes 4325384 | tf_op jit(solution)/shard_map/ppermute | solution.py:242
  1240.2 151.7 %collective-permute-start.8 = (bf16[1,2048,1024]{2,1,0:T(8,128)(2,1)}, bf16[1,2048,1024]{2,1,0:T(8,128)(2,1)}, u32[]{:S(2)}, u32[]{:S(2)}) collective-permute-start(bf16[1,2048,1024]{2,1,0:T(8,128)(2,1)} %get-tuple-element.178), channel_id=1, source_target_pairs={{0,4},{4,0},{1,5},{5,1},{2,6},{6,2},{3,7},{7,3}} | collective-permute-start | bytes 12582920 | tf_op jit(solution)/shard_map/ppermute | solution.py:242
  1298.9 283.8 %collective-permute-start.17 = (bf16[1,2816,256]{2,1,0:T(8,128)(2,1)}, bf16[1,2816,256]{2,1,0:T(8,128)(2,1)}, u32[]{:S(2)}, u32[]{:S(2)}) collective-permute-start(bf16[1,2816,256]{2,1,0:T(8,128)(2,1)} %get-tuple-element.171), channel_id=1, source_target_pairs={{0,4},{4,0},{1,5},{5,1},{2,6},{6,2},{3,7},{7,3}} | collective-permute-start | bytes 4325384 | tf_op jit(solution)/shard_map/ppermute | solution.py:242
  1391.9 104.6 %collective-permute-start.4 = (bf16[1,2048,256]{2,1,0:T(8,128)(2,1)S(1)}, bf16[1,2048,256]{2,1,0:T(8,128)(2,1)S(1)}, u32[]{:S(2)}, u32[]{:S(2)}) collective-permute-start(bf16[1,2048,256]{2,1,0:T(8,128)(2,1)S(1)} %copy-done.4), channel_id=1, source_target_pairs={{0,4},{4,0},{1,5},{5,1},{2,6},{6,2},{3,7},{7,3}} | collective-permute-start | bytes 3145736 | tf_op jit(solution)/shard_map/ppermute | solution.py:242
  1450.3 155.9 %collective-permute-start.65 = (bf16[1,2816,256]{2,1,0:T(8,128)(2,1)}, bf16[1,2816,256]{2,1,0:T(8,128)(2,1)}, u32[]{:S(2)}, u32[]{:S(2)}) collective-permute-start(bf16[1,2816,256]{2,1,0:T(8,128)(2,1)} %get-tuple-element.162), channel_id=1, source_target_pairs={{0,4},{4,0},{1,5},{5,1},{2,6},{6,2},{3,7},{7,3}} | collective-permute-start | bytes 4325384 | tf_op jit(solution)/shard_map/ppermute | solution.py:242
  1472.7 156.3 %collective-permute-start.61 = (bf16[1,2816,256]{2,1,0:T(8,128)(2,1)}, bf16[1,2816,256]{2,1,0:T(8,128)(2,1)}, u32[]{:S(2)}, u32[]{:S(2)}) collective-permute-start(bf16[1,2816,256]{2,1,0:T(8,128)(2,1)} %get-tuple-element.172), channel_id=1, source_target_pairs={{0,4},{4,0},{1,5},{5,1},{2,6},{6,2},{3,7},{7,3}} | collective-permute-start | bytes 4325384 | tf_op jit(solution)/shard_map/ppermute | solution.py:242
  1496.5 32.9 %collective-permute-start.37 = (bf16[1,2816,128]{2,1,0:T(8,128)(2,1)S(1)}, bf16[1,2816,128]{2,1,0:T(8,128)(2,1)S(1)}, u32[]{:S(2)}, u32[]{:S(2)}) collective-permute-start(bf16[1,2816,128]{2,1,0:T(8,128)(2,1)S(1)} %copy-done.6), channel_id=1, source_target_pairs={{0,4},{4,0},{1,5},{5,1},{2,6},{6,2},{3,7},{7,3}} | collective-permute-start | bytes 2162696 | tf_op jit(solution)/shard_map/ppermute | solution.py:242
  1529.5 42.9 %collective-permute-start.11 = (bf16[1,2816,128]{2,1,0:T(8,128)(2,1)S(1)}, bf16[1,2816,128]{2,1,0:T(8,128)(2,1)S(1)}, u32[]{:S(2)}, u32[]{:S(2)}) collective-permute-start(bf16[1,2816,128]{2,1,0:T(8,128)(2,1)S(1)} %copy-done.5), channel_id=1, source_target_pairs={{0,4},{4,0},{1,5},{5,1},{2,6},{6,2},{3,7},{7,3}} | collective-permute-start | bytes 2162696 | tf_op jit(solution)/shard_map/ppermute | solution.py:242
  1549.3 112.3 %collective-permute-start.57 = (bf16[1,2816,256]{2,1,0:T(8,128)(2,1)}, bf16[1,2816,256]{2,1,0:T(8,128)(2,1)}, u32[]{:S(2)}, u32[]{:S(2)}) collective-permute-start(bf16[1,2816,256]{2,1,0:T(8,128)(2,1)} %get-tuple-element.163), channel_id=1, source_target_pairs={{0,4},{4,0},{1,5},{5,1},{2,6},{6,2},{3,7},{7,3}} | collective-permute-start | bytes 4325384 | tf_op jit(solution)/shard_map/ppermute | solution.py:242
  1572.4 111.2 %collective-permute-start.53 = (bf16[1,2816,256]{2,1,0:T(8,128)(2,1)}, bf16[1,2816,256]{2,1,0:T(8,128)(2,1)}, u32[]{:S(2)}, u32[]{:S(2)}) collective-permute-start(bf16[1,2816,256]{2,1,0:T(8,128)(2,1)} %get-tuple-element.164), channel_id=1, source_target_pairs={{0,4},{4,0},{1,5},{5,1},{2,6},{6,2},{3,7},{7,3}} | collective-permute-start | bytes 4325384 | tf_op jit(solution)/shard_map/ppermute | solution.py:242
  1582.7 102.4 %collective-permute-start.49 = (bf16[1,2816,256]{2,1,0:T(8,128)(2,1)}, bf16[1,2816,256]{2,1,0:T(8,128)(2,1)}, u32[]{:S(2)}, u32[]{:S(2)}) collective-permute-start(bf16[1,2816,256]{2,1,0:T(8,128)(2,1)} %get-tuple-element.165), channel_id=1, source_target_pairs={{0,4},{4,0},{1,5},{5,1},{2,6},{6,2},{3,7},{7,3}} | collective-permute-start | bytes 4325384 | tf_op jit(solution)/shard_map/ppermute | solution.py:242
  1606.2 101.2 %collective-permute-start.45 = (bf16[1,2816,256]{2,1,0:T(8,128)(2,1)}, bf16[1,2816,256]{2,1,0:T(8,128)(2,1)}, u32[]{:S(2)}, u32[]{:S(2)}) collective-permute-start(bf16[1,2816,256]{2,1,0:T(8,128)(2,1)} %get-tuple-element.166), channel_id=1, source_target_pairs={{0,4},{4,0},{1,5},{5,1},{2,6},{6,2},{3,7},{7,3}} | collective-permute-start | bytes 4325384 | tf_op jit(solution)/shard_map/ppermute | solution.py:242
  1629.0 100.8 %collective-permute-start.41 = (bf16[1,2816,256]{2,1,0:T(8,128)(2,1)}, bf16[1,2816,256]{2,1,0:T(8,128)(2,1)}, u32[]{:S(2)}, u32[]{:S(2)}) collective-permute-start(bf16[1,2816,256]{2,1,0:T(8,128)(2,1)} %get-tuple-element.167), channel_id=1, source_target_pairs={{0,4},{4,0},{1,5},{5,1},{2,6},{6,2},{3,7},{7,3}} | collective-permute-start | bytes 4325384 | tf_op jit(solution)/shard_map/ppermute | solution.py:242
  1661.6 189.3 %collective-permute-start.34 = (bf16[2,640,1024]{2,1,0:T(8,128)(2,1)}, bf16[2,640,1024]{2,1,0:T(8,128)(2,1)}, u32[]{:S(2)}, u32[]{:S(2)}) collective-permute-start(bf16[2,640,1024]{2,1,0:T(8,128)(2,1)} %get-tuple-element.111), channel_id=1, source_target_pairs={{0,1},{1,0},{2,3},{3,2},{4,5},{5,4},{6,7},{7,6}} | collective-permute-start | bytes 7864328 | tf_op jit(solution)/shard_map/ppermute | solution.py:238
  1683.6 168.7 %collective-permute-start.35 = (bf16[2,640,1024]{2,1,0:T(8,128)(2,1)}, bf16[2,640,1024]{2,1,0:T(8,128)(2,1)}, u32[]{:S(2)}, u32[]{:S(2)}) collective-permute-start(bf16[2,640,1024]{2,1,0:T(8,128)(2,1)} %get-tuple-element.112), channel_id=1, source_target_pairs={{0,2},{1,3},{2,0},{3,1},{4,6},{5,7},{6,4},{7,5}} | collective-permute-start | bytes 7864328 | tf_op jit(solution)/shard_map/ppermute | solution.py:238
  1685.1 167.2 %collective-permute-start.36 = (bf16[2,640,1024]{2,1,0:T(8,128)(2,1)}, bf16[2,640,1024]{2,1,0:T(8,128)(2,1)}, u32[]{:S(2)}, u32[]{:S(2)}) collective-permute-start(bf16[2,640,1024]{2,1,0:T(8,128)(2,1)} %get-tuple-element.113), channel_id=1, source_target_pairs={{0,3},{1,2},{2,1},{3,0},{4,7},{5,6},{6,5},{7,4}} | collective-permute-start | bytes 7864328 | tf_op jit(solution)/shard_map/ppermute | solution.py:238
  1729.9 83.9 %collective-permute-start.31 = (bf16[2,640,256]{2,1,0:T(8,128)(2,1)S(1)}, bf16[2,640,256]{2,1,0:T(8,128)(2,1)S(1)}, u32[]{:S(2)}, u32[]{:S(2)}) collective-permute-start(bf16[2,640,256]{2,1,0:T(8,128)(2,1)S(1)} %copy-done.44), channel_id=1, source_target_pairs={{0,2},{1,3},{2,0},{3,1},{4,6},{5,7},{6,4},{7,5}} | collective-permute-start | bytes 1966088 | tf_op jit(solution)/shard_map/ppermute | solution.py:238
  1731.4 95.4 %collective-permute-start.32 = (bf16[2,640,256]{2,1,0:T(8,128)(2,1)S(1)}, bf16[2,640,256]{2,1,0:T(8,128)(2,1)S(1)}, u32[]{:S(2)}, u32[]{:S(2)}) collective-permute-start(bf16[2,640,256]{2,1,0:T(8,128)(2,1)S(1)} %copy-done.43), channel_id=1, source_target_pairs={{0,3},{1,2},{2,1},{3,0},{4,7},{5,6},{6,5},{7,4}} | collective-permute-start | bytes 1966088 | tf_op jit(solution)/shard_map/ppermute | solution.py:238
  1813.8 36.4 %collective-permute-start.26 = (bf16[2,640,256]{2,1,0:T(8,128)(2,1)}, bf16[2,640,256]{2,1,0:T(8,128)(2,1)S(1)}, u32[]{:S(2)}, u32[]{:S(2)}) collective-permute-start(bf16[2,640,256]{2,1,0:T(8,128)(2,1)} %get-tuple-element.103), channel_id=1, source_target_pairs={{0,1},{1,0},{2,3},{3,2},{4,5},{5,4},{6,7},{7,6}} | collective-permute-start | bytes 1966088 | tf_op jit(solution)/shard_map/ppermute | solution.py:238
  1850.2 36.3 %collective-permute-start.28 = (bf16[2,640,256]{2,1,0:T(8,128)(2,1)}, bf16[2,640,256]{2,1,0:T(8,128)(2,1)S(1)}, u32[]{:S(2)}, u32[]{:S(2)}) collective-permute-start(bf16[2,640,256]{2,1,0:T(8,128)(2,1)} %get-tuple-element.105), channel_id=1, source_target_pairs={{0,3},{1,2},{2,1},{3,0},{4,7},{5,6},{6,5},{7,4}} | collective-permute-start | bytes 1966088 | tf_op jit(solution)/shard_map/ppermute | solution.py:238
  1850.4 37.5 %collective-permute-start.22 = (bf16[2,640,256]{2,1,0:T(8,128)(2,1)}, bf16[2,640,256]{2,1,0:T(8,128)(2,1)S(1)}, u32[]{:S(2)}, u32[]{:S(2)}) collective-permute-start(bf16[2,640,256]{2,1,0:T(8,128)(2,1)} %get-tuple-element.99), channel_id=1, source_target_pairs={{0,1},{1,0},{2,3},{3,2},{4,5},{5,4},{6,7},{7,6}} | collective-permute-start | bytes 1966088 | tf_op jit(solution)/shard_map/ppermute | solution.py:238
  1850.9 37.1 %collective-permute-start.23 = (bf16[2,640,256]{2,1,0:T(8,128)(2,1)}, bf16[2,640,256]{2,1,0:T(8,128)(2,1)S(1)}, u32[]{:S(2)}, u32[]{:S(2)}) collective-permute-start(bf16[2,640,256]{2,1,0:T(8,128)(2,1)} %get-tuple-element.100), channel_id=1, source_target_pairs={{0,2},{1,3},{2,0},{3,1},{4,6},{5,7},{6,4},{7,5}} | collective-permute-start | bytes 1966088 | tf_op jit(solution)/shard_map/ppermute | solution.py:238
  1852.4 51.0 %collective-permute-start.24 = (bf16[2,640,256]{2,1,0:T(8,128)(2,1)}, bf16[2,640,256]{2,1,0:T(8,128)(2,1)}, u32[]{:S(2)}, u32[]{:S(2)}) collective-permute-start(bf16[2,640,256]{2,1,0:T(8,128)(2,1)} %get-tuple-element.101), channel_id=1, source_target_pairs={{0,3},{1,2},{2,1},{3,0},{4,7},{5,6},{6,5},{7,4}} | collective-permute-start | bytes 1966088 | tf_op jit(solution)/shard_map/ppermute | solution.py:238
  1852.4 52.5 %collective-permute-start.18 = (bf16[2,640,256]{2,1,0:T(8,128)(2,1)}, bf16[2,640,256]{2,1,0:T(8,128)(2,1)S(1)}, u32[]{:S(2)}, u32[]{:S(2)}) collective-permute-start(bf16[2,640,256]{2,1,0:T(8,128)(2,1)} %get-tuple-element.95), channel_id=1, source_target_pairs={{0,1},{1,0},{2,3},{3,2},{4,5},{5,4},{6,7},{7,6}} | collective-permute-start | bytes 1966088 | tf_op jit(solution)/shard_map/ppermute | solution.py:238
  1886.5 33.3 %collective-permute-start.19 = (bf16[2,640,256]{2,1,0:T(8,128)(2,1)}, bf16[2,640,256]{2,1,0:T(8,128)(2,1)S(1)}, u32[]{:S(2)}, u32[]{:S(2)}) collective-permute-start(bf16[2,640,256]{2,1,0:T(8,128)(2,1)} %get-tuple-element.96), channel_id=1, source_target_pairs={{0,2},{1,3},{2,0},{3,1},{4,6},{5,7},{6,4},{7,5}} | collective-permute-start | bytes 1966088 | tf_op jit(solution)/shard_map/ppermute | solution.py:238
  1888.0 35.5 %collective-permute-start.20 = (bf16[2,640,256]{2,1,0:T(8,128)(2,1)}, bf16[2,640,256]{2,1,0:T(8,128)(2,1)}, u32[]{:S(2)}, u32[]{:S(2)}) collective-permute-start(bf16[2,640,256]{2,1,0:T(8,128)(2,1)} %get-tuple-element.97), channel_id=1, source_target_pairs={{0,3},{1,2},{2,1},{3,0},{4,7},{5,6},{6,5},{7,4}} | collective-permute-start | bytes 1966088 | tf_op jit(solution)/shard_map/ppermute | solution.py:238
  1888.0 36.0 %collective-permute-start.66 = (bf16[2,640,256]{2,1,0:T(8,128)(2,1)}, bf16[2,640,256]{2,1,0:T(8,128)(2,1)S(1)}, u32[]{:S(2)}, u32[]{:S(2)}) collective-permute-start(bf16[2,640,256]{2,1,0:T(8,128)(2,1)} %get-tuple-element.143), channel_id=1, source_target_pairs={{0,1},{1,0},{2,3},{3,2},{4,5},{5,4},{6,7},{7,6}} | collective-permute-start | bytes 1966088 | tf_op jit(solution)/shard_map/ppermute | solution.py:238
  1903.4 36.5 %collective-permute-start.67 = (bf16[2,640,256]{2,1,0:T(8,128)(2,1)}, bf16[2,640,256]{2,1,0:T(8,128)(2,1)S(1)}, u32[]{:S(2)}, u32[]{:S(2)}) collective-permute-start(bf16[2,640,256]{2,1,0:T(8,128)(2,1)} %get-tuple-element.144), channel_id=1, source_target_pairs={{0,2},{1,3},{2,0},{3,1},{4,6},{5,7},{6,4},{7,5}} | collective-permute-start | bytes 1966088 | tf_op jit(solution)/shard_map/ppermute | solution.py:238
  1904.9 46.5 %collective-permute-start.68 = (bf16[2,640,256]{2,1,0:T(8,128)(2,1)}, bf16[2,640,256]{2,1,0:T(8,128)(2,1)S(1)}, u32[]{:S(2)}, u32[]{:S(2)}) collective-permute-start(bf16[2,640,256]{2,1,0:T(8,128)(2,1)} %get-tuple-element.145), channel_id=1, source_target_pairs={{0,3},{1,2},{2,1},{3,0},{4,7},{5,6},{6,5},{7,4}} | collective-permute-start | bytes 1966088 | tf_op jit(solution)/shard_map/ppermute | solution.py:238
  1919.8 47.7 %collective-permute-start.62 = (bf16[2,640,256]{2,1,0:T(8,128)(2,1)}, bf16[2,640,256]{2,1,0:T(8,128)(2,1)S(1)}, u32[]{:S(2)}, u32[]{:S(2)}) collective-permute-start(bf16[2,640,256]{2,1,0:T(8,128)(2,1)} %get-tuple-element.139), channel_id=1, source_target_pairs={{0,1},{1,0},{2,3},{3,2},{4,5},{5,4},{6,7},{7,6}} | collective-permute-start | bytes 1966088 | tf_op jit(solution)/shard_map/ppermute | solution.py:238
  1923.5 45.3 %collective-permute-start.63 = (bf16[2,640,256]{2,1,0:T(8,128)(2,1)}, bf16[2,640,256]{2,1,0:T(8,128)(2,1)S(1)}, u32[]{:S(2)}, u32[]{:S(2)}) collective-permute-start(bf16[2,640,256]{2,1,0:T(8,128)(2,1)} %get-tuple-element.140), channel_id=1, source_target_pairs={{0,2},{1,3},{2,0},{3,1},{4,6},{5,7},{6,4},{7,5}} | collective-permute-start | bytes 1966088 | tf_op jit(solution)/shard_map/ppermute | solution.py:238
  1924.0 55.6 %collective-permute-start.64 = (bf16[2,640,256]{2,1,0:T(8,128)(2,1)}, bf16[2,640,256]{2,1,0:T(8,128)(2,1)}, u32[]{:S(2)}, u32[]{:S(2)}) collective-permute-start(bf16[2,640,256]{2,1,0:T(8,128)(2,1)} %get-tuple-element.141), channel_id=1, source_target_pairs={{0,3},{1,2},{2,1},{3,0},{4,7},{5,6},{6,5},{7,4}} | collective-permute-start | bytes 1966088 | tf_op jit(solution)/shard_map/ppermute | solution.py:238
  1939.9 55.2 %collective-permute-start.58 = (bf16[2,640,256]{2,1,0:T(8,128)(2,1)}, bf16[2,640,256]{2,1,0:T(8,128)(2,1)S(1)}, u32[]{:S(2)}, u32[]{:S(2)}) collective-permute-start(bf16[2,640,256]{2,1,0:T(8,128)(2,1)} %get-tuple-element.135), channel_id=1, source_target_pairs={{0,1},{1,0},{2,3},{3,2},{4,5},{5,4},{6,7},{7,6}} | collective-permute-start | bytes 1966088 | tf_op jit(solution)/shard_map/ppermute | solution.py:238
  1952.3 44.0 %collective-permute-start.59 = (bf16[2,640,256]{2,1,0:T(8,128)(2,1)}, bf16[2,640,256]{2,1,0:T(8,128)(2,1)S(1)}, u32[]{:S(2)}, u32[]{:S(2)}) collective-permute-start(bf16[2,640,256]{2,1,0:T(8,128)(2,1)} %get-tuple-element.136), channel_id=1, source_target_pairs={{0,2},{1,3},{2,0},{3,1},{4,6},{5,7},{6,4},{7,5}} | collective-permute-start | bytes 1966088 | tf_op jit(solution)/shard_map/ppermute | solution.py:238
  1967.5 44.2 %collective-permute-start.60 = (bf16[2,640,256]{2,1,0:T(8,128)(2,1)}, bf16[2,640,256]{2,1,0:T(8,128)(2,1)}, u32[]{:S(2)}, u32[]{:S(2)}) collective-permute-start(bf16[2,640,256]{2,1,0:T(8,128)(2,1)} %get-tuple-element.137), channel_id=1, source_target_pairs={{0,3},{1,2},{2,1},{3,0},{4,7},{5,6},{6,5},{7,4}} | collective-permute-start | bytes 1966088 | tf_op jit(solution)/shard_map/ppermute | solution.py:238
  1969.6 42.7 %collective-permute-start.54 = (bf16[2,640,256]{2,1,0:T(8,128)(2,1)}, bf16[2,640,256]{2,1,0:T(8,128)(2,1)S(1)}, u32[]{:S(2)}, u32[]{:S(2)}) collective-permute-start(bf16[2,640,256]{2,1,0:T(8,128)(2,1)} %get-tuple-element.131), channel_id=1, source_target_pairs={{0,1},{1,0},{2,3},{3,2},{4,5},{5,4},{6,7},{7,6}} | collective-permute-start | bytes 1966088 | tf_op jit(solution)/shard_map/ppermute | solution.py:238
  1979.6 42.6 %collective-permute-start.55 = (bf16[2,640,256]{2,1,0:T(8,128)(2,1)}, bf16[2,640,256]{2,1,0:T(8,128)(2,1)S(1)}, u32[]{:S(2)}, u32[]{:S(2)}) collective-permute-start(bf16[2,640,256]{2,1,0:T(8,128)(2,1)} %get-tuple-element.132), channel_id=1, source_target_pairs={{0,2},{1,3},{2,0},{3,1},{4,6},{5,7},{6,4},{7,5}} | collective-permute-start | bytes 1966088 | tf_op jit(solution)/shard_map/ppermute | solution.py:238
  1995.1 42.3 %collective-permute-start.56 = (bf16[2,640,256]{2,1,0:T(8,128)(2,1)}, bf16[2,640,256]{2,1,0:T(8,128)(2,1)S(1)}, u32[]{:S(2)}, u32[]{:S(2)}) collective-permute-start(bf16[2,640,256]{2,1,0:T(8,128)(2,1)} %get-tuple-element.133), channel_id=1, source_target_pairs={{0,3},{1,2},{2,1},{3,0},{4,7},{5,6},{6,5},{7,4}} | collective-permute-start | bytes 1966088 | tf_op jit(solution)/shard_map/ppermute | solution.py:238
  1996.3 41.6 %collective-permute-start.50 = (bf16[2,640,256]{2,1,0:T(8,128)(2,1)}, bf16[2,640,256]{2,1,0:T(8,128)(2,1)S(1)}, u32[]{:S(2)}, u32[]{:S(2)}) collective-permute-start(bf16[2,640,256]{2,1,0:T(8,128)(2,1)} %get-tuple-element.127), channel_id=1, source_target_pairs={{0,1},{1,0},{2,3},{3,2},{4,5},{5,4},{6,7},{7,6}} | collective-permute-start | bytes 1966088 | tf_op jit(solution)/shard_map/ppermute | solution.py:238
  2011.7 42.3 %collective-permute-start.51 = (bf16[2,640,256]{2,1,0:T(8,128)(2,1)}, bf16[2,640,256]{2,1,0:T(8,128)(2,1)S(1)}, u32[]{:S(2)}, u32[]{:S(2)}) collective-permute-start(bf16[2,640,256]{2,1,0:T(8,128)(2,1)} %get-tuple-element.128), channel_id=1, source_target_pairs={{0,2},{1,3},{2,0},{3,1},{4,6},{5,7},{6,4},{7,5}} | collective-permute-start | bytes 1966088 | tf_op jit(solution)/shard_map/ppermute | solution.py:238
  2012.3 51.6 %collective-permute-start.52 = (bf16[2,640,256]{2,1,0:T(8,128)(2,1)}, bf16[2,640,256]{2,1,0:T(8,128)(2,1)}, u32[]{:S(2)}, u32[]{:S(2)}) collective-permute-start(bf16[2,640,256]{2,1,0:T(8,128)(2,1)} %get-tuple-element.129), channel_id=1, source_target_pairs={{0,3},{1,2},{2,1},{3,0},{4,7},{5,6},{6,5},{7,4}} | collective-permute-start | bytes 1966088 | tf_op jit(solution)/shard_map/ppermute | solution.py:238
  2022.2 42.2 %collective-permute-start.46 = (bf16[2,640,256]{2,1,0:T(8,128)(2,1)}, bf16[2,640,256]{2,1,0:T(8,128)(2,1)S(1)}, u32[]{:S(2)}, u32[]{:S(2)}) collective-permute-start(bf16[2,640,256]{2,1,0:T(8,128)(2,1)} %get-tuple-element.123), channel_id=1, source_target_pairs={{0,1},{1,0},{2,3},{3,2},{4,5},{5,4},{6,7},{7,6}} | collective-permute-start | bytes 1966088 | tf_op jit(solution)/shard_map/ppermute | solution.py:238
  2037.4 43.2 %collective-permute-start.47 = (bf16[2,640,256]{2,1,0:T(8,128)(2,1)}, bf16[2,640,256]{2,1,0:T(8,128)(2,1)S(1)}, u32[]{:S(2)}, u32[]{:S(2)}) collective-permute-start(bf16[2,640,256]{2,1,0:T(8,128)(2,1)} %get-tuple-element.124), channel_id=1, source_target_pairs={{0,2},{1,3},{2,0},{3,1},{4,6},{5,7},{6,4},{7,5}} | collective-permute-start | bytes 1966088 | tf_op jit(solution)/shard_map/ppermute | solution.py:238
  2038.0 54.0 %collective-permute-start.48 = (bf16[2,640,256]{2,1,0:T(8,128)(2,1)}, bf16[2,640,256]{2,1,0:T(8,128)(2,1)}, u32[]{:S(2)}, u32[]{:S(2)}) collective-permute-start(bf16[2,640,256]{2,1,0:T(8,128)(2,1)} %get-tuple-element.125), channel_id=1, source_target_pairs={{0,3},{1,2},{2,1},{3,0},{4,7},{5,6},{6,5},{7,4}} | collective-permute-start | bytes 1966088 | tf_op jit(solution)/shard_map/ppermute | solution.py:238
  2054.1 54.9 %collective-permute-start.42 = (bf16[2,640,256]{2,1,0:T(8,128)(2,1)}, bf16[2,640,256]{2,1,0:T(8,128)(2,1)S(1)}, u32[]{:S(2)}, u32[]{:S(2)}) collective-permute-start(bf16[2,640,256]{2,1,0:T(8,128)(2,1)} %get-tuple-element.119), channel_id=1, source_target_pairs={{0,1},{1,0},{2,3},{3,2},{4,5},{5,4},{6,7},{7,6}} | collective-permute-start | bytes 1966088 | tf_op jit(solution)/shard_map/ppermute | solution.py:238
  2063.9 45.6 %collective-permute-start.43 = (bf16[2,640,256]{2,1,0:T(8,128)(2,1)}, bf16[2,640,256]{2,1,0:T(8,128)(2,1)S(1)}, u32[]{:S(2)}, u32[]{:S(2)}) collective-permute-start(bf16[2,640,256]{2,1,0:T(8,128)(2,1)} %get-tuple-element.120), channel_id=1, source_target_pairs={{0,2},{1,3},{2,0},{3,1},{4,6},{5,7},{6,4},{7,5}} | collective-permute-start | bytes 1966088 | tf_op jit(solution)/shard_map/ppermute | solution.py:238
  2064.4 55.5 %collective-permute-start.44 = (bf16[2,640,256]{2,1,0:T(8,128)(2,1)}, bf16[2,640,256]{2,1,0:T(8,128)(2,1)S(1)}, u32[]{:S(2)}, u32[]{:S(2)}) collective-permute-start(bf16[2,640,256]{2,1,0:T(8,128)(2,1)} %get-tuple-element.121), channel_id=1, source_target_pairs={{0,3},{1,2},{2,1},{3,0},{4,7},{5,6},{6,5},{7,4}} | collective-permute-start | bytes 1966088 | tf_op jit(solution)/shard_map/ppermute | solution.py:238
  2092.0 43.8 %collective-permute-start.39 = (bf16[2,640,128]{2,1,0:T(8,128)(2,1)}, bf16[2,640,128]{2,1,0:T(8,128)(2,1)S(1)}, u32[]{:S(2)}, u32[]{:S(2)}) collective-permute-start(bf16[2,640,128]{2,1,0:T(8,128)(2,1)} %get-tuple-element.116), channel_id=1, source_target_pairs={{0,2},{1,3},{2,0},{3,1},{4,6},{5,7},{6,4},{7,5}} | collective-permute-start | bytes 983048 | tf_op jit(solution)/shard_map/ppermute | solution.py:238
  2109.0 41.2 %collective-permute-start.13 = (bf16[2,640,128]{2,1,0:T(8,128)(2,1)}, bf16[2,640,128]{2,1,0:T(8,128)(2,1)S(1)}, u32[]{:S(2)}, u32[]{:S(2)}) collective-permute-start(bf16[2,640,128]{2,1,0:T(8,128)(2,1)} %get-tuple-element.92), channel_id=1, source_target_pairs={{0,2},{1,3},{2,0},{3,1},{4,6},{5,7},{6,4},{7,5}} | collective-permute-start | bytes 983048 | tf_op jit(solution)/shard_map/ppermute | solution.py:238
  2109.5 40.7 %collective-permute-start.14 = (bf16[2,640,128]{2,1,0:T(8,128)(2,1)}, bf16[2,640,128]{2,1,0:T(8,128)(2,1)S(1)}, u32[]{:S(2)}, u32[]{:S(2)}) collective-permute-start(bf16[2,640,128]{2,1,0:T(8,128)(2,1)} %get-tuple-element.93), channel_id=1, source_target_pairs={{0,3},{1,2},{2,1},{3,0},{4,7},{5,6},{6,5},{7,4}} | collective-permute-start | bytes 983048 | tf_op jit(solution)/shard_map/ppermute | solution.py:238
  (63 other events, 1130.4 us)

commit v3 on v2

--- a/solution.py
+++ b/solution.py
@@ -123,15 +123,15 @@
     )(*args)
 
 
-def final_kernel(h, p, wd, *outs):
+def final_kernel(h0, h1, p, wd, *outs):
     m = pl.program_id(0) % len(outs)
-    cap = h.shape[2]
-    for lo in range(0, cap, cap // 2):
-        rows = slice(lo, lo + cap // 2)
-        y = (p[0, 0, 0, rows] + mm(h[0, 0, rows], wd[...])).astype(BF16)
-        for j, out in enumerate(outs):
-
-            @pl.when(m == j)
+    half = h0.shape[3]
+    for j, h in enumerate((h0, h1)):
+        rows = slice(j * half, (j + 1) * half)
+        y = (p[0, 0, 0, rows] + mm(h[0, 0, 0], wd[...])).astype(BF16)
+        for t, out in enumerate(outs):
+
+            @pl.when(m == t)
             def _():
                 out[0, rows] = y
 
@@ -141,76 +141,82 @@
     cols = wd.shape[1]
     at, n, m0 = lo // cols, len(masks), masks[0]
     rows = 2 * n * cap
+    halves = h.reshape(2, MASKS, 2, cap // 2, width)
     return call(
         final_kernel, 2 * rows * width * cols, 2 * (rows * width + width * cols) + 6 * rows * cols,
         grid=(2 * n,),
-        in_specs=[
-            pl.BlockSpec((1, 1, cap, width), lambda i: (i // n, m0 + i % n, 0, 0)),
+        in_specs=[pl.BlockSpec((1, 1, 1, cap // 2, width), functools.partial(lambda j, i: (i // n, m0 + i % n, j, 0, 0), j)) for j in range(2)]
+        + [
             pl.BlockSpec((1, 1, 1, cap, cols), lambda i: (k, i // n, m0 + i % n, 0, at)),
             pl.BlockSpec((width, cols), lambda i: (0, 0)),
         ],
         out_specs=[pl.BlockSpec((1, cap, cols), functools.partial(lambda m, i: (jnp.where(i >= n + m, 1, 0), 0, 0), m)) for m in range(n)],
         out_shape=[jax.ShapeDtypeStruct((2, cap, cols), BF16)] * n,
-    )(h, p, wd)
-
-
-def picked(k, ys, pick, gate):
-    total = None
+    )(halves, halves, p, wd)
+
+
+def picked(k, groups, pos, gate):
+    slots = lax.broadcasted_iota(jnp.int32, (TB, groups[0][0].shape[1]), 1)
+    totals = [None] * len(groups)
     for m in range(MASKS):
         e = 2 * m + k
-        term = gate[0, :, e:e + 1] * mm(pick[0, m], ys[m][0])
-        total = term if total is None else total + term
-    return total
-
-
-def combine_first_kernel(k, *refs):
-    refs[-1][...] = picked(k, refs[:MASKS], refs[MASKS], refs[MASKS + 1])
-
-
-def combine_kernel(k, *refs):
-    acc, outs = refs[MASKS + 2], refs[-2:]
+        onehot = (slots == pos[0, :, e:e + 1]).astype(BF16)
+        for j, ys in enumerate(groups):
+            term = gate[0, :, e:e + 1] * mm(onehot, ys[m][0])
+            totals[j] = term if totals[j] is None else totals[j] + term
+    return totals
+
+
+def combine_kernel(k, n, *refs):
+    groups = [refs[MASKS * j:MASKS * (j + 1)] for j in range(n)]
+    totals = picked(k, groups, *refs[MASKS * n:MASKS * n + 2])
+    cols = groups[0][0].shape[2]
     i, blocks = pl.program_id(0), pl.num_programs(0) // 2
-    total = (acc[...] + picked(k, refs[:MASKS], refs[MASKS], refs[MASKS + 1])).astype(BF16)
-    for b, out in enumerate(outs):
-
-        @pl.when(i // blocks == b)
-        def _():
-            out[...] = total
-
-
-def combine(ys, pick, gate, k, lo, model, acc=None, into=None):
-    _, cap, cols = ys[0].shape
-    toks = pick.shape[2]
+    for j, total in enumerate(totals):
+        at = slice(j * cols, (j + 1) * cols)
+        if k == 0:
+            refs[-1][:, at] = total
+            continue
+        total = (refs[MASKS * n + 2][:, at] + total).astype(BF16)
+        for b, out in enumerate(refs[-2:]):
+
+            @pl.when(i // blocks == b)
+            def _():
+                out[:, at] = total
+
+
+def combine(groups, pos, gate, k, lo, model, acc=None, into=None):
+    _, cap, cols = groups[0][0].shape
+    n, wide = len(groups), cols * len(groups)
+    toks = pos.shape[1]
     blocks = toks // TB
-    at = lo // cols
-    in_specs = [pl.BlockSpec((1, cap, cols), lambda i: (i // blocks, 0, 0)) for _ in ys]
-    in_specs += [
-        pl.BlockSpec((1, MASKS, TB, cap), lambda i: (i // blocks, 0, i % blocks, 0)),
-        pl.BlockSpec((1, TB, gate.shape[2]), lambda i: (i // blocks, i % blocks, 0)),
-    ]
-    args = [*ys, pick, gate]
-    flops, nbytes = 2 * 2 * toks * MASKS * cap * cols, 2 * 2 * toks * MASKS * cap + 2 * toks * cols * 6
-    if acc is None:
+    at = lo // wide
+    args = [y for ys in groups for y in ys] + [pos, gate]
+    in_specs = [pl.BlockSpec((1, cap, cols), lambda i: (i // blocks, 0, 0))] * (MASKS * n)
+    in_specs += [pl.BlockSpec((1, TB, pos.shape[2]), lambda i: (i // blocks, i % blocks, 0))] * 2
+    flops, nbytes = 2 * 2 * toks * MASKS * cap * wide, 2 * toks * wide * 6
+    kernel = functools.partial(combine_kernel, k, n)
+    if k == 0:
         kw = filled_further(into, args, in_specs)
         return call(
-            functools.partial(combine_first_kernel, k), flops, nbytes,
+            kernel, flops, nbytes,
             grid=(2 * blocks,), in_specs=in_specs,
-            out_specs=pl.BlockSpec((TB, cols), lambda i: (i, at)),
+            out_specs=pl.BlockSpec((TB, wide), lambda i: (i, at)),
             out_shape=jax.ShapeDtypeStruct((2 * toks, model), F32), **kw,
         )(*args)
     args.append(acc)
-    in_specs.append(pl.BlockSpec((TB, cols), lambda i: (i, at)))
+    in_specs.append(pl.BlockSpec((TB, wide), lambda i: (i, at)))
     kw = {}
     if into is not None:
         kw["input_output_aliases"] = {len(args): 0, len(args) + 1: 1}
         args += into
         in_specs += [pl.BlockSpec(memory_space=pl.ANY)] * 2
     return call(
-        functools.partial(combine_kernel, k), flops, nbytes,
+        kernel, flops, nbytes,
         grid=(2 * blocks,), in_specs=in_specs,
         out_specs=[
-            pl.BlockSpec((TB, cols), lambda i: (jnp.minimum(i, blocks - 1), at)),
-            pl.BlockSpec((TB, cols), lambda i: (jnp.maximum(i - blocks, 0), at)),
+            pl.BlockSpec((TB, wide), lambda i: (jnp.minimum(i, blocks - 1), at)),
+            pl.BlockSpec((TB, wide), lambda i: (jnp.maximum(i - blocks, 0), at)),
         ],
         out_shape=[jax.ShapeDtypeStruct((toks, model), BF16)] * 2, **kw,
     )(*args)
@@ -233,6 +239,7 @@
     down_cuts = [cuts([1024] + [256] * 4), cuts([256] * 7 + [128, 128])]
     late = [(0, n) for n in range(1, 5)] + [(1, n) for n in range(9)]
     halves = [(1, 7), (1, 8)]
+    groups = [[(0, 0)], [(0, 1), (0, 2)], [(0, 3), (0, 4)], [(1, 0), (1, 1)], [(1, 2), (1, 3)], [(1, 4), (1, 5)], [(1, 6)], [(1, 7)], [(1, 8)]]
 
     def ep_swap(value, mask):
         return lax.ppermute(value, "ep", [(i, i ^ mask) for i in range(ep_size)])
@@ -272,7 +279,7 @@
             down[k][n] = tp_swap(w_down, k, lo, hi)
 
         pos, gate, cap = routing(jnp.stack([ids_a, ids_b]), jnp.stack([gates_a, gates_b]), me)
-        gate_t = gate.transpose(0, 2, 1)
+        pos_t, gate_t = pos.transpose(0, 2, 1), gate.transpose(0, 2, 1)
 
         xs = []
         for b, tokens in enumerate((tokens_a, tokens_b)):
@@ -281,9 +288,6 @@
             far = [ep_swap(far[0], 2), ep_swap(far[1], 3)]
             near = dispatch(rows[:4], tokens, cap)
             xs.append([near[0], ep_swap(near[1], 1), *far])
-        slots = jnp.arange(cap, dtype=jnp.int32)
-        picks = [(pos.reshape(2, MASKS, 2, -1)[:, :, k, :, None] == slots).astype(BF16) for k in range(2)]
-
         p, h_l = None, []
         for b in range(2):
             h_l.append(hidden_local(xs[b], w_gate, w_up))
@@ -297,7 +301,7 @@
             for b in range(2):
                 h_r[1] = hidden(xs[b], b, 1, gate1, up1[n], lo, h_r[1])
 
-        acc, outs = None, None
+        acc, outs, back = None, None, {}
         for k, n in [(0, 0)] + late:
             lo, hi = down_cuts[k][n]
             if (k, n) in halves:
@@ -308,10 +312,15 @@
                 far = [y2, y3]
             far = [ep_swap(far[0], 2), ep_swap(far[1], 3)]
             near = [near[0], ep_swap(near[1], 1)]
+            back[k, n] = near + far
+        for group in groups:
+            k, n = group[-1]
+            lo = down_cuts[k][group[0][1]][0]
+            done = [back[item] for item in group]
             if k == 0:
-                acc = combine(near + far, picks[0], gate_t, 0, lo, model, None, acc)
+                acc = combine(done, pos_t, gate_t, 0, lo, model, None, acc)
             else:
-                outs = combine(near + far, picks[1], gate_t, 1, lo, model, acc, outs)
+                outs = combine(done, pos_t, gate_t, 1, lo, model, acc, outs)
         return tuple(outs)
 
     in_specs = (row_spec, row_spec, row_spec, row_spec, row_spec, row_spec, gate_spec, gate_spec, down_spec)

time: 2170 us -> 2180 us (level)
  waiting for transfers between devices: 645 us -> 703 us
  Pallas kernels: 1380 us -> 1340 us
    ppermute x48, waiting for transfers between devices: 320 us -> 382 us  [ep_swap(): return lax.ppermute(value, 'ep', [(i, i ^ mask) for i in range(ep_size)])]
    pallas_call x14 -> x9, Pallas kernels: 225 us -> 164 us  [combine(): call(kernel, flops, nbytes, grid=(2 * blocks,), in_specs=in_specs, out_sp...]
  transfers between devices with their start and end apart: 69 -> 69, of which waited for: 15 -> 22; matrix products, arithmetic and copies ran while one was open for 3% -> 3% of each run, Pallas kernels for 62% -> 60%
where the time goes in v3:
time: 2180 us; the launch traced here: 2170 us
  Pallas kernels  1340 us (61%)
  waiting for transfers between devices  703 us (32%)
  local copies, waits for them, and re-layouts  71.7 us (3%)
  starting transfers between devices  55.5 us (3%)
    ppermute x48, waiting for transfers between devices, ep_swap(): return lax.ppermute(value, 'ep', [(i, i ^ mask) for i in range(ep_size)])  382 us
    pallas_call x16, Pallas kernels, final(): call(final_kernel, 2 * rows * width * cols, 2 * (rows * width + width * c...  336 us
    ppermute x21, waiting for transfers between devices, tp_swap(): return lax.ppermute(piece, 'tp', TP_SWAP)[0]  322 us
    pallas_call x10, Pallas kernels, hidden(): call(hidden_kernel, 4 * rows * model * cols, 2 * (rows * model + 2 * mode...  306 us
    pallas_call x2, Pallas kernels, hidden_local(): call(hidden_kernel, 4 * rows * model * width, 2 * (rows * model + 4 * mod...  259 us
    pallas_call x9, Pallas kernels, combine(): call(kernel, flops, nbytes, grid=(2 * blocks,), in_specs=in_specs, out_sp...  164 us
    pallas_call x2, Pallas kernels, part(): call(part_kernel, 2 * rows * width * model, 2 * (rows * width + 2 * width...  146 us
    pallas_call x4, Pallas kernels, dispatch(): call(dispatch_kernel, 2 * n * 2 * cap * toks * model, toks * model * 2 +...  125 us
  transfers between devices with their start and end apart: 69, of which 22 were waited for; matrix products, arithmetic and copies ran while one was open for 3% of the time, Pallas kernels for 60%

profile of v3, /device:TPU:0, one launch (start us, length us, event | category | flops | bytes accessed | tf_op | source)
XLA Modules:
  0.0 2174.3 jit_solution(2023063557125932528)
XLA Ops:
  14.8 31.1 %shard_map.106 = (bf16[2,640,2048]{2,1,0:T(8,128)(2,1)}, bf16[2,640,2048]{2,1,0:T(8,128)(2,1)}) custom-call(s32[4,1,2048]{2,1,0:T(1,128)} %copy.54.pos_ref, bf16[2048,2048]{1,0:T(8,128)(2,1)} %tok_ref.7), custom_call_target="tpu_custom_call" | custom-call | flops 21474836480 | bytes 18874368 | tf_op jit(solution)/shard_map/pallas_call | solution.py:56
  47.6 31.1 %shard_map.107 = (bf16[2,640,2048]{2,1,0:T(8,128)(2,1)}, bf16[2,640,2048]{2,1,0:T(8,128)(2,1)}) custom-call(s32[4,1,2048]{2,1,0:T(1,128)} %copy.55.pos_ref, bf16[2048,2048]{1,0:T(8,128)(2,1)} %tok_ref.7), custom_call_target="tpu_custom_call" | custom-call | flops 21474836480 | bytes 18874368 | tf_op jit(solution)/shard_map/pallas_call | solution.py:56
  82.2 31.6 %shard_map.104 = (bf16[2,640,2048]{2,1,0:T(8,128)(2,1)}, bf16[2,640,2048]{2,1,0:T(8,128)(2,1)}) custom-call(s32[4,1,2048]{2,1,0:T(1,128)} %copy.52.pos_ref, bf16[2048,2048]{1,0:T(8,128)(2,1)} %tok_ref.5), custom_call_target="tpu_custom_call" | custom-call | flops 21474836480 | bytes 18874368 | tf_op jit(solution)/shard_map/pallas_call | solution.py:56
  114.8 31.0 %shard_map.105 = (bf16[2,640,2048]{2,1,0:T(8,128)(2,1)}, bf16[2,640,2048]{2,1,0:T(8,128)(2,1)}) custom-call(s32[4,1,2048]{2,1,0:T(1,128)} %copy.53.pos_ref, bf16[2048,2048]{1,0:T(8,128)(2,1)} %tok_ref.5), custom_call_target="tpu_custom_call" | custom-call | flops 21474836480 | bytes 18874368 | tf_op jit(solution)/shard_map/pallas_call | solution.py:56
  147.8 9.9 slice.116
  173.3 7.0 fusion.5
  180.2 13.3 fusion.2
  196.7 8.1 fusion.4
  206.4 101.0 %collective-permute-done.7.refs_3_ = bf16[2,640,2048]{2,1,0:T(8,128)(2,1)} collective-permute-done((bf16[2,640,2048]{2,1,0:T(8,128)(2,1)}, bf16[2,640,2048]{2,1,0:T(8,128)(2,1)}, u32[]{:S(2)}, u32[]{:S(2)}) %collective-permute-start.7) | collective-permute-done | bytes 5242912 | tf_op jit(solution)/shard_map/ppermute | solution.py:245
  308.9 129.8 %shard_map.117.h = bf16[2,4,640,2816]{3,2,1,0:T(8,128)(2,1)} custom-call(bf16[2,640,2048]{2,1,0:T(8,128)(2,1)} %get-tuple-element.80.refs_0_, bf16[2,640,2048]{2,1,0:T(8,128)(2,1)} %collective-permute-done.5.refs_1_, bf16[2,640,2048]{2,1,0:T(8,128)(2,1)} %collective-permute-done.6.refs_2_, bf16[2,640,2048]{2,1,0:T(8,128)(2,1)} %collective-permute-done.7.refs_3_, ...), custom_call_target="tpu_custom_call" | custom-call | flops 118111600640 | bytes 95944704 | tf_op jit(solution)/shard_map/pallas_call | solution.py:79
  440.7 91.4 %collective-permute-done.2.refs_3_ = bf16[2,640,2048]{2,1,0:T(8,128)(2,1)} collective-permute-done((bf16[2,640,2048]{2,1,0:T(8,128)(2,1)}, bf16[2,640,2048]{2,1,0:T(8,128)(2,1)}, u32[]{:S(2)}, u32[]{:S(2)}) %collective-permute-start.2) | collective-permute-done | bytes 5242912 | tf_op jit(solution)/shard_map/ppermute | solution.py:245
  533.6 129.5 %shard_map.116.h = bf16[2,4,640,2816]{3,2,1,0:T(8,128)(2,1)} custom-call(bf16[2,640,2048]{2,1,0:T(8,128)(2,1)} %get-tuple-element.76.refs_0_, bf16[2,640,2048]{2,1,0:T(8,128)(2,1)} %collective-permute-done.refs_1_, bf16[2,640,2048]{2,1,0:T(8,128)(2,1)} %collective-permute-done.1.refs_2_, bf16[2,640,2048]{2,1,0:T(8,128)(2,1)} %collective-permute-done.2.refs_3_, ...), custom_call_target="tpu_custom_call" | custom-call | flops 118111600640 | bytes 95944704 | tf_op jit(solution)/shard_map/pallas_call | solution.py:79
  663.1 72.8 %shard_map.118.refs_0_ = f32[2,2,4,640,2048]{4,3,2,1,0:T(8,128)} custom-call(bf16[2,4,640,2816]{3,2,1,0:T(8,128)(2,1)} %shard_map.117.h, bf16[2,2816,2048]{2,1,0:T(8,128)(2,1)} %wd.3), custom_call_target="tpu_custom_call" | custom-call | flops 59055800320 | bytes 93847552 | tf_op jit(solution)/shard_map/pallas_call | solution.py:118
  735.9 72.8 %shard_map.119.p = f32[2,2,4,640,2048]{4,3,2,1,0:T(8,128)} custom-call(bf16[2,4,640,2816]{3,2,1,0:T(8,128)(2,1)} %shard_map.116.h, bf16[2,2816,2048]{2,1,0:T(8,128)(2,1)} %wd.3, f32[2,2,4,640,2048]{4,3,2,1,0:T(8,128)} %shard_map.118.refs_0_), custom_call_target="tpu_custom_call", output_to_operand_aliasing={{}: (2, {})} | custom-call | flops 59055800320 | bytes 93847552 | tf_op jit(solution)/shard_map/pallas_call | solution.py:118
  810.8 67.9 %shard_map.122.refs_6_ = bf16[2,4,640,2816]{3,2,1,0:T(8,128)(2,1)} custom-call(bf16[2,640,2048]{2,1,0:T(8,128)(2,1)} %get-tuple-element.80.refs_0_, bf16[2,640,2048]{2,1,0:T(8,128)(2,1)} %collective-permute-done.5.refs_1_, bf16[2,640,2048]{2,1,0:T(8,128)(2,1)} %collective-permute-done.6.refs_2_, bf16[2,640,2048]{2,1,0:T(8,128)(2,1)} %collective-permute-done.7.refs_3_, ...), custom_call_target="tpu_custom_call" | custom-call | flops 59055800320 | bytes 47972352 | tf_op jit(solution)/shard_map/pallas_call | solution.py:98
  878.6 67.6 %shard_map.123 = bf16[2,4,640,2816]{3,2,1,0:T(8,128)(2,1)} custom-call(bf16[2,640,2048]{2,1,0:T(8,128)(2,1)} %get-tuple-element.76.refs_0_, bf16[2,640,2048]{2,1,0:T(8,128)(2,1)} %collective-permute-done.refs_1_, bf16[2,640,2048]{2,1,0:T(8,128)(2,1)} %collective-permute-done.1.refs_2_, ...), custom_call_target="tpu_custom_call", output_to_operand_aliasing={{}: (6, {})} | custom-call | flops 59055800320 | bytes 47972352 | tf_op jit(solution)/shard_map/pallas_call | solution.py:98
  946.3 203.2 %collective-permute-done.10 = bf16[1,2048,512]{2,1,0:T(8,128)(2,1)S(1)} collective-permute-done((bf16[1,2048,512]{2,1,0:T(8,128)(2,1)}, bf16[1,2048,512]{2,1,0:T(8,128)(2,1)S(1)}, u32[]{:S(2)}, u32[]{:S(2)}) %collective-permute-start.10) | collective-permute-done | bytes 2097184 | tf_op jit(solution)/shard_map/ppermute | solution.py:249
  1151.6 17.0 shard_map.108.refs_6_
  1168.6 17.5 shard_map.109.refs_6_
  1186.1 53.4 %collective-permute-done.9 = bf16[1,2048,1024]{2,1,0:T(8,128)(2,1)} collective-permute-done((bf16[1,2048,1024]{2,1,0:T(8,128)(2,1)}, bf16[1,2048,1024]{2,1,0:T(8,128)(2,1)}, u32[]{:S(2)}, u32[]{:S(2)}) %collective-permute-start.9) | collective-permute-done | bytes 4194336 | tf_op jit(solution)/shard_map/ppermute | solution.py:249
  1241.1 28.3 %shard_map.110.refs_6_ = bf16[2,4,640,2816]{3,2,1,0:T(8,128)(2,1)} custom-call(bf16[2,640,2048]{2,1,0:T(8,128)(2,1)} %get-tuple-element.80.refs_0_, bf16[2,640,2048]{2,1,0:T(8,128)(2,1)} %collective-permute-done.5.refs_1_, bf16[2,640,2048]{2,1,0:T(8,128)(2,1)} %collective-permute-done.6.refs_2_, ...), custom_call_target="tpu_custom_call", output_to_operand_aliasing={{}: (6, {})} | custom-call | flops 21474836480 | bytes 24117248 | tf_op jit(solution)/shard_map/pallas_call | solution.py:98
  1269.4 28.3 %shard_map.111.refs_6_ = bf16[2,4,640,2816]{3,2,1,0:T(8,128)(2,1)} custom-call(bf16[2,640,2048]{2,1,0:T(8,128)(2,1)} %get-tuple-element.76.refs_0_, bf16[2,640,2048]{2,1,0:T(8,128)(2,1)} %collective-permute-done.refs_1_, bf16[2,640,2048]{2,1,0:T(8,128)(2,1)} %collective-permute-done.1.refs_2_, ...), custom_call_target="tpu_custom_call", output_to_operand_aliasing={{}: (6, {})} | custom-call | flops 21474836480 | bytes 24117248 | tf_op jit(solution)/shard_map/pallas_call | solution.py:98
  1298.2 42.2 %shard_map.128 = (bf16[2,640,1024]{2,1,0:T(8,128)(2,1)}, bf16[2,640,1024]{2,1,0:T(8,128)(2,1)}, bf16[2,640,1024]{2,1,0:T(8,128)(2,1)}, bf16[2,640,1024]{2,1,0:T(8,128)(2,1)}) custom-call(bf16[2,4,2,320,2816]{4,3,2,1,0:T(8,128)(2,1)} %bitcast.65, bf16[2,4,2,320,2816]{4,3,2,1,0:T(8,128)(2,1)} %bitcast.66, f32[2,2,4,640,2048]{4,3,2,1,0:T(8,128)} %shard_map.119.p, ...), custom_call_target="tpu_custom_call" | custom-call | flops 29527900160 | bytes 66060288 | tf_op jit(solution)/shard_map/pallas_call | solution.py:145
  1340.4 50.8 %collective-permute-done.8 = bf16[1,2048,1024]{2,1,0:T(8,128)(2,1)} collective-permute-done((bf16[1,2048,1024]{2,1,0:T(8,128)(2,1)}, bf16[1,2048,1024]{2,1,0:T(8,128)(2,1)}, u32[]{:S(2)}, u32[]{:S(2)}) %collective-permute-start.8) | collective-permute-done | bytes 4194336 | tf_op jit(solution)/shard_map/ppermute | solution.py:249
  1392.8 28.3 %shard_map.112.refs_6_ = bf16[2,4,640,2816]{3,2,1,0:T(8,128)(2,1)} custom-call(bf16[2,640,2048]{2,1,0:T(8,128)(2,1)} %get-tuple-element.80.refs_0_, bf16[2,640,2048]{2,1,0:T(8,128)(2,1)} %collective-permute-done.5.refs_1_, bf16[2,640,2048]{2,1,0:T(8,128)(2,1)} %collective-permute-done.6.refs_2_, ...), custom_call_target="tpu_custom_call", output_to_operand_aliasing={{}: (6, {})} | custom-call | flops 21474836480 | bytes 24117248 | tf_op jit(solution)/shard_map/pallas_call | solution.py:98
  1421.1 28.3 %shard_map.113.refs_6_ = bf16[2,4,640,2816]{3,2,1,0:T(8,128)(2,1)} custom-call(bf16[2,640,2048]{2,1,0:T(8,128)(2,1)} %get-tuple-element.76.refs_0_, bf16[2,640,2048]{2,1,0:T(8,128)(2,1)} %collective-permute-done.refs_1_, bf16[2,640,2048]{2,1,0:T(8,128)(2,1)} %collective-permute-done.1.refs_2_, ...), custom_call_target="tpu_custom_call", output_to_operand_aliasing={{}: (6, {})} | custom-call | flops 21474836480 | bytes 24117248 | tf_op jit(solution)/shard_map/pallas_call | solution.py:98
  1449.8 22.9 %shard_map.127 = (bf16[2,640,256]{2,1,0:T(8,128)(2,1)}, bf16[2,640,256]{2,1,0:T(8,128)(2,1)}, bf16[2,640,256]{2,1,0:T(8,128)(2,1)}, bf16[2,640,256]{2,1,0:T(8,128)(2,1)}) custom-call(bf16[2,4,2,320,2816]{4,3,2,1,0:T(8,128)(2,1)} %bitcast.67, bf16[2,4,2,320,2816]{4,3,2,1,0:T(8,128)(2,1)} %bitcast.68, f32[2,2,4,640,2048]{4,3,2,1,0:T(8,128)} %shard_map.119.p, ...), custom_call_target="tpu_custom_call" | custom-call | flops 7381975040 | bytes 38141952 | tf_op jit(solution)/shard_map/pallas_call | solution.py:145
  1474.3 23.2 %shard_map.126 = (bf16[2,640,256]{2,1,0:T(8,128)(2,1)}, bf16[2,640,256]{2,1,0:T(8,128)(2,1)}, bf16[2,640,256]{2,1,0:T(8,128)(2,1)}, bf16[2,640,256]{2,1,0:T(8,128)(2,1)}) custom-call(bf16[2,4,2,320,2816]{4,3,2,1,0:T(8,128)(2,1)} %bitcast.69, bf16[2,4,2,320,2816]{4,3,2,1,0:T(8,128)(2,1)} %bitcast.70, f32[2,2,4,640,2048]{4,3,2,1,0:T(8,128)} %shard_map.119.p, ...), custom_call_target="tpu_custom_call" | custom-call | flops 7381975040 | bytes 38141952 | tf_op jit(solution)/shard_map/pallas_call | solution.py:145
  1498.0 23.0 %shard_map.125 = (bf16[2,640,256]{2,1,0:T(8,128)(2,1)}, bf16[2,640,256]{2,1,0:T(8,128)(2,1)}, bf16[2,640,256]{2,1,0:T(8,128)(2,1)}, bf16[2,640,256]{2,1,0:T(8,128)(2,1)}) custom-call(bf16[2,4,2,320,2816]{4,3,2,1,0:T(8,128)(2,1)} %bitcast.71, bf16[2,4,2,320,2816]{4,3,2,1,0:T(8,128)(2,1)} %bitcast.72, f32[2,2,4,640,2048]{4,3,2,1,0:T(8,128)} %shard_map.119.p, ...), custom_call_target="tpu_custom_call" | custom-call | flops 7381975040 | bytes 38141952 | tf_op jit(solution)/shard_map/pallas_call | solution.py:145
  1522.6 11.4 shard_map.114.refs_6_
  1534.0 11.3 shard_map.115
  1545.3 14.0 collective-permute-done.37
  1560.2 10.0 shard_map.132
  1570.2 10.0 shard_map.133
  1581.4 23.3 %shard_map.124 = (bf16[2,640,256]{2,1,0:T(8,128)(2,1)}, bf16[2,640,256]{2,1,0:T(8,128)(2,1)}, bf16[2,640,256]{2,1,0:T(8,128)(2,1)}, bf16[2,640,256]{2,1,0:T(8,128)(2,1)}) custom-call(bf16[2,4,2,320,2816]{4,3,2,1,0:T(8,128)(2,1)} %bitcast.73, bf16[2,4,2,320,2816]{4,3,2,1,0:T(8,128)(2,1)} %bitcast.74, f32[2,2,4,640,2048]{4,3,2,1,0:T(8,128)} %shard_map.119.p, ...), custom_call_target="tpu_custom_call" | custom-call | flops 7381975040 | bytes 38141952 | tf_op jit(solution)/shard_map/pallas_call | solution.py:145
  1605.6 10.0 shard_map.121
  1616.8 23.0 %shard_map.139 = (bf16[2,640,256]{2,1,0:T(8,128)(2,1)}, bf16[2,640,256]{2,1,0:T(8,128)(2,1)}, bf16[2,640,256]{2,1,0:T(8,128)(2,1)}, bf16[2,640,256]{2,1,0:T(8,128)(2,1)}) custom-call(bf16[2,4,2,320,2816]{4,3,2,1,0:T(8,128)(2,1)} %bitcast.49, bf16[2,4,2,320,2816]{4,3,2,1,0:T(8,128)(2,1)} %bitcast.50, f32[2,2,4,640,2048]{4,3,2,1,0:T(8,128)} %shard_map.119.p, ...), custom_call_target="tpu_custom_call" | custom-call | flops 7381975040 | bytes 38141952 | tf_op jit(solution)/shard_map/pallas_call | solution.py:145
  1640.6 23.0 %shard_map.140 = (bf16[2,640,256]{2,1,0:T(8,128)(2,1)}, bf16[2,640,256]{2,1,0:T(8,128)(2,1)}, bf16[2,640,256]{2,1,0:T(8,128)(2,1)}, bf16[2,640,256]{2,1,0:T(8,128)(2,1)}) custom-call(bf16[2,4,2,320,2816]{4,3,2,1,0:T(8,128)(2,1)} %bitcast.51, bf16[2,4,2,320,2816]{4,3,2,1,0:T(8,128)(2,1)} %bitcast.52, f32[2,2,4,640,2048]{4,3,2,1,0:T(8,128)} %shard_map.119.p, ...), custom_call_target="tpu_custom_call" | custom-call | flops 7381975040 | bytes 38141952 | tf_op jit(solution)/shard_map/pallas_call | solution.py:145
  1663.7 23.0 %shard_map.137 = (bf16[2,640,256]{2,1,0:T(8,128)(2,1)}, bf16[2,640,256]{2,1,0:T(8,128)(2,1)}, bf16[2,640,256]{2,1,0:T(8,128)(2,1)}, bf16[2,640,256]{2,1,0:T(8,128)(2,1)}) custom-call(bf16[2,4,2,320,2816]{4,3,2,1,0:T(8,128)(2,1)} %bitcast.53, bf16[2,4,2,320,2816]{4,3,2,1,0:T(8,128)(2,1)} %bitcast.54, f32[2,2,4,640,2048]{4,3,2,1,0:T(8,128)} %shard_map.119.p, ...), custom_call_target="tpu_custom_call" | custom-call | flops 7381975040 | bytes 38141952 | tf_op jit(solution)/shard_map/pallas_call | solution.py:145
  1686.7 10.0 shard_map.120
  1698.5 23.1 %shard_map.138 = (bf16[2,640,256]{2,1,0:T(8,128)(2,1)}, bf16[2,640,256]{2,1,0:T(8,128)(2,1)}, bf16[2,640,256]{2,1,0:T(8,128)(2,1)}, bf16[2,640,256]{2,1,0:T(8,128)(2,1)}) custom-call(bf16[2,4,2,320,2816]{4,3,2,1,0:T(8,128)(2,1)} %bitcast.57, bf16[2,4,2,320,2816]{4,3,2,1,0:T(8,128)(2,1)} %bitcast.58, f32[2,2,4,640,2048]{4,3,2,1,0:T(8,128)} %shard_map.119.p, ...), custom_call_target="tpu_custom_call" | custom-call | flops 7381975040 | bytes 38141952 | tf_op jit(solution)/shard_map/pallas_call | solution.py:145
  1721.9 23.0 %shard_map.135 = (bf16[2,640,256]{2,1,0:T(8,128)(2,1)}, bf16[2,640,256]{2,1,0:T(8,128)(2,1)}, bf16[2,640,256]{2,1,0:T(8,128)(2,1)}, bf16[2,640,256]{2,1,0:T(8,128)(2,1)}) custom-call(bf16[2,4,2,320,2816]{4,3,2,1,0:T(8,128)(2,1)} %bitcast.59, bf16[2,4,2,320,2816]{4,3,2,1,0:T(8,128)(2,1)} %bitcast.60, f32[2,2,4,640,2048]{4,3,2,1,0:T(8,128)} %shard_map.119.p, ...), custom_call_target="tpu_custom_call" | custom-call | flops 7381975040 | bytes 38141952 | tf_op jit(solution)/shard_map/pallas_call | solution.py:145
  1746.6 23.2 %shard_map.136 = (bf16[2,640,256]{2,1,0:T(8,128)(2,1)}, bf16[2,640,256]{2,1,0:T(8,128)(2,1)}, bf16[2,640,256]{2,1,0:T(8,128)(2,1)}, bf16[2,640,256]{2,1,0:T(8,128)(2,1)}) custom-call(bf16[2,4,2,320,2816]{4,3,2,1,0:T(8,128)(2,1)} %bitcast.61, bf16[2,4,2,320,2816]{4,3,2,1,0:T(8,128)(2,1)} %bitcast.62, f32[2,2,4,640,2048]{4,3,2,1,0:T(8,128)} %shard_map.119.p, ...), custom_call_target="tpu_custom_call" | custom-call | flops 7381975040 | bytes 38141952 | tf_op jit(solution)/shard_map/pallas_call | solution.py:145
  1769.8 57.1 %collective-permute-done.31.refs_6_ = bf16[2,640,256]{2,1,0:T(8,128)(2,1)S(1)} collective-permute-done((bf16[2,640,256]{2,1,0:T(8,128)(2,1)S(1)}, bf16[2,640,256]{2,1,0:T(8,128)(2,1)S(1)}, u32[]{:S(2)}, u32[]{:S(2)}) %collective-permute-start.31) | collective-permute-done | bytes 655392 | tf_op jit(solution)/shard_map/ppermute | solution.py:245
  1826.9 13.0 collective-permute-done.32.refs_7_
  1841.4 23.1 %shard_map.134 = (bf16[2,640,256]{2,1,0:T(8,128)(2,1)}, bf16[2,640,256]{2,1,0:T(8,128)(2,1)}, bf16[2,640,256]{2,1,0:T(8,128)(2,1)}, bf16[2,640,256]{2,1,0:T(8,128)(2,1)}) custom-call(bf16[2,4,2,320,2816]{4,3,2,1,0:T(8,128)(2,1)} %bitcast.63, bf16[2,4,2,320,2816]{4,3,2,1,0:T(8,128)(2,1)} %bitcast.64, f32[2,2,4,640,2048]{4,3,2,1,0:T(8,128)} %shard_map.119.p, ...), custom_call_target="tpu_custom_call" | custom-call | flops 7381975040 | bytes 38141952 | tf_op jit(solution)/shard_map/pallas_call | solution.py:145
  1868.2 32.8 %shard_map.129.refs_10_ = f32[4096,2048]{1,0:T(8,128)} custom-call(bf16[2,640,1024]{2,1,0:T(8,128)(2,1)} %get-tuple-element.104.refs_0_, bf16[2,640,1024]{2,1,0:T(8,128)(2,1)} %collective-permute-done.34.refs_1_, bf16[2,640,1024]{2,1,0:T(8,128)(2,1)} %collective-permute-done.35.refs_2_, bf16[2,640,1024]{2,1,0:T(8,128)(2,1)} %collective-permute-done.36.refs_3_, ...), custom_call_target="tpu_custom_call" | custom-call | flops 21474836480 | bytes 25165824 | tf_op jit(solution)/shard_map/pallas_call | solution.py:201
  1903.1 6.5 collective-permute-done.24.refs_7_
  1911.3 18.6 shard_map.130.refs_10_
  1930.5 7.3 collective-permute-done.20.refs_3_
  1939.5 12.9 collective-permute-done.63.refs_2_
  1952.4 13.5 collective-permute-done.64.refs_3_
  1966.4 18.6 shard_map.131.refs_10_.refs_6_
  1986.7 7.3 collective-permute-done.68.refs_7_
  1995.7 12.8 collective-permute-done.55.refs_2_
  2008.5 20.2 shard_map.141
  2037.4 12.8 collective-permute-done.60.refs_7_
  2051.9 20.2 shard_map.142
  2079.8 13.0 collective-permute-done.51.refs_6_
  2092.8 13.5 collective-permute-done.52.refs_7_
  2106.9 20.0 shard_map.143
  2135.2 12.3 shard_map.144
  2149.1 10.8 shard_map.145
  2163.3 10.8 shard_map.146
  (239 shorter events, 115.2 us)
Async XLA Ops:
  45.8 158.9 %collective-permute-start.5 = (bf16[2,640,2048]{2,1,0:T(8,128)(2,1)}, bf16[2,640,2048]{2,1,0:T(8,128)(2,1)}, u32[]{:S(2)}, u32[]{:S(2)}) collective-permute-start(bf16[2,640,2048]{2,1,0:T(8,128)(2,1)} %get-tuple-element.81), channel_id=1, source_target_pairs={{0,1},{1,0},{2,3},{3,2},{4,5},{5,4},{6,7},{7,6}} | collective-permute-start | bytes 15728648 | tf_op jit(solution)/shard_map/ppermute | solution.py:245
  78.7 126.1 %collective-permute-start.6 = (bf16[2,640,2048]{2,1,0:T(8,128)(2,1)}, bf16[2,640,2048]{2,1,0:T(8,128)(2,1)}, u32[]{:S(2)}, u32[]{:S(2)}) collective-permute-start(bf16[2,640,2048]{2,1,0:T(8,128)(2,1)} %get-tuple-element.82), channel_id=1, source_target_pairs={{0,2},{1,3},{2,0},{3,1},{4,6},{5,7},{6,4},{7,5}} | collective-permute-start | bytes 15728648 | tf_op jit(solution)/shard_map/ppermute | solution.py:245
  81.2 226.2 %collective-permute-start.7 = (bf16[2,640,2048]{2,1,0:T(8,128)(2,1)}, bf16[2,640,2048]{2,1,0:T(8,128)(2,1)}, u32[]{:S(2)}, u32[]{:S(2)}) collective-permute-start(bf16[2,640,2048]{2,1,0:T(8,128)(2,1)} %get-tuple-element.83), channel_id=1, source_target_pairs={{0,3},{1,2},{2,1},{3,0},{4,7},{5,6},{6,5},{7,4}} | collective-permute-start | bytes 15728648 | tf_op jit(solution)/shard_map/ppermute | solution.py:245
  113.8 324.9 %collective-permute-start = (bf16[2,640,2048]{2,1,0:T(8,128)(2,1)}, bf16[2,640,2048]{2,1,0:T(8,128)(2,1)}, u32[]{:S(2)}, u32[]{:S(2)}) collective-permute-start(bf16[2,640,2048]{2,1,0:T(8,128)(2,1)} %get-tuple-element.77), channel_id=1, source_target_pairs={{0,1},{1,0},{2,3},{3,2},{4,5},{5,4},{6,7},{7,6}} | collective-permute-start | bytes 15728648 | tf_op jit(solution)/shard_map/ppermute | solution.py:245
  145.9 293.3 %collective-permute-start.1 = (bf16[2,640,2048]{2,1,0:T(8,128)(2,1)}, bf16[2,640,2048]{2,1,0:T(8,128)(2,1)}, u32[]{:S(2)}, u32[]{:S(2)}) collective-permute-start(bf16[2,640,2048]{2,1,0:T(8,128)(2,1)} %get-tuple-element.78), channel_id=1, source_target_pairs={{0,2},{1,3},{2,0},{3,1},{4,6},{5,7},{6,4},{7,5}} | collective-permute-start | bytes 15728648 | tf_op jit(solution)/shard_map/ppermute | solution.py:245
  204.8 327.3 %collective-permute-start.2 = (bf16[2,640,2048]{2,1,0:T(8,128)(2,1)}, bf16[2,640,2048]{2,1,0:T(8,128)(2,1)}, u32[]{:S(2)}, u32[]{:S(2)}) collective-permute-start(bf16[2,640,2048]{2,1,0:T(8,128)(2,1)} %get-tuple-element.79), channel_id=1, source_target_pairs={{0,3},{1,2},{2,1},{3,0},{4,7},{5,6},{6,5},{7,4}} | collective-permute-start | bytes 15728648 | tf_op jit(solution)/shard_map/ppermute | solution.py:245
  204.8 604.0 %collective-permute-start.15 = (bf16[1,2048,2816]{2,1,0:T(8,128)(2,1)}, bf16[1,2048,2816]{2,1,0:T(8,128)(2,1)}, u32[]{:S(2)}, u32[]{:S(2)}) collective-permute-start(bf16[1,2048,2816]{2,1,0:T(8,128)(2,1)} %get-tuple-element.163), channel_id=1, source_target_pairs={{0,4},{4,0},{1,5},{5,1},{2,6},{6,2},{3,7},{7,3}} | collective-permute-start | bytes 34603016 | tf_op jit(solution)/shard_map/ppermute | solution.py:249
  307.4 501.9 %collective-permute-start.16 = (bf16[1,2048,2816]{2,1,0:T(8,128)(2,1)}, bf16[1,2048,2816]{2,1,0:T(8,128)(2,1)}, u32[]{:S(2)}, u32[]{:S(2)}) collective-permute-start(bf16[1,2048,2816]{2,1,0:T(8,128)(2,1)} %slice.116), channel_id=1, source_target_pairs={{0,4},{4,0},{1,5},{5,1},{2,6},{6,2},{3,7},{7,3}} | collective-permute-start | bytes 34603016 | tf_op jit(solution)/shard_map/ppermute | solution.py:249
  438.6 859.1 %collective-permute-start.33 = (bf16[1,2816,1024]{2,1,0:T(8,128)(2,1)}, bf16[1,2816,1024]{2,1,0:T(8,128)(2,1)}, u32[]{:S(2)}, u32[]{:S(2)}) collective-permute-start(bf16[1,2816,1024]{2,1,0:T(8,128)(2,1)} %slice.121), channel_id=1, source_target_pairs={{0,4},{4,0},{1,5},{5,1},{2,6},{6,2},{3,7},{7,3}} | collective-permute-start | bytes 17301512 | tf_op jit(solution)/shard_map/ppermute | solution.py:249
  439.2 1010.2 %collective-permute-start.29 = (bf16[1,2816,256]{2,1,0:T(8,128)(2,1)}, bf16[1,2816,256]{2,1,0:T(8,128)(2,1)}, u32[]{:S(2)}, u32[]{:S(2)}) collective-permute-start(bf16[1,2816,256]{2,1,0:T(8,128)(2,1)} %get-tuple-element.156), channel_id=1, source_target_pairs={{0,4},{4,0},{1,5},{5,1},{2,6},{6,2},{3,7},{7,3}} | collective-permute-start | bytes 4325384 | tf_op jit(solution)/shard_map/ppermute | solution.py:249
  532.1 619.0 %collective-permute-start.3 = (bf16[1,2048,2816]{2,1,0:T(8,128)(2,1)}, bf16[1,2048,2816]{2,1,0:T(8,128)(2,1)}, u32[]{:S(2)}, u32[]{:S(2)}) collective-permute-start(bf16[1,2048,2816]{2,1,0:T(8,128)(2,1)} %get-tuple-element.164), channel_id=1, source_target_pairs={{0,4},{4,0},{1,5},{5,1},{2,6},{6,2},{3,7},{7,3}} | collective-permute-start | bytes 34603016 | tf_op jit(solution)/shard_map/ppermute | solution.py:249
  808.8 340.8 %collective-permute-start.10 = (bf16[1,2048,512]{2,1,0:T(8,128)(2,1)}, bf16[1,2048,512]{2,1,0:T(8,128)(2,1)S(1)}, u32[]{:S(2)}, u32[]{:S(2)}) collective-permute-start(bf16[1,2048,512]{2,1,0:T(8,128)(2,1)} %slice.113), channel_id=1, source_target_pairs={{0,4},{4,0},{1,5},{5,1},{2,6},{6,2},{3,7},{7,3}} | collective-permute-start | bytes 6291464 | tf_op jit(solution)/shard_map/ppermute | solution.py:249
  809.3 430.2 %collective-permute-start.9 = (bf16[1,2048,1024]{2,1,0:T(8,128)(2,1)}, bf16[1,2048,1024]{2,1,0:T(8,128)(2,1)}, u32[]{:S(2)}, u32[]{:S(2)}) collective-permute-start(bf16[1,2048,1024]{2,1,0:T(8,128)(2,1)} %get-tuple-element.165), channel_id=1, source_target_pairs={{0,4},{4,0},{1,5},{5,1},{2,6},{6,2},{3,7},{7,3}} | collective-permute-start | bytes 12582920 | tf_op jit(solution)/shard_map/ppermute | solution.py:249
  1149.5 323.2 %collective-permute-start.25 = (bf16[1,2816,256]{2,1,0:T(8,128)(2,1)}, bf16[1,2816,256]{2,1,0:T(8,128)(2,1)}, u32[]{:S(2)}, u32[]{:S(2)}) collective-permute-start(bf16[1,2816,256]{2,1,0:T(8,128)(2,1)} %get-tuple-element.157), channel_id=1, source_target_pairs={{0,4},{4,0},{1,5},{5,1},{2,6},{6,2},{3,7},{7,3}} | collective-permute-start | bytes 4325384 | tf_op jit(solution)/shard_map/ppermute | solution.py:249
  1151.1 346.4 %collective-permute-start.21 = (bf16[1,2816,256]{2,1,0:T(8,128)(2,1)}, bf16[1,2816,256]{2,1,0:T(8,128)(2,1)}, u32[]{:S(2)}, u32[]{:S(2)}) collective-permute-start(bf16[1,2816,256]{2,1,0:T(8,128)(2,1)} %get-tuple-element.158), channel_id=1, source_target_pairs={{0,4},{4,0},{1,5},{5,1},{2,6},{6,2},{3,7},{7,3}} | collective-permute-start | bytes 4325384 | tf_op jit(solution)/shard_map/ppermute | solution.py:249
  1239.5 151.7 %collective-permute-start.8 = (bf16[1,2048,1024]{2,1,0:T(8,128)(2,1)}, bf16[1,2048,1024]{2,1,0:T(8,128)(2,1)}, u32[]{:S(2)}, u32[]{:S(2)}) collective-permute-start(bf16[1,2048,1024]{2,1,0:T(8,128)(2,1)} %get-tuple-element.166), channel_id=1, source_target_pairs={{0,4},{4,0},{1,5},{5,1},{2,6},{6,2},{3,7},{7,3}} | collective-permute-start | bytes 12582920 | tf_op jit(solution)/shard_map/ppermute | solution.py:249
  1297.7 282.5 %collective-permute-start.17 = (bf16[1,2816,256]{2,1,0:T(8,128)(2,1)}, bf16[1,2816,256]{2,1,0:T(8,128)(2,1)}, u32[]{:S(2)}, u32[]{:S(2)}) collective-permute-start(bf16[1,2816,256]{2,1,0:T(8,128)(2,1)} %get-tuple-element.159), channel_id=1, source_target_pairs={{0,4},{4,0},{1,5},{5,1},{2,6},{6,2},{3,7},{7,3}} | collective-permute-start | bytes 4325384 | tf_op jit(solution)/shard_map/ppermute | solution.py:249
  1391.2 129.8 %collective-permute-start.4 = (bf16[1,2048,256]{2,1,0:T(8,128)(2,1)}, bf16[1,2048,256]{2,1,0:T(8,128)(2,1)}, u32[]{:S(2)}, u32[]{:S(2)}) collective-permute-start(bf16[1,2048,256]{2,1,0:T(8,128)(2,1)} %slice.106), channel_id=1, source_target_pairs={{0,4},{4,0},{1,5},{5,1},{2,6},{6,2},{3,7},{7,3}} | collective-permute-start | bytes 3145736 | tf_op jit(solution)/shard_map/ppermute | solution.py:249
  1449.4 166.3 %collective-permute-start.61 = (bf16[1,2816,256]{2,1,0:T(8,128)(2,1)}, bf16[1,2816,256]{2,1,0:T(8,128)(2,1)}, u32[]{:S(2)}, u32[]{:S(2)}) collective-permute-start(bf16[1,2816,256]{2,1,0:T(8,128)(2,1)} %get-tuple-element.160), channel_id=1, source_target_pairs={{0,4},{4,0},{1,5},{5,1},{2,6},{6,2},{3,7},{7,3}} | collective-permute-start | bytes 4325384 | tf_op jit(solution)/shard_map/ppermute | solution.py:249
  1472.7 167.0 %collective-permute-start.65 = (bf16[1,2816,256]{2,1,0:T(8,128)(2,1)}, bf16[1,2816,256]{2,1,0:T(8,128)(2,1)}, u32[]{:S(2)}, u32[]{:S(2)}) collective-permute-start(bf16[1,2816,256]{2,1,0:T(8,128)(2,1)} %get-tuple-element.150), channel_id=1, source_target_pairs={{0,4},{4,0},{1,5},{5,1},{2,6},{6,2},{3,7},{7,3}} | collective-permute-start | bytes 4325384 | tf_op jit(solution)/shard_map/ppermute | solution.py:249
  1497.5 166.1 %collective-permute-start.53 = (bf16[1,2816,256]{2,1,0:T(8,128)(2,1)}, bf16[1,2816,256]{2,1,0:T(8,128)(2,1)}, u32[]{:S(2)}, u32[]{:S(2)}) collective-permute-start(bf16[1,2816,256]{2,1,0:T(8,128)(2,1)} %get-tuple-element.152), channel_id=1, source_target_pairs={{0,4},{4,0},{1,5},{5,1},{2,6},{6,2},{3,7},{7,3}} | collective-permute-start | bytes 4325384 | tf_op jit(solution)/shard_map/ppermute | solution.py:249
  1521.0 38.3 %collective-permute-start.37 = (bf16[1,2816,128]{2,1,0:T(8,128)(2,1)S(1)}, bf16[1,2816,128]{2,1,0:T(8,128)(2,1)S(1)}, u32[]{:S(2)}, u32[]{:S(2)}) collective-permute-start(bf16[1,2816,128]{2,1,0:T(8,128)(2,1)S(1)} %copy-done.5), channel_id=1, source_target_pairs={{0,4},{4,0},{1,5},{5,1},{2,6},{6,2},{3,7},{7,3}} | collective-permute-start | bytes 2162696 | tf_op jit(solution)/shard_map/ppermute | solution.py:249
  1559.3 45.4 %collective-permute-start.11 = (bf16[1,2816,128]{2,1,0:T(8,128)(2,1)S(1)}, bf16[1,2816,128]{2,1,0:T(8,128)(2,1)S(1)}, u32[]{:S(2)}, u32[]{:S(2)}) collective-permute-start(bf16[1,2816,128]{2,1,0:T(8,128)(2,1)S(1)} %copy-done.4), channel_id=1, source_target_pairs={{0,4},{4,0},{1,5},{5,1},{2,6},{6,2},{3,7},{7,3}} | collective-permute-start | bytes 2162696 | tf_op jit(solution)/shard_map/ppermute | solution.py:249
  1580.2 116.5 %collective-permute-start.57 = (bf16[1,2816,256]{2,1,0:T(8,128)(2,1)}, bf16[1,2816,256]{2,1,0:T(8,128)(2,1)}, u32[]{:S(2)}, u32[]{:S(2)}) collective-permute-start(bf16[1,2816,256]{2,1,0:T(8,128)(2,1)} %get-tuple-element.151), channel_id=1, source_target_pairs={{0,4},{4,0},{1,5},{5,1},{2,6},{6,2},{3,7},{7,3}} | collective-permute-start | bytes 4325384 | tf_op jit(solution)/shard_map/ppermute | solution.py:249
  1604.8 93.4 %collective-permute-start.45 = (bf16[1,2816,256]{2,1,0:T(8,128)(2,1)}, bf16[1,2816,256]{2,1,0:T(8,128)(2,1)}, u32[]{:S(2)}, u32[]{:S(2)}) collective-permute-start(bf16[1,2816,256]{2,1,0:T(8,128)(2,1)} %get-tuple-element.154), channel_id=1, source_target_pairs={{0,4},{4,0},{1,5},{5,1},{2,6},{6,2},{3,7},{7,3}} | collective-permute-start | bytes 4325384 | tf_op jit(solution)/shard_map/ppermute | solution.py:249
  1615.6 105.9 %collective-permute-start.49 = (bf16[1,2816,256]{2,1,0:T(8,128)(2,1)}, bf16[1,2816,256]{2,1,0:T(8,128)(2,1)}, u32[]{:S(2)}, u32[]{:S(2)}) collective-permute-start(bf16[1,2816,256]{2,1,0:T(8,128)(2,1)} %get-tuple-element.153), channel_id=1, source_target_pairs={{0,4},{4,0},{1,5},{5,1},{2,6},{6,2},{3,7},{7,3}} | collective-permute-start | bytes 4325384 | tf_op jit(solution)/shard_map/ppermute | solution.py:249
  1639.8 105.2 %collective-permute-start.41 = (bf16[1,2816,256]{2,1,0:T(8,128)(2,1)}, bf16[1,2816,256]{2,1,0:T(8,128)(2,1)}, u32[]{:S(2)}, u32[]{:S(2)}) collective-permute-start(bf16[1,2816,256]{2,1,0:T(8,128)(2,1)} %get-tuple-element.155), channel_id=1, source_target_pairs={{0,4},{4,0},{1,5},{5,1},{2,6},{6,2},{3,7},{7,3}} | collective-permute-start | bytes 4325384 | tf_op jit(solution)/shard_map/ppermute | solution.py:249
  1663.6 202.4 %collective-permute-start.34 = (bf16[2,640,1024]{2,1,0:T(8,128)(2,1)}, bf16[2,640,1024]{2,1,0:T(8,128)(2,1)}, u32[]{:S(2)}, u32[]{:S(2)}) collective-permute-start(bf16[2,640,1024]{2,1,0:T(8,128)(2,1)} %get-tuple-element.105), channel_id=1, source_target_pairs={{0,1},{1,0},{2,3},{3,2},{4,5},{5,4},{6,7},{7,6}} | collective-permute-start | bytes 7864328 | tf_op jit(solution)/shard_map/ppermute | solution.py:245
  1696.7 170.8 %collective-permute-start.35 = (bf16[2,640,1024]{2,1,0:T(8,128)(2,1)}, bf16[2,640,1024]{2,1,0:T(8,128)(2,1)}, u32[]{:S(2)}, u32[]{:S(2)}) collective-permute-start(bf16[2,640,1024]{2,1,0:T(8,128)(2,1)} %get-tuple-element.106), channel_id=1, source_target_pairs={{0,2},{1,3},{2,0},{3,1},{4,6},{5,7},{6,4},{7,5}} | collective-permute-start | bytes 7864328 | tf_op jit(solution)/shard_map/ppermute | solution.py:245
  1698.2 169.3 %collective-permute-start.36 = (bf16[2,640,1024]{2,1,0:T(8,128)(2,1)}, bf16[2,640,1024]{2,1,0:T(8,128)(2,1)}, u32[]{:S(2)}, u32[]{:S(2)}) collective-permute-start(bf16[2,640,1024]{2,1,0:T(8,128)(2,1)} %get-tuple-element.107), channel_id=1, source_target_pairs={{0,3},{1,2},{2,1},{3,0},{4,7},{5,6},{6,5},{7,4}} | collective-permute-start | bytes 7864328 | tf_op jit(solution)/shard_map/ppermute | solution.py:245
  1745.0 81.9 %collective-permute-start.31 = (bf16[2,640,256]{2,1,0:T(8,128)(2,1)S(1)}, bf16[2,640,256]{2,1,0:T(8,128)(2,1)S(1)}, u32[]{:S(2)}, u32[]{:S(2)}) collective-permute-start(bf16[2,640,256]{2,1,0:T(8,128)(2,1)S(1)} %copy-done.39), channel_id=1, source_target_pairs={{0,2},{1,3},{2,0},{3,1},{4,6},{5,7},{6,4},{7,5}} | collective-permute-start | bytes 1966088 | tf_op jit(solution)/shard_map/ppermute | solution.py:245
  1746.5 93.3 %collective-permute-start.32 = (bf16[2,640,256]{2,1,0:T(8,128)(2,1)}, bf16[2,640,256]{2,1,0:T(8,128)(2,1)S(1)}, u32[]{:S(2)}, u32[]{:S(2)}) collective-permute-start(bf16[2,640,256]{2,1,0:T(8,128)(2,1)} %get-tuple-element.103), channel_id=1, source_target_pairs={{0,3},{1,2},{2,1},{3,0},{4,7},{5,6},{6,5},{7,4}} | collective-permute-start | bytes 1966088 | tf_op jit(solution)/shard_map/ppermute | solution.py:245
  1826.9 37.6 %collective-permute-start.26 = (bf16[2,640,256]{2,1,0:T(8,128)(2,1)S(1)}, bf16[2,640,256]{2,1,0:T(8,128)(2,1)S(1)}, u32[]{:S(2)}, u32[]{:S(2)}) collective-permute-start(bf16[2,640,256]{2,1,0:T(8,128)(2,1)S(1)} %copy-done.38), channel_id=1, source_target_pairs={{0,1},{1,0},{2,3},{3,2},{4,5},{5,4},{6,7},{7,6}} | collective-permute-start | bytes 1966088 | tf_op jit(solution)/shard_map/ppermute | solution.py:245
  1864.5 36.4 %collective-permute-start.28 = (bf16[2,640,256]{2,1,0:T(8,128)(2,1)}, bf16[2,640,256]{2,1,0:T(8,128)(2,1)S(1)}, u32[]{:S(2)}, u32[]{:S(2)}) collective-permute-start(bf16[2,640,256]{2,1,0:T(8,128)(2,1)} %get-tuple-element.99), channel_id=1, source_target_pairs={{0,3},{1,2},{2,1},{3,0},{4,7},{5,6},{6,5},{7,4}} | collective-permute-start | bytes 1966088 | tf_op jit(solution)/shard_map/ppermute | solution.py:245
  1865.6 37.0 %collective-permute-start.22 = (bf16[2,640,256]{2,1,0:T(8,128)(2,1)}, bf16[2,640,256]{2,1,0:T(8,128)(2,1)S(1)}, u32[]{:S(2)}, u32[]{:S(2)}) collective-permute-start(bf16[2,640,256]{2,1,0:T(8,128)(2,1)} %get-tuple-element.93), channel_id=1, source_target_pairs={{0,1},{1,0},{2,3},{3,2},{4,5},{5,4},{6,7},{7,6}} | collective-permute-start | bytes 1966088 | tf_op jit(solution)/shard_map/ppermute | solution.py:245
  1866.0 36.6 %collective-permute-start.23 = (bf16[2,640,256]{2,1,0:T(8,128)(2,1)}, bf16[2,640,256]{2,1,0:T(8,128)(2,1)S(1)}, u32[]{:S(2)}, u32[]{:S(2)}) collective-permute-start(bf16[2,640,256]{2,1,0:T(8,128)(2,1)} %get-tuple-element.94), channel_id=1, source_target_pairs={{0,2},{1,3},{2,0},{3,1},{4,6},{5,7},{6,4},{7,5}} | collective-permute-start | bytes 1966088 | tf_op jit(solution)/shard_map/ppermute | solution.py:245
  1867.5 42.1 %collective-permute-start.24 = (bf16[2,640,256]{2,1,0:T(8,128)(2,1)}, bf16[2,640,256]{2,1,0:T(8,128)(2,1)S(1)}, u32[]{:S(2)}, u32[]{:S(2)}) collective-permute-start(bf16[2,640,256]{2,1,0:T(8,128)(2,1)} %get-tuple-element.95), channel_id=1, source_target_pairs={{0,3},{1,2},{2,1},{3,0},{4,7},{5,6},{6,5},{7,4}} | collective-permute-start | bytes 1966088 | tf_op jit(solution)/shard_map/ppermute | solution.py:245
  1867.5 42.6 %collective-permute-start.18 = (bf16[2,640,256]{2,1,0:T(8,128)(2,1)}, bf16[2,640,256]{2,1,0:T(8,128)(2,1)S(1)}, u32[]{:S(2)}, u32[]{:S(2)}) collective-permute-start(bf16[2,640,256]{2,1,0:T(8,128)(2,1)} %get-tuple-element.89), channel_id=1, source_target_pairs={{0,1},{1,0},{2,3},{3,2},{4,5},{5,4},{6,7},{7,6}} | collective-permute-start | bytes 1966088 | tf_op jit(solution)/shard_map/ppermute | solution.py:245
  1902.6 35.3 %collective-permute-start.20 = (bf16[2,640,256]{2,1,0:T(8,128)(2,1)}, bf16[2,640,256]{2,1,0:T(8,128)(2,1)}, u32[]{:S(2)}, u32[]{:S(2)}) collective-permute-start(bf16[2,640,256]{2,1,0:T(8,128)(2,1)} %get-tuple-element.91), channel_id=1, source_target_pairs={{0,3},{1,2},{2,1},{3,0},{4,7},{5,6},{6,5},{7,4}} | collective-permute-start | bytes 1966088 | tf_op jit(solution)/shard_map/ppermute | solution.py:245
  1902.6 35.7 %collective-permute-start.62 = (bf16[2,640,256]{2,1,0:T(8,128)(2,1)}, bf16[2,640,256]{2,1,0:T(8,128)(2,1)}, u32[]{:S(2)}, u32[]{:S(2)}) collective-permute-start(bf16[2,640,256]{2,1,0:T(8,128)(2,1)} %get-tuple-element.133), channel_id=1, source_target_pairs={{0,1},{1,0},{2,3},{3,2},{4,5},{5,4},{6,7},{7,6}} | collective-permute-start | bytes 1966088 | tf_op jit(solution)/shard_map/ppermute | solution.py:245
  1909.6 42.7 %collective-permute-start.63 = (bf16[2,640,256]{2,1,0:T(8,128)(2,1)}, bf16[2,640,256]{2,1,0:T(8,128)(2,1)}, u32[]{:S(2)}, u32[]{:S(2)}) collective-permute-start(bf16[2,640,256]{2,1,0:T(8,128)(2,1)} %get-tuple-element.134), channel_id=1, source_target_pairs={{0,2},{1,3},{2,0},{3,1},{4,6},{5,7},{6,4},{7,5}} | collective-permute-start | bytes 1966088 | tf_op jit(solution)/shard_map/ppermute | solution.py:245
  1910.1 55.8 %collective-permute-start.64 = (bf16[2,640,256]{2,1,0:T(8,128)(2,1)}, bf16[2,640,256]{2,1,0:T(8,128)(2,1)}, u32[]{:S(2)}, u32[]{:S(2)}) collective-permute-start(bf16[2,640,256]{2,1,0:T(8,128)(2,1)} %get-tuple-element.135), channel_id=1, source_target_pairs={{0,3},{1,2},{2,1},{3,0},{4,7},{5,6},{6,5},{7,4}} | collective-permute-start | bytes 1966088 | tf_op jit(solution)/shard_map/ppermute | solution.py:245
  1930.0 55.0 %collective-permute-start.66 = (bf16[2,640,256]{2,1,0:T(8,128)(2,1)}, bf16[2,640,256]{2,1,0:T(8,128)(2,1)S(1)}, u32[]{:S(2)}, u32[]{:S(2)}) collective-permute-start(bf16[2,640,256]{2,1,0:T(8,128)(2,1)} %get-tuple-element.137), channel_id=1, source_target_pairs={{0,1},{1,0},{2,3},{3,2},{4,5},{5,4},{6,7},{7,6}} | collective-permute-start | bytes 1966088 | tf_op jit(solution)/shard_map/ppermute | solution.py:245
  1937.8 48.4 %collective-permute-start.67 = (bf16[2,640,256]{2,1,0:T(8,128)(2,1)}, bf16[2,640,256]{2,1,0:T(8,128)(2,1)S(1)}, u32[]{:S(2)}, u32[]{:S(2)}) collective-permute-start(bf16[2,640,256]{2,1,0:T(8,128)(2,1)} %get-tuple-element.138), channel_id=1, source_target_pairs={{0,2},{1,3},{2,0},{3,1},{4,6},{5,7},{6,4},{7,5}} | collective-permute-start | bytes 1966088 | tf_op jit(solution)/shard_map/ppermute | solution.py:245
  1938.3 55.7 %collective-permute-start.68 = (bf16[2,640,256]{2,1,0:T(8,128)(2,1)}, bf16[2,640,256]{2,1,0:T(8,128)(2,1)}, u32[]{:S(2)}, u32[]{:S(2)}) collective-permute-start(bf16[2,640,256]{2,1,0:T(8,128)(2,1)} %get-tuple-element.139), channel_id=1, source_target_pairs={{0,3},{1,2},{2,1},{3,0},{4,7},{5,6},{6,5},{7,4}} | collective-permute-start | bytes 1966088 | tf_op jit(solution)/shard_map/ppermute | solution.py:245
  1952.4 42.1 %collective-permute-start.54 = (bf16[2,640,256]{2,1,0:T(8,128)(2,1)}, bf16[2,640,256]{2,1,0:T(8,128)(2,1)S(1)}, u32[]{:S(2)}, u32[]{:S(2)}) collective-permute-start(bf16[2,640,256]{2,1,0:T(8,128)(2,1)} %get-tuple-element.125), channel_id=1, source_target_pairs={{0,1},{1,0},{2,3},{3,2},{4,5},{5,4},{6,7},{7,6}} | collective-permute-start | bytes 1966088 | tf_op jit(solution)/shard_map/ppermute | solution.py:245
  1965.9 42.5 %collective-permute-start.55 = (bf16[2,640,256]{2,1,0:T(8,128)(2,1)}, bf16[2,640,256]{2,1,0:T(8,128)(2,1)S(1)}, u32[]{:S(2)}, u32[]{:S(2)}) collective-permute-start(bf16[2,640,256]{2,1,0:T(8,128)(2,1)} %get-tuple-element.126), channel_id=1, source_target_pairs={{0,2},{1,3},{2,0},{3,1},{4,6},{5,7},{6,4},{7,5}} | collective-permute-start | bytes 1966088 | tf_op jit(solution)/shard_map/ppermute | solution.py:245
  1985.0 43.6 %collective-permute-start.56 = (bf16[2,640,256]{2,1,0:T(8,128)(2,1)}, bf16[2,640,256]{2,1,0:T(8,128)(2,1)S(1)}, u32[]{:S(2)}, u32[]{:S(2)}) collective-permute-start(bf16[2,640,256]{2,1,0:T(8,128)(2,1)} %get-tuple-element.127), channel_id=1, source_target_pairs={{0,3},{1,2},{2,1},{3,0},{4,7},{5,6},{6,5},{7,4}} | collective-permute-start | bytes 1966088 | tf_op jit(solution)/shard_map/ppermute | solution.py:245
  1986.3 42.9 %collective-permute-start.58 = (bf16[2,640,256]{2,1,0:T(8,128)(2,1)}, bf16[2,640,256]{2,1,0:T(8,128)(2,1)S(1)}, u32[]{:S(2)}, u32[]{:S(2)}) collective-permute-start(bf16[2,640,256]{2,1,0:T(8,128)(2,1)} %get-tuple-element.129), channel_id=1, source_target_pairs={{0,1},{1,0},{2,3},{3,2},{4,5},{5,4},{6,7},{7,6}} | collective-permute-start | bytes 1966088 | tf_op jit(solution)/shard_map/ppermute | solution.py:245
  1994.0 42.5 %collective-permute-start.59 = (bf16[2,640,256]{2,1,0:T(8,128)(2,1)}, bf16[2,640,256]{2,1,0:T(8,128)(2,1)S(1)}, u32[]{:S(2)}, u32[]{:S(2)}) collective-permute-start(bf16[2,640,256]{2,1,0:T(8,128)(2,1)} %get-tuple-element.130), channel_id=1, source_target_pairs={{0,2},{1,3},{2,0},{3,1},{4,6},{5,7},{6,4},{7,5}} | collective-permute-start | bytes 1966088 | tf_op jit(solution)/shard_map/ppermute | solution.py:245
  1994.5 55.7 %collective-permute-start.60 = (bf16[2,640,256]{2,1,0:T(8,128)(2,1)}, bf16[2,640,256]{2,1,0:T(8,128)(2,1)}, u32[]{:S(2)}, u32[]{:S(2)}) collective-permute-start(bf16[2,640,256]{2,1,0:T(8,128)(2,1)} %get-tuple-element.131), channel_id=1, source_target_pairs={{0,3},{1,2},{2,1},{3,0},{4,7},{5,6},{6,5},{7,4}} | collective-permute-start | bytes 1966088 | tf_op jit(solution)/shard_map/ppermute | solution.py:245
  2008.4 42.2 %collective-permute-start.46 = (bf16[2,640,256]{2,1,0:T(8,128)(2,1)}, bf16[2,640,256]{2,1,0:T(8,128)(2,1)S(1)}, u32[]{:S(2)}, u32[]{:S(2)}) collective-permute-start(bf16[2,640,256]{2,1,0:T(8,128)(2,1)} %get-tuple-element.117), channel_id=1, source_target_pairs={{0,1},{1,0},{2,3},{3,2},{4,5},{5,4},{6,7},{7,6}} | collective-permute-start | bytes 1966088 | tf_op jit(solution)/shard_map/ppermute | solution.py:245
  2028.7 43.4 %collective-permute-start.47 = (bf16[2,640,256]{2,1,0:T(8,128)(2,1)}, bf16[2,640,256]{2,1,0:T(8,128)(2,1)S(1)}, u32[]{:S(2)}, u32[]{:S(2)}) collective-permute-start(bf16[2,640,256]{2,1,0:T(8,128)(2,1)} %get-tuple-element.118), channel_id=1, source_target_pairs={{0,2},{1,3},{2,0},{3,1},{4,6},{5,7},{6,4},{7,5}} | collective-permute-start | bytes 1966088 | tf_op jit(solution)/shard_map/ppermute | solution.py:245
  2029.2 48.9 %collective-permute-start.48 = (bf16[2,640,256]{2,1,0:T(8,128)(2,1)}, bf16[2,640,256]{2,1,0:T(8,128)(2,1)S(1)}, u32[]{:S(2)}, u32[]{:S(2)}) collective-permute-start(bf16[2,640,256]{2,1,0:T(8,128)(2,1)} %get-tuple-element.119), channel_id=1, source_target_pairs={{0,3},{1,2},{2,1},{3,0},{4,7},{5,6},{6,5},{7,4}} | collective-permute-start | bytes 1966088 | tf_op jit(solution)/shard_map/ppermute | solution.py:245
  2037.4 41.3 %collective-permute-start.50 = (bf16[2,640,256]{2,1,0:T(8,128)(2,1)}, bf16[2,640,256]{2,1,0:T(8,128)(2,1)S(1)}, u32[]{:S(2)}, u32[]{:S(2)}) collective-permute-start(bf16[2,640,256]{2,1,0:T(8,128)(2,1)} %get-tuple-element.121), channel_id=1, source_target_pairs={{0,1},{1,0},{2,3},{3,2},{4,5},{5,4},{6,7},{7,6}} | collective-permute-start | bytes 1966088 | tf_op jit(solution)/shard_map/ppermute | solution.py:245
  2050.2 42.6 %collective-permute-start.51 = (bf16[2,640,256]{2,1,0:T(8,128)(2,1)}, bf16[2,640,256]{2,1,0:T(8,128)(2,1)}, u32[]{:S(2)}, u32[]{:S(2)}) collective-permute-start(bf16[2,640,256]{2,1,0:T(8,128)(2,1)} %get-tuple-element.122), channel_id=1, source_target_pairs={{0,2},{1,3},{2,0},{3,1},{4,6},{5,7},{6,4},{7,5}} | collective-permute-start | bytes 1966088 | tf_op jit(solution)/shard_map/ppermute | solution.py:245
  2050.7 55.7 %collective-permute-start.52 = (bf16[2,640,256]{2,1,0:T(8,128)(2,1)}, bf16[2,640,256]{2,1,0:T(8,128)(2,1)}, u32[]{:S(2)}, u32[]{:S(2)}) collective-permute-start(bf16[2,640,256]{2,1,0:T(8,128)(2,1)} %get-tuple-element.123), channel_id=1, source_target_pairs={{0,3},{1,2},{2,1},{3,0},{4,7},{5,6},{6,5},{7,4}} | collective-permute-start | bytes 1966088 | tf_op jit(solution)/shard_map/ppermute | solution.py:245
  2072.1 56.0 %collective-permute-start.42 = (bf16[2,640,256]{2,1,0:T(8,128)(2,1)}, bf16[2,640,256]{2,1,0:T(8,128)(2,1)S(1)}, u32[]{:S(2)}, u32[]{:S(2)}) collective-permute-start(bf16[2,640,256]{2,1,0:T(8,128)(2,1)} %get-tuple-element.113), channel_id=1, source_target_pairs={{0,1},{1,0},{2,3},{3,2},{4,5},{5,4},{6,7},{7,6}} | collective-permute-start | bytes 1966088 | tf_op jit(solution)/shard_map/ppermute | solution.py:245
  2078.2 50.4 %collective-permute-start.43 = (bf16[2,640,256]{2,1,0:T(8,128)(2,1)}, bf16[2,640,256]{2,1,0:T(8,128)(2,1)S(1)}, u32[]{:S(2)}, u32[]{:S(2)}) collective-permute-start(bf16[2,640,256]{2,1,0:T(8,128)(2,1)} %get-tuple-element.114), channel_id=1, source_target_pairs={{0,2},{1,3},{2,0},{3,1},{4,6},{5,7},{6,4},{7,5}} | collective-permute-start | bytes 1966088 | tf_op jit(solution)/shard_map/ppermute | solution.py:245
  2078.7 55.7 %collective-permute-start.44 = (bf16[2,640,256]{2,1,0:T(8,128)(2,1)}, bf16[2,640,256]{2,1,0:T(8,128)(2,1)S(1)}, u32[]{:S(2)}, u32[]{:S(2)}) collective-permute-start(bf16[2,640,256]{2,1,0:T(8,128)(2,1)} %get-tuple-element.115), channel_id=1, source_target_pairs={{0,3},{1,2},{2,1},{3,0},{4,7},{5,6},{6,5},{7,4}} | collective-permute-start | bytes 1966088 | tf_op jit(solution)/shard_map/ppermute | solution.py:245
  2092.8 34.0 %collective-permute-start.38 = (bf16[2,640,128]{2,1,0:T(8,128)(2,1)}, bf16[2,640,128]{2,1,0:T(8,128)(2,1)}, u32[]{:S(2)}, u32[]{:S(2)}) collective-permute-start(bf16[2,640,128]{2,1,0:T(8,128)(2,1)} %get-tuple-element.109), channel_id=1, source_target_pairs={{0,1},{1,0},{2,3},{3,2},{4,5},{5,4},{6,7},{7,6}} | collective-permute-start | bytes 983048 | tf_op jit(solution)/shard_map/ppermute | solution.py:245
  2106.3 41.1 %collective-permute-start.39 = (bf16[2,640,128]{2,1,0:T(8,128)(2,1)}, bf16[2,640,128]{2,1,0:T(8,128)(2,1)}, u32[]{:S(2)}, u32[]{:S(2)}) collective-permute-start(bf16[2,640,128]{2,1,0:T(8,128)(2,1)} %get-tuple-element.110), channel_id=1, source_target_pairs={{0,2},{1,3},{2,0},{3,1},{4,6},{5,7},{6,4},{7,5}} | collective-permute-start | bytes 983048 | tf_op jit(solution)/shard_map/ppermute | solution.py:245
  2128.1 31.9 %collective-permute-start.13 = (bf16[2,640,128]{2,1,0:T(8,128)(2,1)}, bf16[2,640,128]{2,1,0:T(8,128)(2,1)S(1)}, u32[]{:S(2)}, u32[]{:S(2)}) collective-permute-start(bf16[2,640,128]{2,1,0:T(8,128)(2,1)} %get-tuple-element.86), channel_id=1, source_target_pairs={{0,2},{1,3},{2,0},{3,1},{4,6},{5,7},{6,4},{7,5}} | collective-permute-start | bytes 983048 | tf_op jit(solution)/shard_map/ppermute | solution.py:245
  2128.6 33.8 %collective-permute-start.14 = (bf16[2,640,128]{2,1,0:T(8,128)(2,1)}, bf16[2,640,128]{2,1,0:T(8,128)(2,1)S(1)}, u32[]{:S(2)}, u32[]{:S(2)}) collective-permute-start(bf16[2,640,128]{2,1,0:T(8,128)(2,1)} %get-tuple-element.87), channel_id=1, source_target_pairs={{0,3},{1,2},{2,1},{3,0},{4,7},{5,6},{6,5},{7,4}} | collective-permute-start | bytes 983048 | tf_op jit(solution)/shard_map/ppermute | solution.py:245
  (52 other events, 1049.5 us)

commit v4 on v3

--- a/solution.py
+++ b/solution.py
@@ -14,15 +14,14 @@
 MASKS = 4
 TN = 256
 TB = 512
-VMEM_LIMIT = 60 * 1024 * 1024
 
 
 def mm(a, b):
     return jnp.dot(a, b, preferred_element_type=F32)
 
 
-def call(kernel, flops, nbytes, **kw):
-    params = pltpu.CompilerParams(vmem_limit_bytes=VMEM_LIMIT)
+def call(kernel, flops, nbytes, limit=60, **kw):
+    params = pltpu.CompilerParams(vmem_limit_bytes=limit * 1024 * 1024)
     cost = pl.CostEstimate(flops=int(flops), bytes_accessed=int(nbytes), transcendentals=0)
     return pl.pallas_call(kernel, compiler_params=params, cost_estimate=cost, **kw)
 
@@ -33,6 +32,12 @@
     args.append(into)
     in_specs.append(pl.BlockSpec(memory_space=pl.ANY))
     return {"input_output_aliases": {len(args) - 1: 0}}
+
+
+def kept(value, args, in_specs, output):
+    args.append(pltpu.with_memory_space_constraint(value, pltpu.VMEM))
+    in_specs.append(pl.BlockSpec(memory_space=pltpu.VMEM))
+    return {"input_output_aliases": {len(args) - 1: output}}
 
 
 def dispatch_kernel(pos_ref, tok_ref, *outs):
@@ -62,14 +67,18 @@
     )(pos, tokens)
 
 
-def hidden_kernel(*refs):
+def hidden_kernel(b, off, *refs):
     xs, (wg, wu), h = refs[:MASKS], refs[MASKS:MASKS + 2], refs[-1]
     g = wg[...].reshape(wg.shape[-2:])
     u = wu[...].reshape(wu.shape[-2:])
     for m in range(MASKS):
         x = xs[m][0]
         a = mm(x, g)
-        h[0, m] = (a * jax.nn.sigmoid(a) * mm(x, u)).astype(BF16)
+        out = (a * jax.nn.sigmoid(a) * mm(x, u)).astype(BF16)
+        if b is None:
+            h[0, m] = out
+        else:
+            h[b, m, :, pl.ds(pl.multiple_of((off + pl.program_id(0)) * TN, TN), TN)] = out
 
 
 def hidden_local(xs, wg, wu):
@@ -77,7 +86,7 @@
     width = wg.shape[2]
     rows = 2 * MASKS * cap
     return call(
-        hidden_kernel, 4 * rows * model * width, 2 * (rows * model + 4 * model * width + rows * width),
+        functools.partial(hidden_kernel, None, 0), 4 * rows * model * width, 2 * (rows * model + 4 * model * width + rows * width),
         grid=(2, width // TN),
         in_specs=[pl.BlockSpec((1, cap, model), lambda k, n: (k, 0, 0)) for _ in xs]
         + [pl.BlockSpec((1, model, TN), lambda k, n: (k, 0, n))] * 2,
@@ -93,10 +102,21 @@
     in_specs = [pl.BlockSpec((1, cap, model), lambda n: (k, 0, 0)) for _ in xs]
     in_specs += [pl.BlockSpec((model, TN), lambda n: (0, n + off)), pl.BlockSpec((model, TN), lambda n: (0, n))]
     args = [*xs, wg, wu]
+    rows = MASKS * cap
+    cost = (4 * rows * model * cols, 2 * (rows * model + 2 * model * cols + rows * cols))
+    if k == 1:
+        kw = {}
+        if into is not None:
+            kw = kept(into, args, in_specs, 0)
+        return call(
+            functools.partial(hidden_kernel, b, off), *cost, 33,
+            grid=(steps,), in_specs=in_specs,
+            out_specs=pl.BlockSpec(memory_space=pltpu.VMEM),
+            out_shape=pltpu.VMEM((2, MASKS, cap, width), BF16), **kw,
+        )(*args)
     kw = filled_further(into, args, in_specs)
-    rows = MASKS * cap
-    return call(
-        hidden_kernel, 4 * rows * model * cols, 2 * (rows * model + 2 * model * cols + rows * cols),
+    return call(
+        functools.partial(hidden_kernel, None, 0), *cost,
         grid=(steps,), in_specs=in_specs,
         out_specs=pl.BlockSpec((1, MASKS, cap, TN), lambda n: (b, 0, 0, n + off)),
         out_shape=jax.ShapeDtypeStruct((2, MASKS, cap, width), BF16), **kw,
@@ -124,35 +144,62 @@
 
 
 def final_kernel(h0, h1, p, wd, *outs):
-    m = pl.program_id(0) % len(outs)
-    half = h0.shape[3]
+    q = pl.program_id(0) % 2
     for j, h in enumerate((h0, h1)):
-        rows = slice(j * half, (j + 1) * half)
-        y = (p[0, 0, 0, rows] + mm(h[0, 0, 0], wd[...])).astype(BF16)
-        for t, out in enumerate(outs):
-
-            @pl.when(m == t)
+        y = (p[0, 0, j] + mm(h[0, 0], wd[...])).astype(BF16)
+        for t in range(2):
+
+            @pl.when(q == t)
             def _():
-                out[0, rows] = y
-
-
-def final(h, p, k, wd, lo, masks):
+                outs[2 * t + j][0] = y
+
+
+def final(h, p, k, wd, lo):
+    _, _, cap, width = h.shape
+    cols = wd.shape[1]
+    at = lo // cols
+    rows = 2 * MASKS * cap
+    return call(
+        final_kernel, 2 * rows * width * cols, 2 * (rows * width + width * cols) + 6 * rows * cols, 57,
+        grid=(4,),
+        in_specs=[pl.BlockSpec((1, 1, cap, width), functools.partial(lambda j, i: (i // 2, 2 * (i % 2) + j, 0, 0), j)) for j in range(2)]
+        + [
+            pl.BlockSpec((1, 1, 2, cap, cols), lambda i: (k, i // 2, i % 2, 0, at)),
+            pl.BlockSpec((width, cols), lambda i: (0, 0)),
+        ],
+        out_specs=[pl.BlockSpec((1, cap, cols), functools.partial(lambda m, i: (jnp.where(i >= 2 + m // 2, 1, 0), 0, 0), m)) for m in range(MASKS)],
+        out_shape=[jax.ShapeDtypeStruct((2, cap, cols), BF16)] * MASKS,
+    )(h, h, p, wd)
+
+
+def final_kept_kernel(masks, p, wd, h, *refs):
+    i, n = pl.program_id(0), len(masks)
+    y = (p[0, 0, 0] + mm(h[i // n, masks[0] + i % n], wd[...])).astype(BF16)
+    for j, out in enumerate(refs[:n]):
+
+        @pl.when(i % n == j)
+        def _():
+            out[0] = y
+
+
+def final_kept(h, p, k, wd, lo, masks):
     _, _, cap, width = h.shape
     cols = wd.shape[1]
     at, n, m0 = lo // cols, len(masks), masks[0]
     rows = 2 * n * cap
-    halves = h.reshape(2, MASKS, 2, cap // 2, width)
-    return call(
-        final_kernel, 2 * rows * width * cols, 2 * (rows * width + width * cols) + 6 * rows * cols,
-        grid=(2 * n,),
-        in_specs=[pl.BlockSpec((1, 1, 1, cap // 2, width), functools.partial(lambda j, i: (i // n, m0 + i % n, j, 0, 0), j)) for j in range(2)]
-        + [
-            pl.BlockSpec((1, 1, 1, cap, cols), lambda i: (k, i // n, m0 + i % n, 0, at)),
-            pl.BlockSpec((width, cols), lambda i: (0, 0)),
-        ],
-        out_specs=[pl.BlockSpec((1, cap, cols), functools.partial(lambda m, i: (jnp.where(i >= n + m, 1, 0), 0, 0), m)) for m in range(n)],
-        out_shape=[jax.ShapeDtypeStruct((2, cap, cols), BF16)] * n,
-    )(halves, halves, p, wd)
+    args = [p, wd]
+    in_specs = [
+        pl.BlockSpec((1, 1, 1, cap, cols), lambda i: (k, i // n, m0 + i % n, 0, at)),
+        pl.BlockSpec((width, cols), lambda i: (0, 0)),
+    ]
+    kw = kept(h, args, in_specs, n)
+    return call(
+        functools.partial(final_kept_kernel, masks), 2 * rows * width * cols, 6 * rows * cols, 33,
+        grid=(2 * n,), in_specs=in_specs,
+        out_specs=[pl.BlockSpec((1, cap, cols), functools.partial(lambda m, i: (jnp.where(i >= n + m, 1, 0), 0, 0), m)) for m in range(n)]
+        + [pl.BlockSpec(memory_space=pltpu.VMEM)],
+        out_shape=[jax.ShapeDtypeStruct((2, cap, cols), BF16)] * n + [pltpu.VMEM(h.shape, BF16)], **kw,
+    )(*args)
 
 
 def picked(k, groups, pos, gate):
@@ -167,7 +214,9 @@
     return totals
 
 
-def combine_kernel(k, n, *refs):
+def combine_kernel(k, n, held, *refs):
+    if held:
+        refs = refs[:-1]
     groups = [refs[MASKS * j:MASKS * (j + 1)] for j in range(n)]
     totals = picked(k, groups, *refs[MASKS * n:MASKS * n + 2])
     cols = groups[0][0].shape[2]
@@ -185,7 +234,7 @@
                 out[:, at] = total
 
 
-def combine(groups, pos, gate, k, lo, model, acc=None, into=None):
+def combine(groups, pos, gate, k, lo, model, acc=None, into=None, held=None):
     _, cap, cols = groups[0][0].shape
     n, wide = len(groups), cols * len(groups)
     toks = pos.shape[1]
@@ -195,30 +244,33 @@
     in_specs = [pl.BlockSpec((1, cap, cols), lambda i: (i // blocks, 0, 0))] * (MASKS * n)
     in_specs += [pl.BlockSpec((1, TB, pos.shape[2]), lambda i: (i // blocks, i % blocks, 0))] * 2
     flops, nbytes = 2 * 2 * toks * MASKS * cap * wide, 2 * toks * wide * 6
-    kernel = functools.partial(combine_kernel, k, n)
+    kernel = functools.partial(combine_kernel, k, n, held is not None)
     if k == 0:
         kw = filled_further(into, args, in_specs)
         return call(
-            kernel, flops, nbytes,
+            kernel, flops, nbytes, 20,
             grid=(2 * blocks,), in_specs=in_specs,
             out_specs=pl.BlockSpec((TB, wide), lambda i: (i, at)),
             out_shape=jax.ShapeDtypeStruct((2 * toks, model), F32), **kw,
         )(*args)
     args.append(acc)
     in_specs.append(pl.BlockSpec((TB, wide), lambda i: (i, at)))
-    kw = {}
+    aliases = {}
     if into is not None:
-        kw["input_output_aliases"] = {len(args): 0, len(args) + 1: 1}
+        aliases = {len(args): 0, len(args) + 1: 1}
         args += into
         in_specs += [pl.BlockSpec(memory_space=pl.ANY)] * 2
-    return call(
-        kernel, flops, nbytes,
+    if held is not None:
+        aliases |= kept(held, args, in_specs, 2)["input_output_aliases"]
+    return call(
+        kernel, flops, nbytes, 33,
         grid=(2 * blocks,), in_specs=in_specs,
         out_specs=[
             pl.BlockSpec((TB, wide), lambda i: (jnp.minimum(i, blocks - 1), at)),
             pl.BlockSpec((TB, wide), lambda i: (jnp.maximum(i - blocks, 0), at)),
-        ],
-        out_shape=[jax.ShapeDtypeStruct((toks, model), BF16)] * 2, **kw,
+        ] + [pl.BlockSpec(memory_space=pltpu.VMEM)] * (held is not None),
+        out_shape=[jax.ShapeDtypeStruct((toks, model), BF16)] * 2 + ([] if held is None else [pltpu.VMEM(held.shape, BF16)]),
+        input_output_aliases=aliases,
     )(*args)
 
 
@@ -236,10 +288,10 @@
     gate_spec = P("ep", None, "tp")
     down_spec = P("ep", "tp", None)
     up1_cuts = cuts([512, 1024, 1024, 256])
-    down_cuts = [cuts([1024] + [256] * 4), cuts([256] * 7 + [128, 128])]
-    late = [(0, n) for n in range(1, 5)] + [(1, n) for n in range(9)]
+    down_cuts = [cuts([1024, 512, 512]), cuts([256] * 7 + [128, 128])]
+    late = [(1, n) for n in range(9)]
     halves = [(1, 7), (1, 8)]
-    groups = [[(0, 0)], [(0, 1), (0, 2)], [(0, 3), (0, 4)], [(1, 0), (1, 1)], [(1, 2), (1, 3)], [(1, 4), (1, 5)], [(1, 6)], [(1, 7)], [(1, 8)]]
+    after = {(1, 3): [[(1, 0), (1, 1)]], (1, 5): [[(1, 2), (1, 3)]], (1, 7): [[(1, 4), (1, 5)]], (1, 8): [[(1, 6)], [(1, 7)], [(1, 8)]]}
 
     def ep_swap(value, mask):
         return lax.ppermute(value, "ep", [(i, i ^ mask) for i in range(ep_size)])
@@ -270,7 +322,8 @@
         gate0 = tp_swap(w_gate, 0)
         up0 = tp_swap(w_up, 0)
         down = [[None] * len(c) for c in down_cuts]
-        down[0][0] = tp_swap(w_down, 0, *down_cuts[0][0])
+        for n, (lo, hi) in enumerate(down_cuts[0]):
+            down[0][n] = tp_swap(w_down, 0, lo, hi)
         gate1 = tp_swap(w_gate, 1)
         for n, (lo, hi) in list(enumerate(up1_cuts))[1:]:
             up1[n] = tp_swap(w_up, 1, lo, hi)
@@ -302,25 +355,34 @@
                 h_r[1] = hidden(xs[b], b, 1, gate1, up1[n], lo, h_r[1])
 
         acc, outs, back = None, None, {}
-        for k, n in [(0, 0)] + late:
-            lo, hi = down_cuts[k][n]
+
+        def finish(k, n):
+            lo, _ = down_cuts[k][n]
             if (k, n) in halves:
-                far = final(h_r[k], p, k, down[k][n], lo, (2, 3))
-                near = final(h_r[k], p, k, down[k][n], lo, (0, 1))
+                *far, h_r[k] = final_kept(h_r[k], p, k, down[k][n], lo, (2, 3))
+                *near, h_r[k] = final_kept(h_r[k], p, k, down[k][n], lo, (0, 1))
             else:
-                *near, y2, y3 = final(h_r[k], p, k, down[k][n], lo, (0, 1, 2, 3))
-                far = [y2, y3]
+                if k == 0:
+                    ys = final(h_r[k], p, k, down[k][n], lo)
+                else:
+                    *ys, h_r[k] = final_kept(h_r[k], p, k, down[k][n], lo, (0, 1, 2, 3))
+                near, far = ys[:2], ys[2:]
             far = [ep_swap(far[0], 2), ep_swap(far[1], 3)]
             near = [near[0], ep_swap(near[1], 1)]
             back[k, n] = near + far
-        for group in groups:
-            k, n = group[-1]
-            lo = down_cuts[k][group[0][1]][0]
-            done = [back[item] for item in group]
-            if k == 0:
-                acc = combine(done, pos_t, gate_t, 0, lo, model, None, acc)
-            else:
-                outs = combine(done, pos_t, gate_t, 1, lo, model, acc, outs)
+
+        for item in (0, 0), (0, 1), (0, 2):
+            finish(*item)
+            acc = combine([back[item]], pos_t, gate_t, 0, down_cuts[0][item[1]][0], model, None, acc)
+        for i, item in enumerate(late):
+            finish(*item)
+            for group in after.get(item, []):
+                outs = combine(
+                    [back[it] for it in group], pos_t, gate_t, 1, down_cuts[1][group[0][1]][0], model, acc, outs,
+                    h_r[1] if i < len(late) - 1 else None,
+                )
+                if i < len(late) - 1:
+                    *outs, h_r[1] = outs
         return tuple(outs)
 
     in_specs = (row_spec, row_spec, row_spec, row_spec, row_spec, row_spec, gate_spec, gate_spec, down_spec)

time: 2180 us -> 2140 us (0.982)
  Pallas kernels: 1340 us -> 1190 us
  waiting for transfers between devices: 703 us -> 775 us
  local copies, waits for them, and re-layouts: 71.7 us -> 107 us
    pallas_call x16 -> x3, Pallas kernels: 336 us -> 90.9 us  [final(): call(final_kernel, 2 * rows * width * cols, 2 * (rows * width + width * c...]
    pallas_call x21 -> x32, Pallas kernels: 730 us -> 828 us  [the longest x2 259 us: hidden_local(): call(functools.partial(hidden_kernel, None, 0), 4 * rows * model * width,...]
    ppermute x21 -> x19, waiting for transfers between devices: 322 us -> 419 us  [tp_swap(): return lax.ppermute(piece, 'tp', TP_SWAP)[0]]
    unnamed x94 -> x104, local copies, waits for them, and re-layouts: 8.91 us -> 43.1 us
    ppermute x48 -> x42, waiting for transfers between devices: 382 us -> 355 us  [ep_swap(): return lax.ppermute(value, 'ep', [(i, i ^ mask) for i in range(ep_size)])]
    slice x8 -> x9, local copies, waits for them, and re-layouts: 51.9 us -> 53.2 us  [tp_swap(): lax.slice(w, (k, 0, lo), (k + 1, w.shape[1], w.shape[2] if hi is None els...]
  transfers between devices with their start and end apart: 69 -> 61, of which waited for: 22 -> 14; matrix products, arithmetic and copies ran while one was open for 3% -> 3% of each run, Pallas kernels for 60% -> 54%
where the time goes in v4:
time: 2140 us; the launch traced here: 2130 us
  Pallas kernels  1190 us (56%)
  waiting for transfers between devices  775 us (36%)
  local copies, waits for them, and re-layouts  107 us (5%)
  starting transfers between devices  51.7 us (2%)
    ppermute x19, waiting for transfers between devices, tp_swap(): return lax.ppermute(piece, 'tp', TP_SWAP)[0]  419 us
    ppermute x42, waiting for transfers between devices, ep_swap(): return lax.ppermute(value, 'ep', [(i, i ^ mask) for i in range(ep_size)])  355 us
    pallas_call x2, Pallas kernels, hidden_local(): call(functools.partial(hidden_kernel, None, 0), 4 * rows * model * width,...  259 us
    pallas_call x8, Pallas kernels, hidden(): call(functools.partial(hidden_kernel, b, off), *cost, 33, grid=(steps,),...  162 us
    pallas_call x2, Pallas kernels, part(): call(part_kernel, 2 * rows * width * model, 2 * (rows * width + 2 * width...  146 us
    pallas_call x2, Pallas kernels, hidden(): call(functools.partial(hidden_kernel, None, 0), *cost, grid=(steps,), in_...  135 us
    pallas_call x4, Pallas kernels, dispatch(): call(dispatch_kernel, 2 * n * 2 * cap * toks * model, toks * model * 2 +...  125 us
    pallas_call x11, Pallas kernels, final_kept(): call(functools.partial(final_kept_kernel, masks), 2 * rows * width * cols...  114 us
  transfers between devices with their start and end apart: 61, of which 14 were waited for; matrix products, arithmetic and copies ran while one was open for 3% of the time, Pallas kernels for 54%

profile of v4, /device:TPU:0, one launch (start us, length us, event | category | flops | bytes accessed | tf_op | source)
XLA Modules:
  0.0 2131.2 jit_solution(2518606417891695800)
XLA Ops:
  3.1 4.6 reduce-window.6
  14.8 31.1 %shard_map.104 = (bf16[2,640,2048]{2,1,0:T(8,128)(2,1)}, bf16[2,640,2048]{2,1,0:T(8,128)(2,1)}) custom-call(s32[4,1,2048]{2,1,0:T(1,128)} %copy.66.pos_ref, bf16[2048,2048]{1,0:T(8,128)(2,1)} %tok_ref.5), custom_call_target="tpu_custom_call" | custom-call | flops 21474836480 | bytes 18874368 | tf_op jit(solution)/shard_map/pallas_call | solution.py:61
  47.7 31.1 %shard_map.105 = (bf16[2,640,2048]{2,1,0:T(8,128)(2,1)}, bf16[2,640,2048]{2,1,0:T(8,128)(2,1)}) custom-call(s32[4,1,2048]{2,1,0:T(1,128)} %copy.67.pos_ref, bf16[2048,2048]{1,0:T(8,128)(2,1)} %tok_ref.5), custom_call_target="tpu_custom_call" | custom-call | flops 21474836480 | bytes 18874368 | tf_op jit(solution)/shard_map/pallas_call | solution.py:61
  82.3 31.6 %shard_map.107 = (bf16[2,640,2048]{2,1,0:T(8,128)(2,1)}, bf16[2,640,2048]{2,1,0:T(8,128)(2,1)}) custom-call(s32[4,1,2048]{2,1,0:T(1,128)} %copy.68.pos_ref, bf16[2048,2048]{1,0:T(8,128)(2,1)} %tok_ref.7), custom_call_target="tpu_custom_call" | custom-call | flops 21474836480 | bytes 18874368 | tf_op jit(solution)/shard_map/pallas_call | solution.py:61
  115.0 31.1 %shard_map.108 = (bf16[2,640,2048]{2,1,0:T(8,128)(2,1)}, bf16[2,640,2048]{2,1,0:T(8,128)(2,1)}) custom-call(s32[4,1,2048]{2,1,0:T(1,128)} %copy.69.pos_ref, bf16[2048,2048]{1,0:T(8,128)(2,1)} %tok_ref.7), custom_call_target="tpu_custom_call" | custom-call | flops 21474836480 | bytes 18874368 | tf_op jit(solution)/shard_map/pallas_call | solution.py:61
  153.3 9.9 slice.113
  165.7 5.8 slice.116
  173.5 7.0 fusion.6
  180.5 6.4 fusion.4
  186.9 8.2 fusion.2
  197.1 8.1 fusion.5
  206.7 100.7 %collective-permute-done.2.refs_3_ = bf16[2,640,2048]{2,1,0:T(8,128)(2,1)} collective-permute-done((bf16[2,640,2048]{2,1,0:T(8,128)(2,1)}, bf16[2,640,2048]{2,1,0:T(8,128)(2,1)}, u32[]{:S(2)}, u32[]{:S(2)}) %collective-permute-start.2) | collective-permute-done | bytes 5242912 | tf_op jit(solution)/shard_map/ppermute | solution.py:297
  308.9 129.7 %shard_map.106.h = bf16[2,4,640,2816]{3,2,1,0:T(8,128)(2,1)} custom-call(bf16[2,640,2048]{2,1,0:T(8,128)(2,1)} %get-tuple-element.81.refs_0_, bf16[2,640,2048]{2,1,0:T(8,128)(2,1)} %collective-permute-done.refs_1_, bf16[2,640,2048]{2,1,0:T(8,128)(2,1)} %collective-permute-done.1.refs_2_, bf16[2,640,2048]{2,1,0:T(8,128)(2,1)} %collective-permute-done.2.refs_3_, ...), custom_call_target="tpu_custom_call" | custom-call | flops 118111600640 | bytes 95944704 | tf_op jit(solution)/shard_map/pallas_call | solution.py:88
  440.7 91.4 %collective-permute-done.5.refs_3_ = bf16[2,640,2048]{2,1,0:T(8,128)(2,1)} collective-permute-done((bf16[2,640,2048]{2,1,0:T(8,128)(2,1)}, bf16[2,640,2048]{2,1,0:T(8,128)(2,1)}, u32[]{:S(2)}, u32[]{:S(2)}) %collective-permute-start.5) | collective-permute-done | bytes 5242912 | tf_op jit(solution)/shard_map/ppermute | solution.py:297
  533.7 129.7 %shard_map.109.h = bf16[2,4,640,2816]{3,2,1,0:T(8,128)(2,1)} custom-call(bf16[2,640,2048]{2,1,0:T(8,128)(2,1)} %get-tuple-element.85.refs_0_, bf16[2,640,2048]{2,1,0:T(8,128)(2,1)} %collective-permute-done.3.refs_1_, bf16[2,640,2048]{2,1,0:T(8,128)(2,1)} %collective-permute-done.4.refs_2_, bf16[2,640,2048]{2,1,0:T(8,128)(2,1)} %collective-permute-done.5.refs_3_, ...), custom_call_target="tpu_custom_call" | custom-call | flops 118111600640 | bytes 95944704 | tf_op jit(solution)/shard_map/pallas_call | solution.py:88
  663.3 72.8 %shard_map.110.refs_0_ = f32[2,2,4,640,2048]{4,3,2,1,0:T(8,128)} custom-call(bf16[2,4,640,2816]{3,2,1,0:T(8,128)(2,1)} %shard_map.109.h, bf16[2,2816,2048]{2,1,0:T(8,128)(2,1)} %wd.3), custom_call_target="tpu_custom_call" | custom-call | flops 59055800320 | bytes 93847552 | tf_op jit(solution)/shard_map/pallas_call | solution.py:138
  736.1 72.8 %shard_map.111.p = f32[2,2,4,640,2048]{4,3,2,1,0:T(8,128)} custom-call(bf16[2,4,640,2816]{3,2,1,0:T(8,128)(2,1)} %shard_map.106.h, bf16[2,2816,2048]{2,1,0:T(8,128)(2,1)} %wd.3, f32[2,2,4,640,2048]{4,3,2,1,0:T(8,128)} %shard_map.110.refs_0_), custom_call_target="tpu_custom_call", output_to_operand_aliasing={{}: (2, {})} | custom-call | flops 59055800320 | bytes 93847552 | tf_op jit(solution)/shard_map/pallas_call | solution.py:138
  808.9 19.3 collective-permute-done.21
  829.7 245.7 %collective-permute-done.22 = bf16[1,2048,2816]{2,1,0:T(8,128)(2,1)} collective-permute-done((bf16[1,2048,2816]{2,1,0:T(8,128)(2,1)}, bf16[1,2048,2816]{2,1,0:T(8,128)(2,1)}, u32[]{:S(2)}, u32[]{:S(2)}) %collective-permute-start.22) | collective-permute-done | bytes 11534368 | tf_op jit(solution)/shard_map/ppermute | solution.py:301
  1076.8 67.8 %shard_map.122.refs_6_ = bf16[2,4,640,2816]{3,2,1,0:T(8,128)(2,1)} custom-call(bf16[2,640,2048]{2,1,0:T(8,128)(2,1)} %get-tuple-element.85.refs_0_, bf16[2,640,2048]{2,1,0:T(8,128)(2,1)} %collective-permute-done.3.refs_1_, bf16[2,640,2048]{2,1,0:T(8,128)(2,1)} %collective-permute-done.4.refs_2_, bf16[2,640,2048]{2,1,0:T(8,128)(2,1)} %collective-permute-done.5.refs_3_, ...), custom_call_target="tpu_custom_call" | custom-call | flops 59055800320 | bytes 47972352 | tf_op jit(solution)/shard_map/pallas_call | solution.py:118
  1144.6 67.6 %shard_map.123.h0.h1 = bf16[2,4,640,2816]{3,2,1,0:T(8,128)(2,1)} custom-call(bf16[2,640,2048]{2,1,0:T(8,128)(2,1)} %get-tuple-element.81.refs_0_, bf16[2,640,2048]{2,1,0:T(8,128)(2,1)} %collective-permute-done.refs_1_, bf16[2,640,2048]{2,1,0:T(8,128)(2,1)} %collective-permute-done.1.refs_2_, ...), custom_call_target="tpu_custom_call", output_to_operand_aliasing={{}: (6, {})} | custom-call | flops 59055800320 | bytes 47972352 | tf_op jit(solution)/shard_map/pallas_call | solution.py:118
  1214.3 15.9 shard_map.112.refs_6_
  1230.2 16.3 shard_map.113.refs_6_
  1247.1 27.2 %shard_map.114.refs_6_ = bf16[2,4,640,2816]{3,2,1,0:T(8,128)(2,1)S(1)} custom-call(bf16[2,640,2048]{2,1,0:T(8,128)(2,1)} %get-tuple-element.85.refs_0_, bf16[2,640,2048]{2,1,0:T(8,128)(2,1)} %collective-permute-done.3.refs_1_, bf16[2,640,2048]{2,1,0:T(8,128)(2,1)} %collective-permute-done.4.refs_2_, ...), custom_call_target="tpu_custom_call", output_to_operand_aliasing={{}: (6, {})} | custom-call | flops 21474836480 | bytes 24117248 | tf_op jit(solution)/shard_map/pallas_call | solution.py:111
  1274.3 27.3 %shard_map.115.refs_6_ = bf16[2,4,640,2816]{3,2,1,0:T(8,128)(2,1)S(1)} custom-call(bf16[2,640,2048]{2,1,0:T(8,128)(2,1)} %get-tuple-element.81.refs_0_, bf16[2,640,2048]{2,1,0:T(8,128)(2,1)} %collective-permute-done.refs_1_, bf16[2,640,2048]{2,1,0:T(8,128)(2,1)} %collective-permute-done.1.refs_2_, ...), custom_call_target="tpu_custom_call", output_to_operand_aliasing={{}: (6, {})} | custom-call | flops 21474836480 | bytes 24117248 | tf_op jit(solution)/shard_map/pallas_call | solution.py:111
  1301.6 4.5 collective-permute-done.11
  1306.6 27.3 %shard_map.116.refs_6_ = bf16[2,4,640,2816]{3,2,1,0:T(8,128)(2,1)S(1)} custom-call(bf16[2,640,2048]{2,1,0:T(8,128)(2,1)} %get-tuple-element.85.refs_0_, bf16[2,640,2048]{2,1,0:T(8,128)(2,1)} %collective-permute-done.3.refs_1_, bf16[2,640,2048]{2,1,0:T(8,128)(2,1)} %collective-permute-done.4.refs_2_, ...), custom_call_target="tpu_custom_call", output_to_operand_aliasing={{}: (6, {})} | custom-call | flops 21474836480 | bytes 24117248 | tf_op jit(solution)/shard_map/pallas_call | solution.py:111
  1333.9 27.3 %shard_map.117.refs_6_ = bf16[2,4,640,2816]{3,2,1,0:T(8,128)(2,1)S(1)} custom-call(bf16[2,640,2048]{2,1,0:T(8,128)(2,1)} %get-tuple-element.81.refs_0_, bf16[2,640,2048]{2,1,0:T(8,128)(2,1)} %collective-permute-done.refs_1_, bf16[2,640,2048]{2,1,0:T(8,128)(2,1)} %collective-permute-done.1.refs_2_, ...), custom_call_target="tpu_custom_call", output_to_operand_aliasing={{}: (6, {})} | custom-call | flops 21474836480 | bytes 24117248 | tf_op jit(solution)/shard_map/pallas_call | solution.py:111
  1361.2 9.5 copy-done
  1370.7 150.0 %collective-permute-done.23 = bf16[1,2816,512]{2,1,0:T(8,128)(2,1)} collective-permute-done((bf16[1,2816,512]{2,1,0:T(8,128)(2,1)}, bf16[1,2816,512]{2,1,0:T(8,128)(2,1)}, u32[]{:S(2)}, u32[]{:S(2)}) %collective-permute-start.23) | collective-permute-done | bytes 2883616 | tf_op jit(solution)/shard_map/ppermute | solution.py:301
  1521.1 24.2 %shard_map.124 = (bf16[2,640,512]{2,1,0:T(8,128)(2,1)}, bf16[2,640,512]{2,1,0:T(8,128)(2,1)}, bf16[2,640,512]{2,1,0:T(8,128)(2,1)}, bf16[2,640,512]{2,1,0:T(8,128)(2,1)}) custom-call(bf16[2,4,640,2816]{3,2,1,0:T(8,128)(2,1)} %shard_map.123.h0.h1, bf16[2,4,640,2816]{3,2,1,0:T(8,128)(2,1)} %shard_map.123.h0.h1, f32[2,2,4,640,2048]{4,3,2,1,0:T(8,128)} %shard_map.111.p, ...), custom_call_target="tpu_custom_call" | custom-call | flops 14763950080 | bytes 47448064 | tf_op jit(solution)/shard_map/pallas_call | solution.py:162
  1547.0 42.2 %shard_map.126 = (bf16[2,640,1024]{2,1,0:T(8,128)(2,1)}, bf16[2,640,1024]{2,1,0:T(8,128)(2,1)}, bf16[2,640,1024]{2,1,0:T(8,128)(2,1)}, bf16[2,640,1024]{2,1,0:T(8,128)(2,1)}) custom-call(bf16[2,4,640,2816]{3,2,1,0:T(8,128)(2,1)} %shard_map.123.h0.h1, bf16[2,4,640,2816]{3,2,1,0:T(8,128)(2,1)} %shard_map.123.h0.h1, f32[2,2,4,640,2048]{4,3,2,1,0:T(8,128)} %shard_map.111.p, ...), custom_call_target="tpu_custom_call" | custom-call | flops 29527900160 | bytes 66060288 | tf_op jit(solution)/shard_map/pallas_call | solution.py:162
  1590.7 24.5 %shard_map.125 = (bf16[2,640,512]{2,1,0:T(8,128)(2,1)}, bf16[2,640,512]{2,1,0:T(8,128)(2,1)}, bf16[2,640,512]{2,1,0:T(8,128)(2,1)}, bf16[2,640,512]{2,1,0:T(8,128)(2,1)}) custom-call(bf16[2,4,640,2816]{3,2,1,0:T(8,128)(2,1)} %shard_map.123.h0.h1, bf16[2,4,640,2816]{3,2,1,0:T(8,128)(2,1)} %shard_map.123.h0.h1, f32[2,2,4,640,2048]{4,3,2,1,0:T(8,128)} %shard_map.111.p, ...), custom_call_target="tpu_custom_call" | custom-call | flops 14763950080 | bytes 47448064 | tf_op jit(solution)/shard_map/pallas_call | solution.py:162
  1615.3 9.2 copy-done.1
  1624.5 10.2 shard_map.118.refs_6_
  1634.7 10.2 shard_map.119.h
  1646.8 12.3 shard_map.120
  1659.2 12.5 shard_map.121
  1672.0 12.4 shard_map.130
  1684.6 12.6 shard_map.131
  1697.1 9.5 copy-done.2
  1709.8 50.5 %collective-permute-done.34.refs_3_ = bf16[2,640,1024]{2,1,0:T(8,128)(2,1)} collective-permute-done((bf16[2,640,1024]{2,1,0:T(8,128)(2,1)}, bf16[2,640,1024]{2,1,0:T(8,128)(2,1)}, u32[]{:S(2)}, u32[]{:S(2)}) %collective-permute-start.34) | collective-permute-done | bytes 2621472 | tf_op jit(solution)/shard_map/ppermute | solution.py:297
  1765.5 32.6 %shard_map.127.refs_6_ = f32[4096,2048]{1,0:T(8,128)} custom-call(bf16[2,640,1024]{2,1,0:T(8,128)(2,1)S(1)} %copy-done.17, bf16[2,640,1024]{2,1,0:T(8,128)(2,1)} %collective-permute-done.32.refs_1_, bf16[2,640,1024]{2,1,0:T(8,128)(2,1)} %collective-permute-done.33.refs_2_, bf16[2,640,1024]{2,1,0:T(8,128)(2,1)} %collective-permute-done.34.refs_3_, ...), custom_call_target="tpu_custom_call" | custom-call | flops 21474836480 | bytes 25165824 | tf_op jit(solution)/shard_map/pallas_call | solution.py:250
  1798.0 47.3 %collective-permute-done.29.refs_2_ = bf16[2,640,512]{2,1,0:T(8,128)(2,1)S(1)} collective-permute-done((bf16[2,640,512]{2,1,0:T(8,128)(2,1)}, bf16[2,640,512]{2,1,0:T(8,128)(2,1)S(1)}, u32[]{:S(2)}, u32[]{:S(2)}) %collective-permute-start.29) | collective-permute-done | bytes 1310752 | tf_op jit(solution)/shard_map/ppermute | solution.py:297
  1845.4 27.1 %collective-permute-done.30.refs_3_ = bf16[2,640,512]{2,1,0:T(8,128)(2,1)S(1)} collective-permute-done((bf16[2,640,512]{2,1,0:T(8,128)(2,1)}, bf16[2,640,512]{2,1,0:T(8,128)(2,1)S(1)}, u32[]{:S(2)}, u32[]{:S(2)}) %collective-permute-start.30) | collective-permute-done | bytes 1310752 | tf_op jit(solution)/shard_map/ppermute | solution.py:297
  1874.0 17.4 shard_map.128.refs_6_
  1899.2 16.2 shard_map.129.refs_10_.refs_6_
  1917.5 5.6 collective-permute-done.19.refs_6_
  1923.5 13.7 collective-permute-done.20.refs_7_
  1938.1 20.0 shard_map.132
  1958.7 12.4 shard_map.133
  1973.3 12.4 shard_map.134
  1990.6 12.7 collective-permute-done.49.refs_7_
  2004.4 20.2 shard_map.135
  2026.6 12.4 shard_map.136
  2039.0 6.7 shard_map.137
  2045.7 6.7 shard_map.138
  2055.5 4.0 collective-permute-done.43.refs_7_
  2060.5 20.0 shard_map.139
  2081.7 6.6 shard_map.140
  2088.3 6.8 shard_map.141
  2099.4 11.4 shard_map.142
  2110.8 10.3 shard_map.143
  2121.1 9.9 shard_map.144
  (233 shorter events, 89.7 us)
Async XLA Ops:
  45.9 159.2 %collective-permute-start = (bf16[2,640,2048]{2,1,0:T(8,128)(2,1)}, bf16[2,640,2048]{2,1,0:T(8,128)(2,1)}, u32[]{:S(2)}, u32[]{:S(2)}) collective-permute-start(bf16[2,640,2048]{2,1,0:T(8,128)(2,1)} %get-tuple-element.82), channel_id=1, source_target_pairs={{0,1},{1,0},{2,3},{3,2},{4,5},{5,4},{6,7},{7,6}} | collective-permute-start | bytes 15728648 | tf_op jit(solution)/shard_map/ppermute | solution.py:297
  78.8 126.3 %collective-permute-start.1 = (bf16[2,640,2048]{2,1,0:T(8,128)(2,1)}, bf16[2,640,2048]{2,1,0:T(8,128)(2,1)}, u32[]{:S(2)}, u32[]{:S(2)}) collective-permute-start(bf16[2,640,2048]{2,1,0:T(8,128)(2,1)} %get-tuple-element.83), channel_id=1, source_target_pairs={{0,2},{1,3},{2,0},{3,1},{4,6},{5,7},{6,4},{7,5}} | collective-permute-start | bytes 15728648 | tf_op jit(solution)/shard_map/ppermute | solution.py:297
  81.3 226.2 %collective-permute-start.2 = (bf16[2,640,2048]{2,1,0:T(8,128)(2,1)}, bf16[2,640,2048]{2,1,0:T(8,128)(2,1)}, u32[]{:S(2)}, u32[]{:S(2)}) collective-permute-start(bf16[2,640,2048]{2,1,0:T(8,128)(2,1)} %get-tuple-element.84), channel_id=1, source_target_pairs={{0,3},{1,2},{2,1},{3,0},{4,7},{5,6},{6,5},{7,4}} | collective-permute-start | bytes 15728648 | tf_op jit(solution)/shard_map/ppermute | solution.py:297
  113.9 324.8 %collective-permute-start.3 = (bf16[2,640,2048]{2,1,0:T(8,128)(2,1)}, bf16[2,640,2048]{2,1,0:T(8,128)(2,1)}, u32[]{:S(2)}, u32[]{:S(2)}) collective-permute-start(bf16[2,640,2048]{2,1,0:T(8,128)(2,1)} %get-tuple-element.86), channel_id=1, source_target_pairs={{0,1},{1,0},{2,3},{3,2},{4,5},{5,4},{6,7},{7,6}} | collective-permute-start | bytes 15728648 | tf_op jit(solution)/shard_map/ppermute | solution.py:297
  146.0 293.2 %collective-permute-start.4 = (bf16[2,640,2048]{2,1,0:T(8,128)(2,1)}, bf16[2,640,2048]{2,1,0:T(8,128)(2,1)}, u32[]{:S(2)}, u32[]{:S(2)}) collective-permute-start(bf16[2,640,2048]{2,1,0:T(8,128)(2,1)} %get-tuple-element.87), channel_id=1, source_target_pairs={{0,2},{1,3},{2,0},{3,1},{4,6},{5,7},{6,4},{7,5}} | collective-permute-start | bytes 15728648 | tf_op jit(solution)/shard_map/ppermute | solution.py:297
  205.1 327.0 %collective-permute-start.5 = (bf16[2,640,2048]{2,1,0:T(8,128)(2,1)}, bf16[2,640,2048]{2,1,0:T(8,128)(2,1)}, u32[]{:S(2)}, u32[]{:S(2)}) collective-permute-start(bf16[2,640,2048]{2,1,0:T(8,128)(2,1)} %get-tuple-element.88), channel_id=1, source_target_pairs={{0,3},{1,2},{2,1},{3,0},{4,7},{5,6},{6,5},{7,4}} | collective-permute-start | bytes 15728648 | tf_op jit(solution)/shard_map/ppermute | solution.py:297
  205.1 1439.8 %collective-permute-start.8 = (bf16[1,2816,256]{2,1,0:T(8,128)(2,1)}, bf16[1,2816,256]{2,1,0:T(8,128)(2,1)}, u32[]{:S(2)}, u32[]{:S(2)}) collective-permute-start(bf16[1,2816,256]{2,1,0:T(8,128)(2,1)} %get-tuple-element.165), channel_id=1, source_target_pairs={{0,4},{4,0},{1,5},{5,1},{2,6},{6,2},{3,7},{7,3}} | collective-permute-start | bytes 4325384 | tf_op jit(solution)/shard_map/ppermute | solution.py:301
  307.4 905.4 %collective-permute-start.9 = (bf16[1,2048,2816]{2,1,0:T(8,128)(2,1)}, bf16[1,2048,2816]{2,1,0:T(8,128)(2,1)}, u32[]{:S(2)}, u32[]{:S(2)}) collective-permute-start(bf16[1,2048,2816]{2,1,0:T(8,128)(2,1)} %get-tuple-element.172), channel_id=1, source_target_pairs={{0,4},{4,0},{1,5},{5,1},{2,6},{6,2},{3,7},{7,3}} | collective-permute-start | bytes 34603016 | tf_op jit(solution)/shard_map/ppermute | solution.py:301
  438.7 1176.6 %collective-permute-start.10 = (bf16[1,2048,256]{2,1,0:T(8,128)(2,1)}, bf16[1,2048,256]{2,1,0:T(8,128)(2,1)}, u32[]{:S(2)}, u32[]{:S(2)}) collective-permute-start(bf16[1,2048,256]{2,1,0:T(8,128)(2,1)} %slice.107), channel_id=1, source_target_pairs={{0,4},{4,0},{1,5},{5,1},{2,6},{6,2},{3,7},{7,3}} | collective-permute-start | bytes 3145736 | tf_op jit(solution)/shard_map/ppermute | solution.py:301
  439.2 388.9 %collective-permute-start.21 = (bf16[1,2048,2816]{2,1,0:T(8,128)(2,1)}, bf16[1,2048,2816]{2,1,0:T(8,128)(2,1)}, u32[]{:S(2)}, u32[]{:S(2)}) collective-permute-start(bf16[1,2048,2816]{2,1,0:T(8,128)(2,1)} %get-tuple-element.171), channel_id=1, source_target_pairs={{0,4},{4,0},{1,5},{5,1},{2,6},{6,2},{3,7},{7,3}} | collective-permute-start | bytes 34603016 | tf_op jit(solution)/shard_map/ppermute | solution.py:301
  532.2 543.2 %collective-permute-start.22 = (bf16[1,2048,2816]{2,1,0:T(8,128)(2,1)}, bf16[1,2048,2816]{2,1,0:T(8,128)(2,1)}, u32[]{:S(2)}, u32[]{:S(2)}) collective-permute-start(bf16[1,2048,2816]{2,1,0:T(8,128)(2,1)} %slice.113), channel_id=1, source_target_pairs={{0,4},{4,0},{1,5},{5,1},{2,6},{6,2},{3,7},{7,3}} | collective-permute-start | bytes 34603016 | tf_op jit(solution)/shard_map/ppermute | solution.py:301
  828.2 418.4 %collective-permute-start.12 = (bf16[1,2048,1024]{2,1,0:T(8,128)(2,1)}, bf16[1,2048,1024]{2,1,0:T(8,128)(2,1)}, u32[]{:S(2)}, u32[]{:S(2)}) collective-permute-start(bf16[1,2048,1024]{2,1,0:T(8,128)(2,1)} %get-tuple-element.173), channel_id=1, source_target_pairs={{0,4},{4,0},{1,5},{5,1},{2,6},{6,2},{3,7},{7,3}} | collective-permute-start | bytes 12582920 | tf_op jit(solution)/shard_map/ppermute | solution.py:301
  1075.3 136.9 %collective-permute-start.13 = (bf16[1,2048,512]{2,1,0:T(8,128)(2,1)}, bf16[1,2048,512]{2,1,0:T(8,128)(2,1)S(1)}, u32[]{:S(2)}, u32[]{:S(2)}) collective-permute-start(bf16[1,2048,512]{2,1,0:T(8,128)(2,1)} %slice.110), channel_id=1, source_target_pairs={{0,4},{4,0},{1,5},{5,1},{2,6},{6,2},{3,7},{7,3}} | collective-permute-start | bytes 6291464 | tf_op jit(solution)/shard_map/ppermute | solution.py:301
  1212.3 93.8 %collective-permute-start.11 = (bf16[1,2048,1024]{2,1,0:T(8,128)(2,1)}, bf16[1,2048,1024]{2,1,0:T(8,128)(2,1)}, u32[]{:S(2)}, u32[]{:S(2)}) collective-permute-start(bf16[1,2048,1024]{2,1,0:T(8,128)(2,1)} %get-tuple-element.174), channel_id=1, source_target_pairs={{0,4},{4,0},{1,5},{5,1},{2,6},{6,2},{3,7},{7,3}} | collective-permute-start | bytes 12582920 | tf_op jit(solution)/shard_map/ppermute | solution.py:301
  1212.8 433.7 %collective-permute-start.17 = (bf16[1,2816,256]{2,1,0:T(8,128)(2,1)}, bf16[1,2816,256]{2,1,0:T(8,128)(2,1)}, u32[]{:S(2)}, u32[]{:S(2)}) collective-permute-start(bf16[1,2816,256]{2,1,0:T(8,128)(2,1)} %get-tuple-element.164), channel_id=1, source_target_pairs={{0,4},{4,0},{1,5},{5,1},{2,6},{6,2},{3,7},{7,3}} | collective-permute-start | bytes 4325384 | tf_op jit(solution)/shard_map/ppermute | solution.py:301
  1246.6 298.6 %collective-permute-start.31 = (bf16[1,2816,1024]{2,1,0:T(8,128)(2,1)}, bf16[1,2816,1024]{2,1,0:T(8,128)(2,1)}, u32[]{:S(2)}, u32[]{:S(2)}) collective-permute-start(bf16[1,2816,1024]{2,1,0:T(8,128)(2,1)} %slice.116), channel_id=1, source_target_pairs={{0,4},{4,0},{1,5},{5,1},{2,6},{6,2},{3,7},{7,3}} | collective-permute-start | bytes 17301512 | tf_op jit(solution)/shard_map/ppermute | solution.py:301
  1306.0 214.7 %collective-permute-start.23 = (bf16[1,2816,512]{2,1,0:T(8,128)(2,1)}, bf16[1,2816,512]{2,1,0:T(8,128)(2,1)}, u32[]{:S(2)}, u32[]{:S(2)}) collective-permute-start(bf16[1,2816,512]{2,1,0:T(8,128)(2,1)} %get-tuple-element.170), channel_id=1, source_target_pairs={{0,4},{4,0},{1,5},{5,1},{2,6},{6,2},{3,7},{7,3}} | collective-permute-start | bytes 8650760 | tf_op jit(solution)/shard_map/ppermute | solution.py:301
  1333.9 186.8 %copy-start.19 = (bf16[1,2816,512]{2,1,0:T(8,128)(2,1)S(1)}, bf16[1,2816,512]{2,1,0:T(8,128)(2,1)}, u32[]{:S(2)}) copy-start(bf16[1,2816,512]{2,1,0:T(8,128)(2,1)} %get-tuple-element.169) | copy-start | bytes 8650756
  1520.8 68.4 %collective-permute-start.27 = (bf16[1,2816,512]{2,1,0:T(8,128)(2,1)S(1)}, bf16[1,2816,512]{2,1,0:T(8,128)(2,1)S(1)}, u32[]{:S(2)}, u32[]{:S(2)}) collective-permute-start(bf16[1,2816,512]{2,1,0:T(8,128)(2,1)S(1)} %copy-done.19), channel_id=1, source_target_pairs={{0,4},{4,0},{1,5},{5,1},{2,6},{6,2},{3,7},{7,3}} | collective-permute-start | bytes 8650760 | tf_op jit(solution)/shard_map/ppermute | solution.py:301
  1545.2 139.1 %collective-permute-start.35 = (bf16[1,2816,256]{2,1,0:T(8,128)(2,1)}, bf16[1,2816,256]{2,1,0:T(8,128)(2,1)}, u32[]{:S(2)}, u32[]{:S(2)}) collective-permute-start(bf16[1,2816,256]{2,1,0:T(8,128)(2,1)} %get-tuple-element.163), channel_id=1, source_target_pairs={{0,4},{4,0},{1,5},{5,1},{2,6},{6,2},{3,7},{7,3}} | collective-permute-start | bytes 4325384 | tf_op jit(solution)/shard_map/ppermute | solution.py:301
  1589.2 82.5 %collective-permute-start.36 = (bf16[1,2816,256]{2,1,0:T(8,128)(2,1)}, bf16[1,2816,256]{2,1,0:T(8,128)(2,1)}, u32[]{:S(2)}, u32[]{:S(2)}) collective-permute-start(bf16[1,2816,256]{2,1,0:T(8,128)(2,1)} %get-tuple-element.162), channel_id=1, source_target_pairs={{0,4},{4,0},{1,5},{5,1},{2,6},{6,2},{3,7},{7,3}} | collective-permute-start | bytes 4325384 | tf_op jit(solution)/shard_map/ppermute | solution.py:301
  1615.3 92.9 %collective-permute-start.32 = (bf16[2,640,1024]{2,1,0:T(8,128)(2,1)}, bf16[2,640,1024]{2,1,0:T(8,128)(2,1)}, u32[]{:S(2)}, u32[]{:S(2)}) collective-permute-start(bf16[2,640,1024]{2,1,0:T(8,128)(2,1)} %get-tuple-element.107), channel_id=1, source_target_pairs={{0,1},{1,0},{2,3},{3,2},{4,5},{5,4},{6,7},{7,6}} | collective-permute-start | bytes 7864328 | tf_op jit(solution)/shard_map/ppermute | solution.py:297
  1645.0 63.3 %collective-permute-start.33 = (bf16[2,640,1024]{2,1,0:T(8,128)(2,1)}, bf16[2,640,1024]{2,1,0:T(8,128)(2,1)}, u32[]{:S(2)}, u32[]{:S(2)}) collective-permute-start(bf16[2,640,1024]{2,1,0:T(8,128)(2,1)} %get-tuple-element.108), channel_id=1, source_target_pairs={{0,2},{1,3},{2,0},{3,1},{4,6},{5,7},{6,4},{7,5}} | collective-permute-start | bytes 7864328 | tf_op jit(solution)/shard_map/ppermute | solution.py:297
  1646.5 113.8 %collective-permute-start.34 = (bf16[2,640,1024]{2,1,0:T(8,128)(2,1)}, bf16[2,640,1024]{2,1,0:T(8,128)(2,1)}, u32[]{:S(2)}, u32[]{:S(2)}) collective-permute-start(bf16[2,640,1024]{2,1,0:T(8,128)(2,1)} %get-tuple-element.109), channel_id=1, source_target_pairs={{0,3},{1,2},{2,1},{3,0},{4,7},{5,6},{6,5},{7,4}} | collective-permute-start | bytes 7864328 | tf_op jit(solution)/shard_map/ppermute | solution.py:297
  1671.7 35.0 %collective-permute-start.28 = (bf16[2,640,512]{2,1,0:T(8,128)(2,1)}, bf16[2,640,512]{2,1,0:T(8,128)(2,1)}, u32[]{:S(2)}, u32[]{:S(2)}) collective-permute-start(bf16[2,640,512]{2,1,0:T(8,128)(2,1)} %get-tuple-element.103), channel_id=1, source_target_pairs={{0,1},{1,0},{2,3},{3,2},{4,5},{5,4},{6,7},{7,6}} | collective-permute-start | bytes 3932168 | tf_op jit(solution)/shard_map/ppermute | solution.py:297
  1684.4 207.6 %collective-permute-start.24 = (bf16[2,640,512]{2,1,0:T(8,128)(2,1)}, bf16[2,640,512]{2,1,0:T(8,128)(2,1)S(1)}, u32[]{:S(2)}, u32[]{:S(2)}) collective-permute-start(bf16[2,640,512]{2,1,0:T(8,128)(2,1)} %get-tuple-element.99), channel_id=1, source_target_pairs={{0,1},{1,0},{2,3},{3,2},{4,5},{5,4},{6,7},{7,6}} | collective-permute-start | bytes 3932168 | tf_op jit(solution)/shard_map/ppermute | solution.py:297
  1706.7 186.0 %collective-permute-start.25 = (bf16[2,640,512]{2,1,0:T(8,128)(2,1)}, bf16[2,640,512]{2,1,0:T(8,128)(2,1)S(1)}, u32[]{:S(2)}, u32[]{:S(2)}) collective-permute-start(bf16[2,640,512]{2,1,0:T(8,128)(2,1)} %get-tuple-element.100), channel_id=1, source_target_pairs={{0,2},{1,3},{2,0},{3,1},{4,6},{5,7},{6,4},{7,5}} | collective-permute-start | bytes 3932168 | tf_op jit(solution)/shard_map/ppermute | solution.py:297
  1708.1 187.0 %collective-permute-start.26 = (bf16[2,640,512]{2,1,0:T(8,128)(2,1)}, bf16[2,640,512]{2,1,0:T(8,128)(2,1)S(1)}, u32[]{:S(2)}, u32[]{:S(2)}) collective-permute-start(bf16[2,640,512]{2,1,0:T(8,128)(2,1)} %get-tuple-element.101), channel_id=1, source_target_pairs={{0,3},{1,2},{2,1},{3,0},{4,7},{5,6},{6,5},{7,4}} | collective-permute-start | bytes 3932168 | tf_op jit(solution)/shard_map/ppermute | solution.py:297
  1708.3 137.1 %collective-permute-start.29 = (bf16[2,640,512]{2,1,0:T(8,128)(2,1)}, bf16[2,640,512]{2,1,0:T(8,128)(2,1)S(1)}, u32[]{:S(2)}, u32[]{:S(2)}) collective-permute-start(bf16[2,640,512]{2,1,0:T(8,128)(2,1)} %get-tuple-element.104), channel_id=1, source_target_pairs={{0,2},{1,3},{2,0},{3,1},{4,6},{5,7},{6,4},{7,5}} | collective-permute-start | bytes 3932168 | tf_op jit(solution)/shard_map/ppermute | solution.py:297
  1760.3 112.2 %collective-permute-start.30 = (bf16[2,640,512]{2,1,0:T(8,128)(2,1)}, bf16[2,640,512]{2,1,0:T(8,128)(2,1)S(1)}, u32[]{:S(2)}, u32[]{:S(2)}) collective-permute-start(bf16[2,640,512]{2,1,0:T(8,128)(2,1)} %get-tuple-element.105), channel_id=1, source_target_pairs={{0,3},{1,2},{2,1},{3,0},{4,7},{5,6},{6,5},{7,4}} | collective-permute-start | bytes 3932168 | tf_op jit(solution)/shard_map/ppermute | solution.py:297
  1765.5 107.0 %copy-start.37 = (bf16[2,640,256]{2,1,0:T(8,128)(2,1)S(1)}, bf16[2,640,256]{2,1,0:T(8,128)(2,1)}, u32[]{:S(2)}) copy-start(bf16[2,640,256]{2,1,0:T(8,128)(2,1)} %get-tuple-element.91) | copy-start | bytes 1966084
  1765.5 108.5 %copy-start.9 = (bf16[2,640,512]{2,1,0:T(8,128)(2,1)S(1)}, bf16[2,640,512]{2,1,0:T(8,128)(2,1)}, u32[]{:S(2)}) copy-start(bf16[2,640,512]{2,1,0:T(8,128)(2,1)} %get-tuple-element.102.refs_0_) | copy-start | bytes 3932164
  1845.4 46.0 %collective-permute-start.14 = (bf16[2,640,256]{2,1,0:T(8,128)(2,1)S(1)}, bf16[2,640,256]{2,1,0:T(8,128)(2,1)S(1)}, u32[]{:S(2)}, u32[]{:S(2)}) collective-permute-start(bf16[2,640,256]{2,1,0:T(8,128)(2,1)S(1)} %copy-done.38), channel_id=1, source_target_pairs={{0,1},{1,0},{2,3},{3,2},{4,5},{5,4},{6,7},{7,6}} | collective-permute-start | bytes 1966088 | tf_op jit(solution)/shard_map/ppermute | solution.py:297
  1872.5 19.4 collective-permute-start.15
  1891.4 66.7 %collective-permute-start.7 = (bf16[1,2816,256]{2,1,0:T(8,128)(2,1)}, bf16[1,2816,256]{2,1,0:T(8,128)(2,1)}, u32[]{:S(2)}, u32[]{:S(2)}) collective-permute-start(bf16[1,2816,256]{2,1,0:T(8,128)(2,1)} %get-tuple-element.166), channel_id=1, source_target_pairs={{0,4},{4,0},{1,5},{5,1},{2,6},{6,2},{3,7},{7,3}} | collective-permute-start | bytes 4325384 | tf_op jit(solution)/shard_map/ppermute | solution.py:301
  1891.9 23.5 %collective-permute-start.16 = (bf16[2,640,256]{2,1,0:T(8,128)(2,1)}, bf16[2,640,256]{2,1,0:T(8,128)(2,1)S(1)}, u32[]{:S(2)}, u32[]{:S(2)}) collective-permute-start(bf16[2,640,256]{2,1,0:T(8,128)(2,1)} %get-tuple-element.92), channel_id=1, source_target_pairs={{0,3},{1,2},{2,1},{3,0},{4,7},{5,6},{6,5},{7,4}} | collective-permute-start | bytes 1966088 | tf_op jit(solution)/shard_map/ppermute | solution.py:297
  1892.0 25.0 %collective-permute-start.18 = (bf16[2,640,256]{2,1,0:T(8,128)(2,1)}, bf16[2,640,256]{2,1,0:T(8,128)(2,1)S(1)}, u32[]{:S(2)}, u32[]{:S(2)}) collective-permute-start(bf16[2,640,256]{2,1,0:T(8,128)(2,1)} %get-tuple-element.95), channel_id=1, source_target_pairs={{0,1},{1,0},{2,3},{3,2},{4,5},{5,4},{6,7},{7,6}} | collective-permute-start | bytes 1966088 | tf_op jit(solution)/shard_map/ppermute | solution.py:297
  1893.7 29.4 %collective-permute-start.19 = (bf16[2,640,256]{2,1,0:T(8,128)(2,1)}, bf16[2,640,256]{2,1,0:T(8,128)(2,1)S(1)}, u32[]{:S(2)}, u32[]{:S(2)}) collective-permute-start(bf16[2,640,256]{2,1,0:T(8,128)(2,1)} %get-tuple-element.96), channel_id=1, source_target_pairs={{0,2},{1,3},{2,0},{3,1},{4,6},{5,7},{6,4},{7,5}} | collective-permute-start | bytes 1966088 | tf_op jit(solution)/shard_map/ppermute | solution.py:297
  1896.2 41.0 %collective-permute-start.20 = (bf16[2,640,256]{2,1,0:T(8,128)(2,1)}, bf16[2,640,256]{2,1,0:T(8,128)(2,1)S(1)}, u32[]{:S(2)}, u32[]{:S(2)}) collective-permute-start(bf16[2,640,256]{2,1,0:T(8,128)(2,1)} %get-tuple-element.97), channel_id=1, source_target_pairs={{0,3},{1,2},{2,1},{3,0},{4,7},{5,6},{6,5},{7,4}} | collective-permute-start | bytes 1966088 | tf_op jit(solution)/shard_map/ppermute | solution.py:297
  1915.4 55.7 %collective-permute-start.40 = (bf16[1,2816,256]{2,1,0:T(8,128)(2,1)}, bf16[1,2816,256]{2,1,0:T(8,128)(2,1)S(1)}, u32[]{:S(2)}, u32[]{:S(2)}) collective-permute-start(bf16[1,2816,256]{2,1,0:T(8,128)(2,1)} %get-tuple-element.161), channel_id=1, source_target_pairs={{0,4},{4,0},{1,5},{5,1},{2,6},{6,2},{3,7},{7,3}} | collective-permute-start | bytes 4325384 | tf_op jit(solution)/shard_map/ppermute | solution.py:301
  1916.9 108.2 %collective-permute-start.51 = (bf16[1,2816,256]{2,1,0:T(8,128)(2,1)}, bf16[1,2816,256]{2,1,0:T(8,128)(2,1)S(1)}, u32[]{:S(2)}, u32[]{:S(2)}) collective-permute-start(bf16[1,2816,256]{2,1,0:T(8,128)(2,1)} %get-tuple-element.160), channel_id=1, source_target_pairs={{0,4},{4,0},{1,5},{5,1},{2,6},{6,2},{3,7},{7,3}} | collective-permute-start | bytes 4325384 | tf_op jit(solution)/shard_map/ppermute | solution.py:301
  1923.1 48.8 %collective-permute-start.44 = (bf16[2,640,256]{2,1,0:T(8,128)(2,1)}, bf16[2,640,256]{2,1,0:T(8,128)(2,1)S(1)}, u32[]{:S(2)}, u32[]{:S(2)}) collective-permute-start(bf16[2,640,256]{2,1,0:T(8,128)(2,1)} %get-tuple-element.124), channel_id=1, source_target_pairs={{0,1},{1,0},{2,3},{3,2},{4,5},{5,4},{6,7},{7,6}} | collective-permute-start | bytes 1966088 | tf_op jit(solution)/shard_map/ppermute | solution.py:297
  1937.2 35.5 %collective-permute-start.45 = (bf16[2,640,256]{2,1,0:T(8,128)(2,1)}, bf16[2,640,256]{2,1,0:T(8,128)(2,1)}, u32[]{:S(2)}, u32[]{:S(2)}) collective-permute-start(bf16[2,640,256]{2,1,0:T(8,128)(2,1)} %get-tuple-element.125), channel_id=1, source_target_pairs={{0,2},{1,3},{2,0},{3,1},{4,6},{5,7},{6,4},{7,5}} | collective-permute-start | bytes 1966088 | tf_op jit(solution)/shard_map/ppermute | solution.py:297
  1958.1 27.6 %collective-permute-start.46 = (bf16[2,640,256]{2,1,0:T(8,128)(2,1)}, bf16[2,640,256]{2,1,0:T(8,128)(2,1)}, u32[]{:S(2)}, u32[]{:S(2)}) collective-permute-start(bf16[2,640,256]{2,1,0:T(8,128)(2,1)} %get-tuple-element.126), channel_id=1, source_target_pairs={{0,3},{1,2},{2,1},{3,0},{4,7},{5,6},{6,5},{7,4}} | collective-permute-start | bytes 1966088 | tf_op jit(solution)/shard_map/ppermute | solution.py:297
  1971.1 16.1 collective-permute-start.47
  1971.9 17.9 collective-permute-start.48
  1972.7 30.6 %collective-permute-start.49 = (bf16[2,640,256]{2,1,0:T(8,128)(2,1)}, bf16[2,640,256]{2,1,0:T(8,128)(2,1)}, u32[]{:S(2)}, u32[]{:S(2)}) collective-permute-start(bf16[2,640,256]{2,1,0:T(8,128)(2,1)} %get-tuple-element.130), channel_id=1, source_target_pairs={{0,3},{1,2},{2,1},{3,0},{4,7},{5,6},{6,5},{7,4}} | collective-permute-start | bytes 1966088 | tf_op jit(solution)/shard_map/ppermute | solution.py:297
  1985.7 38.9 %collective-permute-start.50 = (bf16[1,2816,128]{2,1,0:T(8,128)(2,1)}, bf16[1,2816,128]{2,1,0:T(8,128)(2,1)S(1)}, u32[]{:S(2)}, u32[]{:S(2)}) collective-permute-start(bf16[1,2816,128]{2,1,0:T(8,128)(2,1)} %get-tuple-element.167), channel_id=1, source_target_pairs={{0,4},{4,0},{1,5},{5,1},{2,6},{6,2},{3,7},{7,3}} | collective-permute-start | bytes 2162696 | tf_op jit(solution)/shard_map/ppermute | solution.py:301
  1987.2 38.6 %collective-permute-start.37 = (bf16[2,640,256]{2,1,0:T(8,128)(2,1)}, bf16[2,640,256]{2,1,0:T(8,128)(2,1)S(1)}, u32[]{:S(2)}, u32[]{:S(2)}) collective-permute-start(bf16[2,640,256]{2,1,0:T(8,128)(2,1)} %get-tuple-element.115), channel_id=1, source_target_pairs={{0,1},{1,0},{2,3},{3,2},{4,5},{5,4},{6,7},{7,6}} | collective-permute-start | bytes 1966088 | tf_op jit(solution)/shard_map/ppermute | solution.py:297
  1989.8 62.6 %collective-permute-start.38 = (bf16[2,640,256]{2,1,0:T(8,128)(2,1)}, bf16[2,640,256]{2,1,0:T(8,128)(2,1)S(1)}, u32[]{:S(2)}, u32[]{:S(2)}) collective-permute-start(bf16[2,640,256]{2,1,0:T(8,128)(2,1)} %get-tuple-element.116), channel_id=1, source_target_pairs={{0,2},{1,3},{2,0},{3,1},{4,6},{5,7},{6,4},{7,5}} | collective-permute-start | bytes 1966088 | tf_op jit(solution)/shard_map/ppermute | solution.py:297
  2003.3 50.6 %collective-permute-start.39 = (bf16[2,640,256]{2,1,0:T(8,128)(2,1)}, bf16[2,640,256]{2,1,0:T(8,128)(2,1)}, u32[]{:S(2)}, u32[]{:S(2)}) collective-permute-start(bf16[2,640,256]{2,1,0:T(8,128)(2,1)} %get-tuple-element.117), channel_id=1, source_target_pairs={{0,3},{1,2},{2,1},{3,0},{4,7},{5,6},{6,5},{7,4}} | collective-permute-start | bytes 1966088 | tf_op jit(solution)/shard_map/ppermute | solution.py:297
  2024.6 29.7 %collective-permute-start.41 = (bf16[2,640,256]{2,1,0:T(8,128)(2,1)}, bf16[2,640,256]{2,1,0:T(8,128)(2,1)}, u32[]{:S(2)}, u32[]{:S(2)}) collective-permute-start(bf16[2,640,256]{2,1,0:T(8,128)(2,1)} %get-tuple-element.120), channel_id=1, source_target_pairs={{0,1},{1,0},{2,3},{3,2},{4,5},{5,4},{6,7},{7,6}} | collective-permute-start | bytes 1966088 | tf_op jit(solution)/shard_map/ppermute | solution.py:297
  2025.2 29.2 %collective-permute-start.42 = (bf16[2,640,256]{2,1,0:T(8,128)(2,1)}, bf16[2,640,256]{2,1,0:T(8,128)(2,1)}, u32[]{:S(2)}, u32[]{:S(2)}) collective-permute-start(bf16[2,640,256]{2,1,0:T(8,128)(2,1)} %get-tuple-element.121), channel_id=1, source_target_pairs={{0,2},{1,3},{2,0},{3,1},{4,6},{5,7},{6,4},{7,5}} | collective-permute-start | bytes 1966088 | tf_op jit(solution)/shard_map/ppermute | solution.py:297
  2025.8 33.7 %collective-permute-start.43 = (bf16[2,640,256]{2,1,0:T(8,128)(2,1)}, bf16[2,640,256]{2,1,0:T(8,128)(2,1)}, u32[]{:S(2)}, u32[]{:S(2)}) collective-permute-start(bf16[2,640,256]{2,1,0:T(8,128)(2,1)} %get-tuple-element.122), channel_id=1, source_target_pairs={{0,3},{1,2},{2,1},{3,0},{4,7},{5,6},{6,5},{7,4}} | collective-permute-start | bytes 1966088 | tf_op jit(solution)/shard_map/ppermute | solution.py:297
  2052.4 28.2 %collective-permute-start.6 = (bf16[1,2816,128]{2,1,0:T(8,128)(2,1)S(1)}, bf16[1,2816,128]{2,1,0:T(8,128)(2,1)S(1)}, u32[]{:S(2)}, u32[]{:S(2)}) collective-permute-start(bf16[1,2816,128]{2,1,0:T(8,128)(2,1)S(1)} %copy-done.25), channel_id=1, source_target_pairs={{0,4},{4,0},{1,5},{5,1},{2,6},{6,2},{3,7},{7,3}} | collective-permute-start | bytes 2162696 | tf_op jit(solution)/shard_map/ppermute | solution.py:301
  2053.9 41.2 %collective-permute-start.55 = (bf16[2,640,128]{2,1,0:T(8,128)(2,1)}, bf16[2,640,128]{2,1,0:T(8,128)(2,1)}, u32[]{:S(2)}, u32[]{:S(2)}) collective-permute-start(bf16[2,640,128]{2,1,0:T(8,128)(2,1)} %get-tuple-element.147), channel_id=1, source_target_pairs={{0,1},{1,0},{2,3},{3,2},{4,5},{5,4},{6,7},{7,6}} | collective-permute-start | bytes 983048 | tf_op jit(solution)/shard_map/ppermute | solution.py:297
  2054.3 41.5 %collective-permute-start.58 = (bf16[2,640,256]{2,1,0:T(8,128)(2,1)}, bf16[2,640,256]{2,1,0:T(8,128)(2,1)S(1)}, u32[]{:S(2)}, u32[]{:S(2)}) collective-permute-start(bf16[2,640,256]{2,1,0:T(8,128)(2,1)} %get-tuple-element.151), channel_id=1, source_target_pairs={{0,1},{1,0},{2,3},{3,2},{4,5},{5,4},{6,7},{7,6}} | collective-permute-start | bytes 1966088 | tf_op jit(solution)/shard_map/ppermute | solution.py:297
  2054.4 41.7 %collective-permute-start.59 = (bf16[2,640,256]{2,1,0:T(8,128)(2,1)}, bf16[2,640,256]{2,1,0:T(8,128)(2,1)}, u32[]{:S(2)}, u32[]{:S(2)}) collective-permute-start(bf16[2,640,256]{2,1,0:T(8,128)(2,1)} %get-tuple-element.152), channel_id=1, source_target_pairs={{0,2},{1,3},{2,0},{3,1},{4,6},{5,7},{6,4},{7,5}} | collective-permute-start | bytes 1966088 | tf_op jit(solution)/shard_map/ppermute | solution.py:297
  2059.5 37.8 %collective-permute-start.60 = (bf16[2,640,256]{2,1,0:T(8,128)(2,1)}, bf16[2,640,256]{2,1,0:T(8,128)(2,1)}, u32[]{:S(2)}, u32[]{:S(2)}) collective-permute-start(bf16[2,640,256]{2,1,0:T(8,128)(2,1)} %get-tuple-element.153), channel_id=1, source_target_pairs={{0,3},{1,2},{2,1},{3,0},{4,7},{5,6},{6,5},{7,4}} | collective-permute-start | bytes 1966088 | tf_op jit(solution)/shard_map/ppermute | solution.py:297
  2080.5 30.3 %collective-permute-start.56 = (bf16[2,640,128]{2,1,0:T(8,128)(2,1)}, bf16[2,640,128]{2,1,0:T(8,128)(2,1)}, u32[]{:S(2)}, u32[]{:S(2)}) collective-permute-start(bf16[2,640,128]{2,1,0:T(8,128)(2,1)} %get-tuple-element.148), channel_id=1, source_target_pairs={{0,2},{1,3},{2,0},{3,1},{4,6},{5,7},{6,4},{7,5}} | collective-permute-start | bytes 983048 | tf_op jit(solution)/shard_map/ppermute | solution.py:297
  2095.1 15.7 collective-permute-start.57
  2095.9 25.2 %collective-permute-start.52 = (bf16[2,640,128]{2,1,0:T(8,128)(2,1)}, bf16[2,640,128]{2,1,0:T(8,128)(2,1)S(1)}, u32[]{:S(2)}, u32[]{:S(2)}) collective-permute-start(bf16[2,640,128]{2,1,0:T(8,128)(2,1)} %get-tuple-element.143), channel_id=1, source_target_pairs={{0,1},{1,0},{2,3},{3,2},{4,5},{5,4},{6,7},{7,6}} | collective-permute-start | bytes 983048 | tf_op jit(solution)/shard_map/ppermute | solution.py:297
  2096.1 25.0 %collective-permute-start.53 = (bf16[2,640,128]{2,1,0:T(8,128)(2,1)}, bf16[2,640,128]{2,1,0:T(8,128)(2,1)S(1)}, u32[]{:S(2)}, u32[]{:S(2)}) collective-permute-start(bf16[2,640,128]{2,1,0:T(8,128)(2,1)} %get-tuple-element.144), channel_id=1, source_target_pairs={{0,2},{1,3},{2,0},{3,1},{4,6},{5,7},{6,4},{7,5}} | collective-permute-start | bytes 983048 | tf_op jit(solution)/shard_map/ppermute | solution.py:297
  2097.2 23.9 %collective-permute-start.54 = (bf16[2,640,128]{2,1,0:T(8,128)(2,1)}, bf16[2,640,128]{2,1,0:T(8,128)(2,1)S(1)}, u32[]{:S(2)}, u32[]{:S(2)}) collective-permute-start(bf16[2,640,128]{2,1,0:T(8,128)(2,1)} %get-tuple-element.145), channel_id=1, source_target_pairs={{0,3},{1,2},{2,1},{3,0},{4,7},{5,6},{6,5},{7,4}} | collective-permute-start | bytes 983048 | tf_op jit(solution)/shard_map/ppermute | solution.py:297
  (49 other events, 815.5 us)

commit v5 on v4

--- a/solution.py
+++ b/solution.py
@@ -14,6 +14,7 @@
 MASKS = 4
 TN = 256
 TB = 512
+WIN = 256
 
 
 def mm(a, b):
@@ -173,104 +174,133 @@
 
 
 def final_kept_kernel(masks, p, wd, h, *refs):
-    i, n = pl.program_id(0), len(masks)
-    y = (p[0, 0, 0] + mm(h[i // n, masks[0] + i % n], wd[...])).astype(BF16)
-    for j, out in enumerate(refs[:n]):
-
-        @pl.when(i % n == j)
+    i = pl.program_id(0)
+    per_batch = len(masks) // 2
+    m = masks[0] + 2 * (i % per_batch)
+    _, _, cap, width = h.shape
+    rows = h[i // per_batch, pl.ds(m, 2)].reshape(2 * cap, width)
+    y = (p[0, 0].reshape(2 * cap, -1) + mm(rows, wd[...])).astype(BF16)
+    for q in range(per_batch):
+
+        @pl.when(i % per_batch == q)
         def _():
-            out[0] = y
+            refs[2 * q][0] = y[:cap]
+            refs[2 * q + 1][0] = y[cap:]
 
 
 def final_kept(h, p, k, wd, lo, masks):
     _, _, cap, width = h.shape
     cols = wd.shape[1]
     at, n, m0 = lo // cols, len(masks), masks[0]
+    steps = n // 2
     rows = 2 * n * cap
     args = [p, wd]
     in_specs = [
-        pl.BlockSpec((1, 1, 1, cap, cols), lambda i: (k, i // n, m0 + i % n, 0, at)),
+        pl.BlockSpec((1, 1, 2, cap, cols), lambda i: (k, i // steps, m0 // 2 + i % steps, 0, at)),
         pl.BlockSpec((width, cols), lambda i: (0, 0)),
     ]
     kw = kept(h, args, in_specs, n)
     return call(
         functools.partial(final_kept_kernel, masks), 2 * rows * width * cols, 6 * rows * cols, 33,
-        grid=(2 * n,), in_specs=in_specs,
-        out_specs=[pl.BlockSpec((1, cap, cols), functools.partial(lambda m, i: (jnp.where(i >= n + m, 1, 0), 0, 0), m)) for m in range(n)]
+        grid=(n,), in_specs=in_specs,
+        out_specs=[pl.BlockSpec((1, cap, cols), functools.partial(lambda q, i: (jnp.where(i >= steps + q, 1, 0), 0, 0), m // 2)) for m in range(n)]
         + [pl.BlockSpec(memory_space=pltpu.VMEM)],
         out_shape=[jax.ShapeDtypeStruct((2, cap, cols), BF16)] * n + [pltpu.VMEM(h.shape, BF16)], **kw,
     )(*args)
 
 
-def picked(k, groups, pos, gate):
-    slots = lax.broadcasted_iota(jnp.int32, (TB, groups[0][0].shape[1]), 1)
+def picked(k, groups, pos, gate, lo):
+    slots = lax.broadcasted_iota(jnp.int32, (TB, WIN), 1)
     totals = [None] * len(groups)
     for m in range(MASKS):
         e = 2 * m + k
-        onehot = (slots == pos[0, :, e:e + 1]).astype(BF16)
+        at = pl.multiple_of(lo[m], 16)
+        onehot = (slots == pos[0, :, e:e + 1] - at).astype(BF16)
         for j, ys in enumerate(groups):
-            term = gate[0, :, e:e + 1] * mm(onehot, ys[m][0])
+            term = gate[0, :, e:e + 1] * mm(onehot, ys[m][0, pl.ds(at, WIN)])
             totals[j] = term if totals[j] is None else totals[j] + term
     return totals
 
 
-def combine_kernel(k, n, held, *refs):
-    if held:
-        refs = refs[:-1]
+def combine_kernel(k, n, held, first, last, *refs):
+    total = refs[-1]
+    refs = refs[:-2] if held else refs[:-1]
     groups = [refs[MASKS * j:MASKS * (j + 1)] for j in range(n)]
-    totals = picked(k, groups, *refs[MASKS * n:MASKS * n + 2])
-    cols = groups[0][0].shape[2]
+    pos, gate = refs[MASKS * n:MASKS * n + 2]
+    cap, cols = groups[0][0].shape[1:]
     i, blocks = pl.program_id(0), pl.num_programs(0) // 2
-    for j, total in enumerate(totals):
-        at = slice(j * cols, (j + 1) * cols)
-        if k == 0:
-            refs[-1][:, at] = total
-            continue
-        total = (refs[MASKS * n + 2][:, at] + total).astype(BF16)
-        for b, out in enumerate(refs[-2:]):
-
-            @pl.when(i // blocks == b)
-            def _():
-                out[:, at] = total
-
-
-def combine(groups, pos, gate, k, lo, model, acc=None, into=None, held=None):
+    begin = [(jnp.minimum(first[i * MASKS + m], cap - WIN) // 16) * 16 for m in range(MASKS)]
+    for j, part in enumerate(picked(k, groups, pos, gate, begin)):
+        total[:, j * cols:(j + 1) * cols] = part
+    slots = lax.broadcasted_iota(jnp.int32, (TB, WIN), 1)
+    for m in range(MASKS):
+        e = 2 * m + k
+        end = last[i * MASKS + m]
+
+        @pl.when(end > begin[m] + WIN)
+        def _():
+            def more(step, carry):
+                lo = begin[m] + WIN + step * WIN
+                at = pl.multiple_of(jnp.minimum(lo, cap - WIN), 16)
+                mine = pos[0, :, e:e + 1]
+                onehot = (slots == jnp.where(mine >= lo, mine - at, -1)).astype(BF16)
+                for j, ys in enumerate(groups):
+                    total[:, j * cols:(j + 1) * cols] += gate[0, :, e:e + 1] * mm(onehot, ys[m][0, pl.ds(at, WIN)])
+                return carry
+
+            lax.fori_loop(0, (end - begin[m] - 1) // WIN, more, 0)
+
+    if k == 0:
+        refs[-1][...] = total[...]
+        return
+    result = (refs[MASKS * n + 2][...] + total[...]).astype(BF16)
+    for b, out in enumerate(refs[-2:]):
+
+        @pl.when(i // blocks == b)
+        def _():
+            out[...] = result
+
+
+def combine(groups, table, k, lo, model, acc=None, into=None, held=None):
+    pos, gate, first, last = table
     _, cap, cols = groups[0][0].shape
     n, wide = len(groups), cols * len(groups)
     toks = pos.shape[1]
     blocks = toks // TB
     at = lo // wide
-    args = [y for ys in groups for y in ys] + [pos, gate]
-    in_specs = [pl.BlockSpec((1, cap, cols), lambda i: (i // blocks, 0, 0))] * (MASKS * n)
-    in_specs += [pl.BlockSpec((1, TB, pos.shape[2]), lambda i: (i // blocks, i % blocks, 0))] * 2
-    flops, nbytes = 2 * 2 * toks * MASKS * cap * wide, 2 * toks * wide * 6
-    kernel = functools.partial(combine_kernel, k, n, held is not None)
+    args = [first[k], last[k]] + [y for ys in groups for y in ys] + [pos, gate]
+    in_specs = [pl.BlockSpec((1, cap, cols), lambda i, *_: (i // blocks, 0, 0))] * (MASKS * n)
+    in_specs += [pl.BlockSpec((1, TB, pos.shape[2]), lambda i, *_: (i // blocks, i % blocks, 0))] * 2
+    aliases = {}
     if k == 0:
-        kw = filled_further(into, args, in_specs)
-        return call(
-            kernel, flops, nbytes, 20,
-            grid=(2 * blocks,), in_specs=in_specs,
-            out_specs=pl.BlockSpec((TB, wide), lambda i: (i, at)),
-            out_shape=jax.ShapeDtypeStruct((2 * toks, model), F32), **kw,
-        )(*args)
-    args.append(acc)
-    in_specs.append(pl.BlockSpec((TB, wide), lambda i: (i, at)))
-    aliases = {}
-    if into is not None:
-        aliases = {len(args): 0, len(args) + 1: 1}
-        args += into
-        in_specs += [pl.BlockSpec(memory_space=pl.ANY)] * 2
-    if held is not None:
-        aliases |= kept(held, args, in_specs, 2)["input_output_aliases"]
-    return call(
-        kernel, flops, nbytes, 33,
-        grid=(2 * blocks,), in_specs=in_specs,
-        out_specs=[
-            pl.BlockSpec((TB, wide), lambda i: (jnp.minimum(i, blocks - 1), at)),
-            pl.BlockSpec((TB, wide), lambda i: (jnp.maximum(i - blocks, 0), at)),
-        ] + [pl.BlockSpec(memory_space=pltpu.VMEM)] * (held is not None),
-        out_shape=[jax.ShapeDtypeStruct((toks, model), BF16)] * 2 + ([] if held is None else [pltpu.VMEM(held.shape, BF16)]),
-        input_output_aliases=aliases,
+        if into is not None:
+            aliases |= filled_further(into, args, in_specs)["input_output_aliases"]
+        out_specs = pl.BlockSpec((TB, wide), lambda i, *_: (i, at))
+        out_shape = jax.ShapeDtypeStruct((2 * toks, model), F32)
+    else:
+        args.append(acc)
+        in_specs.append(pl.BlockSpec((TB, wide), lambda i, *_: (i, at)))
+        if into is not None:
+            aliases = {len(args): 0, len(args) + 1: 1}
+            args += into
+            in_specs += [pl.BlockSpec(memory_space=pl.ANY)] * 2
+        out_specs = [
+            pl.BlockSpec((TB, wide), lambda i, *_: (jnp.minimum(i, blocks - 1), at)),
+            pl.BlockSpec((TB, wide), lambda i, *_: (jnp.maximum(i - blocks, 0), at)),
+        ]
+        out_shape = [jax.ShapeDtypeStruct((toks, model), BF16)] * 2
+        if held is not None:
+            aliases |= kept(held, args, in_specs, 2)["input_output_aliases"]
+            out_specs.append(pl.BlockSpec(memory_space=pltpu.VMEM))
+            out_shape.append(pltpu.VMEM(held.shape, BF16))
+    return call(
+        functools.partial(combine_kernel, k, n, held is not None),
+        2 * 2 * toks * MASKS * WIN * wide, 2 * toks * wide * 6, 33 if k else 20,
+        grid_spec=pltpu.PrefetchScalarGridSpec(
+            num_scalar_prefetch=2, grid=(2 * blocks,), in_specs=in_specs, out_specs=out_specs,
+            scratch_shapes=[pltpu.VMEM((TB, wide), F32)],
+        ),
+        out_shape=out_shape, input_output_aliases=aliases,
     )(*args)
 
 
@@ -287,11 +317,12 @@
     row_spec = P(("dp", "ep", "tp"), None)
     gate_spec = P("ep", None, "tp")
     down_spec = P("ep", "tp", None)
-    up1_cuts = cuts([512, 1024, 1024, 256])
+    up1_cuts = cuts([256, 1280, 768, 512])
     down_cuts = [cuts([1024, 512, 512]), cuts([256] * 7 + [128, 128])]
     late = [(1, n) for n in range(9)]
-    halves = [(1, 7), (1, 8)]
-    after = {(1, 3): [[(1, 0), (1, 1)]], (1, 5): [[(1, 2), (1, 3)]], (1, 7): [[(1, 4), (1, 5)]], (1, 8): [[(1, 6)], [(1, 7)], [(1, 8)]]}
+    halves = [(1, n) for n in range(5, 9)]
+    after = {(1, 2): [[(1, 0), (1, 1)]], (1, 4): [[(1, 2)]], (1, 5): [[(1, 3)]], (1, 6): [[(1, 4), (1, 5)]]}
+    after[1, 8] = [[(1, 6)], [(1, 7)], [(1, 8)]]
 
     def ep_swap(value, mask):
         return lax.ppermute(value, "ep", [(i, i ^ mask) for i in range(ep_size)])
@@ -312,7 +343,11 @@
         pos = jnp.cumsum(count, axis=2) - count
         pos = jnp.where(has & (pos < cap), pos, -1)
         gate = jnp.sum(jnp.where(hit, gates[:, None], 0.0), axis=3)
-        return pos, gate, cap
+        used = jnp.sum(count.reshape(2, n_exp, toks // TB, TB), axis=3)
+        upto = jnp.cumsum(used, axis=2)
+        first, last = jnp.minimum(upto - used, cap), jnp.minimum(upto, cap)
+        order = lambda a: a.reshape(2, ep_size, 2, toks // TB).transpose(2, 0, 3, 1).reshape(2, -1)
+        return pos, gate, cap, order(first), order(last)
 
     def group_body(tokens_a, ids_a, gates_a, tokens_b, ids_b, gates_b, w_gate, w_up, w_down):
         me = lax.axis_index("ep")
@@ -331,8 +366,8 @@
             lo, hi = down_cuts[k][n]
             down[k][n] = tp_swap(w_down, k, lo, hi)
 
-        pos, gate, cap = routing(jnp.stack([ids_a, ids_b]), jnp.stack([gates_a, gates_b]), me)
-        pos_t, gate_t = pos.transpose(0, 2, 1), gate.transpose(0, 2, 1)
+        pos, gate, cap, first, last = routing(jnp.stack([ids_a, ids_b]), jnp.stack([gates_a, gates_b]), me)
+        table = pos.transpose(0, 2, 1), gate.transpose(0, 2, 1), first, last
 
         xs = []
         for b, tokens in enumerate((tokens_a, tokens_b)):
@@ -373,12 +408,12 @@
 
         for item in (0, 0), (0, 1), (0, 2):
             finish(*item)
-            acc = combine([back[item]], pos_t, gate_t, 0, down_cuts[0][item[1]][0], model, None, acc)
+            acc = combine([back[item]], table, 0, down_cuts[0][item[1]][0], model, None, acc)
         for i, item in enumerate(late):
             finish(*item)
             for group in after.get(item, []):
                 outs = combine(
-                    [back[it] for it in group], pos_t, gate_t, 1, down_cuts[1][group[0][1]][0], model, acc, outs,
+                    [back[it] for it in group], table, 1, down_cuts[1][group[0][1]][0], model, acc, outs,
                     h_r[1] if i < len(late) - 1 else None,
                 )
                 if i < len(late) - 1:

time: 2140 us -> 2060 us (0.963)
  waiting for transfers between devices: 775 us -> 682 us
  local copies, waits for them, and re-layouts: 107 us -> 152 us
  Pallas kernels: 1190 us -> 1150 us
    ppermute x42, waiting for transfers between devices: 355 us -> 296 us  [ep_swap(): return lax.ppermute(value, 'ep', [(i, i ^ mask) for i in range(ep_size)])]
    unnamed x104 -> x112, local copies, waits for them, and re-layouts: 43.1 us -> 82.3 us
    pallas_call x9 -> x10, Pallas kernels: 158 us -> 124 us  [combine(): call(functools.partial(combine_kernel, k, n, held is not None), 2 * 2 * t...]
    ppermute x19, waiting for transfers between devices: 419 us -> 386 us  [tp_swap(): return lax.ppermute(piece, 'tp', TP_SWAP)[0]]
    pallas_call x11 -> x13, Pallas kernels: 114 us -> 109 us  [final_kept(): call(functools.partial(final_kept_kernel, masks), 2 * rows * width * cols...]
    slice x9 -> x10, local copies, waits for them, and re-layouts: 53.2 us -> 55.2 us  [tp_swap(): lax.slice(w, (k, 0, lo), (k + 1, w.shape[1], w.shape[2] if hi is None els...]
  transfers between devices with their start and end apart: 61 -> 61, of which waited for: 14 -> 11; matrix products, arithmetic and copies ran while one was open for 3% -> 3% of each run, Pallas kernels for 54% -> 54%
where the time goes in v5:
time: 2060 us; the launch traced here: 2050 us
  Pallas kernels  1150 us (56%)
  waiting for transfers between devices  682 us (33%)
  local copies, waits for them, and re-layouts  152 us (7%)
  starting transfers between devices  54.4 us (3%)
    ppermute x19, waiting for transfers between devices, tp_swap(): return lax.ppermute(piece, 'tp', TP_SWAP)[0]  386 us
    ppermute x42, waiting for transfers between devices, ep_swap(): return lax.ppermute(value, 'ep', [(i, i ^ mask) for i in range(ep_size)])  296 us
    pallas_call x2, Pallas kernels, hidden_local(): call(functools.partial(hidden_kernel, None, 0), 4 * rows * model * width,...  260 us
    pallas_call x8, Pallas kernels, hidden(): call(functools.partial(hidden_kernel, b, off), *cost, 33, grid=(steps,),...  161 us
    pallas_call x2, Pallas kernels, part(): call(part_kernel, 2 * rows * width * model, 2 * (rows * width + 2 * width...  146 us
    pallas_call x2, Pallas kernels, hidden(): call(functools.partial(hidden_kernel, None, 0), *cost, grid=(steps,), in_...  135 us
    pallas_call x4, Pallas kernels, dispatch(): call(dispatch_kernel, 2 * n * 2 * cap * toks * model, toks * model * 2 +...  125 us
    pallas_call x10, Pallas kernels, combine(): call(functools.partial(combine_kernel, k, n, held is not None), 2 * 2 * t...  124 us
  transfers between devices with their start and end apart: 61, of which 11 were waited for; matrix products, arithmetic and copies ran while one was open for 3% of the time, Pallas kernels for 54%

profile of v5, /device:TPU:0, one launch (start us, length us, event | category | flops | bytes accessed | tf_op | source)
XLA Modules:
  0.0 2049.5 jit_solution(16276851048055783354)
XLA Ops:
  15.1 31.1 %shard_map.104 = (bf16[2,640,2048]{2,1,0:T(8,128)(2,1)}, bf16[2,640,2048]{2,1,0:T(8,128)(2,1)}) custom-call(s32[4,1,2048]{2,1,0:T(1,128)} %copy.95.pos_ref, bf16[2048,2048]{1,0:T(8,128)(2,1)} %tok_ref.5), custom_call_target="tpu_custom_call" | custom-call | flops 21474836480 | bytes 18874368 | tf_op jit(solution)/shard_map/pallas_call | solution.py:62
  49.3 31.0 %shard_map.105 = (bf16[2,640,2048]{2,1,0:T(8,128)(2,1)}, bf16[2,640,2048]{2,1,0:T(8,128)(2,1)}) custom-call(s32[4,1,2048]{2,1,0:T(1,128)} %copy.96.pos_ref, bf16[2048,2048]{1,0:T(8,128)(2,1)} %tok_ref.5), custom_call_target="tpu_custom_call" | custom-call | flops 21474836480 | bytes 18874368 | tf_op jit(solution)/shard_map/pallas_call | solution.py:62
  83.8 31.3 %shard_map.107 = (bf16[2,640,2048]{2,1,0:T(8,128)(2,1)}, bf16[2,640,2048]{2,1,0:T(8,128)(2,1)}) custom-call(s32[4,1,2048]{2,1,0:T(1,128)} %copy.97.pos_ref, bf16[2048,2048]{1,0:T(8,128)(2,1)} %tok_ref.7), custom_call_target="tpu_custom_call" | custom-call | flops 21474836480 | bytes 18874368 | tf_op jit(solution)/shard_map/pallas_call | solution.py:62
  116.2 31.0 %shard_map.108 = (bf16[2,640,2048]{2,1,0:T(8,128)(2,1)}, bf16[2,640,2048]{2,1,0:T(8,128)(2,1)}) custom-call(s32[4,1,2048]{2,1,0:T(1,128)} %copy.98.pos_ref, bf16[2048,2048]{1,0:T(8,128)(2,1)} %tok_ref.7), custom_call_target="tpu_custom_call" | custom-call | flops 21474836480 | bytes 18874368 | tf_op jit(solution)/shard_map/pallas_call | solution.py:62
  163.6 9.9 slice.151
  187.5 6.2 fusion.3
  193.6 8.2 fusion.2
  204.1 8.1 fusion.4
  213.8 95.2 %collective-permute-done.2.refs_3_ = bf16[2,640,2048]{2,1,0:T(8,128)(2,1)} collective-permute-done((bf16[2,640,2048]{2,1,0:T(8,128)(2,1)}, bf16[2,640,2048]{2,1,0:T(8,128)(2,1)}, u32[]{:S(2)}, u32[]{:S(2)}) %collective-permute-start.2) | collective-permute-done | bytes 5242912 | tf_op jit(solution)/shard_map/ppermute | solution.py:328
  310.5 130.1 %shard_map.106.h = bf16[2,4,640,2816]{3,2,1,0:T(8,128)(2,1)} custom-call(bf16[2,640,2048]{2,1,0:T(8,128)(2,1)} %get-tuple-element.86.refs_0_, bf16[2,640,2048]{2,1,0:T(8,128)(2,1)} %collective-permute-done.refs_1_, bf16[2,640,2048]{2,1,0:T(8,128)(2,1)} %collective-permute-done.1.refs_2_, bf16[2,640,2048]{2,1,0:T(8,128)(2,1)} %collective-permute-done.2.refs_3_, ...), custom_call_target="tpu_custom_call" | custom-call | flops 118111600640 | bytes 95944704 | tf_op jit(solution)/shard_map/pallas_call | solution.py:89
  442.6 91.1 %collective-permute-done.5.refs_3_ = bf16[2,640,2048]{2,1,0:T(8,128)(2,1)} collective-permute-done((bf16[2,640,2048]{2,1,0:T(8,128)(2,1)}, bf16[2,640,2048]{2,1,0:T(8,128)(2,1)}, u32[]{:S(2)}, u32[]{:S(2)}) %collective-permute-start.5) | collective-permute-done | bytes 5242912 | tf_op jit(solution)/shard_map/ppermute | solution.py:328
  535.2 129.6 %shard_map.109.h = bf16[2,4,640,2816]{3,2,1,0:T(8,128)(2,1)} custom-call(bf16[2,640,2048]{2,1,0:T(8,128)(2,1)} %get-tuple-element.90.refs_0_, bf16[2,640,2048]{2,1,0:T(8,128)(2,1)} %collective-permute-done.3.refs_1_, bf16[2,640,2048]{2,1,0:T(8,128)(2,1)} %collective-permute-done.4.refs_2_, bf16[2,640,2048]{2,1,0:T(8,128)(2,1)} %collective-permute-done.5.refs_3_, ...), custom_call_target="tpu_custom_call" | custom-call | flops 118111600640 | bytes 95944704 | tf_op jit(solution)/shard_map/pallas_call | solution.py:89
  664.7 72.8 %shard_map.110.refs_0_ = f32[2,2,4,640,2048]{4,3,2,1,0:T(8,128)} custom-call(bf16[2,4,640,2816]{3,2,1,0:T(8,128)(2,1)} %shard_map.109.h, bf16[2,2816,2048]{2,1,0:T(8,128)(2,1)} %wd.3), custom_call_target="tpu_custom_call" | custom-call | flops 59055800320 | bytes 93847552 | tf_op jit(solution)/shard_map/pallas_call | solution.py:139
  737.6 73.0 %shard_map.111.p = f32[2,2,4,640,2048]{4,3,2,1,0:T(8,128)} custom-call(bf16[2,4,640,2816]{3,2,1,0:T(8,128)(2,1)} %shard_map.106.h, bf16[2,2816,2048]{2,1,0:T(8,128)(2,1)} %wd.3, f32[2,2,4,640,2048]{4,3,2,1,0:T(8,128)} %shard_map.110.refs_0_), custom_call_target="tpu_custom_call", output_to_operand_aliasing={{}: (2, {})} | custom-call | flops 59055800320 | bytes 93847552 | tf_op jit(solution)/shard_map/pallas_call | solution.py:139
  812.6 10.2 shard_map.112.refs_6_
  822.8 10.2 shard_map.113.refs_6_
  833.0 9.5 copy-done
  843.0 233.9 %collective-permute-done.24 = bf16[1,2048,2816]{2,1,0:T(8,128)(2,1)} collective-permute-done((bf16[1,2048,2816]{2,1,0:T(8,128)(2,1)}, bf16[1,2048,2816]{2,1,0:T(8,128)(2,1)}, u32[]{:S(2)}, u32[]{:S(2)}) %collective-permute-start.24) | collective-permute-done | bytes 11534368 | tf_op jit(solution)/shard_map/ppermute | solution.py:332
  1078.3 67.6 %shard_map.122.refs_6_ = bf16[2,4,640,2816]{3,2,1,0:T(8,128)(2,1)} custom-call(bf16[2,640,2048]{2,1,0:T(8,128)(2,1)} %get-tuple-element.90.refs_0_, bf16[2,640,2048]{2,1,0:T(8,128)(2,1)} %collective-permute-done.3.refs_1_, bf16[2,640,2048]{2,1,0:T(8,128)(2,1)} %collective-permute-done.4.refs_2_, bf16[2,640,2048]{2,1,0:T(8,128)(2,1)} %collective-permute-done.5.refs_3_, ...), custom_call_target="tpu_custom_call" | custom-call | flops 59055800320 | bytes 47972352 | tf_op jit(solution)/shard_map/pallas_call | solution.py:119
  1146.0 67.8 %shard_map.123.h0.h1 = bf16[2,4,640,2816]{3,2,1,0:T(8,128)(2,1)} custom-call(bf16[2,640,2048]{2,1,0:T(8,128)(2,1)} %get-tuple-element.86.refs_0_, bf16[2,640,2048]{2,1,0:T(8,128)(2,1)} %collective-permute-done.refs_1_, bf16[2,640,2048]{2,1,0:T(8,128)(2,1)} %collective-permute-done.1.refs_2_, ...), custom_call_target="tpu_custom_call", output_to_operand_aliasing={{}: (6, {})} | custom-call | flops 59055800320 | bytes 47972352 | tf_op jit(solution)/shard_map/pallas_call | solution.py:119
  1213.8 87.8 %collective-permute-done.14 = bf16[1,2048,1280]{2,1,0:T(8,128)(2,1)} collective-permute-done((bf16[1,2048,1280]{2,1,0:T(8,128)(2,1)}, bf16[1,2048,1280]{2,1,0:T(8,128)(2,1)}, u32[]{:S(2)}, u32[]{:S(2)}) %collective-permute-start.14) | collective-permute-done | bytes 5242912 | tf_op jit(solution)/shard_map/ppermute | solution.py:332
  1303.0 9.2 copy-done.1
  1312.3 32.8 %shard_map.114.refs_6_ = bf16[2,4,640,2816]{3,2,1,0:T(8,128)(2,1)S(1)} custom-call(bf16[2,640,2048]{2,1,0:T(8,128)(2,1)} %get-tuple-element.90.refs_0_, bf16[2,640,2048]{2,1,0:T(8,128)(2,1)} %collective-permute-done.3.refs_1_, bf16[2,640,2048]{2,1,0:T(8,128)(2,1)} %collective-permute-done.4.refs_2_, ...), custom_call_target="tpu_custom_call", output_to_operand_aliasing={{}: (6, {})} | custom-call | flops 26843545600 | bytes 27525120 | tf_op jit(solution)/shard_map/pallas_call | solution.py:112
  1345.0 32.8 %shard_map.115.refs_6_ = bf16[2,4,640,2816]{3,2,1,0:T(8,128)(2,1)S(1)} custom-call(bf16[2,640,2048]{2,1,0:T(8,128)(2,1)} %get-tuple-element.86.refs_0_, bf16[2,640,2048]{2,1,0:T(8,128)(2,1)} %collective-permute-done.refs_1_, bf16[2,640,2048]{2,1,0:T(8,128)(2,1)} %collective-permute-done.1.refs_2_, ...), custom_call_target="tpu_custom_call", output_to_operand_aliasing={{}: (6, {})} | custom-call | flops 26843545600 | bytes 27525120 | tf_op jit(solution)/shard_map/pallas_call | solution.py:112
  1378.4 21.9 %shard_map.116.refs_6_ = bf16[2,4,640,2816]{3,2,1,0:T(8,128)(2,1)S(1)} custom-call(bf16[2,640,2048]{2,1,0:T(8,128)(2,1)} %get-tuple-element.90.refs_0_, bf16[2,640,2048]{2,1,0:T(8,128)(2,1)} %collective-permute-done.3.refs_1_, bf16[2,640,2048]{2,1,0:T(8,128)(2,1)} %collective-permute-done.4.refs_2_, ...), custom_call_target="tpu_custom_call", output_to_operand_aliasing={{}: (6, {})} | custom-call | flops 16106127360 | bytes 20709376 | tf_op jit(solution)/shard_map/pallas_call | solution.py:112
  1400.3 21.6 %shard_map.117.refs_6_ = bf16[2,4,640,2816]{3,2,1,0:T(8,128)(2,1)S(1)} custom-call(bf16[2,640,2048]{2,1,0:T(8,128)(2,1)} %get-tuple-element.86.refs_0_, bf16[2,640,2048]{2,1,0:T(8,128)(2,1)} %collective-permute-done.refs_1_, bf16[2,640,2048]{2,1,0:T(8,128)(2,1)} %collective-permute-done.1.refs_2_, ...), custom_call_target="tpu_custom_call", output_to_operand_aliasing={{}: (6, {})} | custom-call | flops 16106127360 | bytes 20709376 | tf_op jit(solution)/shard_map/pallas_call | solution.py:112
  1423.5 15.9 shard_map.118.refs_6_
  1439.4 16.1 shard_map.119.h
  1456.1 11.5 shard_map.120
  1467.5 9.5 copy-done.2
  1477.1 42.0 %shard_map.126 = (bf16[2,640,1024]{2,1,0:T(8,128)(2,1)}, bf16[2,640,1024]{2,1,0:T(8,128)(2,1)}, bf16[2,640,1024]{2,1,0:T(8,128)(2,1)}, bf16[2,640,1024]{2,1,0:T(8,128)(2,1)}) custom-call(bf16[2,4,640,2816]{3,2,1,0:T(8,128)(2,1)} %shard_map.123.h0.h1, bf16[2,4,640,2816]{3,2,1,0:T(8,128)(2,1)} %shard_map.123.h0.h1, f32[2,2,4,640,2048]{4,3,2,1,0:T(8,128)} %shard_map.111.p, ...), custom_call_target="tpu_custom_call" | custom-call | flops 29527900160 | bytes 66060288 | tf_op jit(solution)/shard_map/pallas_call | solution.py:163
  1521.0 24.4 %shard_map.124 = (bf16[2,640,512]{2,1,0:T(8,128)(2,1)}, bf16[2,640,512]{2,1,0:T(8,128)(2,1)}, bf16[2,640,512]{2,1,0:T(8,128)(2,1)}, bf16[2,640,512]{2,1,0:T(8,128)(2,1)}) custom-call(bf16[2,4,640,2816]{3,2,1,0:T(8,128)(2,1)} %shard_map.123.h0.h1, bf16[2,4,640,2816]{3,2,1,0:T(8,128)(2,1)} %shard_map.123.h0.h1, f32[2,2,4,640,2048]{4,3,2,1,0:T(8,128)} %shard_map.111.p, ...), custom_call_target="tpu_custom_call" | custom-call | flops 14763950080 | bytes 47448064 | tf_op jit(solution)/shard_map/pallas_call | solution.py:163
  1545.4 64.7 %collective-permute-done.37 = bf16[1,2816,256]{2,1,0:T(8,128)(2,1)} collective-permute-done((bf16[1,2816,256]{2,1,0:T(8,128)(2,1)}, bf16[1,2816,256]{2,1,0:T(8,128)(2,1)}, u32[]{:S(2)}, u32[]{:S(2)}) %collective-permute-start.37) | collective-permute-done | bytes 1441824 | tf_op jit(solution)/shard_map/ppermute | solution.py:332
  1613.5 9.2 copy-done.3
  1622.7 11.5 shard_map.121
  1634.3 9.5 copy-done.4
  1644.4 24.2 %shard_map.125 = (bf16[2,640,512]{2,1,0:T(8,128)(2,1)}, bf16[2,640,512]{2,1,0:T(8,128)(2,1)}, bf16[2,640,512]{2,1,0:T(8,128)(2,1)}, bf16[2,640,512]{2,1,0:T(8,128)(2,1)}) custom-call(bf16[2,4,640,2816]{3,2,1,0:T(8,128)(2,1)} %shard_map.123.h0.h1, bf16[2,4,640,2816]{3,2,1,0:T(8,128)(2,1)} %shard_map.123.h0.h1, f32[2,2,4,640,2048]{4,3,2,1,0:T(8,128)} %shard_map.111.p, ...), custom_call_target="tpu_custom_call" | custom-call | flops 14763950080 | bytes 47448064 | tf_op jit(solution)/shard_map/pallas_call | solution.py:163
  1670.9 55.3 %collective-permute-done.27.refs_2_ = bf16[2,640,512]{2,1,0:T(8,128)(2,1)S(1)} collective-permute-done((bf16[2,640,512]{2,1,0:T(8,128)(2,1)}, bf16[2,640,512]{2,1,0:T(8,128)(2,1)S(1)}, u32[]{:S(2)}, u32[]{:S(2)}) %collective-permute-start.27) | collective-permute-done | bytes 1310752 | tf_op jit(solution)/shard_map/ppermute | solution.py:328
  1730.6 9.2 copy-done.5
  1739.8 11.7 shard_map.130
  1751.5 9.5 copy-done.6
  1767.8 17.5 shard_map.127.refs_6_
  1786.8 22.9 %collective-permute-done.32.refs_3_ = bf16[2,640,512]{2,1,0:T(8,128)(2,1)} collective-permute-done((bf16[2,640,512]{2,1,0:T(8,128)(2,1)}, bf16[2,640,512]{2,1,0:T(8,128)(2,1)}, u32[]{:S(2)}, u32[]{:S(2)}) %collective-permute-start.32) | collective-permute-done | bytes 1310752 | tf_op jit(solution)/shard_map/ppermute | solution.py:328
  1811.7 11.5 shard_map.128.refs_6_
  1824.8 12.4 shard_map.129.refs_10_.refs_6_
  1840.2 14.6 shard_map.131
  1855.4 11.7 shard_map.132
  1868.6 11.5 shard_map.133
  1885.9 11.9 shard_map.134
  1898.9 6.6 shard_map.135
  1906.1 6.6 shard_map.136
  1916.5 11.9 shard_map.137
  1930.2 6.9 shard_map.138
  1938.4 6.7 shard_map.139
  1945.9 12.5 collective-permute-done.46.refs_6_
  1960.0 12.7 collective-permute-done.47.refs_7_
  1973.4 14.6 shard_map.140
  1989.0 6.1 shard_map.141
  1995.1 6.1 shard_map.142
  2002.5 6.1 shard_map.143
  2009.2 6.5 shard_map.144
  2019.2 10.8 shard_map.145
  2030.1 9.6 shard_map.146
  2039.7 9.4 shard_map.147
  (258 shorter events, 122.8 us)
Async XLA Ops:
  46.3 165.9 %collective-permute-start = (bf16[2,640,2048]{2,1,0:T(8,128)(2,1)}, bf16[2,640,2048]{2,1,0:T(8,128)(2,1)}, u32[]{:S(2)}, u32[]{:S(2)}) collective-permute-start(bf16[2,640,2048]{2,1,0:T(8,128)(2,1)} %get-tuple-element.87), channel_id=1, source_target_pairs={{0,1},{1,0},{2,3},{3,2},{4,5},{5,4},{6,7},{7,6}} | collective-permute-start | bytes 15728648 | tf_op jit(solution)/shard_map/ppermute | solution.py:328
  80.3 131.9 %collective-permute-start.1 = (bf16[2,640,2048]{2,1,0:T(8,128)(2,1)}, bf16[2,640,2048]{2,1,0:T(8,128)(2,1)}, u32[]{:S(2)}, u32[]{:S(2)}) collective-permute-start(bf16[2,640,2048]{2,1,0:T(8,128)(2,1)} %get-tuple-element.88), channel_id=1, source_target_pairs={{0,2},{1,3},{2,0},{3,1},{4,6},{5,7},{6,4},{7,5}} | collective-permute-start | bytes 15728648 | tf_op jit(solution)/shard_map/ppermute | solution.py:328
  82.8 226.2 %collective-permute-start.2 = (bf16[2,640,2048]{2,1,0:T(8,128)(2,1)}, bf16[2,640,2048]{2,1,0:T(8,128)(2,1)}, u32[]{:S(2)}, u32[]{:S(2)}) collective-permute-start(bf16[2,640,2048]{2,1,0:T(8,128)(2,1)} %get-tuple-element.89), channel_id=1, source_target_pairs={{0,3},{1,2},{2,1},{3,0},{4,7},{5,6},{6,5},{7,4}} | collective-permute-start | bytes 15728648 | tf_op jit(solution)/shard_map/ppermute | solution.py:328
  115.1 325.4 %collective-permute-start.3 = (bf16[2,640,2048]{2,1,0:T(8,128)(2,1)}, bf16[2,640,2048]{2,1,0:T(8,128)(2,1)}, u32[]{:S(2)}, u32[]{:S(2)}) collective-permute-start(bf16[2,640,2048]{2,1,0:T(8,128)(2,1)} %get-tuple-element.91), channel_id=1, source_target_pairs={{0,1},{1,0},{2,3},{3,2},{4,5},{5,4},{6,7},{7,6}} | collective-permute-start | bytes 15728648 | tf_op jit(solution)/shard_map/ppermute | solution.py:328
  147.2 293.8 %collective-permute-start.4 = (bf16[2,640,2048]{2,1,0:T(8,128)(2,1)}, bf16[2,640,2048]{2,1,0:T(8,128)(2,1)}, u32[]{:S(2)}, u32[]{:S(2)}) collective-permute-start(bf16[2,640,2048]{2,1,0:T(8,128)(2,1)} %get-tuple-element.92), channel_id=1, source_target_pairs={{0,2},{1,3},{2,0},{3,1},{4,6},{5,7},{6,4},{7,5}} | collective-permute-start | bytes 15728648 | tf_op jit(solution)/shard_map/ppermute | solution.py:328
  178.9 23.0 %slice-start.7 = ((s8[23068672]{0:T(1024)(128)(4,1)}), s8[2097152]{0:T(1024)(128)(4,1)S(1)}, s32[]{:S(2)}) async-start(s8[23068672]{0:T(1024)(128)(4,1)} %bitcast.68), calls=%async_computation.7 | async-start | bytes 4194304
  178.9 23.0 %slice-start.8 = ((s8[23068672]{0:T(1024)(128)(4,1)}), s8[4194304]{0:T(1024)(128)(4,1)S(1)}, s32[]{:S(2)}) async-start(s8[23068672]{0:T(1024)(128)(4,1)} %bitcast.68), calls=%async_computation.8 | async-start | bytes 8388608
  212.2 321.5 %collective-permute-start.5 = (bf16[2,640,2048]{2,1,0:T(8,128)(2,1)}, bf16[2,640,2048]{2,1,0:T(8,128)(2,1)}, u32[]{:S(2)}, u32[]{:S(2)}) collective-permute-start(bf16[2,640,2048]{2,1,0:T(8,128)(2,1)} %get-tuple-element.93), channel_id=1, source_target_pairs={{0,3},{1,2},{2,1},{3,0},{4,7},{5,6},{6,5},{7,4}} | collective-permute-start | bytes 15728648 | tf_op jit(solution)/shard_map/ppermute | solution.py:328
  212.2 1243.3 %collective-permute-start.10 = (bf16[1,2816,256]{2,1,0:T(8,128)(2,1)}, bf16[1,2816,256]{2,1,0:T(8,128)(2,1)}, u32[]{:S(2)}, u32[]{:S(2)}) collective-permute-start(bf16[1,2816,256]{2,1,0:T(8,128)(2,1)} %get-tuple-element.173), channel_id=1, source_target_pairs={{0,4},{4,0},{1,5},{5,1},{2,6},{6,2},{3,7},{7,3}} | collective-permute-start | bytes 4325384 | tf_op jit(solution)/shard_map/ppermute | solution.py:332
  309.0 502.1 %collective-permute-start.11 = (bf16[1,2048,2816]{2,1,0:T(8,128)(2,1)}, bf16[1,2048,2816]{2,1,0:T(8,128)(2,1)}, u32[]{:S(2)}, u32[]{:S(2)}) collective-permute-start(bf16[1,2048,2816]{2,1,0:T(8,128)(2,1)} %get-tuple-element.180), channel_id=1, source_target_pairs={{0,4},{4,0},{1,5},{5,1},{2,6},{6,2},{3,7},{7,3}} | collective-permute-start | bytes 34603016 | tf_op jit(solution)/shard_map/ppermute | solution.py:332
  440.5 370.0 %collective-permute-start.15 = (bf16[1,2048,256]{2,1,0:T(8,128)(2,1)}, bf16[1,2048,256]{2,1,0:T(8,128)(2,1)}, u32[]{:S(2)}, u32[]{:S(2)}) collective-permute-start(bf16[1,2048,256]{2,1,0:T(8,128)(2,1)} %slice.146), channel_id=1, source_target_pairs={{0,4},{4,0},{1,5},{5,1},{2,6},{6,2},{3,7},{7,3}} | collective-permute-start | bytes 3145736 | tf_op jit(solution)/shard_map/ppermute | solution.py:332
  441.1 401.4 %collective-permute-start.23 = (bf16[1,2048,2816]{2,1,0:T(8,128)(2,1)}, bf16[1,2048,2816]{2,1,0:T(8,128)(2,1)}, u32[]{:S(2)}, u32[]{:S(2)}) collective-permute-start(bf16[1,2048,2816]{2,1,0:T(8,128)(2,1)} %get-tuple-element.179), channel_id=1, source_target_pairs={{0,4},{4,0},{1,5},{5,1},{2,6},{6,2},{3,7},{7,3}} | collective-permute-start | bytes 34603016 | tf_op jit(solution)/shard_map/ppermute | solution.py:332
  533.7 543.2 %collective-permute-start.24 = (bf16[1,2048,2816]{2,1,0:T(8,128)(2,1)}, bf16[1,2048,2816]{2,1,0:T(8,128)(2,1)}, u32[]{:S(2)}, u32[]{:S(2)}) collective-permute-start(bf16[1,2048,2816]{2,1,0:T(8,128)(2,1)} %slice.151), channel_id=1, source_target_pairs={{0,4},{4,0},{1,5},{5,1},{2,6},{6,2},{3,7},{7,3}} | collective-permute-start | bytes 34603016 | tf_op jit(solution)/shard_map/ppermute | solution.py:332
  810.5 611.4 %collective-permute-start.12 = (bf16[1,2048,512]{2,1,0:T(8,128)(2,1)}, bf16[1,2048,512]{2,1,0:T(8,128)(2,1)}, u32[]{:S(2)}, u32[]{:S(2)}) collective-permute-start(bf16[1,2048,512]{2,1,0:T(8,128)(2,1)} %slice.143), channel_id=1, source_target_pairs={{0,4},{4,0},{1,5},{5,1},{2,6},{6,2},{3,7},{7,3}} | collective-permute-start | bytes 6291464 | tf_op jit(solution)/shard_map/ppermute | solution.py:332
  811.1 566.7 %collective-permute-start.13 = (bf16[1,2048,768]{2,1,0:T(8,128)(2,1)}, bf16[1,2048,768]{2,1,0:T(8,128)(2,1)}, u32[]{:S(2)}, u32[]{:S(2)}) collective-permute-start(bf16[1,2048,768]{2,1,0:T(8,128)(2,1)} %slice.144), channel_id=1, source_target_pairs={{0,4},{4,0},{1,5},{5,1},{2,6},{6,2},{3,7},{7,3}} | collective-permute-start | bytes 9437192 | tf_op jit(solution)/shard_map/ppermute | solution.py:332
  842.5 459.1 %collective-permute-start.14 = (bf16[1,2048,1280]{2,1,0:T(8,128)(2,1)}, bf16[1,2048,1280]{2,1,0:T(8,128)(2,1)}, u32[]{:S(2)}, u32[]{:S(2)}) collective-permute-start(bf16[1,2048,1280]{2,1,0:T(8,128)(2,1)} %slice.145), channel_id=1, source_target_pairs={{0,4},{4,0},{1,5},{5,1},{2,6},{6,2},{3,7},{7,3}} | collective-permute-start | bytes 15728648 | tf_op jit(solution)/shard_map/ppermute | solution.py:332
  1076.8 442.2 %collective-permute-start.19 = (bf16[1,2816,256]{2,1,0:T(8,128)(2,1)}, bf16[1,2816,256]{2,1,0:T(8,128)(2,1)}, u32[]{:S(2)}, u32[]{:S(2)}) collective-permute-start(bf16[1,2816,256]{2,1,0:T(8,128)(2,1)} %get-tuple-element.172), channel_id=1, source_target_pairs={{0,4},{4,0},{1,5},{5,1},{2,6},{6,2},{3,7},{7,3}} | collective-permute-start | bytes 4325384 | tf_op jit(solution)/shard_map/ppermute | solution.py:332
  1301.6 175.5 %collective-permute-start.33 = (bf16[1,2816,1024]{2,1,0:T(8,128)(2,1)}, bf16[1,2816,1024]{2,1,0:T(8,128)(2,1)}, u32[]{:S(2)}, u32[]{:S(2)}) collective-permute-start(bf16[1,2816,1024]{2,1,0:T(8,128)(2,1)} %slice.154), channel_id=1, source_target_pairs={{0,4},{4,0},{1,5},{5,1},{2,6},{6,2},{3,7},{7,3}} | collective-permute-start | bytes 17301512 | tf_op jit(solution)/shard_map/ppermute | solution.py:332
  1377.8 141.7 %collective-permute-start.25 = (bf16[1,2816,512]{2,1,0:T(8,128)(2,1)}, bf16[1,2816,512]{2,1,0:T(8,128)(2,1)}, u32[]{:S(2)}, u32[]{:S(2)}) collective-permute-start(bf16[1,2816,512]{2,1,0:T(8,128)(2,1)} %get-tuple-element.178), channel_id=1, source_target_pairs={{0,4},{4,0},{1,5},{5,1},{2,6},{6,2},{3,7},{7,3}} | collective-permute-start | bytes 8650760 | tf_op jit(solution)/shard_map/ppermute | solution.py:332
  1421.9 189.8 %collective-permute-start.29 = (bf16[1,2816,512]{2,1,0:T(8,128)(2,1)}, bf16[1,2816,512]{2,1,0:T(8,128)(2,1)}, u32[]{:S(2)}, u32[]{:S(2)}) collective-permute-start(bf16[1,2816,512]{2,1,0:T(8,128)(2,1)} %get-tuple-element.177), channel_id=1, source_target_pairs={{0,4},{4,0},{1,5},{5,1},{2,6},{6,2},{3,7},{7,3}} | collective-permute-start | bytes 8650760 | tf_op jit(solution)/shard_map/ppermute | solution.py:332
  1455.5 154.6 %collective-permute-start.37 = (bf16[1,2816,256]{2,1,0:T(8,128)(2,1)}, bf16[1,2816,256]{2,1,0:T(8,128)(2,1)}, u32[]{:S(2)}, u32[]{:S(2)}) collective-permute-start(bf16[1,2816,256]{2,1,0:T(8,128)(2,1)} %get-tuple-element.171), channel_id=1, source_target_pairs={{0,4},{4,0},{1,5},{5,1},{2,6},{6,2},{3,7},{7,3}} | collective-permute-start | bytes 4325384 | tf_op jit(solution)/shard_map/ppermute | solution.py:332
  1477.1 134.7 %collective-permute-start.16 = (bf16[2,640,256]{2,1,0:T(8,128)(2,1)}, bf16[2,640,256]{2,1,0:T(8,128)(2,1)S(1)}, u32[]{:S(2)}, u32[]{:S(2)}) collective-permute-start(bf16[2,640,256]{2,1,0:T(8,128)(2,1)} %get-tuple-element.95), channel_id=1, source_target_pairs={{0,1},{1,0},{2,3},{3,2},{4,5},{5,4},{6,7},{7,6}} | collective-permute-start | bytes 1966088 | tf_op jit(solution)/shard_map/ppermute | solution.py:328
  1519.1 208.2 %collective-permute-start.34 = (bf16[2,640,1024]{2,1,0:T(8,128)(2,1)}, bf16[2,640,1024]{2,1,0:T(8,128)(2,1)S(1)}, u32[]{:S(2)}, u32[]{:S(2)}) collective-permute-start(bf16[2,640,1024]{2,1,0:T(8,128)(2,1)} %get-tuple-element.112), channel_id=1, source_target_pairs={{0,1},{1,0},{2,3},{3,2},{4,5},{5,4},{6,7},{7,6}} | collective-permute-start | bytes 7864328 | tf_op jit(solution)/shard_map/ppermute | solution.py:328
  1519.6 210.9 %collective-permute-start.35 = (bf16[2,640,1024]{2,1,0:T(8,128)(2,1)}, bf16[2,640,1024]{2,1,0:T(8,128)(2,1)}, u32[]{:S(2)}, u32[]{:S(2)}) collective-permute-start(bf16[2,640,1024]{2,1,0:T(8,128)(2,1)} %get-tuple-element.113), channel_id=1, source_target_pairs={{0,2},{1,3},{2,0},{3,1},{4,6},{5,7},{6,4},{7,5}} | collective-permute-start | bytes 7864328 | tf_op jit(solution)/shard_map/ppermute | solution.py:328
  1610.1 33.7 %collective-permute-start.17 = (bf16[2,640,256]{2,1,0:T(8,128)(2,1)}, bf16[2,640,256]{2,1,0:T(8,128)(2,1)}, u32[]{:S(2)}, u32[]{:S(2)}) collective-permute-start(bf16[2,640,256]{2,1,0:T(8,128)(2,1)} %get-tuple-element.96), channel_id=1, source_target_pairs={{0,2},{1,3},{2,0},{3,1},{4,6},{5,7},{6,4},{7,5}} | collective-permute-start | bytes 1966088 | tf_op jit(solution)/shard_map/ppermute | solution.py:328
  1611.8 32.0 %collective-permute-start.18 = (bf16[2,640,256]{2,1,0:T(8,128)(2,1)}, bf16[2,640,256]{2,1,0:T(8,128)(2,1)}, u32[]{:S(2)}, u32[]{:S(2)}) collective-permute-start(bf16[2,640,256]{2,1,0:T(8,128)(2,1)} %get-tuple-element.97), channel_id=1, source_target_pairs={{0,3},{1,2},{2,1},{3,0},{4,7},{5,6},{6,5},{7,4}} | collective-permute-start | bytes 1966088 | tf_op jit(solution)/shard_map/ppermute | solution.py:328
  1611.8 149.2 %collective-permute-start.36 = (bf16[2,640,1024]{2,1,0:T(8,128)(2,1)}, bf16[2,640,1024]{2,1,0:T(8,128)(2,1)}, u32[]{:S(2)}, u32[]{:S(2)}) collective-permute-start(bf16[2,640,1024]{2,1,0:T(8,128)(2,1)} %get-tuple-element.114), channel_id=1, source_target_pairs={{0,3},{1,2},{2,1},{3,0},{4,7},{5,6},{6,5},{7,4}} | collective-permute-start | bytes 7864328 | tf_op jit(solution)/shard_map/ppermute | solution.py:328
  1643.8 24.8 %collective-permute-start.26 = (bf16[2,640,512]{2,1,0:T(8,128)(2,1)}, bf16[2,640,512]{2,1,0:T(8,128)(2,1)S(1)}, u32[]{:S(2)}, u32[]{:S(2)}) collective-permute-start(bf16[2,640,512]{2,1,0:T(8,128)(2,1)} %get-tuple-element.104), channel_id=1, source_target_pairs={{0,1},{1,0},{2,3},{3,2},{4,5},{5,4},{6,7},{7,6}} | collective-permute-start | bytes 3932168 | tf_op jit(solution)/shard_map/ppermute | solution.py:328
  1643.8 82.4 %collective-permute-start.27 = (bf16[2,640,512]{2,1,0:T(8,128)(2,1)}, bf16[2,640,512]{2,1,0:T(8,128)(2,1)S(1)}, u32[]{:S(2)}, u32[]{:S(2)}) collective-permute-start(bf16[2,640,512]{2,1,0:T(8,128)(2,1)} %get-tuple-element.105), channel_id=1, source_target_pairs={{0,2},{1,3},{2,0},{3,1},{4,6},{5,7},{6,4},{7,5}} | collective-permute-start | bytes 3932168 | tf_op jit(solution)/shard_map/ppermute | solution.py:328
  1669.7 153.5 %collective-permute-start.28 = (bf16[2,640,512]{2,1,0:T(8,128)(2,1)}, bf16[2,640,512]{2,1,0:T(8,128)(2,1)}, u32[]{:S(2)}, u32[]{:S(2)}) collective-permute-start(bf16[2,640,512]{2,1,0:T(8,128)(2,1)} %get-tuple-element.106), channel_id=1, source_target_pairs={{0,3},{1,2},{2,1},{3,0},{4,7},{5,6},{6,5},{7,4}} | collective-permute-start | bytes 3932168 | tf_op jit(solution)/shard_map/ppermute | solution.py:328
  1727.2 58.1 %collective-permute-start.30 = (bf16[2,640,512]{2,1,0:T(8,128)(2,1)}, bf16[2,640,512]{2,1,0:T(8,128)(2,1)}, u32[]{:S(2)}, u32[]{:S(2)}) collective-permute-start(bf16[2,640,512]{2,1,0:T(8,128)(2,1)} %get-tuple-element.108), channel_id=1, source_target_pairs={{0,1},{1,0},{2,3},{3,2},{4,5},{5,4},{6,7},{7,6}} | collective-permute-start | bytes 3932168 | tf_op jit(solution)/shard_map/ppermute | solution.py:328
  1728.7 56.6 %collective-permute-start.31 = (bf16[2,640,512]{2,1,0:T(8,128)(2,1)}, bf16[2,640,512]{2,1,0:T(8,128)(2,1)S(1)}, u32[]{:S(2)}, u32[]{:S(2)}) collective-permute-start(bf16[2,640,512]{2,1,0:T(8,128)(2,1)} %get-tuple-element.109), channel_id=1, source_target_pairs={{0,2},{1,3},{2,0},{3,1},{4,6},{5,7},{6,4},{7,5}} | collective-permute-start | bytes 3932168 | tf_op jit(solution)/shard_map/ppermute | solution.py:328
  1730.4 79.4 %collective-permute-start.32 = (bf16[2,640,512]{2,1,0:T(8,128)(2,1)}, bf16[2,640,512]{2,1,0:T(8,128)(2,1)}, u32[]{:S(2)}, u32[]{:S(2)}) collective-permute-start(bf16[2,640,512]{2,1,0:T(8,128)(2,1)} %get-tuple-element.110), channel_id=1, source_target_pairs={{0,3},{1,2},{2,1},{3,0},{4,7},{5,6},{6,5},{7,4}} | collective-permute-start | bytes 3932168 | tf_op jit(solution)/shard_map/ppermute | solution.py:328
  1761.0 93.8 %collective-permute-start.9 = (bf16[1,2816,256]{2,1,0:T(8,128)(2,1)}, bf16[1,2816,256]{2,1,0:T(8,128)(2,1)}, u32[]{:S(2)}, u32[]{:S(2)}) collective-permute-start(bf16[1,2816,256]{2,1,0:T(8,128)(2,1)} %get-tuple-element.174), channel_id=1, source_target_pairs={{0,4},{4,0},{1,5},{5,1},{2,6},{6,2},{3,7},{7,3}} | collective-permute-start | bytes 4325384 | tf_op jit(solution)/shard_map/ppermute | solution.py:332
  1767.8 43.9 %copy-start.20 = (bf16[2,640,512]{2,1,0:T(8,128)(2,1)S(1)}, bf16[2,640,512]{2,1,0:T(8,128)(2,1)}, u32[]{:S(2)}) copy-start(bf16[2,640,512]{2,1,0:T(8,128)(2,1)} %get-tuple-element.107.refs_0_) | copy-start | bytes 3932164
  1785.3 51.9 %collective-permute-start.20 = (bf16[2,640,256]{2,1,0:T(8,128)(2,1)}, bf16[2,640,256]{2,1,0:T(8,128)(2,1)S(1)}, u32[]{:S(2)}, u32[]{:S(2)}) collective-permute-start(bf16[2,640,256]{2,1,0:T(8,128)(2,1)} %get-tuple-element.100), channel_id=1, source_target_pairs={{0,1},{1,0},{2,3},{3,2},{4,5},{5,4},{6,7},{7,6}} | collective-permute-start | bytes 1966088 | tf_op jit(solution)/shard_map/ppermute | solution.py:328
  1785.3 52.4 %collective-permute-start.21 = (bf16[2,640,256]{2,1,0:T(8,128)(2,1)}, bf16[2,640,256]{2,1,0:T(8,128)(2,1)S(1)}, u32[]{:S(2)}, u32[]{:S(2)}) collective-permute-start(bf16[2,640,256]{2,1,0:T(8,128)(2,1)} %get-tuple-element.101), channel_id=1, source_target_pairs={{0,2},{1,3},{2,0},{3,1},{4,6},{5,7},{6,4},{7,5}} | collective-permute-start | bytes 1966088 | tf_op jit(solution)/shard_map/ppermute | solution.py:328
  1809.8 29.5 %collective-permute-start.22 = (bf16[2,640,256]{2,1,0:T(8,128)(2,1)}, bf16[2,640,256]{2,1,0:T(8,128)(2,1)S(1)}, u32[]{:S(2)}, u32[]{:S(2)}) collective-permute-start(bf16[2,640,256]{2,1,0:T(8,128)(2,1)} %get-tuple-element.102), channel_id=1, source_target_pairs={{0,3},{1,2},{2,1},{3,0},{4,7},{5,6},{6,5},{7,4}} | collective-permute-start | bytes 1966088 | tf_op jit(solution)/shard_map/ppermute | solution.py:328
  1823.2 43.8 %collective-permute-start.8 = (bf16[1,2816,256]{2,1,0:T(8,128)(2,1)}, bf16[1,2816,256]{2,1,0:T(8,128)(2,1)}, u32[]{:S(2)}, u32[]{:S(2)}) collective-permute-start(bf16[1,2816,256]{2,1,0:T(8,128)(2,1)} %get-tuple-element.175), channel_id=1, source_target_pairs={{0,4},{4,0},{1,5},{5,1},{2,6},{6,2},{3,7},{7,3}} | collective-permute-start | bytes 4325384 | tf_op jit(solution)/shard_map/ppermute | solution.py:332
  1837.3 60.5 %collective-permute-start.41 = (bf16[1,2816,256]{2,1,0:T(8,128)(2,1)}, bf16[1,2816,256]{2,1,0:T(8,128)(2,1)S(1)}, u32[]{:S(2)}, u32[]{:S(2)}) collective-permute-start(bf16[1,2816,256]{2,1,0:T(8,128)(2,1)} %get-tuple-element.176), channel_id=1, source_target_pairs={{0,4},{4,0},{1,5},{5,1},{2,6},{6,2},{3,7},{7,3}} | collective-permute-start | bytes 4325384 | tf_op jit(solution)/shard_map/ppermute | solution.py:332
  1837.8 90.6 %collective-permute-start.51 = (bf16[1,2816,256]{2,1,0:T(8,128)(2,1)}, bf16[1,2816,256]{2,1,0:T(8,128)(2,1)}, u32[]{:S(2)}, u32[]{:S(2)}) collective-permute-start(bf16[1,2816,256]{2,1,0:T(8,128)(2,1)} %get-tuple-element.170), channel_id=1, source_target_pairs={{0,4},{4,0},{1,5},{5,1},{2,6},{6,2},{3,7},{7,3}} | collective-permute-start | bytes 4325384 | tf_op jit(solution)/shard_map/ppermute | solution.py:332
  1839.3 28.2 %collective-permute-start.42 = (bf16[2,640,256]{2,1,0:T(8,128)(2,1)}, bf16[2,640,256]{2,1,0:T(8,128)(2,1)S(1)}, u32[]{:S(2)}, u32[]{:S(2)}) collective-permute-start(bf16[2,640,256]{2,1,0:T(8,128)(2,1)} %get-tuple-element.124), channel_id=1, source_target_pairs={{0,1},{1,0},{2,3},{3,2},{4,5},{5,4},{6,7},{7,6}} | collective-permute-start | bytes 1966088 | tf_op jit(solution)/shard_map/ppermute | solution.py:328
  1854.8 25.3 %collective-permute-start.43 = (bf16[2,640,256]{2,1,0:T(8,128)(2,1)}, bf16[2,640,256]{2,1,0:T(8,128)(2,1)S(1)}, u32[]{:S(2)}, u32[]{:S(2)}) collective-permute-start(bf16[2,640,256]{2,1,0:T(8,128)(2,1)} %get-tuple-element.125), channel_id=1, source_target_pairs={{0,2},{1,3},{2,0},{3,1},{4,6},{5,7},{6,4},{7,5}} | collective-permute-start | bytes 1966088 | tf_op jit(solution)/shard_map/ppermute | solution.py:328
  1867.0 17.3 collective-permute-start.44
  1867.5 38.0 %collective-permute-start.48 = (bf16[2,640,256]{2,1,0:T(8,128)(2,1)}, bf16[2,640,256]{2,1,0:T(8,128)(2,1)S(1)}, u32[]{:S(2)}, u32[]{:S(2)}) collective-permute-start(bf16[2,640,256]{2,1,0:T(8,128)(2,1)} %get-tuple-element.137), channel_id=1, source_target_pairs={{0,1},{1,0},{2,3},{3,2},{4,5},{5,4},{6,7},{7,6}} | collective-permute-start | bytes 1966088 | tf_op jit(solution)/shard_map/ppermute | solution.py:328
  1881.0 48.8 %collective-permute-start.38 = (bf16[2,640,256]{2,1,0:T(8,128)(2,1)}, bf16[2,640,256]{2,1,0:T(8,128)(2,1)S(1)}, u32[]{:S(2)}, u32[]{:S(2)}) collective-permute-start(bf16[2,640,256]{2,1,0:T(8,128)(2,1)} %get-tuple-element.120), channel_id=1, source_target_pairs={{0,1},{1,0},{2,3},{3,2},{4,5},{5,4},{6,7},{7,6}} | collective-permute-start | bytes 1966088 | tf_op jit(solution)/shard_map/ppermute | solution.py:328
  1884.4 28.3 %collective-permute-start.49 = (bf16[2,640,256]{2,1,0:T(8,128)(2,1)}, bf16[2,640,256]{2,1,0:T(8,128)(2,1)S(1)}, u32[]{:S(2)}, u32[]{:S(2)}) collective-permute-start(bf16[2,640,256]{2,1,0:T(8,128)(2,1)} %get-tuple-element.138), channel_id=1, source_target_pairs={{0,2},{1,3},{2,0},{3,1},{4,6},{5,7},{6,4},{7,5}} | collective-permute-start | bytes 1966088 | tf_op jit(solution)/shard_map/ppermute | solution.py:328
  1897.7 18.7 collective-permute-start.50
  1905.5 31.6 %collective-permute-start.39 = (bf16[2,640,256]{2,1,0:T(8,128)(2,1)}, bf16[2,640,256]{2,1,0:T(8,128)(2,1)S(1)}, u32[]{:S(2)}, u32[]{:S(2)}) collective-permute-start(bf16[2,640,256]{2,1,0:T(8,128)(2,1)} %get-tuple-element.121), channel_id=1, source_target_pairs={{0,2},{1,3},{2,0},{3,1},{4,6},{5,7},{6,4},{7,5}} | collective-permute-start | bytes 1966088 | tf_op jit(solution)/shard_map/ppermute | solution.py:328
  1912.7 32.4 %collective-permute-start.40 = (bf16[2,640,256]{2,1,0:T(8,128)(2,1)}, bf16[2,640,256]{2,1,0:T(8,128)(2,1)}, u32[]{:S(2)}, u32[]{:S(2)}) collective-permute-start(bf16[2,640,256]{2,1,0:T(8,128)(2,1)} %get-tuple-element.122), channel_id=1, source_target_pairs={{0,3},{1,2},{2,1},{3,0},{4,7},{5,6},{6,5},{7,4}} | collective-permute-start | bytes 1966088 | tf_op jit(solution)/shard_map/ppermute | solution.py:328
  1916.5 29.4 %collective-permute-start.45 = (bf16[2,640,256]{2,1,0:T(8,128)(2,1)}, bf16[2,640,256]{2,1,0:T(8,128)(2,1)}, u32[]{:S(2)}, u32[]{:S(2)}) collective-permute-start(bf16[2,640,256]{2,1,0:T(8,128)(2,1)} %get-tuple-element.133), channel_id=1, source_target_pairs={{0,1},{1,0},{2,3},{3,2},{4,5},{5,4},{6,7},{7,6}} | collective-permute-start | bytes 1966088 | tf_op jit(solution)/shard_map/ppermute | solution.py:328
  1928.4 30.0 %collective-permute-start.46 = (bf16[2,640,256]{2,1,0:T(8,128)(2,1)}, bf16[2,640,256]{2,1,0:T(8,128)(2,1)}, u32[]{:S(2)}, u32[]{:S(2)}) collective-permute-start(bf16[2,640,256]{2,1,0:T(8,128)(2,1)} %get-tuple-element.134), channel_id=1, source_target_pairs={{0,2},{1,3},{2,0},{3,1},{4,6},{5,7},{6,4},{7,5}} | collective-permute-start | bytes 1966088 | tf_op jit(solution)/shard_map/ppermute | solution.py:328
  1929.8 42.8 %collective-permute-start.47 = (bf16[2,640,256]{2,1,0:T(8,128)(2,1)}, bf16[2,640,256]{2,1,0:T(8,128)(2,1)}, u32[]{:S(2)}, u32[]{:S(2)}) collective-permute-start(bf16[2,640,256]{2,1,0:T(8,128)(2,1)} %get-tuple-element.135), channel_id=1, source_target_pairs={{0,3},{1,2},{2,1},{3,0},{4,7},{5,6},{6,5},{7,4}} | collective-permute-start | bytes 1966088 | tf_op jit(solution)/shard_map/ppermute | solution.py:328
  1937.1 50.9 %collective-permute-start.7 = (bf16[1,2816,128]{2,1,0:T(8,128)(2,1)S(1)}, bf16[1,2816,128]{2,1,0:T(8,128)(2,1)S(1)}, u32[]{:S(2)}, u32[]{:S(2)}) collective-permute-start(bf16[1,2816,128]{2,1,0:T(8,128)(2,1)S(1)} %copy-done.30), channel_id=1, source_target_pairs={{0,4},{4,0},{1,5},{5,1},{2,6},{6,2},{3,7},{7,3}} | collective-permute-start | bytes 2162696 | tf_op jit(solution)/shard_map/ppermute | solution.py:332
  1945.1 56.0 %collective-permute-start.6 = (bf16[1,2816,128]{2,1,0:T(8,128)(2,1)S(1)}, bf16[1,2816,128]{2,1,0:T(8,128)(2,1)S(1)}, u32[]{:S(2)}, u32[]{:S(2)}) collective-permute-start(bf16[1,2816,128]{2,1,0:T(8,128)(2,1)S(1)} %copy-done.29), channel_id=1, source_target_pairs={{0,4},{4,0},{1,5},{5,1},{2,6},{6,2},{3,7},{7,3}} | collective-permute-start | bytes 2162696 | tf_op jit(solution)/shard_map/ppermute | solution.py:332
  1945.9 69.8 %collective-permute-start.58 = (bf16[2,640,256]{2,1,0:T(8,128)(2,1)}, bf16[2,640,256]{2,1,0:T(8,128)(2,1)}, u32[]{:S(2)}, u32[]{:S(2)}) collective-permute-start(bf16[2,640,256]{2,1,0:T(8,128)(2,1)} %get-tuple-element.161), channel_id=1, source_target_pairs={{0,1},{1,0},{2,3},{3,2},{4,5},{5,4},{6,7},{7,6}} | collective-permute-start | bytes 1966088 | tf_op jit(solution)/shard_map/ppermute | solution.py:328
  1958.4 57.8 %collective-permute-start.59 = (bf16[2,640,256]{2,1,0:T(8,128)(2,1)}, bf16[2,640,256]{2,1,0:T(8,128)(2,1)}, u32[]{:S(2)}, u32[]{:S(2)}) collective-permute-start(bf16[2,640,256]{2,1,0:T(8,128)(2,1)} %get-tuple-element.162), channel_id=1, source_target_pairs={{0,2},{1,3},{2,0},{3,1},{4,6},{5,7},{6,4},{7,5}} | collective-permute-start | bytes 1966088 | tf_op jit(solution)/shard_map/ppermute | solution.py:328
  1972.7 44.7 %collective-permute-start.60 = (bf16[2,640,256]{2,1,0:T(8,128)(2,1)}, bf16[2,640,256]{2,1,0:T(8,128)(2,1)}, u32[]{:S(2)}, u32[]{:S(2)}) collective-permute-start(bf16[2,640,256]{2,1,0:T(8,128)(2,1)} %get-tuple-element.163), channel_id=1, source_target_pairs={{0,3},{1,2},{2,1},{3,0},{4,7},{5,6},{6,5},{7,4}} | collective-permute-start | bytes 1966088 | tf_op jit(solution)/shard_map/ppermute | solution.py:328
  2001.1 7.5 collective-permute-start.55
  2001.2 28.9 %collective-permute-start.56 = (bf16[2,640,128]{2,1,0:T(8,128)(2,1)}, bf16[2,640,128]{2,1,0:T(8,128)(2,1)S(1)}, u32[]{:S(2)}, u32[]{:S(2)}) collective-permute-start(bf16[2,640,128]{2,1,0:T(8,128)(2,1)} %get-tuple-element.158), channel_id=1, source_target_pairs={{0,2},{1,3},{2,0},{3,1},{4,6},{5,7},{6,4},{7,5}} | collective-permute-start | bytes 983048 | tf_op jit(solution)/shard_map/ppermute | solution.py:328
  2008.6 21.4 %collective-permute-start.57 = (bf16[2,640,128]{2,1,0:T(8,128)(2,1)}, bf16[2,640,128]{2,1,0:T(8,128)(2,1)}, u32[]{:S(2)}, u32[]{:S(2)}) collective-permute-start(bf16[2,640,128]{2,1,0:T(8,128)(2,1)} %get-tuple-element.159), channel_id=1, source_target_pairs={{0,3},{1,2},{2,1},{3,0},{4,7},{5,6},{6,5},{7,4}} | collective-permute-start | bytes 983048 | tf_op jit(solution)/shard_map/ppermute | solution.py:328
  2015.7 24.0 %collective-permute-start.52 = (bf16[2,640,128]{2,1,0:T(8,128)(2,1)}, bf16[2,640,128]{2,1,0:T(8,128)(2,1)S(1)}, u32[]{:S(2)}, u32[]{:S(2)}) collective-permute-start(bf16[2,640,128]{2,1,0:T(8,128)(2,1)} %get-tuple-element.153), channel_id=1, source_target_pairs={{0,1},{1,0},{2,3},{3,2},{4,5},{5,4},{6,7},{7,6}} | collective-permute-start | bytes 983048 | tf_op jit(solution)/shard_map/ppermute | solution.py:328
  2016.2 23.5 %collective-permute-start.53 = (bf16[2,640,128]{2,1,0:T(8,128)(2,1)}, bf16[2,640,128]{2,1,0:T(8,128)(2,1)S(1)}, u32[]{:S(2)}, u32[]{:S(2)}) collective-permute-start(bf16[2,640,128]{2,1,0:T(8,128)(2,1)} %get-tuple-element.154), channel_id=1, source_target_pairs={{0,2},{1,3},{2,0},{3,1},{4,6},{5,7},{6,4},{7,5}} | collective-permute-start | bytes 983048 | tf_op jit(solution)/shard_map/ppermute | solution.py:328
  2017.3 22.4 %collective-permute-start.54 = (bf16[2,640,128]{2,1,0:T(8,128)(2,1)}, bf16[2,640,128]{2,1,0:T(8,128)(2,1)S(1)}, u32[]{:S(2)}, u32[]{:S(2)}) collective-permute-start(bf16[2,640,128]{2,1,0:T(8,128)(2,1)} %get-tuple-element.155), channel_id=1, source_target_pairs={{0,3},{1,2},{2,1},{3,0},{4,7},{5,6},{6,5},{7,4}} | collective-permute-start | bytes 983048 | tf_op jit(solution)/shard_map/ppermute | solution.py:328
  (53 other events, 458.8 us)

commit v6 on v5

--- a/solution.py
+++ b/solution.py
@@ -15,6 +15,7 @@
 TN = 256
 TB = 512
 WIN = 256
+INFO = 128
 
 
 def mm(a, b):
@@ -209,15 +210,23 @@
     )(*args)
 
 
-def picked(k, groups, pos, gate, lo):
+def slot_of(info, e):
+    return info[0, :, e:e + 1].astype(jnp.int32)
+
+
+def gate_of(info, e):
+    return info[0, :, INFO // 2 + e:INFO // 2 + e + 1]
+
+
+def picked(k, groups, info, lo):
     slots = lax.broadcasted_iota(jnp.int32, (TB, WIN), 1)
     totals = [None] * len(groups)
     for m in range(MASKS):
         e = 2 * m + k
         at = pl.multiple_of(lo[m], 16)
-        onehot = (slots == pos[0, :, e:e + 1] - at).astype(BF16)
+        onehot = (slots == slot_of(info, e) - at).astype(BF16)
         for j, ys in enumerate(groups):
-            term = gate[0, :, e:e + 1] * mm(onehot, ys[m][0, pl.ds(at, WIN)])
+            term = gate_of(info, e) * mm(onehot, ys[m][0, pl.ds(at, WIN)])
             totals[j] = term if totals[j] is None else totals[j] + term
     return totals
 
@@ -226,11 +235,11 @@
     total = refs[-1]
     refs = refs[:-2] if held else refs[:-1]
     groups = [refs[MASKS * j:MASKS * (j + 1)] for j in range(n)]
-    pos, gate = refs[MASKS * n:MASKS * n + 2]
+    info = refs[MASKS * n]
     cap, cols = groups[0][0].shape[1:]
     i, blocks = pl.program_id(0), pl.num_programs(0) // 2
     begin = [(jnp.minimum(first[i * MASKS + m], cap - WIN) // 16) * 16 for m in range(MASKS)]
-    for j, part in enumerate(picked(k, groups, pos, gate, begin)):
+    for j, part in enumerate(picked(k, groups, info, begin)):
         total[:, j * cols:(j + 1) * cols] = part
     slots = lax.broadcasted_iota(jnp.int32, (TB, WIN), 1)
     for m in range(MASKS):
@@ -242,10 +251,10 @@
             def more(step, carry):
                 lo = begin[m] + WIN + step * WIN
                 at = pl.multiple_of(jnp.minimum(lo, cap - WIN), 16)
-                mine = pos[0, :, e:e + 1]
+                mine = slot_of(info, e)
                 onehot = (slots == jnp.where(mine >= lo, mine - at, -1)).astype(BF16)
                 for j, ys in enumerate(groups):
-                    total[:, j * cols:(j + 1) * cols] += gate[0, :, e:e + 1] * mm(onehot, ys[m][0, pl.ds(at, WIN)])
+                    total[:, j * cols:(j + 1) * cols] += gate_of(info, e) * mm(onehot, ys[m][0, pl.ds(at, WIN)])
                 return carry
 
             lax.fori_loop(0, (end - begin[m] - 1) // WIN, more, 0)
@@ -253,7 +262,7 @@
     if k == 0:
         refs[-1][...] = total[...]
         return
-    result = (refs[MASKS * n + 2][...] + total[...]).astype(BF16)
+    result = (refs[MASKS * n + 1][...] + total[...]).astype(BF16)
     for b, out in enumerate(refs[-2:]):
 
         @pl.when(i // blocks == b)
@@ -262,15 +271,15 @@
 
 
 def combine(groups, table, k, lo, model, acc=None, into=None, held=None):
-    pos, gate, first, last = table
+    info, first, last = table
     _, cap, cols = groups[0][0].shape
     n, wide = len(groups), cols * len(groups)
-    toks = pos.shape[1]
+    toks = info.shape[1]
     blocks = toks // TB
     at = lo // wide
-    args = [first[k], last[k]] + [y for ys in groups for y in ys] + [pos, gate]
+    args = [first[k], last[k]] + [y for ys in groups for y in ys] + [info]
     in_specs = [pl.BlockSpec((1, cap, cols), lambda i, *_: (i // blocks, 0, 0))] * (MASKS * n)
-    in_specs += [pl.BlockSpec((1, TB, pos.shape[2]), lambda i, *_: (i // blocks, i % blocks, 0))] * 2
+    in_specs += [pl.BlockSpec((1, TB, INFO), lambda i, *_: (i // blocks, i % blocks, 0))]
     aliases = {}
     if k == 0:
         if into is not None:
@@ -322,7 +331,7 @@
     late = [(1, n) for n in range(9)]
     halves = [(1, n) for n in range(5, 9)]
     after = {(1, 2): [[(1, 0), (1, 1)]], (1, 4): [[(1, 2)]], (1, 5): [[(1, 3)]], (1, 6): [[(1, 4), (1, 5)]]}
-    after[1, 8] = [[(1, 6)], [(1, 7)], [(1, 8)]]
+    after[1, 8] = [[(1, 6)], [(1, 7), (1, 8)]]
 
     def ep_swap(value, mask):
         return lax.ppermute(value, "ep", [(i, i ^ mask) for i in range(ep_size)])
@@ -367,7 +376,8 @@
             down[k][n] = tp_swap(w_down, k, lo, hi)
 
         pos, gate, cap, first, last = routing(jnp.stack([ids_a, ids_b]), jnp.stack([gates_a, gates_b]), me)
-        table = pos.transpose(0, 2, 1), gate.transpose(0, 2, 1), first, last
+        info = [jnp.pad(a, ((0, 0), (0, INFO // 2 - a.shape[1]), (0, 0))) for a in (pos.astype(F32), gate)]
+        table = jnp.concatenate(info, axis=1).transpose(0, 2, 1), first, last
 
         xs = []
         for b, tokens in enumerate((tokens_a, tokens_b)):

time: 2060 us -> 2060 us (level)
    unnamed x112 -> x96, local copies, waits for them, and re-layouts: 82.3 us -> 66.7 us
    pallas_call x10 -> x9, Pallas kernels: 124 us -> 115 us  [combine(): call(functools.partial(combine_kernel, k, n, held is not None), 2 * 2 * t...]
  transfers between devices with their start and end apart: 61 -> 61, of which waited for: 11 -> 14; matrix products, arithmetic and copies ran while one was open for 3% -> 3% of each run, Pallas kernels for 54% -> 54%
where the time goes in v6:
time: 2060 us; the launch traced here: 2050 us
  Pallas kernels  1140 us (55%)
  waiting for transfers between devices  701 us (34%)
  local copies, waits for them, and re-layouts  137 us (7%)
  starting transfers between devices  56.4 us (3%)
    ppermute x19, waiting for transfers between devices, tp_swap(): return lax.ppermute(piece, 'tp', TP_SWAP)[0]  386 us
    ppermute x42, waiting for transfers between devices, ep_swap(): return lax.ppermute(value, 'ep', [(i, i ^ mask) for i in range(ep_size)])  315 us
    pallas_call x2, Pallas kernels, hidden_local(): call(functools.partial(hidden_kernel, None, 0), 4 * rows * model * width,...  260 us
    pallas_call x8, Pallas kernels, hidden(): call(functools.partial(hidden_kernel, b, off), *cost, 33, grid=(steps,),...  162 us
    pallas_call x2, Pallas kernels, part(): call(part_kernel, 2 * rows * width * model, 2 * (rows * width + 2 * width...  146 us
    pallas_call x2, Pallas kernels, hidden(): call(functools.partial(hidden_kernel, None, 0), *cost, grid=(steps,), in_...  135 us
    pallas_call x4, Pallas kernels, dispatch(): call(dispatch_kernel, 2 * n * 2 * cap * toks * model, toks * model * 2 +...  125 us
    pallas_call x9, Pallas kernels, combine(): call(functools.partial(combine_kernel, k, n, held is not None), 2 * 2 * t...  115 us
  transfers between devices with their start and end apart: 61, of which 14 were waited for; matrix products, arithmetic and copies ran while one was open for 3% of the time, Pallas kernels for 54%

profile of v6, /device:TPU:0, one launch (start us, length us, event | category | flops | bytes accessed | tf_op | source)
XLA Modules:
  0.0 2048.5 jit_solution(12128221390311385148)
XLA Ops:
  15.1 31.2 %shard_map.104 = (bf16[2,640,2048]{2,1,0:T(8,128)(2,1)}, bf16[2,640,2048]{2,1,0:T(8,128)(2,1)}) custom-call(s32[4,1,2048]{2,1,0:T(1,128)} %copy.93.pos_ref, bf16[2048,2048]{1,0:T(8,128)(2,1)} %tok_ref.5), custom_call_target="tpu_custom_call" | custom-call | flops 21474836480 | bytes 18874368 | tf_op jit(solution)/shard_map/pallas_call | solution.py:63
  49.2 31.1 %shard_map.105 = (bf16[2,640,2048]{2,1,0:T(8,128)(2,1)}, bf16[2,640,2048]{2,1,0:T(8,128)(2,1)}) custom-call(s32[4,1,2048]{2,1,0:T(1,128)} %copy.94.pos_ref, bf16[2048,2048]{1,0:T(8,128)(2,1)} %tok_ref.5), custom_call_target="tpu_custom_call" | custom-call | flops 21474836480 | bytes 18874368 | tf_op jit(solution)/shard_map/pallas_call | solution.py:63
  83.9 31.3 %shard_map.107 = (bf16[2,640,2048]{2,1,0:T(8,128)(2,1)}, bf16[2,640,2048]{2,1,0:T(8,128)(2,1)}) custom-call(s32[4,1,2048]{2,1,0:T(1,128)} %copy.95.pos_ref, bf16[2048,2048]{1,0:T(8,128)(2,1)} %tok_ref.7), custom_call_target="tpu_custom_call" | custom-call | flops 21474836480 | bytes 18874368 | tf_op jit(solution)/shard_map/pallas_call | solution.py:63
  116.3 31.2 %shard_map.108 = (bf16[2,640,2048]{2,1,0:T(8,128)(2,1)}, bf16[2,640,2048]{2,1,0:T(8,128)(2,1)}) custom-call(s32[4,1,2048]{2,1,0:T(1,128)} %copy.96.pos_ref, bf16[2048,2048]{1,0:T(8,128)(2,1)} %tok_ref.7), custom_call_target="tpu_custom_call" | custom-call | flops 21474836480 | bytes 18874368 | tf_op jit(solution)/shard_map/pallas_call | solution.py:63
  165.5 9.8 slice.148
  179.0 6.4 slice.151
  190.0 5.7 fusion.6
  195.7 8.2 fusion.5
  205.9 8.0 fusion.7
  215.5 93.6 %collective-permute-done.2.refs_3_ = bf16[2,640,2048]{2,1,0:T(8,128)(2,1)} collective-permute-done((bf16[2,640,2048]{2,1,0:T(8,128)(2,1)}, bf16[2,640,2048]{2,1,0:T(8,128)(2,1)}, u32[]{:S(2)}, u32[]{:S(2)}) %collective-permute-start.2) | collective-permute-done | bytes 5242912 | tf_op jit(solution)/shard_map/ppermute | solution.py:337
  310.6 130.0 %shard_map.106.h = bf16[2,4,640,2816]{3,2,1,0:T(8,128)(2,1)} custom-call(bf16[2,640,2048]{2,1,0:T(8,128)(2,1)} %get-tuple-element.84.refs_0_, bf16[2,640,2048]{2,1,0:T(8,128)(2,1)} %collective-permute-done.refs_1_, bf16[2,640,2048]{2,1,0:T(8,128)(2,1)} %collective-permute-done.1.refs_2_, bf16[2,640,2048]{2,1,0:T(8,128)(2,1)} %collective-permute-done.2.refs_3_, ...), custom_call_target="tpu_custom_call" | custom-call | flops 118111600640 | bytes 95944704 | tf_op jit(solution)/shard_map/pallas_call | solution.py:90
  442.6 91.1 %collective-permute-done.5.refs_3_ = bf16[2,640,2048]{2,1,0:T(8,128)(2,1)} collective-permute-done((bf16[2,640,2048]{2,1,0:T(8,128)(2,1)}, bf16[2,640,2048]{2,1,0:T(8,128)(2,1)}, u32[]{:S(2)}, u32[]{:S(2)}) %collective-permute-start.5) | collective-permute-done | bytes 5242912 | tf_op jit(solution)/shard_map/ppermute | solution.py:337
  535.3 129.6 %shard_map.109.h = bf16[2,4,640,2816]{3,2,1,0:T(8,128)(2,1)} custom-call(bf16[2,640,2048]{2,1,0:T(8,128)(2,1)} %get-tuple-element.88.refs_0_, bf16[2,640,2048]{2,1,0:T(8,128)(2,1)} %collective-permute-done.3.refs_1_, bf16[2,640,2048]{2,1,0:T(8,128)(2,1)} %collective-permute-done.4.refs_2_, bf16[2,640,2048]{2,1,0:T(8,128)(2,1)} %collective-permute-done.5.refs_3_, ...), custom_call_target="tpu_custom_call" | custom-call | flops 118111600640 | bytes 95944704 | tf_op jit(solution)/shard_map/pallas_call | solution.py:90
  664.9 72.8 %shard_map.110.refs_0_ = f32[2,2,4,640,2048]{4,3,2,1,0:T(8,128)} custom-call(bf16[2,4,640,2816]{3,2,1,0:T(8,128)(2,1)} %shard_map.109.h, bf16[2,2816,2048]{2,1,0:T(8,128)(2,1)} %wd.3), custom_call_target="tpu_custom_call" | custom-call | flops 59055800320 | bytes 93847552 | tf_op jit(solution)/shard_map/pallas_call | solution.py:140
  737.7 72.9 %shard_map.111.p = f32[2,2,4,640,2048]{4,3,2,1,0:T(8,128)} custom-call(bf16[2,4,640,2816]{3,2,1,0:T(8,128)(2,1)} %shard_map.106.h, bf16[2,2816,2048]{2,1,0:T(8,128)(2,1)} %wd.3, f32[2,2,4,640,2048]{4,3,2,1,0:T(8,128)} %shard_map.110.refs_0_), custom_call_target="tpu_custom_call", output_to_operand_aliasing={{}: (2, {})} | custom-call | flops 59055800320 | bytes 93847552 | tf_op jit(solution)/shard_map/pallas_call | solution.py:140
  812.7 10.2 shard_map.112.refs_6_
  822.9 10.2 shard_map.113.refs_6_
  833.1 9.5 copy-done
  843.2 233.8 %collective-permute-done.23 = bf16[1,2048,2816]{2,1,0:T(8,128)(2,1)} collective-permute-done((bf16[1,2048,2816]{2,1,0:T(8,128)(2,1)}, bf16[1,2048,2816]{2,1,0:T(8,128)(2,1)}, u32[]{:S(2)}, u32[]{:S(2)}) %collective-permute-start.23) | collective-permute-done | bytes 11534368 | tf_op jit(solution)/shard_map/ppermute | solution.py:341
  1078.5 67.6 %shard_map.122.refs_6_ = bf16[2,4,640,2816]{3,2,1,0:T(8,128)(2,1)} custom-call(bf16[2,640,2048]{2,1,0:T(8,128)(2,1)} %get-tuple-element.88.refs_0_, bf16[2,640,2048]{2,1,0:T(8,128)(2,1)} %collective-permute-done.3.refs_1_, bf16[2,640,2048]{2,1,0:T(8,128)(2,1)} %collective-permute-done.4.refs_2_, bf16[2,640,2048]{2,1,0:T(8,128)(2,1)} %collective-permute-done.5.refs_3_, ...), custom_call_target="tpu_custom_call" | custom-call | flops 59055800320 | bytes 47972352 | tf_op jit(solution)/shard_map/pallas_call | solution.py:120
  1146.1 67.8 %shard_map.123.h0.h1 = bf16[2,4,640,2816]{3,2,1,0:T(8,128)(2,1)} custom-call(bf16[2,640,2048]{2,1,0:T(8,128)(2,1)} %get-tuple-element.84.refs_0_, bf16[2,640,2048]{2,1,0:T(8,128)(2,1)} %collective-permute-done.refs_1_, bf16[2,640,2048]{2,1,0:T(8,128)(2,1)} %collective-permute-done.1.refs_2_, ...), custom_call_target="tpu_custom_call", output_to_operand_aliasing={{}: (6, {})} | custom-call | flops 59055800320 | bytes 47972352 | tf_op jit(solution)/shard_map/pallas_call | solution.py:120
  1213.9 87.8 %collective-permute-done.13 = bf16[1,2048,1280]{2,1,0:T(8,128)(2,1)} collective-permute-done((bf16[1,2048,1280]{2,1,0:T(8,128)(2,1)}, bf16[1,2048,1280]{2,1,0:T(8,128)(2,1)}, u32[]{:S(2)}, u32[]{:S(2)}) %collective-permute-start.13) | collective-permute-done | bytes 5242912 | tf_op jit(solution)/shard_map/ppermute | solution.py:341
  1303.2 9.2 copy-done.1
  1312.4 32.8 %shard_map.114.refs_6_ = bf16[2,4,640,2816]{3,2,1,0:T(8,128)(2,1)S(1)} custom-call(bf16[2,640,2048]{2,1,0:T(8,128)(2,1)} %get-tuple-element.88.refs_0_, bf16[2,640,2048]{2,1,0:T(8,128)(2,1)} %collective-permute-done.3.refs_1_, bf16[2,640,2048]{2,1,0:T(8,128)(2,1)} %collective-permute-done.4.refs_2_, ...), custom_call_target="tpu_custom_call", output_to_operand_aliasing={{}: (6, {})} | custom-call | flops 26843545600 | bytes 27525120 | tf_op jit(solution)/shard_map/pallas_call | solution.py:113
  1345.2 32.8 %shard_map.115.refs_6_ = bf16[2,4,640,2816]{3,2,1,0:T(8,128)(2,1)S(1)} custom-call(bf16[2,640,2048]{2,1,0:T(8,128)(2,1)} %get-tuple-element.84.refs_0_, bf16[2,640,2048]{2,1,0:T(8,128)(2,1)} %collective-permute-done.refs_1_, bf16[2,640,2048]{2,1,0:T(8,128)(2,1)} %collective-permute-done.1.refs_2_, ...), custom_call_target="tpu_custom_call", output_to_operand_aliasing={{}: (6, {})} | custom-call | flops 26843545600 | bytes 27525120 | tf_op jit(solution)/shard_map/pallas_call | solution.py:113
  1378.5 21.9 %shard_map.116.refs_6_ = bf16[2,4,640,2816]{3,2,1,0:T(8,128)(2,1)S(1)} custom-call(bf16[2,640,2048]{2,1,0:T(8,128)(2,1)} %get-tuple-element.88.refs_0_, bf16[2,640,2048]{2,1,0:T(8,128)(2,1)} %collective-permute-done.3.refs_1_, bf16[2,640,2048]{2,1,0:T(8,128)(2,1)} %collective-permute-done.4.refs_2_, ...), custom_call_target="tpu_custom_call", output_to_operand_aliasing={{}: (6, {})} | custom-call | flops 16106127360 | bytes 20709376 | tf_op jit(solution)/shard_map/pallas_call | solution.py:113
  1400.5 21.6 %shard_map.117.refs_6_ = bf16[2,4,640,2816]{3,2,1,0:T(8,128)(2,1)S(1)} custom-call(bf16[2,640,2048]{2,1,0:T(8,128)(2,1)} %get-tuple-element.84.refs_0_, bf16[2,640,2048]{2,1,0:T(8,128)(2,1)} %collective-permute-done.refs_1_, bf16[2,640,2048]{2,1,0:T(8,128)(2,1)} %collective-permute-done.1.refs_2_, ...), custom_call_target="tpu_custom_call", output_to_operand_aliasing={{}: (6, {})} | custom-call | flops 16106127360 | bytes 20709376 | tf_op jit(solution)/shard_map/pallas_call | solution.py:113
  1423.6 15.9 shard_map.118.refs_6_
  1439.5 16.2 shard_map.119.h
  1456.3 11.5 shard_map.120
  1467.8 9.5 copy-done.2
  1477.3 42.1 %shard_map.126 = (bf16[2,640,1024]{2,1,0:T(8,128)(2,1)}, bf16[2,640,1024]{2,1,0:T(8,128)(2,1)}, bf16[2,640,1024]{2,1,0:T(8,128)(2,1)}, bf16[2,640,1024]{2,1,0:T(8,128)(2,1)}) custom-call(bf16[2,4,640,2816]{3,2,1,0:T(8,128)(2,1)} %shard_map.123.h0.h1, bf16[2,4,640,2816]{3,2,1,0:T(8,128)(2,1)} %shard_map.123.h0.h1, f32[2,2,4,640,2048]{4,3,2,1,0:T(8,128)} %shard_map.111.p, ...), custom_call_target="tpu_custom_call" | custom-call | flops 29527900160 | bytes 66060288 | tf_op jit(solution)/shard_map/pallas_call | solution.py:164
  1521.3 24.4 %shard_map.124 = (bf16[2,640,512]{2,1,0:T(8,128)(2,1)}, bf16[2,640,512]{2,1,0:T(8,128)(2,1)}, bf16[2,640,512]{2,1,0:T(8,128)(2,1)}, bf16[2,640,512]{2,1,0:T(8,128)(2,1)}) custom-call(bf16[2,4,640,2816]{3,2,1,0:T(8,128)(2,1)} %shard_map.123.h0.h1, bf16[2,4,640,2816]{3,2,1,0:T(8,128)(2,1)} %shard_map.123.h0.h1, f32[2,2,4,640,2048]{4,3,2,1,0:T(8,128)} %shard_map.111.p, ...), custom_call_target="tpu_custom_call" | custom-call | flops 14763950080 | bytes 47448064 | tf_op jit(solution)/shard_map/pallas_call | solution.py:164
  1545.7 64.5 %collective-permute-done.36 = bf16[1,2816,256]{2,1,0:T(8,128)(2,1)} collective-permute-done((bf16[1,2816,256]{2,1,0:T(8,128)(2,1)S(1)}, bf16[1,2816,256]{2,1,0:T(8,128)(2,1)}, u32[]{:S(2)}, u32[]{:S(2)}) %collective-permute-start.36) | collective-permute-done | bytes 1441824 | tf_op jit(solution)/shard_map/ppermute | solution.py:341
  1613.6 9.2 copy-done.3
  1622.8 11.4 shard_map.121
  1634.3 9.5 copy-done.4
  1645.9 24.2 %shard_map.125 = (bf16[2,640,512]{2,1,0:T(8,128)(2,1)}, bf16[2,640,512]{2,1,0:T(8,128)(2,1)}, bf16[2,640,512]{2,1,0:T(8,128)(2,1)}, bf16[2,640,512]{2,1,0:T(8,128)(2,1)}) custom-call(bf16[2,4,640,2816]{3,2,1,0:T(8,128)(2,1)} %shard_map.123.h0.h1, bf16[2,4,640,2816]{3,2,1,0:T(8,128)(2,1)} %shard_map.123.h0.h1, f32[2,2,4,640,2048]{4,3,2,1,0:T(8,128)} %shard_map.111.p, ...), custom_call_target="tpu_custom_call" | custom-call | flops 14763950080 | bytes 47448064 | tf_op jit(solution)/shard_map/pallas_call | solution.py:164
  1670.7 55.6 %collective-permute-done.26.refs_2_ = bf16[2,640,512]{2,1,0:T(8,128)(2,1)S(1)} collective-permute-done((bf16[2,640,512]{2,1,0:T(8,128)(2,1)}, bf16[2,640,512]{2,1,0:T(8,128)(2,1)S(1)}, u32[]{:S(2)}, u32[]{:S(2)}) %collective-permute-start.26) | collective-permute-done | bytes 1310752 | tf_op jit(solution)/shard_map/ppermute | solution.py:337
  1729.2 9.2 copy-done.5
  1738.4 11.5 shard_map.130
  1753.4 19.1 shard_map.127.refs_5_
  1772.6 10.0 collective-permute-done.30.refs_2_
  1784.3 25.6 %collective-permute-done.31.refs_3_ = bf16[2,640,512]{2,1,0:T(8,128)(2,1)} collective-permute-done((bf16[2,640,512]{2,1,0:T(8,128)(2,1)}, bf16[2,640,512]{2,1,0:T(8,128)(2,1)}, u32[]{:S(2)}, u32[]{:S(2)}) %collective-permute-start.31) | collective-permute-done | bytes 1310752 | tf_op jit(solution)/shard_map/ppermute | solution.py:337
  1811.8 12.1 shard_map.128.refs_5_
  1825.4 10.9 shard_map.129.refs_9_.refs_5_
  1839.2 14.4 shard_map.131
  1854.1 11.6 shard_map.132
  1867.4 11.5 shard_map.133
  1885.4 11.5 shard_map.134
  1898.1 6.6 shard_map.135
  1905.3 6.6 shard_map.136
  1915.5 11.5 shard_map.137
  1929.1 7.1 shard_map.138
  1937.8 6.7 shard_map.139
  1946.1 11.5 collective-permute-done.45.refs_6_
  1959.5 11.7 collective-permute-done.46.refs_7_
  1973.0 14.4 shard_map.140
  1988.3 6.1 shard_map.141
  1994.4 6.1 shard_map.142
  2001.4 6.1 shard_map.143
  2007.6 6.5 shard_map.144
  2017.0 10.8 shard_map.145
  2037.7 10.4 shard_map.146
  (241 shorter events, 125.2 us)
Async XLA Ops:
  46.3 167.6 %collective-permute-start = (bf16[2,640,2048]{2,1,0:T(8,128)(2,1)}, bf16[2,640,2048]{2,1,0:T(8,128)(2,1)}, u32[]{:S(2)}, u32[]{:S(2)}) collective-permute-start(bf16[2,640,2048]{2,1,0:T(8,128)(2,1)} %get-tuple-element.85), channel_id=1, source_target_pairs={{0,1},{1,0},{2,3},{3,2},{4,5},{5,4},{6,7},{7,6}} | collective-permute-start | bytes 15728648 | tf_op jit(solution)/shard_map/ppermute | solution.py:337
  80.4 133.5 %collective-permute-start.1 = (bf16[2,640,2048]{2,1,0:T(8,128)(2,1)}, bf16[2,640,2048]{2,1,0:T(8,128)(2,1)}, u32[]{:S(2)}, u32[]{:S(2)}) collective-permute-start(bf16[2,640,2048]{2,1,0:T(8,128)(2,1)} %get-tuple-element.86), channel_id=1, source_target_pairs={{0,2},{1,3},{2,0},{3,1},{4,6},{5,7},{6,4},{7,5}} | collective-permute-start | bytes 15728648 | tf_op jit(solution)/shard_map/ppermute | solution.py:337
  82.9 226.2 %collective-permute-start.2 = (bf16[2,640,2048]{2,1,0:T(8,128)(2,1)}, bf16[2,640,2048]{2,1,0:T(8,128)(2,1)}, u32[]{:S(2)}, u32[]{:S(2)}) collective-permute-start(bf16[2,640,2048]{2,1,0:T(8,128)(2,1)} %get-tuple-element.87), channel_id=1, source_target_pairs={{0,3},{1,2},{2,1},{3,0},{4,7},{5,6},{6,5},{7,4}} | collective-permute-start | bytes 15728648 | tf_op jit(solution)/shard_map/ppermute | solution.py:337
  115.3 325.3 %collective-permute-start.3 = (bf16[2,640,2048]{2,1,0:T(8,128)(2,1)}, bf16[2,640,2048]{2,1,0:T(8,128)(2,1)}, u32[]{:S(2)}, u32[]{:S(2)}) collective-permute-start(bf16[2,640,2048]{2,1,0:T(8,128)(2,1)} %get-tuple-element.89), channel_id=1, source_target_pairs={{0,1},{1,0},{2,3},{3,2},{4,5},{5,4},{6,7},{7,6}} | collective-permute-start | bytes 15728648 | tf_op jit(solution)/shard_map/ppermute | solution.py:337
  147.6 293.6 %collective-permute-start.4 = (bf16[2,640,2048]{2,1,0:T(8,128)(2,1)}, bf16[2,640,2048]{2,1,0:T(8,128)(2,1)}, u32[]{:S(2)}, u32[]{:S(2)}) collective-permute-start(bf16[2,640,2048]{2,1,0:T(8,128)(2,1)} %get-tuple-element.90), channel_id=1, source_target_pairs={{0,2},{1,3},{2,0},{3,1},{4,6},{5,7},{6,4},{7,5}} | collective-permute-start | bytes 15728648 | tf_op jit(solution)/shard_map/ppermute | solution.py:337
  186.0 1639.4 %copy-start.6 = (f32[2,2048,128]{2,1,0:T(8,128)}, f32[2,2048,128]{2,1,0:T(8,128)S(1)}, u32[]{:S(2)}) copy-start(f32[2,2048,128]{2,1,0:T(8,128)S(1)} %fusion.refs_4_.refs_8_) | copy-start | bytes 6291460
  213.9 319.9 %collective-permute-start.5 = (bf16[2,640,2048]{2,1,0:T(8,128)(2,1)}, bf16[2,640,2048]{2,1,0:T(8,128)(2,1)}, u32[]{:S(2)}, u32[]{:S(2)}) collective-permute-start(bf16[2,640,2048]{2,1,0:T(8,128)(2,1)} %get-tuple-element.91), channel_id=1, source_target_pairs={{0,3},{1,2},{2,1},{3,0},{4,7},{5,6},{6,5},{7,4}} | collective-permute-start | bytes 15728648 | tf_op jit(solution)/shard_map/ppermute | solution.py:337
  213.9 1241.8 %collective-permute-start.9 = (bf16[1,2816,256]{2,1,0:T(8,128)(2,1)}, bf16[1,2816,256]{2,1,0:T(8,128)(2,1)}, u32[]{:S(2)}, u32[]{:S(2)}) collective-permute-start(bf16[1,2816,256]{2,1,0:T(8,128)(2,1)} %get-tuple-element.174), channel_id=1, source_target_pairs={{0,4},{4,0},{1,5},{5,1},{2,6},{6,2},{3,7},{7,3}} | collective-permute-start | bytes 4325384 | tf_op jit(solution)/shard_map/ppermute | solution.py:341
  309.1 502.1 %collective-permute-start.10 = (bf16[1,2048,2816]{2,1,0:T(8,128)(2,1)}, bf16[1,2048,2816]{2,1,0:T(8,128)(2,1)}, u32[]{:S(2)}, u32[]{:S(2)}) collective-permute-start(bf16[1,2048,2816]{2,1,0:T(8,128)(2,1)} %get-tuple-element.180), channel_id=1, source_target_pairs={{0,4},{4,0},{1,5},{5,1},{2,6},{6,2},{3,7},{7,3}} | collective-permute-start | bytes 34603016 | tf_op jit(solution)/shard_map/ppermute | solution.py:341
  440.6 370.1 %collective-permute-start.14 = (bf16[1,2048,256]{2,1,0:T(8,128)(2,1)}, bf16[1,2048,256]{2,1,0:T(8,128)(2,1)}, u32[]{:S(2)}, u32[]{:S(2)}) collective-permute-start(bf16[1,2048,256]{2,1,0:T(8,128)(2,1)} %slice.143), channel_id=1, source_target_pairs={{0,4},{4,0},{1,5},{5,1},{2,6},{6,2},{3,7},{7,3}} | collective-permute-start | bytes 3145736 | tf_op jit(solution)/shard_map/ppermute | solution.py:341
  441.1 401.5 %collective-permute-start.22 = (bf16[1,2048,2816]{2,1,0:T(8,128)(2,1)}, bf16[1,2048,2816]{2,1,0:T(8,128)(2,1)}, u32[]{:S(2)}, u32[]{:S(2)}) collective-permute-start(bf16[1,2048,2816]{2,1,0:T(8,128)(2,1)} %get-tuple-element.179), channel_id=1, source_target_pairs={{0,4},{4,0},{1,5},{5,1},{2,6},{6,2},{3,7},{7,3}} | collective-permute-start | bytes 34603016 | tf_op jit(solution)/shard_map/ppermute | solution.py:341
  533.8 543.2 %collective-permute-start.23 = (bf16[1,2048,2816]{2,1,0:T(8,128)(2,1)}, bf16[1,2048,2816]{2,1,0:T(8,128)(2,1)}, u32[]{:S(2)}, u32[]{:S(2)}) collective-permute-start(bf16[1,2048,2816]{2,1,0:T(8,128)(2,1)} %slice.148), channel_id=1, source_target_pairs={{0,4},{4,0},{1,5},{5,1},{2,6},{6,2},{3,7},{7,3}} | collective-permute-start | bytes 34603016 | tf_op jit(solution)/shard_map/ppermute | solution.py:341
  810.7 611.4 %collective-permute-start.11 = (bf16[1,2048,512]{2,1,0:T(8,128)(2,1)}, bf16[1,2048,512]{2,1,0:T(8,128)(2,1)}, u32[]{:S(2)}, u32[]{:S(2)}) collective-permute-start(bf16[1,2048,512]{2,1,0:T(8,128)(2,1)} %slice.140), channel_id=1, source_target_pairs={{0,4},{4,0},{1,5},{5,1},{2,6},{6,2},{3,7},{7,3}} | collective-permute-start | bytes 6291464 | tf_op jit(solution)/shard_map/ppermute | solution.py:341
  811.2 566.7 %collective-permute-start.12 = (bf16[1,2048,768]{2,1,0:T(8,128)(2,1)}, bf16[1,2048,768]{2,1,0:T(8,128)(2,1)}, u32[]{:S(2)}, u32[]{:S(2)}) collective-permute-start(bf16[1,2048,768]{2,1,0:T(8,128)(2,1)} %slice.141), channel_id=1, source_target_pairs={{0,4},{4,0},{1,5},{5,1},{2,6},{6,2},{3,7},{7,3}} | collective-permute-start | bytes 9437192 | tf_op jit(solution)/shard_map/ppermute | solution.py:341
  842.6 459.0 %collective-permute-start.13 = (bf16[1,2048,1280]{2,1,0:T(8,128)(2,1)}, bf16[1,2048,1280]{2,1,0:T(8,128)(2,1)}, u32[]{:S(2)}, u32[]{:S(2)}) collective-permute-start(bf16[1,2048,1280]{2,1,0:T(8,128)(2,1)} %slice.142), channel_id=1, source_target_pairs={{0,4},{4,0},{1,5},{5,1},{2,6},{6,2},{3,7},{7,3}} | collective-permute-start | bytes 15728648 | tf_op jit(solution)/shard_map/ppermute | solution.py:341
  1077.0 442.4 %collective-permute-start.18 = (bf16[1,2816,256]{2,1,0:T(8,128)(2,1)}, bf16[1,2816,256]{2,1,0:T(8,128)(2,1)}, u32[]{:S(2)}, u32[]{:S(2)}) collective-permute-start(bf16[1,2816,256]{2,1,0:T(8,128)(2,1)} %get-tuple-element.173), channel_id=1, source_target_pairs={{0,4},{4,0},{1,5},{5,1},{2,6},{6,2},{3,7},{7,3}} | collective-permute-start | bytes 4325384 | tf_op jit(solution)/shard_map/ppermute | solution.py:341
  1301.7 175.6 %collective-permute-start.32 = (bf16[1,2816,1024]{2,1,0:T(8,128)(2,1)}, bf16[1,2816,1024]{2,1,0:T(8,128)(2,1)}, u32[]{:S(2)}, u32[]{:S(2)}) collective-permute-start(bf16[1,2816,1024]{2,1,0:T(8,128)(2,1)} %slice.151), channel_id=1, source_target_pairs={{0,4},{4,0},{1,5},{5,1},{2,6},{6,2},{3,7},{7,3}} | collective-permute-start | bytes 17301512 | tf_op jit(solution)/shard_map/ppermute | solution.py:341
  1378.0 141.9 %collective-permute-start.24 = (bf16[1,2816,512]{2,1,0:T(8,128)(2,1)}, bf16[1,2816,512]{2,1,0:T(8,128)(2,1)}, u32[]{:S(2)}, u32[]{:S(2)}) collective-permute-start(bf16[1,2816,512]{2,1,0:T(8,128)(2,1)} %get-tuple-element.178), channel_id=1, source_target_pairs={{0,4},{4,0},{1,5},{5,1},{2,6},{6,2},{3,7},{7,3}} | collective-permute-start | bytes 8650760 | tf_op jit(solution)/shard_map/ppermute | solution.py:341
  1422.0 189.8 %collective-permute-start.28 = (bf16[1,2816,512]{2,1,0:T(8,128)(2,1)}, bf16[1,2816,512]{2,1,0:T(8,128)(2,1)}, u32[]{:S(2)}, u32[]{:S(2)}) collective-permute-start(bf16[1,2816,512]{2,1,0:T(8,128)(2,1)} %get-tuple-element.177), channel_id=1, source_target_pairs={{0,4},{4,0},{1,5},{5,1},{2,6},{6,2},{3,7},{7,3}} | collective-permute-start | bytes 8650760 | tf_op jit(solution)/shard_map/ppermute | solution.py:341
  1455.7 154.4 %collective-permute-start.36 = (bf16[1,2816,256]{2,1,0:T(8,128)(2,1)S(1)}, bf16[1,2816,256]{2,1,0:T(8,128)(2,1)}, u32[]{:S(2)}, u32[]{:S(2)}) collective-permute-start(bf16[1,2816,256]{2,1,0:T(8,128)(2,1)S(1)} %copy-done.23), channel_id=1, source_target_pairs={{0,4},{4,0},{1,5},{5,1},{2,6},{6,2},{3,7},{7,3}} | collective-permute-start | bytes 4325384 | tf_op jit(solution)/shard_map/ppermute | solution.py:341
  1477.3 134.6 %collective-permute-start.15 = (bf16[2,640,256]{2,1,0:T(8,128)(2,1)}, bf16[2,640,256]{2,1,0:T(8,128)(2,1)S(1)}, u32[]{:S(2)}, u32[]{:S(2)}) collective-permute-start(bf16[2,640,256]{2,1,0:T(8,128)(2,1)} %get-tuple-element.93), channel_id=1, source_target_pairs={{0,1},{1,0},{2,3},{3,2},{4,5},{5,4},{6,7},{7,6}} | collective-permute-start | bytes 1966088 | tf_op jit(solution)/shard_map/ppermute | solution.py:337
  1519.3 208.0 %collective-permute-start.33 = (bf16[2,640,1024]{2,1,0:T(8,128)(2,1)}, bf16[2,640,1024]{2,1,0:T(8,128)(2,1)}, u32[]{:S(2)}, u32[]{:S(2)}) collective-permute-start(bf16[2,640,1024]{2,1,0:T(8,128)(2,1)} %get-tuple-element.110), channel_id=1, source_target_pairs={{0,1},{1,0},{2,3},{3,2},{4,5},{5,4},{6,7},{7,6}} | collective-permute-start | bytes 7864328 | tf_op jit(solution)/shard_map/ppermute | solution.py:337
  1519.8 209.2 %collective-permute-start.34 = (bf16[2,640,1024]{2,1,0:T(8,128)(2,1)}, bf16[2,640,1024]{2,1,0:T(8,128)(2,1)}, u32[]{:S(2)}, u32[]{:S(2)}) collective-permute-start(bf16[2,640,1024]{2,1,0:T(8,128)(2,1)} %get-tuple-element.111), channel_id=1, source_target_pairs={{0,2},{1,3},{2,0},{3,1},{4,6},{5,7},{6,4},{7,5}} | collective-permute-start | bytes 7864328 | tf_op jit(solution)/shard_map/ppermute | solution.py:337
  1610.2 33.6 %collective-permute-start.16 = (bf16[2,640,256]{2,1,0:T(8,128)(2,1)}, bf16[2,640,256]{2,1,0:T(8,128)(2,1)S(1)}, u32[]{:S(2)}, u32[]{:S(2)}) collective-permute-start(bf16[2,640,256]{2,1,0:T(8,128)(2,1)} %get-tuple-element.94), channel_id=1, source_target_pairs={{0,2},{1,3},{2,0},{3,1},{4,6},{5,7},{6,4},{7,5}} | collective-permute-start | bytes 1966088 | tf_op jit(solution)/shard_map/ppermute | solution.py:337
  1611.9 32.7 %collective-permute-start.17 = (bf16[2,640,256]{2,1,0:T(8,128)(2,1)}, bf16[2,640,256]{2,1,0:T(8,128)(2,1)}, u32[]{:S(2)}, u32[]{:S(2)}) collective-permute-start(bf16[2,640,256]{2,1,0:T(8,128)(2,1)} %get-tuple-element.95), channel_id=1, source_target_pairs={{0,3},{1,2},{2,1},{3,0},{4,7},{5,6},{6,5},{7,4}} | collective-permute-start | bytes 1966088 | tf_op jit(solution)/shard_map/ppermute | solution.py:337
  1611.9 138.0 %collective-permute-start.35 = (bf16[2,640,1024]{2,1,0:T(8,128)(2,1)}, bf16[2,640,1024]{2,1,0:T(8,128)(2,1)}, u32[]{:S(2)}, u32[]{:S(2)}) collective-permute-start(bf16[2,640,1024]{2,1,0:T(8,128)(2,1)} %get-tuple-element.112), channel_id=1, source_target_pairs={{0,3},{1,2},{2,1},{3,0},{4,7},{5,6},{6,5},{7,4}} | collective-permute-start | bytes 7864328 | tf_op jit(solution)/shard_map/ppermute | solution.py:337
  1644.6 25.5 %collective-permute-start.25 = (bf16[2,640,512]{2,1,0:T(8,128)(2,1)}, bf16[2,640,512]{2,1,0:T(8,128)(2,1)S(1)}, u32[]{:S(2)}, u32[]{:S(2)}) collective-permute-start(bf16[2,640,512]{2,1,0:T(8,128)(2,1)} %get-tuple-element.102), channel_id=1, source_target_pairs={{0,1},{1,0},{2,3},{3,2},{4,5},{5,4},{6,7},{7,6}} | collective-permute-start | bytes 3932168 | tf_op jit(solution)/shard_map/ppermute | solution.py:337
  1644.6 81.7 %collective-permute-start.26 = (bf16[2,640,512]{2,1,0:T(8,128)(2,1)}, bf16[2,640,512]{2,1,0:T(8,128)(2,1)S(1)}, u32[]{:S(2)}, u32[]{:S(2)}) collective-permute-start(bf16[2,640,512]{2,1,0:T(8,128)(2,1)} %get-tuple-element.103), channel_id=1, source_target_pairs={{0,2},{1,3},{2,0},{3,1},{4,6},{5,7},{6,4},{7,5}} | collective-permute-start | bytes 3932168 | tf_op jit(solution)/shard_map/ppermute | solution.py:337
  1670.1 153.8 %collective-permute-start.27 = (bf16[2,640,512]{2,1,0:T(8,128)(2,1)}, bf16[2,640,512]{2,1,0:T(8,128)(2,1)}, u32[]{:S(2)}, u32[]{:S(2)}) collective-permute-start(bf16[2,640,512]{2,1,0:T(8,128)(2,1)} %get-tuple-element.104), channel_id=1, source_target_pairs={{0,3},{1,2},{2,1},{3,0},{4,7},{5,6},{6,5},{7,4}} | collective-permute-start | bytes 3932168 | tf_op jit(solution)/shard_map/ppermute | solution.py:337
  1727.3 45.2 %collective-permute-start.29 = (bf16[2,640,512]{2,1,0:T(8,128)(2,1)}, bf16[2,640,512]{2,1,0:T(8,128)(2,1)}, u32[]{:S(2)}, u32[]{:S(2)}) collective-permute-start(bf16[2,640,512]{2,1,0:T(8,128)(2,1)} %get-tuple-element.106), channel_id=1, source_target_pairs={{0,1},{1,0},{2,3},{3,2},{4,5},{5,4},{6,7},{7,6}} | collective-permute-start | bytes 3932168 | tf_op jit(solution)/shard_map/ppermute | solution.py:337
  1727.4 55.2 %collective-permute-start.30 = (bf16[2,640,512]{2,1,0:T(8,128)(2,1)}, bf16[2,640,512]{2,1,0:T(8,128)(2,1)}, u32[]{:S(2)}, u32[]{:S(2)}) collective-permute-start(bf16[2,640,512]{2,1,0:T(8,128)(2,1)} %get-tuple-element.107), channel_id=1, source_target_pairs={{0,2},{1,3},{2,0},{3,1},{4,6},{5,7},{6,4},{7,5}} | collective-permute-start | bytes 3932168 | tf_op jit(solution)/shard_map/ppermute | solution.py:337
  1729.1 80.8 %collective-permute-start.31 = (bf16[2,640,512]{2,1,0:T(8,128)(2,1)}, bf16[2,640,512]{2,1,0:T(8,128)(2,1)}, u32[]{:S(2)}, u32[]{:S(2)}) collective-permute-start(bf16[2,640,512]{2,1,0:T(8,128)(2,1)} %get-tuple-element.108), channel_id=1, source_target_pairs={{0,3},{1,2},{2,1},{3,0},{4,7},{5,6},{6,5},{7,4}} | collective-permute-start | bytes 3932168 | tf_op jit(solution)/shard_map/ppermute | solution.py:337
  1749.9 103.7 %collective-permute-start.8 = (bf16[1,2816,256]{2,1,0:T(8,128)(2,1)}, bf16[1,2816,256]{2,1,0:T(8,128)(2,1)}, u32[]{:S(2)}, u32[]{:S(2)}) collective-permute-start(bf16[1,2816,256]{2,1,0:T(8,128)(2,1)} %get-tuple-element.175), channel_id=1, source_target_pairs={{0,4},{4,0},{1,5},{5,1},{2,6},{6,2},{3,7},{7,3}} | collective-permute-start | bytes 4325384 | tf_op jit(solution)/shard_map/ppermute | solution.py:341
  1753.4 56.5 %copy-start.40 = (bf16[2,640,256]{2,1,0:T(8,128)(2,1)S(1)}, bf16[2,640,256]{2,1,0:T(8,128)(2,1)}, u32[]{:S(2)}) copy-start(bf16[2,640,256]{2,1,0:T(8,128)(2,1)} %get-tuple-element.100) | copy-start | bytes 1966084
  1753.4 58.4 %copy-start.12 = (bf16[2,640,512]{2,1,0:T(8,128)(2,1)S(1)}, bf16[2,640,512]{2,1,0:T(8,128)(2,1)}, u32[]{:S(2)}) copy-start(bf16[2,640,512]{2,1,0:T(8,128)(2,1)} %get-tuple-element.105.refs_0_) | copy-start | bytes 3932164
  1772.5 63.7 %collective-permute-start.19 = (bf16[2,640,256]{2,1,0:T(8,128)(2,1)}, bf16[2,640,256]{2,1,0:T(8,128)(2,1)S(1)}, u32[]{:S(2)}, u32[]{:S(2)}) collective-permute-start(bf16[2,640,256]{2,1,0:T(8,128)(2,1)} %get-tuple-element.98), channel_id=1, source_target_pairs={{0,1},{1,0},{2,3},{3,2},{4,5},{5,4},{6,7},{7,6}} | collective-permute-start | bytes 1966088 | tf_op jit(solution)/shard_map/ppermute | solution.py:337
  1782.6 54.2 %collective-permute-start.20 = (bf16[2,640,256]{2,1,0:T(8,128)(2,1)S(1)}, bf16[2,640,256]{2,1,0:T(8,128)(2,1)S(1)}, u32[]{:S(2)}, u32[]{:S(2)}) collective-permute-start(bf16[2,640,256]{2,1,0:T(8,128)(2,1)S(1)} %copy-done.41), channel_id=1, source_target_pairs={{0,2},{1,3},{2,0},{3,1},{4,6},{5,7},{6,4},{7,5}} | collective-permute-start | bytes 1966088 | tf_op jit(solution)/shard_map/ppermute | solution.py:337
  1809.9 28.4 %collective-permute-start.21 = (bf16[2,640,256]{2,1,0:T(8,128)(2,1)S(1)}, bf16[2,640,256]{2,1,0:T(8,128)(2,1)S(1)}, u32[]{:S(2)}, u32[]{:S(2)}) collective-permute-start(bf16[2,640,256]{2,1,0:T(8,128)(2,1)S(1)} %copy-done.40), channel_id=1, source_target_pairs={{0,3},{1,2},{2,1},{3,0},{4,7},{5,6},{6,5},{7,4}} | collective-permute-start | bytes 1966088 | tf_op jit(solution)/shard_map/ppermute | solution.py:337
  1823.9 41.9 %collective-permute-start.7 = (bf16[1,2816,256]{2,1,0:T(8,128)(2,1)}, bf16[1,2816,256]{2,1,0:T(8,128)(2,1)}, u32[]{:S(2)}, u32[]{:S(2)}) collective-permute-start(bf16[1,2816,256]{2,1,0:T(8,128)(2,1)} %get-tuple-element.176), channel_id=1, source_target_pairs={{0,4},{4,0},{1,5},{5,1},{2,6},{6,2},{3,7},{7,3}} | collective-permute-start | bytes 4325384 | tf_op jit(solution)/shard_map/ppermute | solution.py:341
  1836.3 60.6 %collective-permute-start.40 = (bf16[1,2816,256]{2,1,0:T(8,128)(2,1)}, bf16[1,2816,256]{2,1,0:T(8,128)(2,1)S(1)}, u32[]{:S(2)}, u32[]{:S(2)}) collective-permute-start(bf16[1,2816,256]{2,1,0:T(8,128)(2,1)} %get-tuple-element.171), channel_id=1, source_target_pairs={{0,4},{4,0},{1,5},{5,1},{2,6},{6,2},{3,7},{7,3}} | collective-permute-start | bytes 4325384 | tf_op jit(solution)/shard_map/ppermute | solution.py:341
  1836.8 90.2 %collective-permute-start.50 = (bf16[1,2816,256]{2,1,0:T(8,128)(2,1)}, bf16[1,2816,256]{2,1,0:T(8,128)(2,1)}, u32[]{:S(2)}, u32[]{:S(2)}) collective-permute-start(bf16[1,2816,256]{2,1,0:T(8,128)(2,1)} %get-tuple-element.170), channel_id=1, source_target_pairs={{0,4},{4,0},{1,5},{5,1},{2,6},{6,2},{3,7},{7,3}} | collective-permute-start | bytes 4325384 | tf_op jit(solution)/shard_map/ppermute | solution.py:341
  1838.3 27.9 %collective-permute-start.41 = (bf16[2,640,256]{2,1,0:T(8,128)(2,1)}, bf16[2,640,256]{2,1,0:T(8,128)(2,1)S(1)}, u32[]{:S(2)}, u32[]{:S(2)}) collective-permute-start(bf16[2,640,256]{2,1,0:T(8,128)(2,1)} %get-tuple-element.122), channel_id=1, source_target_pairs={{0,1},{1,0},{2,3},{3,2},{4,5},{5,4},{6,7},{7,6}} | collective-permute-start | bytes 1966088 | tf_op jit(solution)/shard_map/ppermute | solution.py:337
  1853.6 25.3 %collective-permute-start.42 = (bf16[2,640,256]{2,1,0:T(8,128)(2,1)}, bf16[2,640,256]{2,1,0:T(8,128)(2,1)S(1)}, u32[]{:S(2)}, u32[]{:S(2)}) collective-permute-start(bf16[2,640,256]{2,1,0:T(8,128)(2,1)} %get-tuple-element.123), channel_id=1, source_target_pairs={{0,2},{1,3},{2,0},{3,1},{4,6},{5,7},{6,4},{7,5}} | collective-permute-start | bytes 1966088 | tf_op jit(solution)/shard_map/ppermute | solution.py:337
  1865.8 17.5 collective-permute-start.43
  1866.2 38.5 %collective-permute-start.47 = (bf16[2,640,256]{2,1,0:T(8,128)(2,1)}, bf16[2,640,256]{2,1,0:T(8,128)(2,1)S(1)}, u32[]{:S(2)}, u32[]{:S(2)}) collective-permute-start(bf16[2,640,256]{2,1,0:T(8,128)(2,1)} %get-tuple-element.135), channel_id=1, source_target_pairs={{0,1},{1,0},{2,3},{3,2},{4,5},{5,4},{6,7},{7,6}} | collective-permute-start | bytes 1966088 | tf_op jit(solution)/shard_map/ppermute | solution.py:337
  1879.7 49.3 %collective-permute-start.37 = (bf16[2,640,256]{2,1,0:T(8,128)(2,1)}, bf16[2,640,256]{2,1,0:T(8,128)(2,1)S(1)}, u32[]{:S(2)}, u32[]{:S(2)}) collective-permute-start(bf16[2,640,256]{2,1,0:T(8,128)(2,1)} %get-tuple-element.118), channel_id=1, source_target_pairs={{0,1},{1,0},{2,3},{3,2},{4,5},{5,4},{6,7},{7,6}} | collective-permute-start | bytes 1966088 | tf_op jit(solution)/shard_map/ppermute | solution.py:337
  1883.3 28.6 %collective-permute-start.48 = (bf16[2,640,256]{2,1,0:T(8,128)(2,1)}, bf16[2,640,256]{2,1,0:T(8,128)(2,1)S(1)}, u32[]{:S(2)}, u32[]{:S(2)}) collective-permute-start(bf16[2,640,256]{2,1,0:T(8,128)(2,1)} %get-tuple-element.136), channel_id=1, source_target_pairs={{0,2},{1,3},{2,0},{3,1},{4,6},{5,7},{6,4},{7,5}} | collective-permute-start | bytes 1966088 | tf_op jit(solution)/shard_map/ppermute | solution.py:337
  1897.0 18.1 collective-permute-start.49
  1904.7 31.4 %collective-permute-start.38 = (bf16[2,640,256]{2,1,0:T(8,128)(2,1)}, bf16[2,640,256]{2,1,0:T(8,128)(2,1)S(1)}, u32[]{:S(2)}, u32[]{:S(2)}) collective-permute-start(bf16[2,640,256]{2,1,0:T(8,128)(2,1)} %get-tuple-element.119), channel_id=1, source_target_pairs={{0,2},{1,3},{2,0},{3,1},{4,6},{5,7},{6,4},{7,5}} | collective-permute-start | bytes 1966088 | tf_op jit(solution)/shard_map/ppermute | solution.py:337
  1911.9 32.5 %collective-permute-start.39 = (bf16[2,640,256]{2,1,0:T(8,128)(2,1)}, bf16[2,640,256]{2,1,0:T(8,128)(2,1)S(1)}, u32[]{:S(2)}, u32[]{:S(2)}) collective-permute-start(bf16[2,640,256]{2,1,0:T(8,128)(2,1)} %get-tuple-element.120), channel_id=1, source_target_pairs={{0,3},{1,2},{2,1},{3,0},{4,7},{5,6},{6,5},{7,4}} | collective-permute-start | bytes 1966088 | tf_op jit(solution)/shard_map/ppermute | solution.py:337
  1915.1 30.7 %collective-permute-start.44 = (bf16[2,640,256]{2,1,0:T(8,128)(2,1)}, bf16[2,640,256]{2,1,0:T(8,128)(2,1)}, u32[]{:S(2)}, u32[]{:S(2)}) collective-permute-start(bf16[2,640,256]{2,1,0:T(8,128)(2,1)} %get-tuple-element.131), channel_id=1, source_target_pairs={{0,1},{1,0},{2,3},{3,2},{4,5},{5,4},{6,7},{7,6}} | collective-permute-start | bytes 1966088 | tf_op jit(solution)/shard_map/ppermute | solution.py:337
  1927.0 30.5 %collective-permute-start.45 = (bf16[2,640,256]{2,1,0:T(8,128)(2,1)}, bf16[2,640,256]{2,1,0:T(8,128)(2,1)}, u32[]{:S(2)}, u32[]{:S(2)}) collective-permute-start(bf16[2,640,256]{2,1,0:T(8,128)(2,1)} %get-tuple-element.132), channel_id=1, source_target_pairs={{0,2},{1,3},{2,0},{3,1},{4,6},{5,7},{6,4},{7,5}} | collective-permute-start | bytes 1966088 | tf_op jit(solution)/shard_map/ppermute | solution.py:337
  1929.1 42.2 %collective-permute-start.46 = (bf16[2,640,256]{2,1,0:T(8,128)(2,1)}, bf16[2,640,256]{2,1,0:T(8,128)(2,1)}, u32[]{:S(2)}, u32[]{:S(2)}) collective-permute-start(bf16[2,640,256]{2,1,0:T(8,128)(2,1)} %get-tuple-element.133), channel_id=1, source_target_pairs={{0,3},{1,2},{2,1},{3,0},{4,7},{5,6},{6,5},{7,4}} | collective-permute-start | bytes 1966088 | tf_op jit(solution)/shard_map/ppermute | solution.py:337
  1936.2 51.2 %collective-permute-start.6 = (bf16[1,2816,128]{2,1,0:T(8,128)(2,1)S(1)}, bf16[1,2816,128]{2,1,0:T(8,128)(2,1)S(1)}, u32[]{:S(2)}, u32[]{:S(2)}) collective-permute-start(bf16[1,2816,128]{2,1,0:T(8,128)(2,1)S(1)} %copy-done.25), channel_id=1, source_target_pairs={{0,4},{4,0},{1,5},{5,1},{2,6},{6,2},{3,7},{7,3}} | collective-permute-start | bytes 2162696 | tf_op jit(solution)/shard_map/ppermute | solution.py:341
  1945.3 55.2 %collective-permute-start.54 = (bf16[1,2816,128]{2,1,0:T(8,128)(2,1)S(1)}, bf16[1,2816,128]{2,1,0:T(8,128)(2,1)S(1)}, u32[]{:S(2)}, u32[]{:S(2)}) collective-permute-start(bf16[1,2816,128]{2,1,0:T(8,128)(2,1)S(1)} %copy-done.24), channel_id=1, source_target_pairs={{0,4},{4,0},{1,5},{5,1},{2,6},{6,2},{3,7},{7,3}} | collective-permute-start | bytes 2162696 | tf_op jit(solution)/shard_map/ppermute | solution.py:341
  1945.7 69.3 %collective-permute-start.58 = (bf16[2,640,256]{2,1,0:T(8,128)(2,1)}, bf16[2,640,256]{2,1,0:T(8,128)(2,1)}, u32[]{:S(2)}, u32[]{:S(2)}) collective-permute-start(bf16[2,640,256]{2,1,0:T(8,128)(2,1)} %get-tuple-element.159), channel_id=1, source_target_pairs={{0,1},{1,0},{2,3},{3,2},{4,5},{5,4},{6,7},{7,6}} | collective-permute-start | bytes 1966088 | tf_op jit(solution)/shard_map/ppermute | solution.py:337
  1957.5 57.9 %collective-permute-start.59 = (bf16[2,640,256]{2,1,0:T(8,128)(2,1)}, bf16[2,640,256]{2,1,0:T(8,128)(2,1)}, u32[]{:S(2)}, u32[]{:S(2)}) collective-permute-start(bf16[2,640,256]{2,1,0:T(8,128)(2,1)} %get-tuple-element.160), channel_id=1, source_target_pairs={{0,2},{1,3},{2,0},{3,1},{4,6},{5,7},{6,4},{7,5}} | collective-permute-start | bytes 1966088 | tf_op jit(solution)/shard_map/ppermute | solution.py:337
  1971.2 45.0 %collective-permute-start.60 = (bf16[2,640,256]{2,1,0:T(8,128)(2,1)}, bf16[2,640,256]{2,1,0:T(8,128)(2,1)}, u32[]{:S(2)}, u32[]{:S(2)}) collective-permute-start(bf16[2,640,256]{2,1,0:T(8,128)(2,1)} %get-tuple-element.161), channel_id=1, source_target_pairs={{0,3},{1,2},{2,1},{3,0},{4,7},{5,6},{6,5},{7,4}} | collective-permute-start | bytes 1966088 | tf_op jit(solution)/shard_map/ppermute | solution.py:337
  2000.5 13.6 collective-permute-start.51
  2000.5 27.3 %collective-permute-start.52 = (bf16[2,640,128]{2,1,0:T(8,128)(2,1)}, bf16[2,640,128]{2,1,0:T(8,128)(2,1)S(1)}, u32[]{:S(2)}, u32[]{:S(2)}) collective-permute-start(bf16[2,640,128]{2,1,0:T(8,128)(2,1)} %get-tuple-element.150), channel_id=1, source_target_pairs={{0,2},{1,3},{2,0},{3,1},{4,6},{5,7},{6,4},{7,5}} | collective-permute-start | bytes 983048 | tf_op jit(solution)/shard_map/ppermute | solution.py:337
  2014.1 13.7 collective-permute-start.53
  2015.1 12.8 collective-permute-start.55
  2015.4 16.6 collective-permute-start.56
  2016.3 21.4 %collective-permute-start.57 = (bf16[2,640,128]{2,1,0:T(8,128)(2,1)}, bf16[2,640,128]{2,1,0:T(8,128)(2,1)S(1)}, u32[]{:S(2)}, u32[]{:S(2)}) collective-permute-start(bf16[2,640,128]{2,1,0:T(8,128)(2,1)} %get-tuple-element.157), channel_id=1, source_target_pairs={{0,3},{1,2},{2,1},{3,0},{4,7},{5,6},{6,5},{7,4}} | collective-permute-start | bytes 983048 | tf_op jit(solution)/shard_map/ppermute | solution.py:337
  (45 other events, 458.9 us)
